TPU v7x, 256 devices: a whole 4x4x8 slice. The times are simulated.
256 devices in a mesh: grp: 4 (over y), dev: 64 (over z, x, core).
Axes of the slice: x: 4, y: 4, z: 8, core: 2. Of those that a mesh axis runs over, the one named last changes fastest.
Arguments:
- pool_latent: bfloat16 [512, 256, 512], P(('grp', 'dev')), may hold values from -6 to 6
- pool_rope: bfloat16 [512, 64, 256], P(('grp', 'dev')), may hold values from -6 to 6
- q_nope: bfloat16 [1024, 16384], P(None, 'dev'), may hold values from -6 to 6
- q_rope: bfloat16 [1024, 8192], P(None, 'dev'), may hold values from -9 to 9
- w_uk: bfloat16 [512, 16384], P(None, 'dev'), may hold values from -0.25 to 0.25
- w_uv: bfloat16 [512, 16384], P(None, 'dev'), may hold values from -0.25 to 0.25
- w_o: bfloat16 [16384, 7168], P('dev'), may hold values from -0.046875 to 0.046875
- block_table: int32 [64, 8], replicated, may hold values from 0 to 511, as said below
- lengths: int32 [64], replicated, may hold values from 2 to 2048, as said below
- preempted: int32 [32], replicated, may hold values from 0 to 63, as said below
- assignment: int32 [32], replicated, may hold values from 0 to 3, as said below
Outputs:
- mixed: bfloat16 [1024, 7168], P('grp', 'dev')
Inputs may be any that keep to these rules, and one draw needn't show every extreme that they name: `preempted`: distinct slots. `assignment`: each group receives exactly 8 requests. `block_table`: every page number 0 to 511 appears exactly once in the table; page p lies on the device with index p // 2 along grp+dev, at position p % 2 there. For every group and every index along dev, exactly 1 of the pages listed for the slots of that group's requests lie on devices with that index along dev. `lengths`: in every draw all requests of one group hold more than (7) * 256 tokens.
All inputs are finite; a program needn't handle non-finite values.
Results may differ from a plain program's by a relative error of at most 0.015.
Values may be sent and summed in bfloat16 or wider, within the bound.
No kernel may reach another device: no remote copies, remote signals or barrier semaphores. Data moves between devices by JAX's collectives and lax.ppermute only.
A program may use at most 128 MiB of HBM per device.

v0:
```python
import functools
import math

import jax
import jax.numpy as jnp
from jax import lax
from jax.experimental import pallas as pl
from jax.experimental.pallas import tpu as pltpu
from jax.sharding import Mesh
from jax.sharding import PartitionSpec as P

DR = 64
DN = 128
DV = 128
NEG = -1e30
NZ, NX, NC = 8, 4, 2
NXC = NX * NC
DEV = ("z", "x", "c")
GRP_DEV = ("grp", "z", "x", "c")
XC = ("x", "c")
SMEM = pltpu.SMEM
VMEM = pltpu.VMEM
F32 = jnp.float32
BF16 = jnp.bfloat16
NT = (((1,), (1,)), ((), ()))


def spec(space):
    return pl.BlockSpec(memory_space=space)


SEND, PICK, PLACE, SPOT, RANK, VALID, MEMBER, COUNT, SPARE = 0, 4, 5, 6, 8, 16, 24, 32, 40
META = 41
TAIL = 16


def fill_table(meta, ids, table, lengths, preempted, assignment, *, groups, block, pages_dev):
    group, column = ids[0], ids[1]
    blocks = table.shape[0]
    columns = NZ * NXC
    me = group * columns + column
    place = column & (NXC - 1)
    plane = lax.shift_right_logical(column, NXC.bit_length() - 1)
    for i in range(SPARE):
        meta[i] = 0
    meta[PLACE] = place
    meta[SPOT] = lax.shift_right_logical(place, NC.bit_length() - 1)

    def one_request(i, carry):
        slot = preempted[i]
        owner = assignment[i]
        rank = meta[COUNT + owner]
        meta[COUNT + owner] = rank + 1
        ahead = SEND + ((owner - group) & (groups - 1))
        for b in range(blocks):
            page = table[b, slot]
            holder = lax.shift_right_logical(page, pages_dev.bit_length() - 1)
            meta[jnp.where(holder == me, ahead, SPARE)] = page & (pages_dev - 1)

        @pl.when(owner == group)
        def _():
            length = lengths[slot]
            meta[MEMBER + rank] = i
            for b in range(blocks):
                holder = lax.shift_right_logical(table[b, slot], pages_dev.bit_length() - 1)
                col = holder & (columns - 1)
                row = lax.shift_right_logical(holder, columns.bit_length() - 1)
                z = (lax.shift_right_logical(col, NXC.bit_length() - 1) - plane) & (NZ - 1)
                near = (col & (NXC - 1)) == place
                meta[jnp.where(near, RANK + z, SPARE)] = rank
                meta[jnp.where(near, VALID + z, SPARE)] = jnp.clip(length - b * block, 0, block)
                meta[jnp.where(col == column, PICK, SPARE)] = (group - row) & (groups - 1)

        return carry

    lax.fori_loop(0, preempted.shape[0], one_request, 0)


def prepare_kernel(ids, *refs, groups):
    tables_hbm, (latent_hbm, rope_hbm, q_nope, q_rope, w_uk, w_uv), rest = refs[:4], refs[4:10], refs[10:]
    meta, copies = rest[:2]
    outs = rest[2 : 2 + groups]
    table, lengths, preempted, assignment, latent, rope, sem, row_sem, table_sem, w_sem = rest[2 + groups :]
    tables = (table, lengths, preempted, assignment)
    pages_dev, block, _ = latent.shape
    half = rope.shape[1] // 2
    q_rows = q_nope.shape[0] // preempted.shape[0]
    depth = w_uk.shape[0]
    queries = copies.shape[1] - 4 * depth
    rows = queries // 3
    for_all = [
        pltpu.make_async_copy(
            w.at[:, pl.ds(h * DN, DN)],
            copies.at[k, pl.ds(queries + (2 * i + h) * depth, depth), :],
            w_sem.at[k, 2 * i + h],
        )
        for i, w in enumerate((w_uk, w_uv))
        for h in range(2)
        for k in range(copies.shape[0])
    ]
    loads = [
        pltpu.make_async_copy(latent_hbm, latent, sem.at[0]),
        pltpu.make_async_copy(rope_hbm, rope, sem.at[1]),
    ]
    first = [
        pltpu.make_async_copy(src, dst, table_sem.at[i])
        for i, (src, dst) in enumerate(zip(tables_hbm, tables))
    ]
    for load in first + loads + for_all:
        load.start()
    for load in first:
        load.wait()
    fill_table(
        meta, ids, table, lengths, preempted, assignment,
        groups=groups, block=block, pages_dev=pages_dev,
    )
    moves = []
    for r in range(rows // q_rows):
        start = pl.multiple_of(meta[MEMBER + r] * q_rows, q_rows)
        for j in range(3):
            source = q_rope if j == 2 else q_nope.at[:, pl.ds(j * DN, DN)]
            moves.append(
                pltpu.make_async_copy(
                    source.at[pl.ds(start, q_rows), :],
                    copies.at[0, pl.ds(j * rows + r * q_rows, q_rows), :],
                    row_sem.at[r, j],
                )
            )
    for move in moves:
        move.start()
    for load in loads:
        load.wait()
    for k, out in enumerate(outs):
        page = meta[SEND + k]
        out[:block, :] = latent[page]
        out[block:, :block] = rope[page, :half, :]
        out[block:, block:] = rope[page, half:, :]
    for move in moves:
        move.wait()
    for k in range(1, copies.shape[0]):
        copies[k, :queries, :] = copies[0, :queries, :]
    for load in for_all:
        load.wait()


def pick_kernel(meta, *rest):
    sources, (first, second) = rest[:-2], rest[-2:]
    half = first.shape[0]
    for k, source in enumerate(sources):

        @pl.when(meta[PICK] == k)
        def _():
            first[...] = source[:half, :]
            second[...] = source[half:, :]


def placed(near, far, s, meta):
    return (near, far)[s % NC].at[meta[SPOT] ^ (s // NC)]


def query_kernel(meta, near, far, out, got, sem):
    per_group = out.shape[0]
    pair = out.shape[1] // NXC
    q_rows = pair // 2
    width = out.shape[2] - 2 * DR
    rows = per_group * q_rows
    loads = [
        pltpu.make_async_copy(
            placed(near, far, s, meta).at[pl.ds(0, got.shape[1]), :], got.at[s], sem.at[s]
        )
        for s in range(NXC)
    ]
    for load in loads:
        load.start()
    lane = lax.broadcasted_iota(jnp.int32, (rows, 2 * DR), 1)
    for s in range(NXC):
        loads[s].wait()
        hi = got[s, 2 * rows : 3 * rows, :]
        for h in range(2):
            live = (lane >= h * DR) & (lane < (h + 1) * DR)
            tail = jnp.where(live, hi, jnp.zeros_like(hi))
            key = 3 * rows + h * width
            lat = lax.dot_general(
                got[s, h * rows : (h + 1) * rows, :],
                got[s, key : key + width, :],
                NT,
                preferred_element_type=F32,
            ).astype(BF16)
            lo = s * pair + h * q_rows
            out[:, lo : lo + q_rows, :width] = lat.reshape(per_group, q_rows, width)
            out[:, lo : lo + q_rows, width:] = tail.reshape(per_group, q_rows, 2 * DR)


def three_parts(x):
    high = x.astype(BF16).astype(F32)
    rest = x - high
    middle = rest.astype(BF16).astype(F32)
    return [high, middle, rest - middle]


def stored_stats(stats):
    rows = [p for s in stats for p in three_parts(s)]
    fill = jnp.zeros((TAIL - len(rows), rows[0].shape[1]), F32)
    return jnp.concatenate(rows + [fill], axis=0).astype(BF16)


def read_stats(tail):
    tail = tail.astype(F32)
    return [tail[3 * h : 3 * h + 1] + tail[3 * h + 1 : 3 * h + 2] + tail[3 * h + 2 : 3 * h + 3] for h in range(2)]


def attention_kernel(meta, query, *rest, scale):
    near, far, firsts, seconds = *rest[:2], rest[2 : 2 + NZ], rest[2 + NZ : -9]
    keep, send, acc, top, total, pages, w_uv, sem, w_sem = rest[-9:]
    per_group, heads_rows, width = acc.shape
    pair = heads_rows // NXC
    q_rows = pair // 2
    rows = per_group * q_rows
    block = pages.shape[1] * 8 // 9

    middle = NZ // 2
    split = pages.shape[1] // 2
    loads = [
        [
            pltpu.make_async_copy(firsts[z], pages.at[z, pl.ds(0, split), :], sem.at[z, 0]),
            pltpu.make_async_copy(seconds[z], pages.at[z, pl.ds(split, split), :], sem.at[z, 1]),
        ]
        for z in range(NZ)
    ]
    order = [0] + [z for k in range(1, middle) for z in (k, NZ - k)] + [middle]
    loads_w = [
        pltpu.make_async_copy(
            placed(near, far, s, meta).at[pl.ds(near.shape[1] - 2 * width, 2 * width), :],
            w_uv.at[s],
            w_sem.at[s],
        )
        for s in range(NXC)
    ]
    for load in [load for z in order for load in loads[z]] + loads_w:
        load.start()

    acc[...] = jnp.zeros_like(acc)
    top[...] = jnp.full_like(top, NEG)
    total[...] = jnp.zeros_like(total)

    for z in order:
        r = meta[RANK + z]
        valid = meta[VALID + z]
        for load in loads[z]:
            load.wait()

        @pl.when(valid > 0)
        def _():
            latent = pages[z, :block, :]
            tail = pages[z, block:, :]
            rope = jnp.concatenate([tail[:, :block], tail[:, block:]], axis=0)
            rope = jnp.concatenate([rope, rope], axis=0)
            q = query[r]
            score = lax.dot_general(q[:, :width], latent, NT, preferred_element_type=F32)
            score = score + jnp.dot(q[:, width:], rope, preferred_element_type=F32)
            token = lax.broadcasted_iota(jnp.int32, score.shape, 1)
            live = token < valid
            score = jnp.where(live, score * scale, NEG)
            old = top[r][:, :1]
            new = jnp.maximum(old, jnp.max(score, axis=1, keepdims=True))
            expo = jnp.where(live, jnp.exp(score - new), 0.0)
            fade = jnp.exp(old - new)
            top[r] = jnp.broadcast_to(new, top.shape[1:])
            total[r] = total[r] * fade + jnp.sum(expo, axis=1, keepdims=True)
            acc[r] = acc[r] * fade + jnp.dot(
                expo.astype(BF16), latent, preferred_element_type=F32
            )

    for s in range(NXC):
        out = keep if s % 2 == 0 else send
        loads_w[s].wait()
        stats = []
        for h in range(2):
            lo = s * pair + h * q_rows
            weight = total[:, lo : lo + q_rows, :].reshape(rows, total.shape[2])
            high = top[:, lo : lo + q_rows, :].reshape(rows, top.shape[2])
            value = acc[:, lo : lo + q_rows, :].reshape(rows, width)
            some = weight > 0.0
            safe = jnp.where(some, weight, 1.0)
            value = (value * (1.0 / safe)[:, :1]).astype(BF16)
            head = jnp.dot(value, w_uv[s, h * width : (h + 1) * width, :], preferred_element_type=F32)
            out[s // 2, :rows, h * DV : (h + 1) * DV] = head.astype(BF16)
            stat = jnp.where(some, high + jnp.log(safe), NEG)
            stats.append(stat.T[:1, :])
        out[s // 2, rows:, :] = stored_stats(stats)


def merge(parts, tails):
    rows = parts[0].shape[0]
    stats = [read_stats(t) for t in tails]
    high = [functools.reduce(jnp.maximum, [s[h] for s in stats]) for h in range(2)]
    shares = [[jnp.exp(s[h] - high[h]) for s in stats] for h in range(2)]
    whole = [functools.reduce(jnp.add, shares[h]) for h in range(2)]
    lines = [w / whole[h] for h in range(2) for w in shares[h]]
    fill = jnp.zeros((128 - len(lines), rows), F32)
    table = jnp.concatenate(lines + [fill], axis=0).T
    halves = []
    for h in range(2):
        sides = [p[:, h * DV : (h + 1) * DV].astype(F32) for p in parts]
        first = h * len(parts)
        halves.append(sum(table[:, first + i : first + i + 1] * p for i, p in enumerate(sides)))
    return halves, [high[h] + jnp.log(whole[h]) for h in range(2)]


def chip_kernel(keep, got, *outs):
    for k, out in enumerate(outs):
        rows = out.shape[0] - TAIL
        halves, stats = merge(
            [keep[k, :rows, :], got[k, :rows, :]], [keep[k, rows:, :], got[k, rows:, :]]
        )
        for h, half in enumerate(halves):
            out[:rows, h * DV : (h + 1) * DV] = half.astype(BF16)
        out[rows:, :] = stored_stats(stats)


def heads_kernel(*refs):
    parts, out = refs[:-1], refs[-1]
    rows = out.shape[0]
    halves, _ = merge([p[:rows, :] for p in parts], [p[rows:, :] for p in parts])
    for h, half in enumerate(halves):
        out[:, h * DV : (h + 1) * DV] = half.astype(BF16)


def columns_kernel(meta, w_hbm, mine, theirs, wide, tall, sem):
    load = pltpu.make_async_copy(w_hbm, wide, sem)
    load.start()
    load.wait()
    step = 256
    for i in range(wide.shape[1] // step):
        tall[i * step : (i + 1) * step, :] = wide[:, i * step : (i + 1) * step].T
    share = mine.shape[2]
    core = meta[PLACE] & (NC - 1)
    for x in range(NX):
        for z in range(NZ):
            at = ((z * NX + x) * NC) * share
            for c, (own, other) in enumerate(((mine, theirs), (theirs, mine))):

                @pl.when(core == c)
                def _():
                    own[x, z] = tall[at : at + share, :]
                    other[x, z] = tall[at + share : at + 2 * share, :]


def output_kernel(mine_hbm, theirs_hbm, near, far, out, mine, theirs, sem):
    loads = []
    for i, (src, dst) in enumerate(((mine_hbm, mine), (theirs_hbm, theirs))):
        for x in range(NX):
            loads.append(pltpu.make_async_copy(src.at[x], dst.at[x], sem.at[i, x]))
    for load in loads:
        load.start()
    share = mine.shape[2]
    for x in range(NX):
        loads[x].wait()
        loads[NX + x].wait()
        for z in range(0, NZ, 2):
            first = mine[x, z : z + 2].reshape(2 * share, -1)
            second = theirs[x, z : z + 2].reshape(2 * share, -1)
            mixed = lax.dot_general(first, near[...], NT, preferred_element_type=F32)
            mixed = mixed + lax.dot_general(second, far[...], NT, preferred_element_type=F32)
            out[x, z : z + 2] = mixed.astype(BF16).reshape(2, share, -1)


def after(x, *others):
    return lax.optimization_barrier((x, *others))[0]


def in_hbm(x):
    return pltpu.with_memory_space_constraint(x, pltpu.HBM)


def sent(x, axis, size, k):
    return lax.ppermute(x, axis, [(i, i ^ k) for i in range(size)])


def shifted(x, k):
    return lax.ppermute(x, "z", [(i, (i + k) % NZ) for i in range(NZ)])


def local(
    pool_latent,
    pool_rope,
    q_nope,
    q_rope,
    w_uk,
    w_uv,
    w_o,
    block_table,
    lengths,
    preempted,
    assignment,
):
    groups = lax.axis_size("grp")
    group = lax.axis_index("grp")
    column = lax.axis_index(DEV)
    place = lax.axis_index(XC)
    pages_dev, block, width = pool_latent.shape
    requests = preempted.shape[0]
    blocks = block_table.shape[1]
    per_group = requests // groups
    query_rows = q_nope.shape[0] // requests
    rows = per_group * query_rows
    pair = 2 * query_rows
    scale = 1.0 / math.sqrt(DN + DR)
    page_rows = block + DR // 2

    small = pltpu.CompilerParams(vmem_limit_bytes=16 << 20)
    ids = jnp.stack([group, column]).astype(jnp.int32)
    page_type = jax.ShapeDtypeStruct((page_rows, width), BF16)
    meta, copies, *packed = pl.pallas_call(
        functools.partial(prepare_kernel, groups=groups),
        out_shape=[
            jax.ShapeDtypeStruct((META,), jnp.int32),
            jax.ShapeDtypeStruct((NX, 3 * rows + 4 * width, DN), BF16),
        ]
        + [page_type] * groups,
        in_specs=[spec(SMEM)] + [spec(pltpu.HBM)] * 10,
        out_specs=[spec(SMEM)] + [spec(VMEM)] * (1 + groups),
        scratch_shapes=[
            SMEM(block_table.T.shape, jnp.int32),
            SMEM(lengths.shape, jnp.int32),
            SMEM(preempted.shape, jnp.int32),
            SMEM(assignment.shape, jnp.int32),
            VMEM(pool_latent.shape, BF16),
            VMEM(pool_rope.shape, BF16),
            pltpu.SemaphoreType.DMA((2,)),
            pltpu.SemaphoreType.DMA((per_group, 3)),
            pltpu.SemaphoreType.DMA((4,)),
            pltpu.SemaphoreType.DMA((NX, 4)),
        ],
        compiler_params=small,
        name="prepare",
    )(ids, *[in_hbm(a) for a in (block_table.T, lengths, preempted, assignment, pool_latent, pool_rope, q_nope, q_rope, w_uk, w_uv)])

    arrived = [packed[0]] + [
        lax.ppermute(packed[k], "grp", [(i, (i + k) % groups) for i in range(groups)])
        for k in range(1, groups)
    ]
    near_x = lax.all_to_all(copies, "x", split_axis=0, concat_axis=0)

    share = w_o.shape[1] // (NZ * NXC)
    column_type = jax.ShapeDtypeStruct((NX, NZ, share, w_o.shape[0]), BF16)
    mine, other = pl.pallas_call(
        columns_kernel,
        out_shape=[column_type] * 2,
        in_specs=[spec(SMEM), spec(pltpu.HBM)],
        out_specs=[spec(VMEM)] * 2,
        scratch_shapes=[
            VMEM(w_o.shape, BF16),
            VMEM(w_o.shape[::-1], BF16),
            pltpu.SemaphoreType.DMA,
        ],
        compiler_params=pltpu.CompilerParams(vmem_limit_bytes=24 << 20),
        name="columns",
    )(meta, in_hbm(w_o))
    arrived, mine, other = lax.optimization_barrier((arrived, mine, other))

    half_page = jax.ShapeDtypeStruct((page_rows // 2, width), BF16)
    halves = pl.pallas_call(
        pick_kernel,
        out_shape=[half_page] * 2,
        in_specs=[spec(SMEM)] + [spec(VMEM)] * groups,
        out_specs=[spec(VMEM)] * 2,
        compiler_params=small,
        name="pick",
    )(meta, *arrived)

    below, above = [halves], [halves]
    for k in range(1, NZ // 2):
        below.append([shifted(h, 1) for h in below[-1]])
        above.append([shifted(h, -1) for h in above[-1]])
    middle = [shifted(below[-1][0], 1), shifted(above[-1][1], -1)]
    pages = [halves] + above[1:] + [middle] + below[:0:-1]

    theirs = sent(after(other, above[2], below[2]), "c", NC, 1)
    far_x = sent(after(near_x, above[3], below[3]), "c", NC, 1)

    query = pl.pallas_call(
        query_kernel,
        out_shape=jax.ShapeDtypeStruct((per_group, NXC * pair, width + 2 * DR), BF16),
        in_specs=[spec(SMEM)] + [spec(pl.ANY)] * 2,
        out_specs=spec(VMEM),
        scratch_shapes=[
            VMEM((NXC, 3 * rows + 2 * width, DN), BF16),
            pltpu.SemaphoreType.DMA((NXC,)),
        ],
        compiler_params=small,
        name="query",
    )(meta, in_hbm(near_x), in_hbm(far_x))

    half_type = jax.ShapeDtypeStruct((NX, rows + TAIL, 2 * DV), BF16)
    keep, send = pl.pallas_call(
        functools.partial(attention_kernel, scale=scale),
        out_shape=[half_type, half_type],
        in_specs=[spec(SMEM), spec(VMEM)] + [spec(pl.ANY)] * (2 + 2 * NZ),
        out_specs=[spec(VMEM)] * 2,
        scratch_shapes=[
            VMEM((per_group, NXC * pair, width), F32),
            VMEM((per_group, NXC * pair, 128), F32),
            VMEM((per_group, NXC * pair, 128), F32),
            VMEM((NZ, page_rows, width), BF16),
            VMEM((NXC, 2 * width, DV), BF16),
            pltpu.SemaphoreType.DMA((NZ, 2)),
            pltpu.SemaphoreType.DMA((NXC,)),
        ],
        compiler_params=pltpu.CompilerParams(vmem_limit_bytes=32 << 20),
        name="attention",
    )(meta, query, in_hbm(near_x), in_hbm(far_x), *[p[0] for p in pages], *[p[1] for p in pages])

    got = sent(send, "c", NC, 1)
    part_type = jax.ShapeDtypeStruct((rows + TAIL, 2 * DV), BF16)
    chip = pl.pallas_call(
        chip_kernel,
        out_shape=[part_type] * NX,
        in_specs=[spec(VMEM)] * 2,
        out_specs=[spec(VMEM)] * NX,
        compiler_params=small,
        name="chip",
    )(keep, got)
    heads = pl.pallas_call(
        heads_kernel,
        out_shape=jax.ShapeDtypeStruct((rows, 2 * DV), BF16),
        in_specs=[spec(VMEM)] * NX,
        out_specs=spec(VMEM),
        compiler_params=small,
        name="heads",
    )(chip[0], *[sent(chip[k], "x", NX, k) for k in range(1, NX)])
    mixed = pl.pallas_call(
        output_kernel,
        out_shape=jax.ShapeDtypeStruct((NX, NZ, share, rows), BF16),
        in_specs=[spec(pl.ANY)] * 2 + [spec(VMEM)] * 2,
        out_specs=spec(VMEM),
        scratch_shapes=[
            VMEM(mine.shape, BF16),
            VMEM(mine.shape, BF16),
            pltpu.SemaphoreType.DMA((2, NX)),
        ],
        compiler_params=small,
        name="output",
    )(in_hbm(mine), in_hbm(theirs), heads, sent(heads, "c", NC, 1))
    mixed = lax.all_to_all(mixed, "x", split_axis=0, concat_axis=0)
    mixed = mixed.astype(F32).sum(axis=0).astype(BF16)
    mixed = lax.all_to_all(mixed, "z", split_axis=0, concat_axis=0, tiled=True)
    mixed = mixed.reshape(NZ, -1, rows).astype(F32).sum(axis=0)
    return mixed.T.astype(BF16)


def solution(mesh):
    split = Mesh(mesh.devices.reshape(mesh.shape["grp"], NZ, NX, NC), GRP_DEV)
    return jax.shard_map(
        local,
        mesh=split,
        in_specs=(
            P(GRP_DEV, None, None),
            P(GRP_DEV, None, None),
            P(None, DEV),
            P(None, DEV),
            P(None, DEV),
            P(None, DEV),
            P(DEV, None),
            P(),
            P(),
            P(),
            P(),
        ),
        out_specs=P("grp", DEV),
        check_vma=False,
    )
```

profile of v0, /device:TPU:1, one launch (start us, length us, event | category | flops | bytes accessed | tf_op | source)
XLA Modules:
  0.0 153.7 jit_solution(867175671374258837)
XLA Ops:
  0.1 6.1 %prepare.1 = (s32[41]{0:T(128)S(1)}, bf16[4,2816,128]{2,1,0:T(8,128)(2,1)}, bf16[288,512]{1,0:T(8,128)(2,1)S(1)}, bf16[288,512]{1,0:T(8,128)(2,1)S(1)}, bf16[288...) custom-call(s32[2]{0:T(128)S(1)} %pad_add_fusion.ids, s32[8,64]{1,0:T(8,128)} %bitcast.4, s32[64]{0:T(128)} %refs_1_.1, ...), custom_call_target="tpu_custom_call" | custom-call | tf_op jit(solution)/shard_map/prepare/pallas_call | solution.py:414
  6.2 4.9 %all-to-all-start = ((bf16[4,2816,128]{2,1,0:T(8,128)(2,1)}), bf16[4,2816,128]{2,1,0:T(8,128)(2,1)}, u32[]{:S(2)}, u32[]{:S(2)}) async-start(bf16[4,2816,128]{2,1,0:T(8,128)(2,1)} %get-tuple-element.45), calls=%async_computation | async-start | bytes 5767168 | tf_op jit(solution)/shard_map/all_to_all | solution.py:443
  11.0 2.0 %collective-permute-start = (bf16[288,512]{1,0:T(8,128)(2,1)S(1)}, bf16[288,512]{1,0:T(8,128)(2,1)S(1)}, u32[]{:S(2)}, u32[]{:S(2)}) collective-permute-start(bf16[288,512]{1,0:T(8,128)(2,1)S(1)} %get-tuple-element.30), channel_id=1, source_target_pairs={{0,64},{64,128},{128,192},{192,0},{1,65},{65,129},{129,193},{193,1... | collective-permute-start | bytes 884744 | tf_op jit(solution)/shard_map/ppermute | solution.py:440
  13.0 2.6 %collective-permute-start.1 = (bf16[288,512]{1,0:T(8,128)(2,1)S(1)}, bf16[288,512]{1,0:T(8,128)(2,1)S(1)}, u32[]{:S(2)}, u32[]{:S(2)}) collective-permute-start(bf16[288,512]{1,0:T(8,128)(2,1)S(1)} %get-tuple-element.31), channel_id=1, source_target_pairs={{0,128},{64,192},{128,0},{192,64},{1,129},{65,193},{129,1},{193,65... | collective-permute-start | bytes 884744 | tf_op jit(solution)/shard_map/ppermute | solution.py:440
  15.6 1.1 collective-permute-start.2
  16.7 3.9 %columns.1 = (bf16[4,8,112,256]{3,2,1,0:T(8,128)(2,1)S(1)}, bf16[4,8,112,256]{3,2,1,0:T(8,128)(2,1)S(1)}) custom-call(s32[41]{0:T(128)S(1)} %get-tuple-element.33.meta, bf16[256,7168]{1,0:T(8,128)(2,1)} %w_hbm.1), custom_call_target="tpu_custom_call" | custom-call | tf_op jit(solution)/shard_map/columns/pallas_call | solution.py:447
  20.6 1.2 copy-done
  21.9 1.3 copy-done.1
  23.2 5.1 %collective-permute-done.1.rest_2_ = bf16[288,512]{1,0:T(8,128)(2,1)S(1)} collective-permute-done((bf16[288,512]{1,0:T(8,128)(2,1)S(1)}, bf16[288,512]{1,0:T(8,128)(2,1)S(1)}, u32[]{:S(2)}, u32[]{:S(2)}) %collective-permute-start.1) | collective-permute-done | bytes 294944 | tf_op jit(solution)/shard_map/ppermute | solution.py:440
  28.9 1.7 %collective-permute-start.7 = (bf16[144,512]{1,0:T(8,128)(2,1)S(1)}, bf16[144,512]{1,0:T(8,128)(2,1)S(1)}, u32[]{:S(2)}, u32[]{:S(2)}) collective-permute-start(bf16[144,512]{1,0:T(8,128)(2,1)S(1)} %get-tuple-element.42.rest_2_), channel_id=1, source_target_pairs={{0,8},{8,16},{16,24},{24,32},{32,40},{40,48},{48,56},{56,0},{1,9},... | collective-permute-start | bytes 442376 | tf_op jit(solution)/shard_map/ppermute | solution.py:381
  30.7 4.0 %collective-permute-start.3 = (bf16[144,512]{1,0:T(8,128)(2,1)S(1)}, bf16[144,512]{1,0:T(8,128)(2,1)S(1)}, u32[]{:S(2)}, u32[]{:S(2)}) collective-permute-start(bf16[144,512]{1,0:T(8,128)(2,1)S(1)} %get-tuple-element.42.rest_2_), channel_id=1, source_target_pairs={{0,56},{8,0},{16,8},{24,16},{32,24},{40,32},{48,40},{56,48},{1,57}... | collective-permute-start | bytes 442376 | tf_op jit(solution)/shard_map/ppermute | solution.py:381
  34.7 2.7 %collective-permute-start.5 = (bf16[144,512]{1,0:T(8,128)(2,1)S(1)}, bf16[144,512]{1,0:T(8,128)(2,1)S(1)}, u32[]{:S(2)}, u32[]{:S(2)}) collective-permute-start(bf16[144,512]{1,0:T(8,128)(2,1)S(1)} %get-tuple-element.43.rest_10_), channel_id=1, source_target_pairs={{0,56},{8,0},{16,8},{24,16},{32,24},{40,32},{48,40},{56,48},{1,57}... | collective-permute-start | bytes 442376 | tf_op jit(solution)/shard_map/ppermute | solution.py:381
  37.5 2.8 %collective-permute-start.4 = (bf16[144,512]{1,0:T(8,128)(2,1)S(1)}, bf16[144,512]{1,0:T(8,128)(2,1)S(1)}, u32[]{:S(2)}, u32[]{:S(2)}) collective-permute-start(bf16[144,512]{1,0:T(8,128)(2,1)S(1)} %collective-permute-done.3.rest_3_), channel_id=1, source_target_pairs={{0,56},{8,0},{16,8},{24,16},{32,24},{40,32},{48,40},{56,48},{1,57}... | collective-permute-start | bytes 442376 | tf_op jit(solution)/shard_map/ppermute | solution.py:381
  40.8 3.0 %collective-permute-start.6 = (bf16[144,512]{1,0:T(8,128)(2,1)S(1)}, bf16[144,512]{1,0:T(8,128)(2,1)S(1)}, u32[]{:S(2)}, u32[]{:S(2)}) collective-permute-start(bf16[144,512]{1,0:T(8,128)(2,1)S(1)} %collective-permute-done.5.rest_11_), channel_id=1, source_target_pairs={{0,56},{8,0},{16,8},{24,16},{32,24},{40,32},{48,40},{56,48},{1,57}... | collective-permute-start | bytes 442376 | tf_op jit(solution)/shard_map/ppermute | solution.py:381
  44.2 3.0 %collective-permute-start.12 = (bf16[144,512]{1,0:T(8,128)(2,1)S(1)}, bf16[144,512]{1,0:T(8,128)(2,1)S(1)}, u32[]{:S(2)}, u32[]{:S(2)}) collective-permute-start(bf16[144,512]{1,0:T(8,128)(2,1)S(1)} %collective-permute-done.4.rest_4_), channel_id=1, source_target_pairs={{0,56},{8,0},{16,8},{24,16},{32,24},{40,32},{48,40},{56,48},{1,57}... | collective-permute-start | bytes 442376 | tf_op jit(solution)/shard_map/ppermute | solution.py:381
  47.4 3.5 %collective-permute-start.13 = (bf16[144,512]{1,0:T(8,128)(2,1)S(1)}, bf16[144,512]{1,0:T(8,128)(2,1)S(1)}, u32[]{:S(2)}, u32[]{:S(2)}) collective-permute-start(bf16[144,512]{1,0:T(8,128)(2,1)S(1)} %collective-permute-done.6.rest_12_), channel_id=1, source_target_pairs={{0,56},{8,0},{16,8},{24,16},{32,24},{40,32},{48,40},{56,48},{1,57}... | collective-permute-start | bytes 442376 | tf_op jit(solution)/shard_map/ppermute | solution.py:381
  51.0 2.6 %collective-permute-done.15.rest_15_ = bf16[144,512]{1,0:T(8,128)(2,1)S(1)} collective-permute-done((bf16[144,512]{1,0:T(8,128)(2,1)S(1)}, bf16[144,512]{1,0:T(8,128)(2,1)S(1)}, u32[]{:S(2)}, u32[]{:S(2)}) %collective-permute-start.15) | collective-permute-done | bytes 147488 | tf_op jit(solution)/shard_map/ppermute | solution.py:381
  53.8 4.2 %collective-permute-start.16 = (bf16[4,2816,128]{2,1,0:T(8,128)(2,1)}, bf16[4,2816,128]{2,1,0:T(8,128)(2,1)S(1)}, u32[]{:S(2)}, u32[]{:S(2)}) collective-permute-start(bf16[4,2816,128]{2,1,0:T(8,128)(2,1)} %all-to-all-done.near.rest_0_), channel_id=1, source_target_pairs={{0,1},{1,0},{2,3},{3,2},{4,5},{5,4},{6,7},{7,6},{8,9},{9,8},{10,11... | collective-permute-start | bytes 8650760 | tf_op jit(solution)/shard_map/ppermute | solution.py:377
  58.1 2.9 %collective-permute-start.18 = (bf16[144,512]{1,0:T(8,128)(2,1)S(1)}, bf16[144,512]{1,0:T(8,128)(2,1)S(1)}, u32[]{:S(2)}, u32[]{:S(2)}) collective-permute-start(bf16[144,512]{1,0:T(8,128)(2,1)S(1)} %collective-permute-done.13.rest_13_), channel_id=1, source_target_pairs={{0,56},{8,0},{16,8},{24,16},{32,24},{40,32},{48,40},{56,48},{1,57}... | collective-permute-start | bytes 442376 | tf_op jit(solution)/shard_map/ppermute | solution.py:381
  61.0 2.2 %collective-permute-done.16.far.rest_1_ = bf16[4,2816,128]{2,1,0:T(8,128)(2,1)S(1)} collective-permute-done((bf16[4,2816,128]{2,1,0:T(8,128)(2,1)}, bf16[4,2816,128]{2,1,0:T(8,128)(2,1)S(1)}, u32[]{:S(2)}, u32[]{:S(2)}) %collective-permute-start.16) | collective-permute-done | bytes 2883616 | tf_op jit(solution)/shard_map/ppermute | solution.py:377
  63.1 1.6 %copy-done.2 = bf16[4,2816,128]{2,1,0:T(8,128)(2,1)} copy-done((bf16[4,2816,128]{2,1,0:T(8,128)(2,1)}, bf16[4,2816,128]{2,1,0:T(8,128)(2,1)S(1)}, u32[]{:S(2)}) %copy-start.2) | copy-done | bytes 2883608
  64.7 4.2 %query.1 = bf16[8,512,640]{2,1,0:T(8,128)(2,1)S(1)} custom-call(s32[41]{0:T(128)S(1)} %get-tuple-element.33.meta, bf16[4,2816,128]{2,1,0:T(8,128)(2,1)} %all-to-all-done.near.rest_0_, bf16[4,2816,128]{2,1,0:T(8,128)(2,1)} %copy-done.2), custom_call_target="tpu_custom_call" | custom-call | tf_op jit(solution)/shard_map/query/pallas_call | solution.py:482
  68.9 15.7 %attention.1 = (bf16[4,272,256]{2,1,0:T(8,128)(2,1)S(1)}, bf16[4,272,256]{2,1,0:T(8,128)(2,1)S(1)}) custom-call(s32[41]{0:T(128)S(1)} %get-tuple-element.33.meta, bf16[8,512,640]{2,1,0:T(8,128)(2,1)S(1)} %query.1, bf16[4,2816,128]{2,1,0:T(8,128)(2,1)} %all-to-all-done.near.rest_0_, bf16[4,2816,128]{2,1,0:T(8,128)(2,1)} %copy-done.2, ...), custom_call_target="tpu_custom_call" | custom-call | tf_op jit(solution)/shard_map/attention/pallas_call | solution.py:496
  84.6 1.6 %collective-permute-start.19 = (bf16[4,272,256]{2,1,0:T(8,128)(2,1)S(1)}, bf16[4,272,256]{2,1,0:T(8,128)(2,1)S(1)}, u32[]{:S(2)}, u32[]{:S(2)}) collective-permute-start(bf16[4,272,256]{2,1,0:T(8,128)(2,1)S(1)} %get-tuple-element.48), channel_id=1, source_target_pairs={{0,1},{1,0},{2,3},{3,2},{4,5},{5,4},{6,7},{7,6},{8,9},{9,8},{10,11... | collective-permute-start | bytes 1671176 | tf_op jit(solution)/shard_map/ppermute | solution.py:377
  86.1 1.6 %collective-permute-done.19.got = bf16[4,272,256]{2,1,0:T(8,128)(2,1)S(1)} collective-permute-done((bf16[4,272,256]{2,1,0:T(8,128)(2,1)S(1)}, bf16[4,272,256]{2,1,0:T(8,128)(2,1)S(1)}, u32[]{:S(2)}, u32[]{:S(2)}) %collective-permute-start.19) | collective-permute-done | bytes 557088 | tf_op jit(solution)/shard_map/ppermute | solution.py:377
  88.8 3.7 %collective-permute-start.22 = (bf16[272,256]{1,0:T(8,128)(2,1)S(1)}, bf16[272,256]{1,0:T(8,128)(2,1)S(1)}, u32[]{:S(2)}, u32[]{:S(2)}) collective-permute-start(bf16[272,256]{1,0:T(8,128)(2,1)S(1)} %get-tuple-element.52), channel_id=1, source_target_pairs={{0,6},{2,4},{4,2},{6,0},{1,7},{3,5},{5,3},{7,1},{8,14},{10,12},{12... | collective-permute-start | bytes 417800 | tf_op jit(solution)/shard_map/ppermute | solution.py:377
  92.6 1.0 collective-permute-done.20.refs_1_
  93.6 1.3 collective-permute-done.21.refs_2_
  94.9 4.0 %collective-permute-done.22.refs_3_ = bf16[272,256]{1,0:T(8,128)(2,1)S(1)} collective-permute-done((bf16[272,256]{1,0:T(8,128)(2,1)S(1)}, bf16[272,256]{1,0:T(8,128)(2,1)S(1)}, u32[]{:S(2)}, u32[]{:S(2)}) %collective-permute-start.22) | collective-permute-done | bytes 139296 | tf_op jit(solution)/shard_map/ppermute | solution.py:377
  101.3 3.6 %output.1 = bf16[4,8,112,256]{3,2,1,0:T(8,128)(2,1)S(1)} custom-call(bf16[4,8,112,256]{3,2,1,0:T(8,128)(2,1)} %copy-done, bf16[4,8,112,256]{3,2,1,0:T(8,128)(2,1)} %copy-done.3, bf16[256,256]{1,0:T(8,128)(2,1)S(1)} %heads.1.near, bf16[256,256]{1,0:T(8,128)(2,1)S(1)} %collective-permute-done.23.far), custom_call_target="tpu_custom_call" | custom-call | tf_op jit(solution)/shard_map/output/pallas_call | solution.py:532
  104.9 27.6 %all_to_all.15 = bf16[4,8,112,256]{3,2,1,0:T(8,128)(2,1)S(1)} all-to-all(bf16[4,8,112,256]{3,2,1,0:T(8,128)(2,1)S(1)} %output.1), channel_id=1, replica_groups=mesh['grp'=4,'z'=8,'x'=4,'c'=2] {'x'}, dimensions={0} | all-to-all | bytes 3670016 | tf_op jit(solution)/shard_map/all_to_all | solution.py:545
  133.0 20.0 %all_to_all.16 = bf16[8,112,256]{2,1,0:T(8,128)(2,1)S(1)} all-to-all(bf16[8,112,256]{2,1,0:T(8,128)(2,1)S(1)} %reduce_sum.24), channel_id=1, replica_groups=mesh['grp'=4,'z'=8,'x'=4,'c'=2] {'z'}, dimensions={0} | all-to-all | bytes 917504 | tf_op jit(solution)/shard_map/all_to_all | solution.py:547
  (39 shorter events, 6.9 us)
Async XLA Ops:
  6.2 47.6 %all-to-all-start = ((bf16[4,2816,128]{2,1,0:T(8,128)(2,1)}), bf16[4,2816,128]{2,1,0:T(8,128)(2,1)}, u32[]{:S(2)}, u32[]{:S(2)}) async-start(bf16[4,2816,128]{2,1,0:T(8,128)(2,1)} %get-tuple-element.45), calls=%async_computation | async-start | bytes 5767168 | tf_op jit(solution)/shard_map/all_to_all | solution.py:443
  11.0 12.2 %collective-permute-start = (bf16[288,512]{1,0:T(8,128)(2,1)S(1)}, bf16[288,512]{1,0:T(8,128)(2,1)S(1)}, u32[]{:S(2)}, u32[]{:S(2)}) collective-permute-start(bf16[288,512]{1,0:T(8,128)(2,1)S(1)} %get-tuple-element.30), channel_id=1, source_target_pairs={{0,64},{64,128},{128,192},{192,0},{1,65},{65,129},{129,193},{193,1... | collective-permute-start | bytes 884744 | tf_op jit(solution)/shard_map/ppermute | solution.py:440
  13.0 15.4 %collective-permute-start.1 = (bf16[288,512]{1,0:T(8,128)(2,1)S(1)}, bf16[288,512]{1,0:T(8,128)(2,1)S(1)}, u32[]{:S(2)}, u32[]{:S(2)}) collective-permute-start(bf16[288,512]{1,0:T(8,128)(2,1)S(1)} %get-tuple-element.31), channel_id=1, source_target_pairs={{0,128},{64,192},{128,0},{192,64},{1,129},{65,193},{129,1},{193,65... | collective-permute-start | bytes 884744 | tf_op jit(solution)/shard_map/ppermute | solution.py:440
  15.6 12.7 %collective-permute-start.2 = (bf16[288,512]{1,0:T(8,128)(2,1)S(1)}, bf16[288,512]{1,0:T(8,128)(2,1)S(1)}, u32[]{:S(2)}, u32[]{:S(2)}) collective-permute-start(bf16[288,512]{1,0:T(8,128)(2,1)S(1)} %get-tuple-element.32), channel_id=1, source_target_pairs={{0,192},{64,0},{128,64},{192,128},{1,193},{65,1},{129,65},{193,129... | collective-permute-start | bytes 884744 | tf_op jit(solution)/shard_map/ppermute | solution.py:440
  20.6 1.2 copy-start
  21.9 1.3 copy-start.1
  28.9 8.6 %collective-permute-start.7 = (bf16[144,512]{1,0:T(8,128)(2,1)S(1)}, bf16[144,512]{1,0:T(8,128)(2,1)S(1)}, u32[]{:S(2)}, u32[]{:S(2)}) collective-permute-start(bf16[144,512]{1,0:T(8,128)(2,1)S(1)} %get-tuple-element.42.rest_2_), channel_id=1, source_target_pairs={{0,8},{8,16},{16,24},{24,32},{32,40},{40,48},{48,56},{56,0},{1,9},... | collective-permute-start | bytes 442376 | tf_op jit(solution)/shard_map/ppermute | solution.py:381
  30.7 6.9 %collective-permute-start.3 = (bf16[144,512]{1,0:T(8,128)(2,1)S(1)}, bf16[144,512]{1,0:T(8,128)(2,1)S(1)}, u32[]{:S(2)}, u32[]{:S(2)}) collective-permute-start(bf16[144,512]{1,0:T(8,128)(2,1)S(1)} %get-tuple-element.42.rest_2_), channel_id=1, source_target_pairs={{0,56},{8,0},{16,8},{24,16},{32,24},{40,32},{48,40},{56,48},{1,57}... | collective-permute-start | bytes 442376 | tf_op jit(solution)/shard_map/ppermute | solution.py:381
  34.7 6.2 %collective-permute-start.9 = (bf16[144,512]{1,0:T(8,128)(2,1)S(1)}, bf16[144,512]{1,0:T(8,128)(2,1)S(1)}, u32[]{:S(2)}, u32[]{:S(2)}) collective-permute-start(bf16[144,512]{1,0:T(8,128)(2,1)S(1)} %get-tuple-element.43.rest_10_), channel_id=1, source_target_pairs={{0,8},{8,16},{16,24},{24,32},{32,40},{40,48},{48,56},{56,0},{1,9},... | collective-permute-start | bytes 442376 | tf_op jit(solution)/shard_map/ppermute | solution.py:381
  34.7 6.2 %collective-permute-start.5 = (bf16[144,512]{1,0:T(8,128)(2,1)S(1)}, bf16[144,512]{1,0:T(8,128)(2,1)S(1)}, u32[]{:S(2)}, u32[]{:S(2)}) collective-permute-start(bf16[144,512]{1,0:T(8,128)(2,1)S(1)} %get-tuple-element.43.rest_10_), channel_id=1, source_target_pairs={{0,56},{8,0},{16,8},{24,16},{32,24},{40,32},{48,40},{56,48},{1,57}... | collective-permute-start | bytes 442376 | tf_op jit(solution)/shard_map/ppermute | solution.py:381
  37.5 6.6 %collective-permute-start.8 = (bf16[144,512]{1,0:T(8,128)(2,1)S(1)}, bf16[144,512]{1,0:T(8,128)(2,1)S(1)}, u32[]{:S(2)}, u32[]{:S(2)}) collective-permute-start(bf16[144,512]{1,0:T(8,128)(2,1)S(1)} %collective-permute-done.7.rest_9_), channel_id=1, source_target_pairs={{0,8},{8,16},{16,24},{24,32},{32,40},{40,48},{48,56},{56,0},{1,9},... | collective-permute-start | bytes 442376 | tf_op jit(solution)/shard_map/ppermute | solution.py:381
  37.5 6.6 %collective-permute-start.4 = (bf16[144,512]{1,0:T(8,128)(2,1)S(1)}, bf16[144,512]{1,0:T(8,128)(2,1)S(1)}, u32[]{:S(2)}, u32[]{:S(2)}) collective-permute-start(bf16[144,512]{1,0:T(8,128)(2,1)S(1)} %collective-permute-done.3.rest_3_), channel_id=1, source_target_pairs={{0,56},{8,0},{16,8},{24,16},{32,24},{40,32},{48,40},{56,48},{1,57}... | collective-permute-start | bytes 442376 | tf_op jit(solution)/shard_map/ppermute | solution.py:381
  40.8 6.5 %collective-permute-start.10 = (bf16[144,512]{1,0:T(8,128)(2,1)S(1)}, bf16[144,512]{1,0:T(8,128)(2,1)S(1)}, u32[]{:S(2)}, u32[]{:S(2)}) collective-permute-start(bf16[144,512]{1,0:T(8,128)(2,1)S(1)} %collective-permute-done.9.rest_17_), channel_id=1, source_target_pairs={{0,8},{8,16},{16,24},{24,32},{32,40},{40,48},{48,56},{56,0},{1,9},... | collective-permute-start | bytes 442376 | tf_op jit(solution)/shard_map/ppermute | solution.py:381
  40.8 6.6 %collective-permute-start.6 = (bf16[144,512]{1,0:T(8,128)(2,1)S(1)}, bf16[144,512]{1,0:T(8,128)(2,1)S(1)}, u32[]{:S(2)}, u32[]{:S(2)}) collective-permute-start(bf16[144,512]{1,0:T(8,128)(2,1)S(1)} %collective-permute-done.5.rest_11_), channel_id=1, source_target_pairs={{0,56},{8,0},{16,8},{24,16},{32,24},{40,32},{48,40},{56,48},{1,57}... | collective-permute-start | bytes 442376 | tf_op jit(solution)/shard_map/ppermute | solution.py:381
  44.2 6.8 %collective-permute-start.14 = (bf16[144,512]{1,0:T(8,128)(2,1)S(1)}, bf16[144,512]{1,0:T(8,128)(2,1)S(1)}, u32[]{:S(2)}, u32[]{:S(2)}) collective-permute-start(bf16[144,512]{1,0:T(8,128)(2,1)S(1)} %collective-permute-done.8.rest_8_), channel_id=1, source_target_pairs={{0,8},{8,16},{16,24},{24,32},{32,40},{40,48},{48,56},{56,0},{1,9},... | collective-permute-start | bytes 442376 | tf_op jit(solution)/shard_map/ppermute | solution.py:381
  44.2 6.8 %collective-permute-start.12 = (bf16[144,512]{1,0:T(8,128)(2,1)S(1)}, bf16[144,512]{1,0:T(8,128)(2,1)S(1)}, u32[]{:S(2)}, u32[]{:S(2)}) collective-permute-start(bf16[144,512]{1,0:T(8,128)(2,1)S(1)} %collective-permute-done.4.rest_4_), channel_id=1, source_target_pairs={{0,56},{8,0},{16,8},{24,16},{32,24},{40,32},{48,40},{56,48},{1,57}... | collective-permute-start | bytes 442376 | tf_op jit(solution)/shard_map/ppermute | solution.py:381
  47.3 6.2 %collective-permute-start.15 = (bf16[144,512]{1,0:T(8,128)(2,1)S(1)}, bf16[144,512]{1,0:T(8,128)(2,1)S(1)}, u32[]{:S(2)}, u32[]{:S(2)}) collective-permute-start(bf16[144,512]{1,0:T(8,128)(2,1)S(1)} %collective-permute-done.10.rest_16_), channel_id=1, source_target_pairs={{0,8},{8,16},{16,24},{24,32},{32,40},{40,48},{48,56},{56,0},{1,9},... | collective-permute-start | bytes 442376 | tf_op jit(solution)/shard_map/ppermute | solution.py:381
  47.4 6.3 %collective-permute-start.13 = (bf16[144,512]{1,0:T(8,128)(2,1)S(1)}, bf16[144,512]{1,0:T(8,128)(2,1)S(1)}, u32[]{:S(2)}, u32[]{:S(2)}) collective-permute-start(bf16[144,512]{1,0:T(8,128)(2,1)S(1)} %collective-permute-done.6.rest_12_), channel_id=1, source_target_pairs={{0,56},{8,0},{16,8},{24,16},{32,24},{40,32},{48,40},{56,48},{1,57}... | collective-permute-start | bytes 442376 | tf_op jit(solution)/shard_map/ppermute | solution.py:381
  53.8 9.4 %collective-permute-start.16 = (bf16[4,2816,128]{2,1,0:T(8,128)(2,1)}, bf16[4,2816,128]{2,1,0:T(8,128)(2,1)S(1)}, u32[]{:S(2)}, u32[]{:S(2)}) collective-permute-start(bf16[4,2816,128]{2,1,0:T(8,128)(2,1)} %all-to-all-done.near.rest_0_), channel_id=1, source_target_pairs={{0,1},{1,0},{2,3},{3,2},{4,5},{5,4},{6,7},{7,6},{8,9},{9,8},{10,11... | collective-permute-start | bytes 8650760 | tf_op jit(solution)/shard_map/ppermute | solution.py:377
  58.0 42.1 %collective-permute-start.11 = (bf16[4,8,112,256]{3,2,1,0:T(8,128)(2,1)}, bf16[4,8,112,256]{3,2,1,0:T(8,128)(2,1)S(1)}, u32[]{:S(2)}, u32[]{:S(2)}) collective-permute-start(bf16[4,8,112,256]{3,2,1,0:T(8,128)(2,1)} %copy-done.1), channel_id=1, source_target_pairs={{0,1},{1,0},{2,3},{3,2},{4,5},{5,4},{6,7},{7,6},{8,9},{9,8},{10,11... | collective-permute-start | bytes 5505032 | tf_op jit(solution)/shard_map/ppermute | solution.py:377
  58.1 10.8 %collective-permute-start.17 = (bf16[144,512]{1,0:T(8,128)(2,1)S(1)}, bf16[144,512]{1,0:T(8,128)(2,1)S(1)}, u32[]{:S(2)}, u32[]{:S(2)}) collective-permute-start(bf16[144,512]{1,0:T(8,128)(2,1)S(1)} %collective-permute-done.14.rest_7_), channel_id=1, source_target_pairs={{0,8},{8,16},{16,24},{24,32},{32,40},{40,48},{48,56},{56,0},{1,9},... | collective-permute-start | bytes 442376 | tf_op jit(solution)/shard_map/ppermute | solution.py:381
  58.1 10.8 %collective-permute-start.18 = (bf16[144,512]{1,0:T(8,128)(2,1)S(1)}, bf16[144,512]{1,0:T(8,128)(2,1)S(1)}, u32[]{:S(2)}, u32[]{:S(2)}) collective-permute-start(bf16[144,512]{1,0:T(8,128)(2,1)S(1)} %collective-permute-done.13.rest_13_), channel_id=1, source_target_pairs={{0,56},{8,0},{16,8},{24,16},{32,24},{40,32},{48,40},{56,48},{1,57}... | collective-permute-start | bytes 442376 | tf_op jit(solution)/shard_map/ppermute | solution.py:381
  63.1 1.6 %copy-start.2 = (bf16[4,2816,128]{2,1,0:T(8,128)(2,1)}, bf16[4,2816,128]{2,1,0:T(8,128)(2,1)S(1)}, u32[]{:S(2)}) copy-start(bf16[4,2816,128]{2,1,0:T(8,128)(2,1)S(1)} %collective-permute-done.16.far.rest_1_) | copy-start | bytes 8650756
  84.6 3.2 %collective-permute-start.19 = (bf16[4,272,256]{2,1,0:T(8,128)(2,1)S(1)}, bf16[4,272,256]{2,1,0:T(8,128)(2,1)S(1)}, u32[]{:S(2)}, u32[]{:S(2)}) collective-permute-start(bf16[4,272,256]{2,1,0:T(8,128)(2,1)S(1)} %get-tuple-element.48), channel_id=1, source_target_pairs={{0,1},{1,0},{2,3},{3,2},{4,5},{5,4},{6,7},{7,6},{8,9},{9,8},{10,11... | collective-permute-start | bytes 1671176 | tf_op jit(solution)/shard_map/ppermute | solution.py:377
  88.6 5.0 %collective-permute-start.20 = (bf16[272,256]{1,0:T(8,128)(2,1)S(1)}, bf16[272,256]{1,0:T(8,128)(2,1)S(1)}, u32[]{:S(2)}, u32[]{:S(2)}) collective-permute-start(bf16[272,256]{1,0:T(8,128)(2,1)S(1)} %get-tuple-element.50), channel_id=1, source_target_pairs={{0,2},{2,0},{4,6},{6,4},{1,3},{3,1},{5,7},{7,5},{8,10},{10,8},{12,... | collective-permute-start | bytes 417800 | tf_op jit(solution)/shard_map/ppermute | solution.py:377
  88.8 6.1 %collective-permute-start.21 = (bf16[272,256]{1,0:T(8,128)(2,1)S(1)}, bf16[272,256]{1,0:T(8,128)(2,1)S(1)}, u32[]{:S(2)}, u32[]{:S(2)}) collective-permute-start(bf16[272,256]{1,0:T(8,128)(2,1)S(1)} %get-tuple-element.51), channel_id=1, source_target_pairs={{0,4},{2,6},{4,0},{6,2},{1,5},{3,7},{5,1},{7,3},{8,12},{10,14},{12... | collective-permute-start | bytes 417800 | tf_op jit(solution)/shard_map/ppermute | solution.py:377
  88.8 10.1 %collective-permute-start.22 = (bf16[272,256]{1,0:T(8,128)(2,1)S(1)}, bf16[272,256]{1,0:T(8,128)(2,1)S(1)}, u32[]{:S(2)}, u32[]{:S(2)}) collective-permute-start(bf16[272,256]{1,0:T(8,128)(2,1)S(1)} %get-tuple-element.52), channel_id=1, source_target_pairs={{0,6},{2,4},{4,2},{6,0},{1,7},{3,5},{5,3},{7,1},{8,14},{10,12},{12... | collective-permute-start | bytes 417800 | tf_op jit(solution)/shard_map/ppermute | solution.py:377
  99.5 1.6 %collective-permute-start.23 = (bf16[256,256]{1,0:T(8,128)(2,1)S(1)}, bf16[256,256]{1,0:T(8,128)(2,1)S(1)}, u32[]{:S(2)}, u32[]{:S(2)}) collective-permute-start(bf16[256,256]{1,0:T(8,128)(2,1)S(1)} %heads.1.near), channel_id=1, source_target_pairs={{0,1},{1,0},{2,3},{3,2},{4,5},{5,4},{6,7},{7,6},{8,9},{9,8},{10,11... | collective-permute-start | bytes 393224 | tf_op jit(solution)/shard_map/ppermute | solution.py:377
  100.1 1.2 copy-start.3
where the time goes:
time: 156 us; the launch traced here: 154 us
  blocking collectives  47.6 us (31%)
  starting transfers between devices  44.5 us (29%)
  Pallas kernels  35.5 us (23%)
  waiting for transfers between devices  20.3 us (13%)
  local copies, waits for them, and re-layouts  4.41 us (3%)
    all_to_all x1, blocking collectives, local(): mixed = lax.all_to_all(mixed, 'x', split_axis=0, concat_axis=0)  27.6 us
    ppermute x14, starting transfers between devices, shifted(): return lax.ppermute(x, 'z', [(i, (i + k) % NZ) for i in range(NZ)])  23.6 us
    all_to_all x1, blocking collectives, local(): mixed = lax.all_to_all(mixed, 'z', split_axis=0, concat_axis=0, tiled=True)  20 us
    pallas_call x1, Pallas kernels, local(): pl.pallas_call(functools.partial(attention_kernel, scale=scale), out_shap...  15.7 us
    ppermute x7, waiting for transfers between devices, sent(): return lax.ppermute(x, axis, [(i, i ^ k) for i in range(size)])  11 us
    ppermute x7, starting transfers between devices, sent(): return lax.ppermute(x, axis, [(i, i ^ k) for i in range(size)])  10.4 us
    pallas_call x1, Pallas kernels, local(): pl.pallas_call(functools.partial(prepare_kernel, groups=groups), out_shap...  6.1 us
    ppermute x3, starting transfers between devices, local(): lax.ppermute(packed[k], 'grp', [(i, (i + k) % groups) for i in range(grou...  5.64 us
  transfers between devices with their start and end apart: 25, of which 14 were waited for; matrix products, arithmetic and copies ran while one was open for 0% of the time, Pallas kernels for 17%

commit v1 on v0

--- a/solution.py
+++ b/solution.py
@@ -326,43 +326,35 @@
         out[:, h * DV : (h + 1) * DV] = half.astype(BF16)
 
 
-def columns_kernel(meta, w_hbm, mine, theirs, wide, tall, sem):
+def columns_kernel(w_hbm, out, wide, tall, sem):
     load = pltpu.make_async_copy(w_hbm, wide, sem)
     load.start()
     load.wait()
     step = 256
     for i in range(wide.shape[1] // step):
         tall[i * step : (i + 1) * step, :] = wide[:, i * step : (i + 1) * step].T
-    share = mine.shape[2]
-    core = meta[PLACE] & (NC - 1)
-    for x in range(NX):
-        for z in range(NZ):
-            at = ((z * NX + x) * NC) * share
-            for c, (own, other) in enumerate(((mine, theirs), (theirs, mine))):
-
-                @pl.when(core == c)
-                def _():
-                    own[x, z] = tall[at : at + share, :]
-                    other[x, z] = tall[at + share : at + 2 * share, :]
-
-
-def output_kernel(mine_hbm, theirs_hbm, near, far, out, mine, theirs, sem):
-    loads = []
-    for i, (src, dst) in enumerate(((mine_hbm, mine), (theirs_hbm, theirs))):
-        for x in range(NX):
-            loads.append(pltpu.make_async_copy(src.at[x], dst.at[x], sem.at[i, x]))
+    share = out.shape[1] // NZ
+    for z in range(NZ):
+        for s in range(NXC):
+            at = (z * NXC + s) * share
+            out[s, z * share : (z + 1) * share, :] = tall[at : at + share, :]
+
+
+def output_kernel(meta, source, *refs):
+    near, far, out, weights, sem = refs[:NX], *refs[NX:]
+    loads = [
+        pltpu.make_async_copy(source.at[meta[PLACE] ^ s], weights.at[s], sem.at[s])
+        for s in range(NXC)
+    ]
     for load in loads:
         load.start()
-    share = mine.shape[2]
-    for x in range(NX):
-        loads[x].wait()
-        loads[NX + x].wait()
-        for z in range(0, NZ, 2):
-            first = mine[x, z : z + 2].reshape(2 * share, -1)
-            second = theirs[x, z : z + 2].reshape(2 * share, -1)
-            mixed = lax.dot_general(first, near[...], NT, preferred_element_type=F32)
-            mixed = mixed + lax.dot_general(second, far[...], NT, preferred_element_type=F32)
-            out[x, z : z + 2] = mixed.astype(BF16).reshape(2, share, -1)
+    mixed = None
+    for s, load in enumerate(loads):
+        heads = near[s // NC][...] if s % NC == 0 else far[s // NC]
+        load.wait()
+        term = lax.dot_general(weights[s], heads, NT, preferred_element_type=F32)
+        mixed = term if mixed is None else mixed + term
+    out[...] = mixed.astype(BF16)
 
 
 def after(x, *others):
@@ -443,12 +435,11 @@
     near_x = lax.all_to_all(copies, "x", split_axis=0, concat_axis=0)
 
     share = w_o.shape[1] // (NZ * NXC)
-    column_type = jax.ShapeDtypeStruct((NX, NZ, share, w_o.shape[0]), BF16)
-    mine, other = pl.pallas_call(
+    w_cols = pl.pallas_call(
         columns_kernel,
-        out_shape=[column_type] * 2,
-        in_specs=[spec(SMEM), spec(pltpu.HBM)],
-        out_specs=[spec(VMEM)] * 2,
+        out_shape=jax.ShapeDtypeStruct((NXC, NZ * share, w_o.shape[0]), BF16),
+        in_specs=[spec(pltpu.HBM)],
+        out_specs=spec(VMEM),
         scratch_shapes=[
             VMEM(w_o.shape, BF16),
             VMEM(w_o.shape[::-1], BF16),
@@ -456,8 +447,8 @@
         ],
         compiler_params=pltpu.CompilerParams(vmem_limit_bytes=24 << 20),
         name="columns",
-    )(meta, in_hbm(w_o))
-    arrived, mine, other = lax.optimization_barrier((arrived, mine, other))
+    )(in_hbm(after(w_o, packed[0])))
+    arrived, w_cols = lax.optimization_barrier((arrived, w_cols))
 
     half_page = jax.ShapeDtypeStruct((page_rows // 2, width), BF16)
     halves = pl.pallas_call(
@@ -476,8 +467,9 @@
     middle = [shifted(below[-1][0], 1), shifted(above[-1][1], -1)]
     pages = [halves] + above[1:] + [middle] + below[:0:-1]
 
-    theirs = sent(after(other, above[2], below[2]), "c", NC, 1)
-    far_x = sent(after(near_x, above[3], below[3]), "c", NC, 1)
+    far_x = sent(after(near_x, above[2], below[2]), "c", NC, 1)
+    w_cols = after(w_cols, near_x, above[3], below[3])
+    weights = lax.all_to_all(w_cols, XC, split_axis=0, concat_axis=0)
 
     query = pl.pallas_call(
         query_kernel,
@@ -529,21 +521,17 @@
         compiler_params=small,
         name="heads",
     )(chip[0], *[sent(chip[k], "x", NX, k) for k in range(1, NX)])
+    near = [heads] + [sent(heads, "x", NX, k) for k in range(1, NX)]
+    far = sent(jnp.stack(near), "c", NC, 1)
     mixed = pl.pallas_call(
         output_kernel,
-        out_shape=jax.ShapeDtypeStruct((NX, NZ, share, rows), BF16),
-        in_specs=[spec(pl.ANY)] * 2 + [spec(VMEM)] * 2,
+        out_shape=jax.ShapeDtypeStruct((NZ * share, rows), BF16),
+        in_specs=[spec(SMEM), spec(pl.ANY)] + [spec(VMEM)] * (NX + 1),
         out_specs=spec(VMEM),
-        scratch_shapes=[
-            VMEM(mine.shape, BF16),
-            VMEM(mine.shape, BF16),
-            pltpu.SemaphoreType.DMA((2, NX)),
-        ],
+        scratch_shapes=[VMEM(weights.shape, BF16), pltpu.SemaphoreType.DMA((NXC,))],
         compiler_params=small,
         name="output",
-    )(in_hbm(mine), in_hbm(theirs), heads, sent(heads, "c", NC, 1))
-    mixed = lax.all_to_all(mixed, "x", split_axis=0, concat_axis=0)
-    mixed = mixed.astype(F32).sum(axis=0).astype(BF16)
+    )(meta, in_hbm(weights), *near, far)
     mixed = lax.all_to_all(mixed, "z", split_axis=0, concat_axis=0, tiled=True)
     mixed = mixed.reshape(NZ, -1, rows).astype(F32).sum(axis=0)
     return mixed.T.astype(BF16)

time: 156 us -> 154 us (0.987); the launches traced: 154 us -> 154 us
  blocking collectives: 47.6 us -> 20.8 us
  waiting for transfers between devices: 20.3 us -> 41.8 us
  starting transfers between devices: 44.5 us -> 52.3 us
  local copies, waits for them, and re-layouts: 4.41 us -> 1.77 us
    all_to_all x1 -> x0, blocking collectives: 27.6 us -> none  [local(): mixed = lax.all_to_all(mixed, 'x', split_axis=0, concat_axis=0)]
    ppermute x7 -> x9, waiting for transfers between devices: 11 us -> 25.7 us  [sent(): return lax.ppermute(x, axis, [(i, i ^ k) for i in range(size)])]
    all_to_all x0 -> x1, starting transfers between devices: none -> 5.4 us  [local(): weights = lax.all_to_all(w_cols, XC, split_axis=0, concat_axis=0)]
    ppermute x14, waiting for transfers between devices: 4.11 us -> 9.31 us  [shifted(): return lax.ppermute(x, 'z', [(i, (i + k) % NZ) for i in range(NZ)])]
    ppermute x7 -> x9, starting transfers between devices: 10.4 us -> 13.6 us  [sent(): return lax.ppermute(x, axis, [(i, i ^ k) for i in range(size)])]
    unnamed x8 -> x2, local copies, waits for them, and re-layouts: 4.41 us -> 1.77 us
    ppermute x3, waiting for transfers between devices: 5.15 us -> 6.83 us  [local(): lax.ppermute(packed[k], 'grp', [(i, (i + k) % groups) for i in range(grou...]
  transfers between devices with their start and end apart: 25 -> 28, of which waited for: 14 -> 15; matrix products, arithmetic and copies ran while one was open for 0% -> 0% of each run, Pallas kernels for 17% -> 17%
where the time goes in v1:
time: 154 us
  starting transfers between devices  52.3 us (34%)
  waiting for transfers between devices  41.8 us (27%)
  Pallas kernels  36.5 us (24%)
  blocking collectives  20.8 us (14%)
  local copies, waits for them, and re-layouts  1.77 us (1%)
    ppermute x9, waiting for transfers between devices, sent(): return lax.ppermute(x, axis, [(i, i ^ k) for i in range(size)])  25.7 us
    ppermute x14, starting transfers between devices, shifted(): return lax.ppermute(x, 'z', [(i, (i + k) % NZ) for i in range(NZ)])  22.8 us
    all_to_all x1, blocking collectives, local(): mixed = lax.all_to_all(mixed, 'z', split_axis=0, concat_axis=0, tiled=True)  20.8 us
    pallas_call x1, Pallas kernels, local(): pl.pallas_call(functools.partial(attention_kernel, scale=scale), out_shap...  16.8 us
    ppermute x9, starting transfers between devices, sent(): return lax.ppermute(x, axis, [(i, i ^ k) for i in range(size)])  13.6 us
    ppermute x14, waiting for transfers between devices, shifted(): return lax.ppermute(x, 'z', [(i, (i + k) % NZ) for i in range(NZ)])  9.31 us
    ppermute x3, waiting for transfers between devices, local(): lax.ppermute(packed[k], 'grp', [(i, (i + k) % groups) for i in range(grou...  6.83 us
    pallas_call x1, Pallas kernels, local(): pl.pallas_call(functools.partial(prepare_kernel, groups=groups), out_shap...  6.1 us
  transfers between devices with their start and end apart: 28, of which 15 were waited for; matrix products, arithmetic and copies ran while one was open for 0% of the time, Pallas kernels for 17%

profile of v1, /device:TPU:1, one launch (start us, length us, event | category | flops | bytes accessed | tf_op | source)
XLA Modules:
  0.0 154.1 jit_solution(14419339062902994066)
XLA Ops:
  0.1 6.1 %prepare.1 = (s32[41]{0:T(128)S(1)}, bf16[4,2816,128]{2,1,0:T(8,128)(2,1)}, bf16[288,512]{1,0:T(8,128)(2,1)S(1)}, bf16[288,512]{1,0:T(8,128)(2,1)S(1)}, bf16[288...) custom-call(s32[2]{0:T(128)S(1)} %pad_add_fusion.ids, s32[8,64]{1,0:T(8,128)} %bitcast.14, s32[64]{0:T(128)} %refs_1_.1, ...), custom_call_target="tpu_custom_call" | custom-call | tf_op jit(solution)/shard_map/prepare/pallas_call | solution.py:406
  6.2 4.9 %all-to-all-start = ((bf16[4,2816,128]{2,1,0:T(8,128)(2,1)}), bf16[4,2816,128]{2,1,0:T(8,128)(2,1)}, u32[]{:S(2)}, u32[]{:S(2)}) async-start(bf16[4,2816,128]{2,1,0:T(8,128)(2,1)} %get-tuple-element.34), calls=%async_computation | async-start | bytes 5767168 | tf_op jit(solution)/shard_map/all_to_all | solution.py:435
  11.0 2.0 %collective-permute-start = (bf16[288,512]{1,0:T(8,128)(2,1)S(1)}, bf16[288,512]{1,0:T(8,128)(2,1)S(1)}, u32[]{:S(2)}, u32[]{:S(2)}) collective-permute-start(bf16[288,512]{1,0:T(8,128)(2,1)S(1)} %get-tuple-element.29), channel_id=1, source_target_pairs={{0,64},{64,128},{128,192},{192,0},{1,65},{65,129},{129,193},{193,1... | collective-permute-start | bytes 884744 | tf_op jit(solution)/shard_map/ppermute | solution.py:432
  13.1 2.6 %collective-permute-start.1 = (bf16[288,512]{1,0:T(8,128)(2,1)S(1)}, bf16[288,512]{1,0:T(8,128)(2,1)S(1)}, u32[]{:S(2)}, u32[]{:S(2)}) collective-permute-start(bf16[288,512]{1,0:T(8,128)(2,1)S(1)} %get-tuple-element.30), channel_id=1, source_target_pairs={{0,128},{64,192},{128,0},{192,64},{1,129},{65,193},{129,1},{193,65... | collective-permute-start | bytes 884744 | tf_op jit(solution)/shard_map/ppermute | solution.py:432
  16.7 3.0 %columns.1 = bf16[8,896,256]{2,1,0:T(8,128)(2,1)S(1)} custom-call(bf16[256,7168]{1,0:T(8,128)(2,1)} %w_hbm), custom_call_target="tpu_custom_call" | custom-call | tf_op jit(solution)/shard_map/columns/pallas_call | solution.py:438
  19.8 1.8 %copy-done = bf16[8,896,256]{2,1,0:T(8,128)(2,1)} copy-done((bf16[8,896,256]{2,1,0:T(8,128)(2,1)}, bf16[8,896,256]{2,1,0:T(8,128)(2,1)S(1)}, u32[]{:S(2)}) %copy-start) | copy-done | bytes 3670040
  21.6 6.8 %collective-permute-done.1.rest_2_ = bf16[288,512]{1,0:T(8,128)(2,1)S(1)} collective-permute-done((bf16[288,512]{1,0:T(8,128)(2,1)S(1)}, bf16[288,512]{1,0:T(8,128)(2,1)S(1)}, u32[]{:S(2)}, u32[]{:S(2)}) %collective-permute-start.1) | collective-permute-done | bytes 294944 | tf_op jit(solution)/shard_map/ppermute | solution.py:432
  29.0 1.7 %collective-permute-start.9 = (bf16[144,512]{1,0:T(8,128)(2,1)S(1)}, bf16[144,512]{1,0:T(8,128)(2,1)S(1)}, u32[]{:S(2)}, u32[]{:S(2)}) collective-permute-start(bf16[144,512]{1,0:T(8,128)(2,1)S(1)} %get-tuple-element.39.rest_2_), channel_id=1, source_target_pairs={{0,8},{8,16},{16,24},{24,32},{32,40},{40,48},{48,56},{56,0},{1,9},... | collective-permute-start | bytes 442376 | tf_op jit(solution)/shard_map/ppermute | solution.py:373
  30.7 4.0 %collective-permute-start.3 = (bf16[144,512]{1,0:T(8,128)(2,1)S(1)}, bf16[144,512]{1,0:T(8,128)(2,1)S(1)}, u32[]{:S(2)}, u32[]{:S(2)}) collective-permute-start(bf16[144,512]{1,0:T(8,128)(2,1)S(1)} %get-tuple-element.39.rest_2_), channel_id=1, source_target_pairs={{0,56},{8,0},{16,8},{24,16},{32,24},{40,32},{48,40},{56,48},{1,57}... | collective-permute-start | bytes 442376 | tf_op jit(solution)/shard_map/ppermute | solution.py:373
  34.7 2.7 %collective-permute-start.6 = (bf16[144,512]{1,0:T(8,128)(2,1)S(1)}, bf16[144,512]{1,0:T(8,128)(2,1)S(1)}, u32[]{:S(2)}, u32[]{:S(2)}) collective-permute-start(bf16[144,512]{1,0:T(8,128)(2,1)S(1)} %get-tuple-element.40.rest_10_), channel_id=1, source_target_pairs={{0,56},{8,0},{16,8},{24,16},{32,24},{40,32},{48,40},{56,48},{1,57}... | collective-permute-start | bytes 442376 | tf_op jit(solution)/shard_map/ppermute | solution.py:373
  37.6 2.8 %collective-permute-start.4 = (bf16[144,512]{1,0:T(8,128)(2,1)S(1)}, bf16[144,512]{1,0:T(8,128)(2,1)S(1)}, u32[]{:S(2)}, u32[]{:S(2)}) collective-permute-start(bf16[144,512]{1,0:T(8,128)(2,1)S(1)} %collective-permute-done.3.rest_3_), channel_id=1, source_target_pairs={{0,56},{8,0},{16,8},{24,16},{32,24},{40,32},{48,40},{56,48},{1,57}... | collective-permute-start | bytes 442376 | tf_op jit(solution)/shard_map/ppermute | solution.py:373
  40.9 3.0 %collective-permute-start.7 = (bf16[144,512]{1,0:T(8,128)(2,1)S(1)}, bf16[144,512]{1,0:T(8,128)(2,1)S(1)}, u32[]{:S(2)}, u32[]{:S(2)}) collective-permute-start(bf16[144,512]{1,0:T(8,128)(2,1)S(1)} %collective-permute-done.6.rest_11_), channel_id=1, source_target_pairs={{0,56},{8,0},{16,8},{24,16},{32,24},{40,32},{48,40},{56,48},{1,57}... | collective-permute-start | bytes 442376 | tf_op jit(solution)/shard_map/ppermute | solution.py:373
  44.2 3.2 %collective-permute-done.13.rest_16_ = bf16[144,512]{1,0:T(8,128)(2,1)S(1)} collective-permute-done((bf16[144,512]{1,0:T(8,128)(2,1)S(1)}, bf16[144,512]{1,0:T(8,128)(2,1)S(1)}, u32[]{:S(2)}, u32[]{:S(2)}) %collective-permute-start.13) | collective-permute-done | bytes 147488 | tf_op jit(solution)/shard_map/ppermute | solution.py:373
  47.5 2.9 %collective-permute-start.15 = (bf16[4,2816,128]{2,1,0:T(8,128)(2,1)}, bf16[4,2816,128]{2,1,0:T(8,128)(2,1)}, u32[]{:S(2)}, u32[]{:S(2)}) collective-permute-start(bf16[4,2816,128]{2,1,0:T(8,128)(2,1)} %all-to-all-done.near.rest_0_), channel_id=1, source_target_pairs={{0,1},{1,0},{2,3},{3,2},{4,5},{5,4},{6,7},{7,6},{8,9},{9,8},{10,11... | collective-permute-start | bytes 8650760 | tf_op jit(solution)/shard_map/ppermute | solution.py:369
  50.4 3.2 %collective-permute-start.5 = (bf16[144,512]{1,0:T(8,128)(2,1)S(1)}, bf16[144,512]{1,0:T(8,128)(2,1)S(1)}, u32[]{:S(2)}, u32[]{:S(2)}) collective-permute-start(bf16[144,512]{1,0:T(8,128)(2,1)S(1)} %collective-permute-done.4.rest_4_), channel_id=1, source_target_pairs={{0,56},{8,0},{16,8},{24,16},{32,24},{40,32},{48,40},{56,48},{1,57}... | collective-permute-start | bytes 442376 | tf_op jit(solution)/shard_map/ppermute | solution.py:373
  53.6 2.7 %collective-permute-start.8 = (bf16[144,512]{1,0:T(8,128)(2,1)S(1)}, bf16[144,512]{1,0:T(8,128)(2,1)S(1)}, u32[]{:S(2)}, u32[]{:S(2)}) collective-permute-start(bf16[144,512]{1,0:T(8,128)(2,1)S(1)} %collective-permute-done.7.rest_12_), channel_id=1, source_target_pairs={{0,56},{8,0},{16,8},{24,16},{32,24},{40,32},{48,40},{56,48},{1,57}... | collective-permute-start | bytes 442376 | tf_op jit(solution)/shard_map/ppermute | solution.py:373
  56.2 1.5 collective-permute-done.11.rest_7_
  57.8 2.9 %collective-permute-done.14.rest_15_ = bf16[144,512]{1,0:T(8,128)(2,1)S(1)} collective-permute-done((bf16[144,512]{1,0:T(8,128)(2,1)S(1)}, bf16[144,512]{1,0:T(8,128)(2,1)S(1)}, u32[]{:S(2)}, u32[]{:S(2)}) %collective-permute-start.14) | collective-permute-done | bytes 147488 | tf_op jit(solution)/shard_map/ppermute | solution.py:373
  60.7 5.4 %all-to-all-start.1 = ((bf16[8,896,256]{2,1,0:T(8,128)(2,1)}), bf16[8,896,256]{2,1,0:T(8,128)(2,1)}, u32[]{:S(2)}, u32[]{:S(2)}) async-start(bf16[8,896,256]{2,1,0:T(8,128)(2,1)} %copy-done), calls=%async_computation.1 | async-start | bytes 7340032 | tf_op jit(solution)/shard_map/all_to_all | solution.py:472
  66.1 2.4 %collective-permute-start.16 = (bf16[144,512]{1,0:T(8,128)(2,1)S(1)}, bf16[144,512]{1,0:T(8,128)(2,1)S(1)}, u32[]{:S(2)}, u32[]{:S(2)}) collective-permute-start(bf16[144,512]{1,0:T(8,128)(2,1)S(1)} %collective-permute-done.11.rest_7_), channel_id=1, source_target_pairs={{0,8},{8,16},{16,24},{24,32},{32,40},{40,48},{48,56},{56,0},{1,9},... | collective-permute-start | bytes 442376 | tf_op jit(solution)/shard_map/ppermute | solution.py:373
  68.8 4.2 %query.1 = bf16[8,512,640]{2,1,0:T(8,128)(2,1)S(1)} custom-call(s32[41]{0:T(128)S(1)} %get-tuple-element.27.meta, bf16[4,2816,128]{2,1,0:T(8,128)(2,1)} %all-to-all-done.near.rest_0_, bf16[4,2816,128]{2,1,0:T(8,128)(2,1)} %collective-permute-done.15.far.rest_1_), custom_call_target="tpu_custom_call" | custom-call | tf_op jit(solution)/shard_map/query/pallas_call | solution.py:474
  73.6 16.8 %attention.1 = (bf16[4,272,256]{2,1,0:T(8,128)(2,1)S(1)}, bf16[4,272,256]{2,1,0:T(8,128)(2,1)S(1)}) custom-call(s32[41]{0:T(128)S(1)} %get-tuple-element.27.meta, bf16[8,512,640]{2,1,0:T(8,128)(2,1)S(1)} %query.1, bf16[4,2816,128]{2,1,0:T(8,128)(2,1)} %all-to-all-done.near.rest_0_, bf16[4,2816,128]{2,1,0:T(8,128)(2,1)} %collective-permute-done.15.far.rest_1_, ...), custom_call_target="tpu_custom_call" | custom-call | tf_op jit(solution)/shard_map/attention/pallas_call | solution.py:488
  91.6 1.6 %collective-permute-done.18.got = bf16[4,272,256]{2,1,0:T(8,128)(2,1)S(1)} collective-permute-done((bf16[4,272,256]{2,1,0:T(8,128)(2,1)S(1)}, bf16[4,272,256]{2,1,0:T(8,128)(2,1)S(1)}, u32[]{:S(2)}, u32[]{:S(2)}) %collective-permute-start.18) | collective-permute-done | bytes 557088 | tf_op jit(solution)/shard_map/ppermute | solution.py:369
  95.5 2.4 %collective-permute-start.20 = (bf16[272,256]{1,0:T(8,128)(2,1)S(1)}, bf16[272,256]{1,0:T(8,128)(2,1)S(1)}, u32[]{:S(2)}, u32[]{:S(2)}) collective-permute-start(bf16[272,256]{1,0:T(8,128)(2,1)S(1)} %get-tuple-element.47), channel_id=1, source_target_pairs={{0,4},{2,6},{4,0},{6,2},{1,5},{3,7},{5,1},{7,3},{8,12},{10,14},{12... | collective-permute-start | bytes 417800 | tf_op jit(solution)/shard_map/ppermute | solution.py:369
  98.0 12.8 %collective-permute-done.19.refs_1_ = bf16[272,256]{1,0:T(8,128)(2,1)S(1)} collective-permute-done((bf16[272,256]{1,0:T(8,128)(2,1)S(1)}, bf16[272,256]{1,0:T(8,128)(2,1)S(1)}, u32[]{:S(2)}, u32[]{:S(2)}) %collective-permute-start.19) | collective-permute-done | bytes 139296 | tf_op jit(solution)/shard_map/ppermute | solution.py:369
  110.8 4.5 %collective-permute-done.20.refs_2_ = bf16[272,256]{1,0:T(8,128)(2,1)S(1)} collective-permute-done((bf16[272,256]{1,0:T(8,128)(2,1)S(1)}, bf16[272,256]{1,0:T(8,128)(2,1)S(1)}, u32[]{:S(2)}, u32[]{:S(2)}) %collective-permute-start.20) | collective-permute-done | bytes 139296 | tf_op jit(solution)/shard_map/ppermute | solution.py:369
  119.2 3.6 %collective-permute-done.24.refs_3_ = bf16[256,256]{1,0:T(8,128)(2,1)S(1)} collective-permute-done((bf16[256,256]{1,0:T(8,128)(2,1)S(1)}, bf16[256,256]{1,0:T(8,128)(2,1)S(1)}, u32[]{:S(2)}, u32[]{:S(2)}) %collective-permute-start.24) | collective-permute-done | bytes 131104 | tf_op jit(solution)/shard_map/ppermute | solution.py:369
  122.8 1.7 %collective-permute-done.22.refs_1_ = bf16[256,256]{1,0:T(8,128)(2,1)S(1)} collective-permute-done((bf16[256,256]{1,0:T(8,128)(2,1)S(1)}, bf16[256,256]{1,0:T(8,128)(2,1)S(1)}, u32[]{:S(2)}, u32[]{:S(2)}) %collective-permute-start.22) | collective-permute-done | bytes 131104 | tf_op jit(solution)/shard_map/ppermute | solution.py:369
  124.6 2.1 %collective-permute-start.25 = (bf16[4,256,256]{2,1,0:T(8,128)(2,1)S(1)}, bf16[4,256,256]{2,1,0:T(8,128)(2,1)S(1)}, u32[]{:S(2)}, u32[]{:S(2)}) collective-permute-start(bf16[4,256,256]{2,1,0:T(8,128)(2,1)S(1)} %pad_maximum_fusion), channel_id=1, source_target_pairs={{0,1},{1,0},{2,3},{3,2},{4,5},{5,4},{6,7},{7,6},{8,9},{9,8},{10,11... | collective-permute-start | bytes 1572872 | tf_op jit(solution)/shard_map/ppermute | solution.py:369
  126.7 1.5 collective-permute-done.25.refs_4_
  128.2 4.4 %output.1 = bf16[896,256]{1,0:T(8,128)(2,1)S(1)} custom-call(s32[41]{0:T(128)S(1)} %get-tuple-element.27.meta, bf16[8,896,256]{2,1,0:T(8,128)(2,1)} %all-to-all-done.1.source, bf16[256,256]{1,0:T(8,128)(2,1)S(1)} %heads.1.refs_0_, bf16[256,256]{1,0:T(8,128)(2,1)S(1)} %collective-permute-done.22.refs_1_, ...), custom_call_target="tpu_custom_call" | custom-call | tf_op jit(solution)/shard_map/output/pallas_call | solution.py:526
  132.6 20.8 %all_to_all.19 = bf16[8,112,256]{2,1,0:T(8,128)(2,1)S(1)} all-to-all(bf16[8,112,256]{2,1,0:T(8,128)(2,1)S(1)} %bitcast.9), channel_id=1, replica_groups=mesh['grp'=4,'z'=8,'x'=4,'c'=2] {'z'}, dimensions={0} | all-to-all | bytes 917504 | tf_op jit(solution)/shard_map/all_to_all | solution.py:535
  (38 shorter events, 12.1 us)
Async XLA Ops:
  6.2 41.3 %all-to-all-start = ((bf16[4,2816,128]{2,1,0:T(8,128)(2,1)}), bf16[4,2816,128]{2,1,0:T(8,128)(2,1)}, u32[]{:S(2)}, u32[]{:S(2)}) async-start(bf16[4,2816,128]{2,1,0:T(8,128)(2,1)} %get-tuple-element.34), calls=%async_computation | async-start | bytes 5767168 | tf_op jit(solution)/shard_map/all_to_all | solution.py:435
  11.0 10.5 %collective-permute-start = (bf16[288,512]{1,0:T(8,128)(2,1)S(1)}, bf16[288,512]{1,0:T(8,128)(2,1)S(1)}, u32[]{:S(2)}, u32[]{:S(2)}) collective-permute-start(bf16[288,512]{1,0:T(8,128)(2,1)S(1)} %get-tuple-element.29), channel_id=1, source_target_pairs={{0,64},{64,128},{128,192},{192,0},{1,65},{65,129},{129,193},{193,1... | collective-permute-start | bytes 884744 | tf_op jit(solution)/shard_map/ppermute | solution.py:432
  13.1 15.4 %collective-permute-start.1 = (bf16[288,512]{1,0:T(8,128)(2,1)S(1)}, bf16[288,512]{1,0:T(8,128)(2,1)S(1)}, u32[]{:S(2)}, u32[]{:S(2)}) collective-permute-start(bf16[288,512]{1,0:T(8,128)(2,1)S(1)} %get-tuple-element.30), channel_id=1, source_target_pairs={{0,128},{64,192},{128,0},{192,64},{1,129},{65,193},{129,1},{193,65... | collective-permute-start | bytes 884744 | tf_op jit(solution)/shard_map/ppermute | solution.py:432
  15.7 12.7 %collective-permute-start.2 = (bf16[288,512]{1,0:T(8,128)(2,1)S(1)}, bf16[288,512]{1,0:T(8,128)(2,1)S(1)}, u32[]{:S(2)}, u32[]{:S(2)}) collective-permute-start(bf16[288,512]{1,0:T(8,128)(2,1)S(1)} %get-tuple-element.31), channel_id=1, source_target_pairs={{0,192},{64,0},{128,64},{192,128},{1,193},{65,1},{129,65},{193,129... | collective-permute-start | bytes 884744 | tf_op jit(solution)/shard_map/ppermute | solution.py:432
  19.8 1.8 %copy-start = (bf16[8,896,256]{2,1,0:T(8,128)(2,1)}, bf16[8,896,256]{2,1,0:T(8,128)(2,1)S(1)}, u32[]{:S(2)}) copy-start(bf16[8,896,256]{2,1,0:T(8,128)(2,1)S(1)} %columns.1) | copy-start | bytes 11010052
  29.0 8.6 %collective-permute-start.9 = (bf16[144,512]{1,0:T(8,128)(2,1)S(1)}, bf16[144,512]{1,0:T(8,128)(2,1)S(1)}, u32[]{:S(2)}, u32[]{:S(2)}) collective-permute-start(bf16[144,512]{1,0:T(8,128)(2,1)S(1)} %get-tuple-element.39.rest_2_), channel_id=1, source_target_pairs={{0,8},{8,16},{16,24},{24,32},{32,40},{40,48},{48,56},{56,0},{1,9},... | collective-permute-start | bytes 442376 | tf_op jit(solution)/shard_map/ppermute | solution.py:373
  30.7 6.9 %collective-permute-start.3 = (bf16[144,512]{1,0:T(8,128)(2,1)S(1)}, bf16[144,512]{1,0:T(8,128)(2,1)S(1)}, u32[]{:S(2)}, u32[]{:S(2)}) collective-permute-start(bf16[144,512]{1,0:T(8,128)(2,1)S(1)} %get-tuple-element.39.rest_2_), channel_id=1, source_target_pairs={{0,56},{8,0},{16,8},{24,16},{32,24},{40,32},{48,40},{56,48},{1,57}... | collective-permute-start | bytes 442376 | tf_op jit(solution)/shard_map/ppermute | solution.py:373
  34.7 6.2 %collective-permute-start.12 = (bf16[144,512]{1,0:T(8,128)(2,1)S(1)}, bf16[144,512]{1,0:T(8,128)(2,1)S(1)}, u32[]{:S(2)}, u32[]{:S(2)}) collective-permute-start(bf16[144,512]{1,0:T(8,128)(2,1)S(1)} %get-tuple-element.40.rest_10_), channel_id=1, source_target_pairs={{0,8},{8,16},{16,24},{24,32},{32,40},{40,48},{48,56},{56,0},{1,9},... | collective-permute-start | bytes 442376 | tf_op jit(solution)/shard_map/ppermute | solution.py:373
  34.7 6.2 %collective-permute-start.6 = (bf16[144,512]{1,0:T(8,128)(2,1)S(1)}, bf16[144,512]{1,0:T(8,128)(2,1)S(1)}, u32[]{:S(2)}, u32[]{:S(2)}) collective-permute-start(bf16[144,512]{1,0:T(8,128)(2,1)S(1)} %get-tuple-element.40.rest_10_), channel_id=1, source_target_pairs={{0,56},{8,0},{16,8},{24,16},{32,24},{40,32},{48,40},{56,48},{1,57}... | collective-permute-start | bytes 442376 | tf_op jit(solution)/shard_map/ppermute | solution.py:373
  37.6 6.6 %collective-permute-start.10 = (bf16[144,512]{1,0:T(8,128)(2,1)S(1)}, bf16[144,512]{1,0:T(8,128)(2,1)S(1)}, u32[]{:S(2)}, u32[]{:S(2)}) collective-permute-start(bf16[144,512]{1,0:T(8,128)(2,1)S(1)} %collective-permute-done.9.rest_9_), channel_id=1, source_target_pairs={{0,8},{8,16},{16,24},{24,32},{32,40},{40,48},{48,56},{56,0},{1,9},... | collective-permute-start | bytes 442376 | tf_op jit(solution)/shard_map/ppermute | solution.py:373
  37.6 6.6 %collective-permute-start.4 = (bf16[144,512]{1,0:T(8,128)(2,1)S(1)}, bf16[144,512]{1,0:T(8,128)(2,1)S(1)}, u32[]{:S(2)}, u32[]{:S(2)}) collective-permute-start(bf16[144,512]{1,0:T(8,128)(2,1)S(1)} %collective-permute-done.3.rest_3_), channel_id=1, source_target_pairs={{0,56},{8,0},{16,8},{24,16},{32,24},{40,32},{48,40},{56,48},{1,57}... | collective-permute-start | bytes 442376 | tf_op jit(solution)/shard_map/ppermute | solution.py:373
  40.9 6.5 %collective-permute-start.13 = (bf16[144,512]{1,0:T(8,128)(2,1)S(1)}, bf16[144,512]{1,0:T(8,128)(2,1)S(1)}, u32[]{:S(2)}, u32[]{:S(2)}) collective-permute-start(bf16[144,512]{1,0:T(8,128)(2,1)S(1)} %collective-permute-done.12.rest_17_), channel_id=1, source_target_pairs={{0,8},{8,16},{16,24},{24,32},{32,40},{40,48},{48,56},{56,0},{1,9},... | collective-permute-start | bytes 442376 | tf_op jit(solution)/shard_map/ppermute | solution.py:373
  40.9 6.6 %collective-permute-start.7 = (bf16[144,512]{1,0:T(8,128)(2,1)S(1)}, bf16[144,512]{1,0:T(8,128)(2,1)S(1)}, u32[]{:S(2)}, u32[]{:S(2)}) collective-permute-start(bf16[144,512]{1,0:T(8,128)(2,1)S(1)} %collective-permute-done.6.rest_11_), channel_id=1, source_target_pairs={{0,56},{8,0},{16,8},{24,16},{32,24},{40,32},{48,40},{56,48},{1,57}... | collective-permute-start | bytes 442376 | tf_op jit(solution)/shard_map/ppermute | solution.py:373
  47.5 21.3 %collective-permute-start.15 = (bf16[4,2816,128]{2,1,0:T(8,128)(2,1)}, bf16[4,2816,128]{2,1,0:T(8,128)(2,1)}, u32[]{:S(2)}, u32[]{:S(2)}) collective-permute-start(bf16[4,2816,128]{2,1,0:T(8,128)(2,1)} %all-to-all-done.near.rest_0_), channel_id=1, source_target_pairs={{0,1},{1,0},{2,3},{3,2},{4,5},{5,4},{6,7},{7,6},{8,9},{9,8},{10,11... | collective-permute-start | bytes 8650760 | tf_op jit(solution)/shard_map/ppermute | solution.py:369
  50.4 7.4 %collective-permute-start.11 = (bf16[144,512]{1,0:T(8,128)(2,1)S(1)}, bf16[144,512]{1,0:T(8,128)(2,1)S(1)}, u32[]{:S(2)}, u32[]{:S(2)}) collective-permute-start(bf16[144,512]{1,0:T(8,128)(2,1)S(1)} %collective-permute-done.10.rest_8_), channel_id=1, source_target_pairs={{0,8},{8,16},{16,24},{24,32},{32,40},{40,48},{48,56},{56,0},{1,9},... | collective-permute-start | bytes 442376 | tf_op jit(solution)/shard_map/ppermute | solution.py:373
  50.4 7.4 %collective-permute-start.5 = (bf16[144,512]{1,0:T(8,128)(2,1)S(1)}, bf16[144,512]{1,0:T(8,128)(2,1)S(1)}, u32[]{:S(2)}, u32[]{:S(2)}) collective-permute-start(bf16[144,512]{1,0:T(8,128)(2,1)S(1)} %collective-permute-done.4.rest_4_), channel_id=1, source_target_pairs={{0,56},{8,0},{16,8},{24,16},{32,24},{40,32},{48,40},{56,48},{1,57}... | collective-permute-start | bytes 442376 | tf_op jit(solution)/shard_map/ppermute | solution.py:373
  53.6 7.1 %collective-permute-start.14 = (bf16[144,512]{1,0:T(8,128)(2,1)S(1)}, bf16[144,512]{1,0:T(8,128)(2,1)S(1)}, u32[]{:S(2)}, u32[]{:S(2)}) collective-permute-start(bf16[144,512]{1,0:T(8,128)(2,1)S(1)} %collective-permute-done.13.rest_16_), channel_id=1, source_target_pairs={{0,8},{8,16},{16,24},{24,32},{32,40},{40,48},{48,56},{56,0},{1,9},... | collective-permute-start | bytes 442376 | tf_op jit(solution)/shard_map/ppermute | solution.py:373
  53.6 7.1 %collective-permute-start.8 = (bf16[144,512]{1,0:T(8,128)(2,1)S(1)}, bf16[144,512]{1,0:T(8,128)(2,1)S(1)}, u32[]{:S(2)}, u32[]{:S(2)}) collective-permute-start(bf16[144,512]{1,0:T(8,128)(2,1)S(1)} %collective-permute-done.7.rest_12_), channel_id=1, source_target_pairs={{0,56},{8,0},{16,8},{24,16},{32,24},{40,32},{48,40},{56,48},{1,57}... | collective-permute-start | bytes 442376 | tf_op jit(solution)/shard_map/ppermute | solution.py:373
  60.7 66.0 %all-to-all-start.1 = ((bf16[8,896,256]{2,1,0:T(8,128)(2,1)}), bf16[8,896,256]{2,1,0:T(8,128)(2,1)}, u32[]{:S(2)}, u32[]{:S(2)}) async-start(bf16[8,896,256]{2,1,0:T(8,128)(2,1)} %copy-done), calls=%async_computation.1 | async-start | bytes 7340032 | tf_op jit(solution)/shard_map/all_to_all | solution.py:472
  66.1 6.9 %collective-permute-start.16 = (bf16[144,512]{1,0:T(8,128)(2,1)S(1)}, bf16[144,512]{1,0:T(8,128)(2,1)S(1)}, u32[]{:S(2)}, u32[]{:S(2)}) collective-permute-start(bf16[144,512]{1,0:T(8,128)(2,1)S(1)} %collective-permute-done.11.rest_7_), channel_id=1, source_target_pairs={{0,8},{8,16},{16,24},{24,32},{32,40},{40,48},{48,56},{56,0},{1,9},... | collective-permute-start | bytes 442376 | tf_op jit(solution)/shard_map/ppermute | solution.py:373
  68.5 5.1 %collective-permute-start.17 = (bf16[144,512]{1,0:T(8,128)(2,1)S(1)}, bf16[144,512]{1,0:T(8,128)(2,1)S(1)}, u32[]{:S(2)}, u32[]{:S(2)}) collective-permute-start(bf16[144,512]{1,0:T(8,128)(2,1)S(1)} %collective-permute-done.8.rest_13_), channel_id=1, source_target_pairs={{0,56},{8,0},{16,8},{24,16},{32,24},{40,32},{48,40},{56,48},{1,57}... | collective-permute-start | bytes 442376 | tf_op jit(solution)/shard_map/ppermute | solution.py:373
  90.3 2.9 %collective-permute-start.18 = (bf16[4,272,256]{2,1,0:T(8,128)(2,1)S(1)}, bf16[4,272,256]{2,1,0:T(8,128)(2,1)S(1)}, u32[]{:S(2)}, u32[]{:S(2)}) collective-permute-start(bf16[4,272,256]{2,1,0:T(8,128)(2,1)S(1)} %get-tuple-element.44), channel_id=1, source_target_pairs={{0,1},{1,0},{2,3},{3,2},{4,5},{5,4},{6,7},{7,6},{8,9},{9,8},{10,11... | collective-permute-start | bytes 1671176 | tf_op jit(solution)/shard_map/ppermute | solution.py:369
  94.1 16.7 %collective-permute-start.19 = (bf16[272,256]{1,0:T(8,128)(2,1)S(1)}, bf16[272,256]{1,0:T(8,128)(2,1)S(1)}, u32[]{:S(2)}, u32[]{:S(2)}) collective-permute-start(bf16[272,256]{1,0:T(8,128)(2,1)S(1)} %get-tuple-element.46), channel_id=1, source_target_pairs={{0,2},{2,0},{4,6},{6,4},{1,3},{3,1},{5,7},{7,5},{8,10},{10,8},{12,... | collective-permute-start | bytes 417800 | tf_op jit(solution)/shard_map/ppermute | solution.py:369
  95.5 19.8 %collective-permute-start.20 = (bf16[272,256]{1,0:T(8,128)(2,1)S(1)}, bf16[272,256]{1,0:T(8,128)(2,1)S(1)}, u32[]{:S(2)}, u32[]{:S(2)}) collective-permute-start(bf16[272,256]{1,0:T(8,128)(2,1)S(1)} %get-tuple-element.47), channel_id=1, source_target_pairs={{0,4},{2,6},{4,0},{6,2},{1,5},{3,7},{5,1},{7,3},{8,12},{10,14},{12... | collective-permute-start | bytes 417800 | tf_op jit(solution)/shard_map/ppermute | solution.py:369
  97.9 17.4 %collective-permute-start.21 = (bf16[272,256]{1,0:T(8,128)(2,1)S(1)}, bf16[272,256]{1,0:T(8,128)(2,1)S(1)}, u32[]{:S(2)}, u32[]{:S(2)}) collective-permute-start(bf16[272,256]{1,0:T(8,128)(2,1)S(1)} %get-tuple-element.48), channel_id=1, source_target_pairs={{0,6},{2,4},{4,2},{6,0},{1,7},{3,5},{5,3},{7,1},{8,14},{10,12},{12... | collective-permute-start | bytes 417800 | tf_op jit(solution)/shard_map/ppermute | solution.py:369
  115.9 6.9 %collective-permute-start.24 = (bf16[256,256]{1,0:T(8,128)(2,1)S(1)}, bf16[256,256]{1,0:T(8,128)(2,1)S(1)}, u32[]{:S(2)}, u32[]{:S(2)}) collective-permute-start(bf16[256,256]{1,0:T(8,128)(2,1)S(1)} %heads.1.refs_0_), channel_id=1, source_target_pairs={{0,6},{2,4},{4,2},{6,0},{1,7},{3,5},{5,3},{7,1},{8,14},{10,12},{12... | collective-permute-start | bytes 393224 | tf_op jit(solution)/shard_map/ppermute | solution.py:369
  116.9 5.9 %collective-permute-start.23 = (bf16[256,256]{1,0:T(8,128)(2,1)S(1)}, bf16[256,256]{1,0:T(8,128)(2,1)S(1)}, u32[]{:S(2)}, u32[]{:S(2)}) collective-permute-start(bf16[256,256]{1,0:T(8,128)(2,1)S(1)} %heads.1.refs_0_), channel_id=1, source_target_pairs={{0,4},{2,6},{4,0},{6,2},{1,5},{3,7},{5,1},{7,3},{8,12},{10,14},{12... | collective-permute-start | bytes 393224 | tf_op jit(solution)/shard_map/ppermute | solution.py:369
  118.0 6.5 %collective-permute-start.22 = (bf16[256,256]{1,0:T(8,128)(2,1)S(1)}, bf16[256,256]{1,0:T(8,128)(2,1)S(1)}, u32[]{:S(2)}, u32[]{:S(2)}) collective-permute-start(bf16[256,256]{1,0:T(8,128)(2,1)S(1)} %heads.1.refs_0_), channel_id=1, source_target_pairs={{0,2},{2,0},{4,6},{6,4},{1,3},{3,1},{5,7},{7,5},{8,10},{10,8},{12,... | collective-permute-start | bytes 393224 | tf_op jit(solution)/shard_map/ppermute | solution.py:369
  124.6 3.7 %collective-permute-start.25 = (bf16[4,256,256]{2,1,0:T(8,128)(2,1)S(1)}, bf16[4,256,256]{2,1,0:T(8,128)(2,1)S(1)}, u32[]{:S(2)}, u32[]{:S(2)}) collective-permute-start(bf16[4,256,256]{2,1,0:T(8,128)(2,1)S(1)} %pad_maximum_fusion), channel_id=1, source_target_pairs={{0,1},{1,0},{2,3},{3,2},{4,5},{5,4},{6,7},{7,6},{8,9},{9,8},{10,11... | collective-permute-start | bytes 1572872 | tf_op jit(solution)/shard_map/ppermute | solution.py:369

commit v2 on v1

--- a/solution.py
+++ b/solution.py
@@ -468,7 +468,7 @@
     pages = [halves] + above[1:] + [middle] + below[:0:-1]
 
     far_x = sent(after(near_x, above[2], below[2]), "c", NC, 1)
-    w_cols = after(w_cols, near_x, above[3], below[3])
+    w_cols = after(w_cols, near_x)
     weights = lax.all_to_all(w_cols, XC, split_axis=0, concat_axis=0)
 
     query = pl.pallas_call(

time: 154 us -> 144 us (0.935)
  waiting for transfers between devices: 41.8 us -> 32.5 us
  starting transfers between devices: 52.3 us -> 50.7 us
    ppermute x9, waiting for transfers between devices: 25.7 us -> 18.5 us  [sent(): return lax.ppermute(x, axis, [(i, i ^ k) for i in range(size)])]
    ppermute x14, waiting for transfers between devices: 9.31 us -> 7.11 us  [shifted(): return lax.ppermute(x, 'z', [(i, (i + k) % NZ) for i in range(NZ)])]
  transfers between devices with their start and end apart: 28 -> 28, of which waited for: 15 -> 13; matrix products, arithmetic and copies ran while one was open for 0% -> 0% of each run, Pallas kernels for 17% -> 18%
where the time goes in v2:
time: 144 us
  starting transfers between devices  50.7 us (35%)
  Pallas kernels  36.5 us (25%)
  waiting for transfers between devices  32.5 us (23%)
  blocking collectives  21.1 us (15%)
  local copies, waits for them, and re-layouts  1.77 us (1%)
    ppermute x14, starting transfers between devices, shifted(): return lax.ppermute(x, 'z', [(i, (i + k) % NZ) for i in range(NZ)])  21.3 us
    all_to_all x1, blocking collectives, local(): mixed = lax.all_to_all(mixed, 'z', split_axis=0, concat_axis=0, tiled=True)  21.1 us
    ppermute x9, waiting for transfers between devices, sent(): return lax.ppermute(x, axis, [(i, i ^ k) for i in range(size)])  18.5 us
    pallas_call x1, Pallas kernels, local(): pl.pallas_call(functools.partial(attention_kernel, scale=scale), out_shap...  16.8 us
    ppermute x9, starting transfers between devices, sent(): return lax.ppermute(x, axis, [(i, i ^ k) for i in range(size)])  13.9 us
    ppermute x14, waiting for transfers between devices, shifted(): return lax.ppermute(x, 'z', [(i, (i + k) % NZ) for i in range(NZ)])  7.11 us
    ppermute x3, waiting for transfers between devices, local(): lax.ppermute(packed[k], 'grp', [(i, (i + k) % groups) for i in range(grou...  6.83 us
    pallas_call x1, Pallas kernels, local(): pl.pallas_call(functools.partial(prepare_kernel, groups=groups), out_shap...  6.1 us
  transfers between devices with their start and end apart: 28, of which 13 were waited for; matrix products, arithmetic and copies ran while one was open for 0% of the time, Pallas kernels for 18%

profile of v2, /device:TPU:1, one launch (start us, length us, event | category | flops | bytes accessed | tf_op | source)
XLA Modules:
  0.0 143.5 jit_solution(4479786598537826311)
XLA Ops:
  0.1 6.1 %prepare.1 = (s32[41]{0:T(128)S(1)}, bf16[4,2816,128]{2,1,0:T(8,128)(2,1)}, bf16[288,512]{1,0:T(8,128)(2,1)S(1)}, bf16[288,512]{1,0:T(8,128)(2,1)S(1)}, bf16[288...) custom-call(s32[2]{0:T(128)S(1)} %pad_add_fusion.ids, s32[8,64]{1,0:T(8,128)} %bitcast.14, s32[64]{0:T(128)} %refs_1_.1, ...), custom_call_target="tpu_custom_call" | custom-call | tf_op jit(solution)/shard_map/prepare/pallas_call | solution.py:406
  6.2 4.9 %all-to-all-start = ((bf16[4,2816,128]{2,1,0:T(8,128)(2,1)}), bf16[4,2816,128]{2,1,0:T(8,128)(2,1)}, u32[]{:S(2)}, u32[]{:S(2)}) async-start(bf16[4,2816,128]{2,1,0:T(8,128)(2,1)} %get-tuple-element.34), calls=%async_computation | async-start | bytes 5767168 | tf_op jit(solution)/shard_map/all_to_all | solution.py:435
  11.0 2.0 %collective-permute-start = (bf16[288,512]{1,0:T(8,128)(2,1)S(1)}, bf16[288,512]{1,0:T(8,128)(2,1)S(1)}, u32[]{:S(2)}, u32[]{:S(2)}) collective-permute-start(bf16[288,512]{1,0:T(8,128)(2,1)S(1)} %get-tuple-element.29), channel_id=1, source_target_pairs={{0,64},{64,128},{128,192},{192,0},{1,65},{65,129},{129,193},{193,1... | collective-permute-start | bytes 884744 | tf_op jit(solution)/shard_map/ppermute | solution.py:432
  13.1 2.6 %collective-permute-start.1 = (bf16[288,512]{1,0:T(8,128)(2,1)S(1)}, bf16[288,512]{1,0:T(8,128)(2,1)S(1)}, u32[]{:S(2)}, u32[]{:S(2)}) collective-permute-start(bf16[288,512]{1,0:T(8,128)(2,1)S(1)} %get-tuple-element.30), channel_id=1, source_target_pairs={{0,128},{64,192},{128,0},{192,64},{1,129},{65,193},{129,1},{193,65... | collective-permute-start | bytes 884744 | tf_op jit(solution)/shard_map/ppermute | solution.py:432
  16.7 3.0 %columns.1 = bf16[8,896,256]{2,1,0:T(8,128)(2,1)S(1)} custom-call(bf16[256,7168]{1,0:T(8,128)(2,1)} %w_hbm), custom_call_target="tpu_custom_call" | custom-call | tf_op jit(solution)/shard_map/columns/pallas_call | solution.py:438
  19.8 1.8 %copy-done = bf16[8,896,256]{2,1,0:T(8,128)(2,1)} copy-done((bf16[8,896,256]{2,1,0:T(8,128)(2,1)}, bf16[8,896,256]{2,1,0:T(8,128)(2,1)S(1)}, u32[]{:S(2)}) %copy-start) | copy-done | bytes 3670040
  21.6 6.8 %collective-permute-done.1.rest_2_ = bf16[288,512]{1,0:T(8,128)(2,1)S(1)} collective-permute-done((bf16[288,512]{1,0:T(8,128)(2,1)S(1)}, bf16[288,512]{1,0:T(8,128)(2,1)S(1)}, u32[]{:S(2)}, u32[]{:S(2)}) %collective-permute-start.1) | collective-permute-done | bytes 294944 | tf_op jit(solution)/shard_map/ppermute | solution.py:432
  29.0 1.7 %collective-permute-start.7 = (bf16[144,512]{1,0:T(8,128)(2,1)S(1)}, bf16[144,512]{1,0:T(8,128)(2,1)S(1)}, u32[]{:S(2)}, u32[]{:S(2)}) collective-permute-start(bf16[144,512]{1,0:T(8,128)(2,1)S(1)} %get-tuple-element.40.rest_2_), channel_id=1, source_target_pairs={{0,8},{8,16},{16,24},{24,32},{32,40},{40,48},{48,56},{56,0},{1,9},... | collective-permute-start | bytes 442376 | tf_op jit(solution)/shard_map/ppermute | solution.py:373
  30.7 4.0 %collective-permute-start.3 = (bf16[144,512]{1,0:T(8,128)(2,1)S(1)}, bf16[144,512]{1,0:T(8,128)(2,1)S(1)}, u32[]{:S(2)}, u32[]{:S(2)}) collective-permute-start(bf16[144,512]{1,0:T(8,128)(2,1)S(1)} %get-tuple-element.40.rest_2_), channel_id=1, source_target_pairs={{0,56},{8,0},{16,8},{24,16},{32,24},{40,32},{48,40},{56,48},{1,57}... | collective-permute-start | bytes 442376 | tf_op jit(solution)/shard_map/ppermute | solution.py:373
  34.7 2.7 %collective-permute-start.5 = (bf16[144,512]{1,0:T(8,128)(2,1)S(1)}, bf16[144,512]{1,0:T(8,128)(2,1)S(1)}, u32[]{:S(2)}, u32[]{:S(2)}) collective-permute-start(bf16[144,512]{1,0:T(8,128)(2,1)S(1)} %get-tuple-element.41.rest_10_), channel_id=1, source_target_pairs={{0,56},{8,0},{16,8},{24,16},{32,24},{40,32},{48,40},{56,48},{1,57}... | collective-permute-start | bytes 442376 | tf_op jit(solution)/shard_map/ppermute | solution.py:373
  37.6 2.8 %collective-permute-start.4 = (bf16[144,512]{1,0:T(8,128)(2,1)S(1)}, bf16[144,512]{1,0:T(8,128)(2,1)S(1)}, u32[]{:S(2)}, u32[]{:S(2)}) collective-permute-start(bf16[144,512]{1,0:T(8,128)(2,1)S(1)} %collective-permute-done.3.rest_3_), channel_id=1, source_target_pairs={{0,56},{8,0},{16,8},{24,16},{32,24},{40,32},{48,40},{56,48},{1,57}... | collective-permute-start | bytes 442376 | tf_op jit(solution)/shard_map/ppermute | solution.py:373
  40.9 3.0 %collective-permute-start.6 = (bf16[144,512]{1,0:T(8,128)(2,1)S(1)}, bf16[144,512]{1,0:T(8,128)(2,1)S(1)}, u32[]{:S(2)}, u32[]{:S(2)}) collective-permute-start(bf16[144,512]{1,0:T(8,128)(2,1)S(1)} %collective-permute-done.5.rest_11_), channel_id=1, source_target_pairs={{0,56},{8,0},{16,8},{24,16},{32,24},{40,32},{48,40},{56,48},{1,57}... | collective-permute-start | bytes 442376 | tf_op jit(solution)/shard_map/ppermute | solution.py:373
  44.2 3.2 %collective-permute-done.10.rest_16_ = bf16[144,512]{1,0:T(8,128)(2,1)S(1)} collective-permute-done((bf16[144,512]{1,0:T(8,128)(2,1)S(1)}, bf16[144,512]{1,0:T(8,128)(2,1)S(1)}, u32[]{:S(2)}, u32[]{:S(2)}) %collective-permute-start.10) | collective-permute-done | bytes 147488 | tf_op jit(solution)/shard_map/ppermute | solution.py:373
  47.5 2.9 %collective-permute-start.11 = (bf16[4,2816,128]{2,1,0:T(8,128)(2,1)}, bf16[4,2816,128]{2,1,0:T(8,128)(2,1)}, u32[]{:S(2)}, u32[]{:S(2)}) collective-permute-start(bf16[4,2816,128]{2,1,0:T(8,128)(2,1)} %all-to-all-done.near.rest_0_), channel_id=1, source_target_pairs={{0,1},{1,0},{2,3},{3,2},{4,5},{5,4},{6,7},{7,6},{8,9},{9,8},{10,11... | collective-permute-start | bytes 8650760 | tf_op jit(solution)/shard_map/ppermute | solution.py:369
  50.4 4.9 %all-to-all-start.1 = ((bf16[8,896,256]{2,1,0:T(8,128)(2,1)}), bf16[8,896,256]{2,1,0:T(8,128)(2,1)}, u32[]{:S(2)}, u32[]{:S(2)}) async-start(bf16[8,896,256]{2,1,0:T(8,128)(2,1)} %copy-done), calls=%async_computation.1 | async-start | bytes 7340032 | tf_op jit(solution)/shard_map/all_to_all | solution.py:472
  55.3 3.0 %collective-permute-start.15 = (bf16[144,512]{1,0:T(8,128)(2,1)S(1)}, bf16[144,512]{1,0:T(8,128)(2,1)S(1)}, u32[]{:S(2)}, u32[]{:S(2)}) collective-permute-start(bf16[144,512]{1,0:T(8,128)(2,1)S(1)} %collective-permute-done.6.rest_12_), channel_id=1, source_target_pairs={{0,56},{8,0},{16,8},{24,16},{32,24},{40,32},{48,40},{56,48},{1,57}... | collective-permute-start | bytes 442376 | tf_op jit(solution)/shard_map/ppermute | solution.py:373
  58.3 1.4 %collective-permute-start.12 = (bf16[144,512]{1,0:T(8,128)(2,1)S(1)}, bf16[144,512]{1,0:T(8,128)(2,1)S(1)}, u32[]{:S(2)}, u32[]{:S(2)}) collective-permute-start(bf16[144,512]{1,0:T(8,128)(2,1)S(1)} %collective-permute-done.4.rest_4_), channel_id=1, source_target_pairs={{0,56},{8,0},{16,8},{24,16},{32,24},{40,32},{48,40},{56,48},{1,57}... | collective-permute-start | bytes 442376 | tf_op jit(solution)/shard_map/ppermute | solution.py:373
  59.7 2.8 %collective-permute-done.13.rest_7_ = bf16[144,512]{1,0:T(8,128)(2,1)S(1)} collective-permute-done((bf16[144,512]{1,0:T(8,128)(2,1)S(1)}, bf16[144,512]{1,0:T(8,128)(2,1)S(1)}, u32[]{:S(2)}, u32[]{:S(2)}) %collective-permute-start.13) | collective-permute-done | bytes 147488 | tf_op jit(solution)/shard_map/ppermute | solution.py:373
  62.6 2.7 %collective-permute-start.16 = (bf16[144,512]{1,0:T(8,128)(2,1)S(1)}, bf16[144,512]{1,0:T(8,128)(2,1)S(1)}, u32[]{:S(2)}, u32[]{:S(2)}) collective-permute-start(bf16[144,512]{1,0:T(8,128)(2,1)S(1)} %collective-permute-done.15.rest_13_), channel_id=1, source_target_pairs={{0,56},{8,0},{16,8},{24,16},{32,24},{40,32},{48,40},{56,48},{1,57}... | collective-permute-start | bytes 442376 | tf_op jit(solution)/shard_map/ppermute | solution.py:373
  65.3 4.2 %query.1 = bf16[8,512,640]{2,1,0:T(8,128)(2,1)S(1)} custom-call(s32[41]{0:T(128)S(1)} %get-tuple-element.27.meta, bf16[4,2816,128]{2,1,0:T(8,128)(2,1)} %all-to-all-done.near.rest_0_, bf16[4,2816,128]{2,1,0:T(8,128)(2,1)} %collective-permute-done.11.far.rest_1_), custom_call_target="tpu_custom_call" | custom-call | tf_op jit(solution)/shard_map/query/pallas_call | solution.py:474
  69.5 16.8 %attention.1 = (bf16[4,272,256]{2,1,0:T(8,128)(2,1)S(1)}, bf16[4,272,256]{2,1,0:T(8,128)(2,1)S(1)}) custom-call(s32[41]{0:T(128)S(1)} %get-tuple-element.27.meta, bf16[8,512,640]{2,1,0:T(8,128)(2,1)S(1)} %query.1, bf16[4,2816,128]{2,1,0:T(8,128)(2,1)} %all-to-all-done.near.rest_0_, bf16[4,2816,128]{2,1,0:T(8,128)(2,1)} %collective-permute-done.11.far.rest_1_, ...), custom_call_target="tpu_custom_call" | custom-call | tf_op jit(solution)/shard_map/attention/pallas_call | solution.py:488
  87.6 1.6 %collective-permute-done.18.got = bf16[4,272,256]{2,1,0:T(8,128)(2,1)S(1)} collective-permute-done((bf16[4,272,256]{2,1,0:T(8,128)(2,1)S(1)}, bf16[4,272,256]{2,1,0:T(8,128)(2,1)S(1)}, u32[]{:S(2)}, u32[]{:S(2)}) %collective-permute-start.18) | collective-permute-done | bytes 557088 | tf_op jit(solution)/shard_map/ppermute | solution.py:369
  90.0 1.8 %collective-permute-start.19 = (bf16[272,256]{1,0:T(8,128)(2,1)S(1)}, bf16[272,256]{1,0:T(8,128)(2,1)S(1)}, u32[]{:S(2)}, u32[]{:S(2)}) collective-permute-start(bf16[272,256]{1,0:T(8,128)(2,1)S(1)} %get-tuple-element.46), channel_id=1, source_target_pairs={{0,2},{2,0},{4,6},{6,4},{1,3},{3,1},{5,7},{7,5},{8,10},{10,8},{12,... | collective-permute-start | bytes 417800 | tf_op jit(solution)/shard_map/ppermute | solution.py:369
  91.8 2.4 %collective-permute-start.20 = (bf16[272,256]{1,0:T(8,128)(2,1)S(1)}, bf16[272,256]{1,0:T(8,128)(2,1)S(1)}, u32[]{:S(2)}, u32[]{:S(2)}) collective-permute-start(bf16[272,256]{1,0:T(8,128)(2,1)S(1)} %get-tuple-element.47), channel_id=1, source_target_pairs={{0,4},{2,6},{4,0},{6,2},{1,5},{3,7},{5,1},{7,3},{8,12},{10,14},{12... | collective-permute-start | bytes 417800 | tf_op jit(solution)/shard_map/ppermute | solution.py:369
  94.3 5.7 %collective-permute-done.19.refs_1_ = bf16[272,256]{1,0:T(8,128)(2,1)S(1)} collective-permute-done((bf16[272,256]{1,0:T(8,128)(2,1)S(1)}, bf16[272,256]{1,0:T(8,128)(2,1)S(1)}, u32[]{:S(2)}, u32[]{:S(2)}) %collective-permute-start.19) | collective-permute-done | bytes 139296 | tf_op jit(solution)/shard_map/ppermute | solution.py:369
  100.0 4.5 %collective-permute-done.20.refs_2_ = bf16[272,256]{1,0:T(8,128)(2,1)S(1)} collective-permute-done((bf16[272,256]{1,0:T(8,128)(2,1)S(1)}, bf16[272,256]{1,0:T(8,128)(2,1)S(1)}, u32[]{:S(2)}, u32[]{:S(2)}) %collective-permute-start.20) | collective-permute-done | bytes 139296 | tf_op jit(solution)/shard_map/ppermute | solution.py:369
  108.4 3.6 %collective-permute-done.24.refs_3_ = bf16[256,256]{1,0:T(8,128)(2,1)S(1)} collective-permute-done((bf16[256,256]{1,0:T(8,128)(2,1)S(1)}, bf16[256,256]{1,0:T(8,128)(2,1)S(1)}, u32[]{:S(2)}, u32[]{:S(2)}) %collective-permute-start.24) | collective-permute-done | bytes 131104 | tf_op jit(solution)/shard_map/ppermute | solution.py:369
  111.9 1.7 %collective-permute-done.22.refs_1_ = bf16[256,256]{1,0:T(8,128)(2,1)S(1)} collective-permute-done((bf16[256,256]{1,0:T(8,128)(2,1)S(1)}, bf16[256,256]{1,0:T(8,128)(2,1)S(1)}, u32[]{:S(2)}, u32[]{:S(2)}) %collective-permute-start.22) | collective-permute-done | bytes 131104 | tf_op jit(solution)/shard_map/ppermute | solution.py:369
  113.7 2.1 %collective-permute-start.25 = (bf16[4,256,256]{2,1,0:T(8,128)(2,1)S(1)}, bf16[4,256,256]{2,1,0:T(8,128)(2,1)S(1)}, u32[]{:S(2)}, u32[]{:S(2)}) collective-permute-start(bf16[4,256,256]{2,1,0:T(8,128)(2,1)S(1)} %pad_maximum_fusion), channel_id=1, source_target_pairs={{0,1},{1,0},{2,3},{3,2},{4,5},{5,4},{6,7},{7,6},{8,9},{9,8},{10,11... | collective-permute-start | bytes 1572872 | tf_op jit(solution)/shard_map/ppermute | solution.py:369
  115.8 1.5 %collective-permute-done.25.refs_4_ = bf16[4,256,256]{2,1,0:T(8,128)(2,1)S(1)} collective-permute-done((bf16[4,256,256]{2,1,0:T(8,128)(2,1)S(1)}, bf16[4,256,256]{2,1,0:T(8,128)(2,1)S(1)}, u32[]{:S(2)}, u32[]{:S(2)}) %collective-permute-start.25) | collective-permute-done | bytes 524320 | tf_op jit(solution)/shard_map/ppermute | solution.py:369
  117.4 4.4 %output.1 = bf16[896,256]{1,0:T(8,128)(2,1)S(1)} custom-call(s32[41]{0:T(128)S(1)} %get-tuple-element.27.meta, bf16[8,896,256]{2,1,0:T(8,128)(2,1)} %all-to-all-done.1.source, bf16[256,256]{1,0:T(8,128)(2,1)S(1)} %heads.1.refs_0_, bf16[256,256]{1,0:T(8,128)(2,1)S(1)} %collective-permute-done.22.refs_1_, ...), custom_call_target="tpu_custom_call" | custom-call | tf_op jit(solution)/shard_map/output/pallas_call | solution.py:526
  121.7 21.1 %all_to_all.19 = bf16[8,112,256]{2,1,0:T(8,128)(2,1)S(1)} all-to-all(bf16[8,112,256]{2,1,0:T(8,128)(2,1)S(1)} %bitcast.9), channel_id=1, replica_groups=mesh['grp'=4,'z'=8,'x'=4,'c'=2] {'z'}, dimensions={0} | all-to-all | bytes 917504 | tf_op jit(solution)/shard_map/all_to_all | solution.py:535
  (38 shorter events, 9.8 us)
Async XLA Ops:
  6.2 41.3 %all-to-all-start = ((bf16[4,2816,128]{2,1,0:T(8,128)(2,1)}), bf16[4,2816,128]{2,1,0:T(8,128)(2,1)}, u32[]{:S(2)}, u32[]{:S(2)}) async-start(bf16[4,2816,128]{2,1,0:T(8,128)(2,1)} %get-tuple-element.34), calls=%async_computation | async-start | bytes 5767168 | tf_op jit(solution)/shard_map/all_to_all | solution.py:435
  11.0 10.5 %collective-permute-start = (bf16[288,512]{1,0:T(8,128)(2,1)S(1)}, bf16[288,512]{1,0:T(8,128)(2,1)S(1)}, u32[]{:S(2)}, u32[]{:S(2)}) collective-permute-start(bf16[288,512]{1,0:T(8,128)(2,1)S(1)} %get-tuple-element.29), channel_id=1, source_target_pairs={{0,64},{64,128},{128,192},{192,0},{1,65},{65,129},{129,193},{193,1... | collective-permute-start | bytes 884744 | tf_op jit(solution)/shard_map/ppermute | solution.py:432
  13.1 15.4 %collective-permute-start.1 = (bf16[288,512]{1,0:T(8,128)(2,1)S(1)}, bf16[288,512]{1,0:T(8,128)(2,1)S(1)}, u32[]{:S(2)}, u32[]{:S(2)}) collective-permute-start(bf16[288,512]{1,0:T(8,128)(2,1)S(1)} %get-tuple-element.30), channel_id=1, source_target_pairs={{0,128},{64,192},{128,0},{192,64},{1,129},{65,193},{129,1},{193,65... | collective-permute-start | bytes 884744 | tf_op jit(solution)/shard_map/ppermute | solution.py:432
  15.7 12.7 %collective-permute-start.2 = (bf16[288,512]{1,0:T(8,128)(2,1)S(1)}, bf16[288,512]{1,0:T(8,128)(2,1)S(1)}, u32[]{:S(2)}, u32[]{:S(2)}) collective-permute-start(bf16[288,512]{1,0:T(8,128)(2,1)S(1)} %get-tuple-element.31), channel_id=1, source_target_pairs={{0,192},{64,0},{128,64},{192,128},{1,193},{65,1},{129,65},{193,129... | collective-permute-start | bytes 884744 | tf_op jit(solution)/shard_map/ppermute | solution.py:432
  19.8 1.8 %copy-start = (bf16[8,896,256]{2,1,0:T(8,128)(2,1)}, bf16[8,896,256]{2,1,0:T(8,128)(2,1)S(1)}, u32[]{:S(2)}) copy-start(bf16[8,896,256]{2,1,0:T(8,128)(2,1)S(1)} %columns.1) | copy-start | bytes 11010052
  29.0 8.6 %collective-permute-start.7 = (bf16[144,512]{1,0:T(8,128)(2,1)S(1)}, bf16[144,512]{1,0:T(8,128)(2,1)S(1)}, u32[]{:S(2)}, u32[]{:S(2)}) collective-permute-start(bf16[144,512]{1,0:T(8,128)(2,1)S(1)} %get-tuple-element.40.rest_2_), channel_id=1, source_target_pairs={{0,8},{8,16},{16,24},{24,32},{32,40},{40,48},{48,56},{56,0},{1,9},... | collective-permute-start | bytes 442376 | tf_op jit(solution)/shard_map/ppermute | solution.py:373
  30.7 6.9 %collective-permute-start.3 = (bf16[144,512]{1,0:T(8,128)(2,1)S(1)}, bf16[144,512]{1,0:T(8,128)(2,1)S(1)}, u32[]{:S(2)}, u32[]{:S(2)}) collective-permute-start(bf16[144,512]{1,0:T(8,128)(2,1)S(1)} %get-tuple-element.40.rest_2_), channel_id=1, source_target_pairs={{0,56},{8,0},{16,8},{24,16},{32,24},{40,32},{48,40},{56,48},{1,57}... | collective-permute-start | bytes 442376 | tf_op jit(solution)/shard_map/ppermute | solution.py:373
  34.7 6.2 %collective-permute-start.9 = (bf16[144,512]{1,0:T(8,128)(2,1)S(1)}, bf16[144,512]{1,0:T(8,128)(2,1)S(1)}, u32[]{:S(2)}, u32[]{:S(2)}) collective-permute-start(bf16[144,512]{1,0:T(8,128)(2,1)S(1)} %get-tuple-element.41.rest_10_), channel_id=1, source_target_pairs={{0,8},{8,16},{16,24},{24,32},{32,40},{40,48},{48,56},{56,0},{1,9},... | collective-permute-start | bytes 442376 | tf_op jit(solution)/shard_map/ppermute | solution.py:373
  34.7 6.2 %collective-permute-start.5 = (bf16[144,512]{1,0:T(8,128)(2,1)S(1)}, bf16[144,512]{1,0:T(8,128)(2,1)S(1)}, u32[]{:S(2)}, u32[]{:S(2)}) collective-permute-start(bf16[144,512]{1,0:T(8,128)(2,1)S(1)} %get-tuple-element.41.rest_10_), channel_id=1, source_target_pairs={{0,56},{8,0},{16,8},{24,16},{32,24},{40,32},{48,40},{56,48},{1,57}... | collective-permute-start | bytes 442376 | tf_op jit(solution)/shard_map/ppermute | solution.py:373
  37.6 6.6 %collective-permute-start.8 = (bf16[144,512]{1,0:T(8,128)(2,1)S(1)}, bf16[144,512]{1,0:T(8,128)(2,1)S(1)}, u32[]{:S(2)}, u32[]{:S(2)}) collective-permute-start(bf16[144,512]{1,0:T(8,128)(2,1)S(1)} %collective-permute-done.7.rest_9_), channel_id=1, source_target_pairs={{0,8},{8,16},{16,24},{24,32},{32,40},{40,48},{48,56},{56,0},{1,9},... | collective-permute-start | bytes 442376 | tf_op jit(solution)/shard_map/ppermute | solution.py:373
  37.6 6.6 %collective-permute-start.4 = (bf16[144,512]{1,0:T(8,128)(2,1)S(1)}, bf16[144,512]{1,0:T(8,128)(2,1)S(1)}, u32[]{:S(2)}, u32[]{:S(2)}) collective-permute-start(bf16[144,512]{1,0:T(8,128)(2,1)S(1)} %collective-permute-done.3.rest_3_), channel_id=1, source_target_pairs={{0,56},{8,0},{16,8},{24,16},{32,24},{40,32},{48,40},{56,48},{1,57}... | collective-permute-start | bytes 442376 | tf_op jit(solution)/shard_map/ppermute | solution.py:373
  40.9 6.5 %collective-permute-start.10 = (bf16[144,512]{1,0:T(8,128)(2,1)S(1)}, bf16[144,512]{1,0:T(8,128)(2,1)S(1)}, u32[]{:S(2)}, u32[]{:S(2)}) collective-permute-start(bf16[144,512]{1,0:T(8,128)(2,1)S(1)} %collective-permute-done.9.rest_17_), channel_id=1, source_target_pairs={{0,8},{8,16},{16,24},{24,32},{32,40},{40,48},{48,56},{56,0},{1,9},... | collective-permute-start | bytes 442376 | tf_op jit(solution)/shard_map/ppermute | solution.py:373
  40.9 6.6 %collective-permute-start.6 = (bf16[144,512]{1,0:T(8,128)(2,1)S(1)}, bf16[144,512]{1,0:T(8,128)(2,1)S(1)}, u32[]{:S(2)}, u32[]{:S(2)}) collective-permute-start(bf16[144,512]{1,0:T(8,128)(2,1)S(1)} %collective-permute-done.5.rest_11_), channel_id=1, source_target_pairs={{0,56},{8,0},{16,8},{24,16},{32,24},{40,32},{48,40},{56,48},{1,57}... | collective-permute-start | bytes 442376 | tf_op jit(solution)/shard_map/ppermute | solution.py:373
  47.5 17.8 %collective-permute-start.11 = (bf16[4,2816,128]{2,1,0:T(8,128)(2,1)}, bf16[4,2816,128]{2,1,0:T(8,128)(2,1)}, u32[]{:S(2)}, u32[]{:S(2)}) collective-permute-start(bf16[4,2816,128]{2,1,0:T(8,128)(2,1)} %all-to-all-done.near.rest_0_), channel_id=1, source_target_pairs={{0,1},{1,0},{2,3},{3,2},{4,5},{5,4},{6,7},{7,6},{8,9},{9,8},{10,11... | collective-permute-start | bytes 8650760 | tf_op jit(solution)/shard_map/ppermute | solution.py:369
  50.4 65.5 %all-to-all-start.1 = ((bf16[8,896,256]{2,1,0:T(8,128)(2,1)}), bf16[8,896,256]{2,1,0:T(8,128)(2,1)}, u32[]{:S(2)}, u32[]{:S(2)}) async-start(bf16[8,896,256]{2,1,0:T(8,128)(2,1)} %copy-done), calls=%async_computation.1 | async-start | bytes 7340032 | tf_op jit(solution)/shard_map/all_to_all | solution.py:472
  55.3 7.3 %collective-permute-start.13 = (bf16[144,512]{1,0:T(8,128)(2,1)S(1)}, bf16[144,512]{1,0:T(8,128)(2,1)S(1)}, u32[]{:S(2)}, u32[]{:S(2)}) collective-permute-start(bf16[144,512]{1,0:T(8,128)(2,1)S(1)} %collective-permute-done.8.rest_8_), channel_id=1, source_target_pairs={{0,8},{8,16},{16,24},{24,32},{32,40},{40,48},{48,56},{56,0},{1,9},... | collective-permute-start | bytes 442376 | tf_op jit(solution)/shard_map/ppermute | solution.py:373
  55.3 7.3 %collective-permute-start.15 = (bf16[144,512]{1,0:T(8,128)(2,1)S(1)}, bf16[144,512]{1,0:T(8,128)(2,1)S(1)}, u32[]{:S(2)}, u32[]{:S(2)}) collective-permute-start(bf16[144,512]{1,0:T(8,128)(2,1)S(1)} %collective-permute-done.6.rest_12_), channel_id=1, source_target_pairs={{0,56},{8,0},{16,8},{24,16},{32,24},{40,32},{48,40},{56,48},{1,57}... | collective-permute-start | bytes 442376 | tf_op jit(solution)/shard_map/ppermute | solution.py:373
  58.3 11.2 %collective-permute-start.12 = (bf16[144,512]{1,0:T(8,128)(2,1)S(1)}, bf16[144,512]{1,0:T(8,128)(2,1)S(1)}, u32[]{:S(2)}, u32[]{:S(2)}) collective-permute-start(bf16[144,512]{1,0:T(8,128)(2,1)S(1)} %collective-permute-done.4.rest_4_), channel_id=1, source_target_pairs={{0,56},{8,0},{16,8},{24,16},{32,24},{40,32},{48,40},{56,48},{1,57}... | collective-permute-start | bytes 442376 | tf_op jit(solution)/shard_map/ppermute | solution.py:373
  59.7 9.7 %collective-permute-start.17 = (bf16[144,512]{1,0:T(8,128)(2,1)S(1)}, bf16[144,512]{1,0:T(8,128)(2,1)S(1)}, u32[]{:S(2)}, u32[]{:S(2)}) collective-permute-start(bf16[144,512]{1,0:T(8,128)(2,1)S(1)} %collective-permute-done.10.rest_16_), channel_id=1, source_target_pairs={{0,8},{8,16},{16,24},{24,32},{32,40},{40,48},{48,56},{56,0},{1,9},... | collective-permute-start | bytes 442376 | tf_op jit(solution)/shard_map/ppermute | solution.py:373
  62.6 6.9 %collective-permute-start.14 = (bf16[144,512]{1,0:T(8,128)(2,1)S(1)}, bf16[144,512]{1,0:T(8,128)(2,1)S(1)}, u32[]{:S(2)}, u32[]{:S(2)}) collective-permute-start(bf16[144,512]{1,0:T(8,128)(2,1)S(1)} %collective-permute-done.13.rest_7_), channel_id=1, source_target_pairs={{0,8},{8,16},{16,24},{24,32},{32,40},{40,48},{48,56},{56,0},{1,9},... | collective-permute-start | bytes 442376 | tf_op jit(solution)/shard_map/ppermute | solution.py:373
  62.6 6.9 %collective-permute-start.16 = (bf16[144,512]{1,0:T(8,128)(2,1)S(1)}, bf16[144,512]{1,0:T(8,128)(2,1)S(1)}, u32[]{:S(2)}, u32[]{:S(2)}) collective-permute-start(bf16[144,512]{1,0:T(8,128)(2,1)S(1)} %collective-permute-done.15.rest_13_), channel_id=1, source_target_pairs={{0,56},{8,0},{16,8},{24,16},{32,24},{40,32},{48,40},{56,48},{1,57}... | collective-permute-start | bytes 442376 | tf_op jit(solution)/shard_map/ppermute | solution.py:373
  86.3 2.9 %collective-permute-start.18 = (bf16[4,272,256]{2,1,0:T(8,128)(2,1)S(1)}, bf16[4,272,256]{2,1,0:T(8,128)(2,1)S(1)}, u32[]{:S(2)}, u32[]{:S(2)}) collective-permute-start(bf16[4,272,256]{2,1,0:T(8,128)(2,1)S(1)} %get-tuple-element.44), channel_id=1, source_target_pairs={{0,1},{1,0},{2,3},{3,2},{4,5},{5,4},{6,7},{7,6},{8,9},{9,8},{10,11... | collective-permute-start | bytes 1671176 | tf_op jit(solution)/shard_map/ppermute | solution.py:369
  90.0 9.9 %collective-permute-start.19 = (bf16[272,256]{1,0:T(8,128)(2,1)S(1)}, bf16[272,256]{1,0:T(8,128)(2,1)S(1)}, u32[]{:S(2)}, u32[]{:S(2)}) collective-permute-start(bf16[272,256]{1,0:T(8,128)(2,1)S(1)} %get-tuple-element.46), channel_id=1, source_target_pairs={{0,2},{2,0},{4,6},{6,4},{1,3},{3,1},{5,7},{7,5},{8,10},{10,8},{12,... | collective-permute-start | bytes 417800 | tf_op jit(solution)/shard_map/ppermute | solution.py:369
  91.8 12.6 %collective-permute-start.20 = (bf16[272,256]{1,0:T(8,128)(2,1)S(1)}, bf16[272,256]{1,0:T(8,128)(2,1)S(1)}, u32[]{:S(2)}, u32[]{:S(2)}) collective-permute-start(bf16[272,256]{1,0:T(8,128)(2,1)S(1)} %get-tuple-element.47), channel_id=1, source_target_pairs={{0,4},{2,6},{4,0},{6,2},{1,5},{3,7},{5,1},{7,3},{8,12},{10,14},{12... | collective-permute-start | bytes 417800 | tf_op jit(solution)/shard_map/ppermute | solution.py:369
  94.2 10.2 %collective-permute-start.21 = (bf16[272,256]{1,0:T(8,128)(2,1)S(1)}, bf16[272,256]{1,0:T(8,128)(2,1)S(1)}, u32[]{:S(2)}, u32[]{:S(2)}) collective-permute-start(bf16[272,256]{1,0:T(8,128)(2,1)S(1)} %get-tuple-element.48), channel_id=1, source_target_pairs={{0,6},{2,4},{4,2},{6,0},{1,7},{3,5},{5,3},{7,1},{8,14},{10,12},{12... | collective-permute-start | bytes 417800 | tf_op jit(solution)/shard_map/ppermute | solution.py:369
  105.0 6.9 %collective-permute-start.24 = (bf16[256,256]{1,0:T(8,128)(2,1)S(1)}, bf16[256,256]{1,0:T(8,128)(2,1)S(1)}, u32[]{:S(2)}, u32[]{:S(2)}) collective-permute-start(bf16[256,256]{1,0:T(8,128)(2,1)S(1)} %heads.1.refs_0_), channel_id=1, source_target_pairs={{0,6},{2,4},{4,2},{6,0},{1,7},{3,5},{5,3},{7,1},{8,14},{10,12},{12... | collective-permute-start | bytes 393224 | tf_op jit(solution)/shard_map/ppermute | solution.py:369
  106.0 5.9 %collective-permute-start.23 = (bf16[256,256]{1,0:T(8,128)(2,1)S(1)}, bf16[256,256]{1,0:T(8,128)(2,1)S(1)}, u32[]{:S(2)}, u32[]{:S(2)}) collective-permute-start(bf16[256,256]{1,0:T(8,128)(2,1)S(1)} %heads.1.refs_0_), channel_id=1, source_target_pairs={{0,4},{2,6},{4,0},{6,2},{1,5},{3,7},{5,1},{7,3},{8,12},{10,14},{12... | collective-permute-start | bytes 393224 | tf_op jit(solution)/shard_map/ppermute | solution.py:369
  107.2 6.4 %collective-permute-start.22 = (bf16[256,256]{1,0:T(8,128)(2,1)S(1)}, bf16[256,256]{1,0:T(8,128)(2,1)S(1)}, u32[]{:S(2)}, u32[]{:S(2)}) collective-permute-start(bf16[256,256]{1,0:T(8,128)(2,1)S(1)} %heads.1.refs_0_), channel_id=1, source_target_pairs={{0,2},{2,0},{4,6},{6,4},{1,3},{3,1},{5,7},{7,5},{8,10},{10,8},{12,... | collective-permute-start | bytes 393224 | tf_op jit(solution)/shard_map/ppermute | solution.py:369
  113.7 3.7 %collective-permute-start.25 = (bf16[4,256,256]{2,1,0:T(8,128)(2,1)S(1)}, bf16[4,256,256]{2,1,0:T(8,128)(2,1)S(1)}, u32[]{:S(2)}, u32[]{:S(2)}) collective-permute-start(bf16[4,256,256]{2,1,0:T(8,128)(2,1)S(1)} %pad_maximum_fusion), channel_id=1, source_target_pairs={{0,1},{1,0},{2,3},{3,2},{4,5},{5,4},{6,7},{7,6},{8,9},{9,8},{10,11... | collective-permute-start | bytes 1572872 | tf_op jit(solution)/shard_map/ppermute | solution.py:369

commit v3 on v2

--- a/solution.py
+++ b/solution.py
@@ -13,6 +13,7 @@
 DN = 128
 DV = 128
 NEG = -1e30
+LOG2E = math.log2(math.e)
 NZ, NX, NC = 8, 4, 2
 NXC = NX * NC
 DEV = ("z", "x", "c")
@@ -213,21 +214,20 @@
     near, far, firsts, seconds = *rest[:2], rest[2 : 2 + NZ], rest[2 + NZ : -9]
     keep, send, acc, top, total, pages, w_uv, sem, w_sem = rest[-9:]
     per_group, heads_rows, width = acc.shape
-    pair = heads_rows // NXC
-    q_rows = pair // 2
+    q_rows = heads_rows // (2 * NXC)
     rows = per_group * q_rows
     block = pages.shape[1] * 8 // 9
 
     middle = NZ // 2
+    order = [0] + [z for k in range(1, middle) for z in (k, NZ - k)] + [middle]
     split = pages.shape[1] // 2
     loads = [
         [
-            pltpu.make_async_copy(firsts[z], pages.at[z, pl.ds(0, split), :], sem.at[z, 0]),
-            pltpu.make_async_copy(seconds[z], pages.at[z, pl.ds(split, split), :], sem.at[z, 1]),
+            pltpu.make_async_copy(firsts[z], pages.at[i, pl.ds(0, split), :], sem.at[i, 0]),
+            pltpu.make_async_copy(seconds[z], pages.at[i, pl.ds(split, split), :], sem.at[i, 1]),
         ]
-        for z in range(NZ)
-    ]
-    order = [0] + [z for k in range(1, middle) for z in (k, NZ - k)] + [middle]
+        for i, z in enumerate(order)
+    ]
     loads_w = [
         pltpu.make_async_copy(
             placed(near, far, s, meta).at[pl.ds(near.shape[1] - 2 * width, 2 * width), :],
@@ -236,58 +236,87 @@
         )
         for s in range(NXC)
     ]
-    for load in [load for z in order for load in loads[z]] + loads_w:
+    for load in [load for pair in loads for load in pair] + loads_w:
         load.start()
 
-    acc[...] = jnp.zeros_like(acc)
-    top[...] = jnp.full_like(top, NEG)
-    total[...] = jnp.zeros_like(total)
-
-    for z in order:
-        r = meta[RANK + z]
-        valid = meta[VALID + z]
-        for load in loads[z]:
-            load.wait()
-
-        @pl.when(valid > 0)
+    ranks = [meta[RANK + z] for z in order]
+    valids = [meta[VALID + z] for z in order]
+    for r in range(per_group):
+        held = [(ranks[z] == r) & (valids[z] > 0) for z in range(NZ)]
+
+        @pl.when(jnp.logical_not(functools.reduce(jnp.logical_or, held)))
         def _():
-            latent = pages[z, :block, :]
-            tail = pages[z, block:, :]
-            rope = jnp.concatenate([tail[:, :block], tail[:, block:]], axis=0)
-            rope = jnp.concatenate([rope, rope], axis=0)
-            q = query[r]
-            score = lax.dot_general(q[:, :width], latent, NT, preferred_element_type=F32)
-            score = score + jnp.dot(q[:, width:], rope, preferred_element_type=F32)
-            token = lax.broadcasted_iota(jnp.int32, score.shape, 1)
-            live = token < valid
-            score = jnp.where(live, score * scale, NEG)
+            acc[r] = jnp.zeros(acc.shape[1:], F32)
+            top[r] = jnp.full(top.shape[1:], NEG, F32)
+            total[r] = jnp.zeros(total.shape[1:], F32)
+
+    def one_page(i, r, valid, first):
+        latent = pages[i, :block, :]
+        tail = pages[i, block:, :]
+        rope = jnp.concatenate([tail[:, :block], tail[:, block:]], axis=0)
+        rope = jnp.concatenate([rope, rope], axis=0)
+        q = query[r]
+        score = lax.dot_general(q[:, :width], latent, NT, preferred_element_type=F32)
+        score = score + jnp.dot(q[:, width:], rope, preferred_element_type=F32)
+        token = lax.broadcasted_iota(jnp.int32, score.shape, 1)
+        score = jnp.where(token < valid, score * (scale * LOG2E), NEG)
+        new = jnp.max(score, axis=1, keepdims=True)
+        if not first:
             old = top[r][:, :1]
-            new = jnp.maximum(old, jnp.max(score, axis=1, keepdims=True))
-            expo = jnp.where(live, jnp.exp(score - new), 0.0)
-            fade = jnp.exp(old - new)
-            top[r] = jnp.broadcast_to(new, top.shape[1:])
-            total[r] = total[r] * fade + jnp.sum(expo, axis=1, keepdims=True)
-            acc[r] = acc[r] * fade + jnp.dot(
-                expo.astype(BF16), latent, preferred_element_type=F32
-            )
-
+            new = jnp.maximum(old, new)
+            fade = jnp.exp2(old - new)
+        expo = jnp.exp2(score - new)
+        weight = jnp.sum(expo, axis=1, keepdims=True)
+        value = jnp.dot(expo.astype(BF16), latent, preferred_element_type=F32)
+        top[r] = jnp.broadcast_to(new, top.shape[1:])
+        if first:
+            total[r] = jnp.broadcast_to(weight, total.shape[1:])
+            acc[r] = value
+        else:
+            total[r] = total[r] * fade + weight
+            acc[r] = acc[r] * fade + value
+
+    def one_step(i, carry):
+        z = jnp.where(i & 1 == 1, (i + 1) // 2, (NZ - i // 2) & (NZ - 1))
+        r, valid = meta[RANK + z], meta[VALID + z]
+        earlier = [(p < i) & (ranks[p] == r) & (valids[p] > 0) for p in range(NZ)]
+        again = functools.reduce(jnp.logical_or, earlier)
+
+        @pl.when((valid > 0) & jnp.logical_not(again))
+        def _():
+            one_page(i, r, valid, True)
+
+        @pl.when((valid > 0) & again)
+        def _():
+            one_page(i, r, valid, False)
+
+        return carry
+
+    for load in [load for pair in loads for load in pair]:
+        load.wait()
+    lax.fori_loop(0, NZ, one_step, 0)
+
+    lane = lax.broadcasted_iota(jnp.int32, (rows, total.shape[2]), 1)
+    weights = jnp.zeros(lane.shape, F32)
+    highs = jnp.full(lane.shape, NEG, F32)
+    for j in range(2 * NXC):
+        part = slice(j * q_rows, (j + 1) * q_rows)
+        weights = jnp.where(lane == j, total[:, part, :].reshape(lane.shape), weights)
+        highs = jnp.where(lane == j, top[:, part, :].reshape(lane.shape), highs)
+    some = weights > 0.0
+    safe = jnp.where(some, weights, 1.0)
+    shares = 1.0 / safe
+    stats = jnp.where(some, highs * (1.0 / LOG2E) + jnp.log(safe), NEG).T
     for s in range(NXC):
         out = keep if s % 2 == 0 else send
         loads_w[s].wait()
-        stats = []
         for h in range(2):
-            lo = s * pair + h * q_rows
-            weight = total[:, lo : lo + q_rows, :].reshape(rows, total.shape[2])
-            high = top[:, lo : lo + q_rows, :].reshape(rows, top.shape[2])
-            value = acc[:, lo : lo + q_rows, :].reshape(rows, width)
-            some = weight > 0.0
-            safe = jnp.where(some, weight, 1.0)
-            value = (value * (1.0 / safe)[:, :1]).astype(BF16)
+            j = 2 * s + h
+            value = acc[:, j * q_rows : (j + 1) * q_rows, :].reshape(rows, width)
+            value = (value * shares[:, j : j + 1]).astype(BF16)
             head = jnp.dot(value, w_uv[s, h * width : (h + 1) * width, :], preferred_element_type=F32)
             out[s // 2, :rows, h * DV : (h + 1) * DV] = head.astype(BF16)
-            stat = jnp.where(some, high + jnp.log(safe), NEG)
-            stats.append(stat.T[:1, :])
-        out[s // 2, rows:, :] = stored_stats(stats)
+        out[s // 2, rows:, :] = stored_stats([stats[2 * s + h : 2 * s + h + 1, :] for h in range(2)])
 
 
 def merge(parts, tails):
@@ -340,19 +369,13 @@
             out[s, z * share : (z + 1) * share, :] = tall[at : at + share, :]
 
 
-def output_kernel(meta, source, *refs):
-    near, far, out, weights, sem = refs[:NX], *refs[NX:]
-    loads = [
-        pltpu.make_async_copy(source.at[meta[PLACE] ^ s], weights.at[s], sem.at[s])
-        for s in range(NXC)
-    ]
-    for load in loads:
-        load.start()
+def output_kernel(meta, weights, *refs):
+    near, far, out = refs[:NX], *refs[NX:]
     mixed = None
-    for s, load in enumerate(loads):
+    for s in range(NXC):
         heads = near[s // NC][...] if s % NC == 0 else far[s // NC]
-        load.wait()
-        term = lax.dot_general(weights[s], heads, NT, preferred_element_type=F32)
+        weight = weights[meta[PLACE] ^ s]
+        term = lax.dot_general(weight, heads, NT, preferred_element_type=F32)
         mixed = term if mixed is None else mixed + term
     out[...] = mixed.astype(BF16)
 
@@ -521,17 +544,17 @@
         compiler_params=small,
         name="heads",
     )(chip[0], *[sent(chip[k], "x", NX, k) for k in range(1, NX)])
+    heads, weights = lax.optimization_barrier((heads, weights))
     near = [heads] + [sent(heads, "x", NX, k) for k in range(1, NX)]
     far = sent(jnp.stack(near), "c", NC, 1)
     mixed = pl.pallas_call(
         output_kernel,
         out_shape=jax.ShapeDtypeStruct((NZ * share, rows), BF16),
-        in_specs=[spec(SMEM), spec(pl.ANY)] + [spec(VMEM)] * (NX + 1),
+        in_specs=[spec(SMEM)] + [spec(VMEM)] * (NX + 2),
         out_specs=spec(VMEM),
-        scratch_shapes=[VMEM(weights.shape, BF16), pltpu.SemaphoreType.DMA((NXC,))],
         compiler_params=small,
         name="output",
-    )(meta, in_hbm(weights), *near, far)
+    )(meta, weights, *near, far)
     mixed = lax.all_to_all(mixed, "z", split_axis=0, concat_axis=0, tiled=True)
     mixed = mixed.reshape(NZ, -1, rows).astype(F32).sum(axis=0)
     return mixed.T.astype(BF16)

time: 144 us -> 143 us (level)
  Pallas kernels: 36.5 us -> 31.9 us
  waiting for transfers between devices: 32.5 us -> 35.6 us
    pallas_call x1, Pallas kernels: 16.8 us -> 13.3 us  [local(): pl.pallas_call(functools.partial(attention_kernel, scale=scale), out_shap...]
    ppermute x9, waiting for transfers between devices: 18.5 us -> 21.6 us  [sent(): return lax.ppermute(x, axis, [(i, i ^ k) for i in range(size)])]
  transfers between devices with their start and end apart: 28 -> 28, of which waited for: 13 -> 13; matrix products, arithmetic and copies ran while one was open for 0% -> 0% of each run, Pallas kernels for 18% -> 16%
where the time goes in v3:
time: 143 us; the launch traced here: 142 us
  starting transfers between devices  51.1 us (36%)
  waiting for transfers between devices  35.6 us (25%)
  Pallas kernels  31.9 us (22%)
  blocking collectives  21.1 us (15%)
  local copies, waits for them, and re-layouts  1.77 us (1%)
    ppermute x9, waiting for transfers between devices, sent(): return lax.ppermute(x, axis, [(i, i ^ k) for i in range(size)])  21.6 us
    ppermute x14, starting transfers between devices, shifted(): return lax.ppermute(x, 'z', [(i, (i + k) % NZ) for i in range(NZ)])  21.3 us
    all_to_all x1, blocking collectives, local(): mixed = lax.all_to_all(mixed, 'z', split_axis=0, concat_axis=0, tiled=True)  21.1 us
    ppermute x9, starting transfers between devices, sent(): return lax.ppermute(x, axis, [(i, i ^ k) for i in range(size)])  14.3 us
    pallas_call x1, Pallas kernels, local(): pl.pallas_call(functools.partial(attention_kernel, scale=scale), out_shap...  13.3 us
    ppermute x14, waiting for transfers between devices, shifted(): return lax.ppermute(x, 'z', [(i, (i + k) % NZ) for i in range(NZ)])  7.11 us
    ppermute x3, waiting for transfers between devices, local(): lax.ppermute(packed[k], 'grp', [(i, (i + k) % groups) for i in range(grou...  6.83 us
    pallas_call x1, Pallas kernels, local(): pl.pallas_call(functools.partial(prepare_kernel, groups=groups), out_shap...  6.1 us
  transfers between devices with their start and end apart: 28, of which 13 were waited for; matrix products, arithmetic and copies ran while one was open for 0% of the time, Pallas kernels for 16%

profile of v3, /device:TPU:1, one launch (start us, length us, event | category | flops | bytes accessed | tf_op | source)
XLA Modules:
  0.0 142.4 jit_solution(14788425045230952825)
XLA Ops:
  0.1 6.1 %prepare.1 = (s32[41]{0:T(128)S(1)}, bf16[4,2816,128]{2,1,0:T(8,128)(2,1)}, bf16[288,512]{1,0:T(8,128)(2,1)S(1)}, bf16[288,512]{1,0:T(8,128)(2,1)S(1)}, bf16[288...) custom-call(s32[2]{0:T(128)S(1)} %pad_add_fusion.ids, s32[8,64]{1,0:T(8,128)} %bitcast.14, s32[64]{0:T(128)} %refs_1_.1, ...), custom_call_target="tpu_custom_call" | custom-call | tf_op jit(solution)/shard_map/prepare/pallas_call | solution.py:429
  6.2 4.9 %all-to-all-start = ((bf16[4,2816,128]{2,1,0:T(8,128)(2,1)}), bf16[4,2816,128]{2,1,0:T(8,128)(2,1)}, u32[]{:S(2)}, u32[]{:S(2)}) async-start(bf16[4,2816,128]{2,1,0:T(8,128)(2,1)} %get-tuple-element.30), calls=%async_computation | async-start | bytes 5767168 | tf_op jit(solution)/shard_map/all_to_all | solution.py:458
  11.0 2.0 %collective-permute-start = (bf16[288,512]{1,0:T(8,128)(2,1)S(1)}, bf16[288,512]{1,0:T(8,128)(2,1)S(1)}, u32[]{:S(2)}, u32[]{:S(2)}) collective-permute-start(bf16[288,512]{1,0:T(8,128)(2,1)S(1)} %get-tuple-element.32), channel_id=1, source_target_pairs={{0,64},{64,128},{128,192},{192,0},{1,65},{65,129},{129,193},{193,1... | collective-permute-start | bytes 884744 | tf_op jit(solution)/shard_map/ppermute | solution.py:455
  13.1 2.6 %collective-permute-start.1 = (bf16[288,512]{1,0:T(8,128)(2,1)S(1)}, bf16[288,512]{1,0:T(8,128)(2,1)S(1)}, u32[]{:S(2)}, u32[]{:S(2)}) collective-permute-start(bf16[288,512]{1,0:T(8,128)(2,1)S(1)} %get-tuple-element.33), channel_id=1, source_target_pairs={{0,128},{64,192},{128,0},{192,64},{1,129},{65,193},{129,1},{193,65... | collective-permute-start | bytes 884744 | tf_op jit(solution)/shard_map/ppermute | solution.py:455
  16.7 3.0 %columns.1 = bf16[8,896,256]{2,1,0:T(8,128)(2,1)S(1)} custom-call(bf16[256,7168]{1,0:T(8,128)(2,1)} %w_hbm), custom_call_target="tpu_custom_call" | custom-call | tf_op jit(solution)/shard_map/columns/pallas_call | solution.py:461
  19.8 1.8 %copy-done = bf16[8,896,256]{2,1,0:T(8,128)(2,1)} copy-done((bf16[8,896,256]{2,1,0:T(8,128)(2,1)}, bf16[8,896,256]{2,1,0:T(8,128)(2,1)S(1)}, u32[]{:S(2)}) %copy-start) | copy-done | bytes 3670040
  21.6 6.8 %collective-permute-done.1.rest_2_ = bf16[288,512]{1,0:T(8,128)(2,1)S(1)} collective-permute-done((bf16[288,512]{1,0:T(8,128)(2,1)S(1)}, bf16[288,512]{1,0:T(8,128)(2,1)S(1)}, u32[]{:S(2)}, u32[]{:S(2)}) %collective-permute-start.1) | collective-permute-done | bytes 294944 | tf_op jit(solution)/shard_map/ppermute | solution.py:455
  29.0 1.7 %collective-permute-start.7 = (bf16[144,512]{1,0:T(8,128)(2,1)S(1)}, bf16[144,512]{1,0:T(8,128)(2,1)S(1)}, u32[]{:S(2)}, u32[]{:S(2)}) collective-permute-start(bf16[144,512]{1,0:T(8,128)(2,1)S(1)} %get-tuple-element.40.rest_2_), channel_id=1, source_target_pairs={{0,8},{8,16},{16,24},{24,32},{32,40},{40,48},{48,56},{56,0},{1,9},... | collective-permute-start | bytes 442376 | tf_op jit(solution)/shard_map/ppermute | solution.py:396
  30.7 4.0 %collective-permute-start.3 = (bf16[144,512]{1,0:T(8,128)(2,1)S(1)}, bf16[144,512]{1,0:T(8,128)(2,1)S(1)}, u32[]{:S(2)}, u32[]{:S(2)}) collective-permute-start(bf16[144,512]{1,0:T(8,128)(2,1)S(1)} %get-tuple-element.40.rest_2_), channel_id=1, source_target_pairs={{0,56},{8,0},{16,8},{24,16},{32,24},{40,32},{48,40},{56,48},{1,57}... | collective-permute-start | bytes 442376 | tf_op jit(solution)/shard_map/ppermute | solution.py:396
  34.7 2.7 %collective-permute-start.5 = (bf16[144,512]{1,0:T(8,128)(2,1)S(1)}, bf16[144,512]{1,0:T(8,128)(2,1)S(1)}, u32[]{:S(2)}, u32[]{:S(2)}) collective-permute-start(bf16[144,512]{1,0:T(8,128)(2,1)S(1)} %get-tuple-element.41.rest_10_), channel_id=1, source_target_pairs={{0,56},{8,0},{16,8},{24,16},{32,24},{40,32},{48,40},{56,48},{1,57}... | collective-permute-start | bytes 442376 | tf_op jit(solution)/shard_map/ppermute | solution.py:396
  37.6 2.8 %collective-permute-start.4 = (bf16[144,512]{1,0:T(8,128)(2,1)S(1)}, bf16[144,512]{1,0:T(8,128)(2,1)S(1)}, u32[]{:S(2)}, u32[]{:S(2)}) collective-permute-start(bf16[144,512]{1,0:T(8,128)(2,1)S(1)} %collective-permute-done.3.rest_3_), channel_id=1, source_target_pairs={{0,56},{8,0},{16,8},{24,16},{32,24},{40,32},{48,40},{56,48},{1,57}... | collective-permute-start | bytes 442376 | tf_op jit(solution)/shard_map/ppermute | solution.py:396
  40.9 3.0 %collective-permute-start.6 = (bf16[144,512]{1,0:T(8,128)(2,1)S(1)}, bf16[144,512]{1,0:T(8,128)(2,1)S(1)}, u32[]{:S(2)}, u32[]{:S(2)}) collective-permute-start(bf16[144,512]{1,0:T(8,128)(2,1)S(1)} %collective-permute-done.5.rest_11_), channel_id=1, source_target_pairs={{0,56},{8,0},{16,8},{24,16},{32,24},{40,32},{48,40},{56,48},{1,57}... | collective-permute-start | bytes 442376 | tf_op jit(solution)/shard_map/ppermute | solution.py:396
  44.2 3.2 %collective-permute-done.10.rest_16_ = bf16[144,512]{1,0:T(8,128)(2,1)S(1)} collective-permute-done((bf16[144,512]{1,0:T(8,128)(2,1)S(1)}, bf16[144,512]{1,0:T(8,128)(2,1)S(1)}, u32[]{:S(2)}, u32[]{:S(2)}) %collective-permute-start.10) | collective-permute-done | bytes 147488 | tf_op jit(solution)/shard_map/ppermute | solution.py:396
  47.5 2.9 %collective-permute-start.11 = (bf16[4,2816,128]{2,1,0:T(8,128)(2,1)}, bf16[4,2816,128]{2,1,0:T(8,128)(2,1)}, u32[]{:S(2)}, u32[]{:S(2)}) collective-permute-start(bf16[4,2816,128]{2,1,0:T(8,128)(2,1)} %all-to-all-done.near.rest_0_), channel_id=1, source_target_pairs={{0,1},{1,0},{2,3},{3,2},{4,5},{5,4},{6,7},{7,6},{8,9},{9,8},{10,11... | collective-permute-start | bytes 8650760 | tf_op jit(solution)/shard_map/ppermute | solution.py:392
  50.4 4.9 %all-to-all-start.1 = ((bf16[8,896,256]{2,1,0:T(8,128)(2,1)}), bf16[8,896,256]{2,1,0:T(8,128)(2,1)}, u32[]{:S(2)}, u32[]{:S(2)}) async-start(bf16[8,896,256]{2,1,0:T(8,128)(2,1)} %copy-done), calls=%async_computation.1 | async-start | bytes 7340032 | tf_op jit(solution)/shard_map/all_to_all | solution.py:495
  55.3 3.0 %collective-permute-start.15 = (bf16[144,512]{1,0:T(8,128)(2,1)S(1)}, bf16[144,512]{1,0:T(8,128)(2,1)S(1)}, u32[]{:S(2)}, u32[]{:S(2)}) collective-permute-start(bf16[144,512]{1,0:T(8,128)(2,1)S(1)} %collective-permute-done.6.rest_12_), channel_id=1, source_target_pairs={{0,56},{8,0},{16,8},{24,16},{32,24},{40,32},{48,40},{56,48},{1,57}... | collective-permute-start | bytes 442376 | tf_op jit(solution)/shard_map/ppermute | solution.py:396
  58.3 1.4 %collective-permute-start.12 = (bf16[144,512]{1,0:T(8,128)(2,1)S(1)}, bf16[144,512]{1,0:T(8,128)(2,1)S(1)}, u32[]{:S(2)}, u32[]{:S(2)}) collective-permute-start(bf16[144,512]{1,0:T(8,128)(2,1)S(1)} %collective-permute-done.4.rest_4_), channel_id=1, source_target_pairs={{0,56},{8,0},{16,8},{24,16},{32,24},{40,32},{48,40},{56,48},{1,57}... | collective-permute-start | bytes 442376 | tf_op jit(solution)/shard_map/ppermute | solution.py:396
  59.7 2.8 %collective-permute-done.13.rest_7_ = bf16[144,512]{1,0:T(8,128)(2,1)S(1)} collective-permute-done((bf16[144,512]{1,0:T(8,128)(2,1)S(1)}, bf16[144,512]{1,0:T(8,128)(2,1)S(1)}, u32[]{:S(2)}, u32[]{:S(2)}) %collective-permute-start.13) | collective-permute-done | bytes 147488 | tf_op jit(solution)/shard_map/ppermute | solution.py:396
  62.6 2.7 %collective-permute-start.16 = (bf16[144,512]{1,0:T(8,128)(2,1)S(1)}, bf16[144,512]{1,0:T(8,128)(2,1)S(1)}, u32[]{:S(2)}, u32[]{:S(2)}) collective-permute-start(bf16[144,512]{1,0:T(8,128)(2,1)S(1)} %collective-permute-done.15.rest_13_), channel_id=1, source_target_pairs={{0,56},{8,0},{16,8},{24,16},{32,24},{40,32},{48,40},{56,48},{1,57}... | collective-permute-start | bytes 442376 | tf_op jit(solution)/shard_map/ppermute | solution.py:396
  65.3 4.2 %query.1 = bf16[8,512,640]{2,1,0:T(8,128)(2,1)S(1)} custom-call(s32[41]{0:T(128)S(1)} %get-tuple-element.29.meta, bf16[4,2816,128]{2,1,0:T(8,128)(2,1)} %all-to-all-done.near.rest_0_, bf16[4,2816,128]{2,1,0:T(8,128)(2,1)} %collective-permute-done.11.far.rest_1_), custom_call_target="tpu_custom_call" | custom-call | tf_op jit(solution)/shard_map/query/pallas_call | solution.py:497
  69.5 13.3 %attention.1 = (bf16[4,272,256]{2,1,0:T(8,128)(2,1)S(1)}, bf16[4,272,256]{2,1,0:T(8,128)(2,1)S(1)}) custom-call(s32[41]{0:T(128)S(1)} %get-tuple-element.29.meta, bf16[8,512,640]{2,1,0:T(8,128)(2,1)S(1)} %query.1, bf16[4,2816,128]{2,1,0:T(8,128)(2,1)} %all-to-all-done.near.rest_0_, bf16[4,2816,128]{2,1,0:T(8,128)(2,1)} %collective-permute-done.11.far.rest_1_, ...), custom_call_target="tpu_custom_call" | custom-call | tf_op jit(solution)/shard_map/attention/pallas_call | solution.py:511
  82.8 2.0 %collective-permute-start.18 = (bf16[4,272,256]{2,1,0:T(8,128)(2,1)S(1)}, bf16[4,272,256]{2,1,0:T(8,128)(2,1)S(1)}, u32[]{:S(2)}, u32[]{:S(2)}) collective-permute-start(bf16[4,272,256]{2,1,0:T(8,128)(2,1)S(1)} %get-tuple-element.44), channel_id=1, source_target_pairs={{0,1},{1,0},{2,3},{3,2},{4,5},{5,4},{6,7},{7,6},{8,9},{9,8},{10,11... | collective-permute-start | bytes 1671176 | tf_op jit(solution)/shard_map/ppermute | solution.py:392
  84.9 1.6 %collective-permute-done.18.got = bf16[4,272,256]{2,1,0:T(8,128)(2,1)S(1)} collective-permute-done((bf16[4,272,256]{2,1,0:T(8,128)(2,1)S(1)}, bf16[4,272,256]{2,1,0:T(8,128)(2,1)S(1)}, u32[]{:S(2)}, u32[]{:S(2)}) %collective-permute-start.18) | collective-permute-done | bytes 557088 | tf_op jit(solution)/shard_map/ppermute | solution.py:392
  88.1 3.2 %collective-permute-start.21 = (bf16[272,256]{1,0:T(8,128)(2,1)S(1)}, bf16[272,256]{1,0:T(8,128)(2,1)S(1)}, u32[]{:S(2)}, u32[]{:S(2)}) collective-permute-start(bf16[272,256]{1,0:T(8,128)(2,1)S(1)} %get-tuple-element.48), channel_id=1, source_target_pairs={{0,6},{2,4},{4,2},{6,0},{1,7},{3,5},{5,3},{7,1},{8,14},{10,12},{12... | collective-permute-start | bytes 417800 | tf_op jit(solution)/shard_map/ppermute | solution.py:392
  91.3 8.7 %collective-permute-done.19.refs_1_ = bf16[272,256]{1,0:T(8,128)(2,1)S(1)} collective-permute-done((bf16[272,256]{1,0:T(8,128)(2,1)S(1)}, bf16[272,256]{1,0:T(8,128)(2,1)S(1)}, u32[]{:S(2)}, u32[]{:S(2)}) %collective-permute-start.19) | collective-permute-done | bytes 139296 | tf_op jit(solution)/shard_map/ppermute | solution.py:392
  100.0 4.5 %collective-permute-done.20.refs_2_ = bf16[272,256]{1,0:T(8,128)(2,1)S(1)} collective-permute-done((bf16[272,256]{1,0:T(8,128)(2,1)S(1)}, bf16[272,256]{1,0:T(8,128)(2,1)S(1)}, u32[]{:S(2)}, u32[]{:S(2)}) %collective-permute-start.20) | collective-permute-done | bytes 139296 | tf_op jit(solution)/shard_map/ppermute | solution.py:392
  108.4 3.6 %collective-permute-done.24.refs_3_ = bf16[256,256]{1,0:T(8,128)(2,1)S(1)} collective-permute-done((bf16[256,256]{1,0:T(8,128)(2,1)S(1)}, bf16[256,256]{1,0:T(8,128)(2,1)S(1)}, u32[]{:S(2)}, u32[]{:S(2)}) %collective-permute-start.24) | collective-permute-done | bytes 131104 | tf_op jit(solution)/shard_map/ppermute | solution.py:392
  112.0 1.7 %collective-permute-done.22.refs_1_ = bf16[256,256]{1,0:T(8,128)(2,1)S(1)} collective-permute-done((bf16[256,256]{1,0:T(8,128)(2,1)S(1)}, bf16[256,256]{1,0:T(8,128)(2,1)S(1)}, u32[]{:S(2)}, u32[]{:S(2)}) %collective-permute-start.22) | collective-permute-done | bytes 131104 | tf_op jit(solution)/shard_map/ppermute | solution.py:392
  113.8 2.1 %collective-permute-start.25 = (bf16[4,256,256]{2,1,0:T(8,128)(2,1)S(1)}, bf16[4,256,256]{2,1,0:T(8,128)(2,1)S(1)}, u32[]{:S(2)}, u32[]{:S(2)}) collective-permute-start(bf16[4,256,256]{2,1,0:T(8,128)(2,1)S(1)} %pad_maximum_fusion), channel_id=1, source_target_pairs={{0,1},{1,0},{2,3},{3,2},{4,5},{5,4},{6,7},{7,6},{8,9},{9,8},{10,11... | collective-permute-start | bytes 1572872 | tf_op jit(solution)/shard_map/ppermute | solution.py:392
  115.9 1.5 %collective-permute-done.25.refs_4_ = bf16[4,256,256]{2,1,0:T(8,128)(2,1)S(1)} collective-permute-done((bf16[4,256,256]{2,1,0:T(8,128)(2,1)S(1)}, bf16[4,256,256]{2,1,0:T(8,128)(2,1)S(1)}, u32[]{:S(2)}, u32[]{:S(2)}) %collective-permute-start.25) | collective-permute-done | bytes 524320 | tf_op jit(solution)/shard_map/ppermute | solution.py:392
  117.4 3.2 %output.1 = bf16[896,256]{1,0:T(8,128)(2,1)S(1)} custom-call(s32[41]{0:T(128)S(1)} %get-tuple-element.29.meta, bf16[8,896,256]{2,1,0:T(8,128)(2,1)} %all-to-all-done.1.weights, bf16[256,256]{1,0:T(8,128)(2,1)S(1)} %heads.1.refs_0_, bf16[256,256]{1,0:T(8,128)(2,1)S(1)} %collective-permute-done.22.refs_1_, ...), custom_call_target="tpu_custom_call" | custom-call | tf_op jit(solution)/shard_map/output/pallas_call | solution.py:550
  120.6 21.1 %all_to_all.19 = bf16[8,112,256]{2,1,0:T(8,128)(2,1)S(1)} all-to-all(bf16[8,112,256]{2,1,0:T(8,128)(2,1)S(1)} %bitcast.9), channel_id=1, replica_groups=mesh['grp'=4,'z'=8,'x'=4,'c'=2] {'z'}, dimensions={0} | all-to-all | bytes 917504 | tf_op jit(solution)/shard_map/all_to_all | solution.py:558
  (38 shorter events, 9.2 us)
Async XLA Ops:
  6.2 41.3 %all-to-all-start = ((bf16[4,2816,128]{2,1,0:T(8,128)(2,1)}), bf16[4,2816,128]{2,1,0:T(8,128)(2,1)}, u32[]{:S(2)}, u32[]{:S(2)}) async-start(bf16[4,2816,128]{2,1,0:T(8,128)(2,1)} %get-tuple-element.30), calls=%async_computation | async-start | bytes 5767168 | tf_op jit(solution)/shard_map/all_to_all | solution.py:458
  11.0 10.5 %collective-permute-start = (bf16[288,512]{1,0:T(8,128)(2,1)S(1)}, bf16[288,512]{1,0:T(8,128)(2,1)S(1)}, u32[]{:S(2)}, u32[]{:S(2)}) collective-permute-start(bf16[288,512]{1,0:T(8,128)(2,1)S(1)} %get-tuple-element.32), channel_id=1, source_target_pairs={{0,64},{64,128},{128,192},{192,0},{1,65},{65,129},{129,193},{193,1... | collective-permute-start | bytes 884744 | tf_op jit(solution)/shard_map/ppermute | solution.py:455
  13.1 15.4 %collective-permute-start.1 = (bf16[288,512]{1,0:T(8,128)(2,1)S(1)}, bf16[288,512]{1,0:T(8,128)(2,1)S(1)}, u32[]{:S(2)}, u32[]{:S(2)}) collective-permute-start(bf16[288,512]{1,0:T(8,128)(2,1)S(1)} %get-tuple-element.33), channel_id=1, source_target_pairs={{0,128},{64,192},{128,0},{192,64},{1,129},{65,193},{129,1},{193,65... | collective-permute-start | bytes 884744 | tf_op jit(solution)/shard_map/ppermute | solution.py:455
  15.7 12.7 %collective-permute-start.2 = (bf16[288,512]{1,0:T(8,128)(2,1)S(1)}, bf16[288,512]{1,0:T(8,128)(2,1)S(1)}, u32[]{:S(2)}, u32[]{:S(2)}) collective-permute-start(bf16[288,512]{1,0:T(8,128)(2,1)S(1)} %get-tuple-element.34), channel_id=1, source_target_pairs={{0,192},{64,0},{128,64},{192,128},{1,193},{65,1},{129,65},{193,129... | collective-permute-start | bytes 884744 | tf_op jit(solution)/shard_map/ppermute | solution.py:455
  19.8 1.8 %copy-start = (bf16[8,896,256]{2,1,0:T(8,128)(2,1)}, bf16[8,896,256]{2,1,0:T(8,128)(2,1)S(1)}, u32[]{:S(2)}) copy-start(bf16[8,896,256]{2,1,0:T(8,128)(2,1)S(1)} %columns.1) | copy-start | bytes 11010052
  29.0 8.6 %collective-permute-start.7 = (bf16[144,512]{1,0:T(8,128)(2,1)S(1)}, bf16[144,512]{1,0:T(8,128)(2,1)S(1)}, u32[]{:S(2)}, u32[]{:S(2)}) collective-permute-start(bf16[144,512]{1,0:T(8,128)(2,1)S(1)} %get-tuple-element.40.rest_2_), channel_id=1, source_target_pairs={{0,8},{8,16},{16,24},{24,32},{32,40},{40,48},{48,56},{56,0},{1,9},... | collective-permute-start | bytes 442376 | tf_op jit(solution)/shard_map/ppermute | solution.py:396
  30.7 6.9 %collective-permute-start.3 = (bf16[144,512]{1,0:T(8,128)(2,1)S(1)}, bf16[144,512]{1,0:T(8,128)(2,1)S(1)}, u32[]{:S(2)}, u32[]{:S(2)}) collective-permute-start(bf16[144,512]{1,0:T(8,128)(2,1)S(1)} %get-tuple-element.40.rest_2_), channel_id=1, source_target_pairs={{0,56},{8,0},{16,8},{24,16},{32,24},{40,32},{48,40},{56,48},{1,57}... | collective-permute-start | bytes 442376 | tf_op jit(solution)/shard_map/ppermute | solution.py:396
  34.7 6.2 %collective-permute-start.9 = (bf16[144,512]{1,0:T(8,128)(2,1)S(1)}, bf16[144,512]{1,0:T(8,128)(2,1)S(1)}, u32[]{:S(2)}, u32[]{:S(2)}) collective-permute-start(bf16[144,512]{1,0:T(8,128)(2,1)S(1)} %get-tuple-element.41.rest_10_), channel_id=1, source_target_pairs={{0,8},{8,16},{16,24},{24,32},{32,40},{40,48},{48,56},{56,0},{1,9},... | collective-permute-start | bytes 442376 | tf_op jit(solution)/shard_map/ppermute | solution.py:396
  34.7 6.2 %collective-permute-start.5 = (bf16[144,512]{1,0:T(8,128)(2,1)S(1)}, bf16[144,512]{1,0:T(8,128)(2,1)S(1)}, u32[]{:S(2)}, u32[]{:S(2)}) collective-permute-start(bf16[144,512]{1,0:T(8,128)(2,1)S(1)} %get-tuple-element.41.rest_10_), channel_id=1, source_target_pairs={{0,56},{8,0},{16,8},{24,16},{32,24},{40,32},{48,40},{56,48},{1,57}... | collective-permute-start | bytes 442376 | tf_op jit(solution)/shard_map/ppermute | solution.py:396
  37.6 6.6 %collective-permute-start.8 = (bf16[144,512]{1,0:T(8,128)(2,1)S(1)}, bf16[144,512]{1,0:T(8,128)(2,1)S(1)}, u32[]{:S(2)}, u32[]{:S(2)}) collective-permute-start(bf16[144,512]{1,0:T(8,128)(2,1)S(1)} %collective-permute-done.7.rest_9_), channel_id=1, source_target_pairs={{0,8},{8,16},{16,24},{24,32},{32,40},{40,48},{48,56},{56,0},{1,9},... | collective-permute-start | bytes 442376 | tf_op jit(solution)/shard_map/ppermute | solution.py:396
  37.6 6.6 %collective-permute-start.4 = (bf16[144,512]{1,0:T(8,128)(2,1)S(1)}, bf16[144,512]{1,0:T(8,128)(2,1)S(1)}, u32[]{:S(2)}, u32[]{:S(2)}) collective-permute-start(bf16[144,512]{1,0:T(8,128)(2,1)S(1)} %collective-permute-done.3.rest_3_), channel_id=1, source_target_pairs={{0,56},{8,0},{16,8},{24,16},{32,24},{40,32},{48,40},{56,48},{1,57}... | collective-permute-start | bytes 442376 | tf_op jit(solution)/shard_map/ppermute | solution.py:396
  40.9 6.5 %collective-permute-start.10 = (bf16[144,512]{1,0:T(8,128)(2,1)S(1)}, bf16[144,512]{1,0:T(8,128)(2,1)S(1)}, u32[]{:S(2)}, u32[]{:S(2)}) collective-permute-start(bf16[144,512]{1,0:T(8,128)(2,1)S(1)} %collective-permute-done.9.rest_17_), channel_id=1, source_target_pairs={{0,8},{8,16},{16,24},{24,32},{32,40},{40,48},{48,56},{56,0},{1,9},... | collective-permute-start | bytes 442376 | tf_op jit(solution)/shard_map/ppermute | solution.py:396
  40.9 6.6 %collective-permute-start.6 = (bf16[144,512]{1,0:T(8,128)(2,1)S(1)}, bf16[144,512]{1,0:T(8,128)(2,1)S(1)}, u32[]{:S(2)}, u32[]{:S(2)}) collective-permute-start(bf16[144,512]{1,0:T(8,128)(2,1)S(1)} %collective-permute-done.5.rest_11_), channel_id=1, source_target_pairs={{0,56},{8,0},{16,8},{24,16},{32,24},{40,32},{48,40},{56,48},{1,57}... | collective-permute-start | bytes 442376 | tf_op jit(solution)/shard_map/ppermute | solution.py:396
  47.5 17.8 %collective-permute-start.11 = (bf16[4,2816,128]{2,1,0:T(8,128)(2,1)}, bf16[4,2816,128]{2,1,0:T(8,128)(2,1)}, u32[]{:S(2)}, u32[]{:S(2)}) collective-permute-start(bf16[4,2816,128]{2,1,0:T(8,128)(2,1)} %all-to-all-done.near.rest_0_), channel_id=1, source_target_pairs={{0,1},{1,0},{2,3},{3,2},{4,5},{5,4},{6,7},{7,6},{8,9},{9,8},{10,11... | collective-permute-start | bytes 8650760 | tf_op jit(solution)/shard_map/ppermute | solution.py:392
  50.4 54.7 %all-to-all-start.1 = ((bf16[8,896,256]{2,1,0:T(8,128)(2,1)}), bf16[8,896,256]{2,1,0:T(8,128)(2,1)}, u32[]{:S(2)}, u32[]{:S(2)}) async-start(bf16[8,896,256]{2,1,0:T(8,128)(2,1)} %copy-done), calls=%async_computation.1 | async-start | bytes 7340032 | tf_op jit(solution)/shard_map/all_to_all | solution.py:495
  55.3 7.3 %collective-permute-start.13 = (bf16[144,512]{1,0:T(8,128)(2,1)S(1)}, bf16[144,512]{1,0:T(8,128)(2,1)S(1)}, u32[]{:S(2)}, u32[]{:S(2)}) collective-permute-start(bf16[144,512]{1,0:T(8,128)(2,1)S(1)} %collective-permute-done.8.rest_8_), channel_id=1, source_target_pairs={{0,8},{8,16},{16,24},{24,32},{32,40},{40,48},{48,56},{56,0},{1,9},... | collective-permute-start | bytes 442376 | tf_op jit(solution)/shard_map/ppermute | solution.py:396
  55.3 7.3 %collective-permute-start.15 = (bf16[144,512]{1,0:T(8,128)(2,1)S(1)}, bf16[144,512]{1,0:T(8,128)(2,1)S(1)}, u32[]{:S(2)}, u32[]{:S(2)}) collective-permute-start(bf16[144,512]{1,0:T(8,128)(2,1)S(1)} %collective-permute-done.6.rest_12_), channel_id=1, source_target_pairs={{0,56},{8,0},{16,8},{24,16},{32,24},{40,32},{48,40},{56,48},{1,57}... | collective-permute-start | bytes 442376 | tf_op jit(solution)/shard_map/ppermute | solution.py:396
  58.3 11.2 %collective-permute-start.12 = (bf16[144,512]{1,0:T(8,128)(2,1)S(1)}, bf16[144,512]{1,0:T(8,128)(2,1)S(1)}, u32[]{:S(2)}, u32[]{:S(2)}) collective-permute-start(bf16[144,512]{1,0:T(8,128)(2,1)S(1)} %collective-permute-done.4.rest_4_), channel_id=1, source_target_pairs={{0,56},{8,0},{16,8},{24,16},{32,24},{40,32},{48,40},{56,48},{1,57}... | collective-permute-start | bytes 442376 | tf_op jit(solution)/shard_map/ppermute | solution.py:396
  59.7 9.7 %collective-permute-start.17 = (bf16[144,512]{1,0:T(8,128)(2,1)S(1)}, bf16[144,512]{1,0:T(8,128)(2,1)S(1)}, u32[]{:S(2)}, u32[]{:S(2)}) collective-permute-start(bf16[144,512]{1,0:T(8,128)(2,1)S(1)} %collective-permute-done.10.rest_16_), channel_id=1, source_target_pairs={{0,8},{8,16},{16,24},{24,32},{32,40},{40,48},{48,56},{56,0},{1,9},... | collective-permute-start | bytes 442376 | tf_op jit(solution)/shard_map/ppermute | solution.py:396
  62.6 6.9 %collective-permute-start.14 = (bf16[144,512]{1,0:T(8,128)(2,1)S(1)}, bf16[144,512]{1,0:T(8,128)(2,1)S(1)}, u32[]{:S(2)}, u32[]{:S(2)}) collective-permute-start(bf16[144,512]{1,0:T(8,128)(2,1)S(1)} %collective-permute-done.13.rest_7_), channel_id=1, source_target_pairs={{0,8},{8,16},{16,24},{24,32},{32,40},{40,48},{48,56},{56,0},{1,9},... | collective-permute-start | bytes 442376 | tf_op jit(solution)/shard_map/ppermute | solution.py:396
  62.6 6.9 %collective-permute-start.16 = (bf16[144,512]{1,0:T(8,128)(2,1)S(1)}, bf16[144,512]{1,0:T(8,128)(2,1)S(1)}, u32[]{:S(2)}, u32[]{:S(2)}) collective-permute-start(bf16[144,512]{1,0:T(8,128)(2,1)S(1)} %collective-permute-done.15.rest_13_), channel_id=1, source_target_pairs={{0,56},{8,0},{16,8},{24,16},{32,24},{40,32},{48,40},{56,48},{1,57}... | collective-permute-start | bytes 442376 | tf_op jit(solution)/shard_map/ppermute | solution.py:396
  82.8 3.6 %collective-permute-start.18 = (bf16[4,272,256]{2,1,0:T(8,128)(2,1)S(1)}, bf16[4,272,256]{2,1,0:T(8,128)(2,1)S(1)}, u32[]{:S(2)}, u32[]{:S(2)}) collective-permute-start(bf16[4,272,256]{2,1,0:T(8,128)(2,1)S(1)} %get-tuple-element.44), channel_id=1, source_target_pairs={{0,1},{1,0},{2,3},{3,2},{4,5},{5,4},{6,7},{7,6},{8,9},{9,8},{10,11... | collective-permute-start | bytes 1671176 | tf_op jit(solution)/shard_map/ppermute | solution.py:392
  87.3 12.7 %collective-permute-start.19 = (bf16[272,256]{1,0:T(8,128)(2,1)S(1)}, bf16[272,256]{1,0:T(8,128)(2,1)S(1)}, u32[]{:S(2)}, u32[]{:S(2)}) collective-permute-start(bf16[272,256]{1,0:T(8,128)(2,1)S(1)} %get-tuple-element.46), channel_id=1, source_target_pairs={{0,2},{2,0},{4,6},{6,4},{1,3},{3,1},{5,7},{7,5},{8,10},{10,8},{12,... | collective-permute-start | bytes 417800 | tf_op jit(solution)/shard_map/ppermute | solution.py:392
  87.4 17.1 %collective-permute-start.20 = (bf16[272,256]{1,0:T(8,128)(2,1)S(1)}, bf16[272,256]{1,0:T(8,128)(2,1)S(1)}, u32[]{:S(2)}, u32[]{:S(2)}) collective-permute-start(bf16[272,256]{1,0:T(8,128)(2,1)S(1)} %get-tuple-element.47), channel_id=1, source_target_pairs={{0,4},{2,6},{4,0},{6,2},{1,5},{3,7},{5,1},{7,3},{8,12},{10,14},{12... | collective-permute-start | bytes 417800 | tf_op jit(solution)/shard_map/ppermute | solution.py:392
  88.1 16.4 %collective-permute-start.21 = (bf16[272,256]{1,0:T(8,128)(2,1)S(1)}, bf16[272,256]{1,0:T(8,128)(2,1)S(1)}, u32[]{:S(2)}, u32[]{:S(2)}) collective-permute-start(bf16[272,256]{1,0:T(8,128)(2,1)S(1)} %get-tuple-element.48), channel_id=1, source_target_pairs={{0,6},{2,4},{4,2},{6,0},{1,7},{3,5},{5,3},{7,1},{8,14},{10,12},{12... | collective-permute-start | bytes 417800 | tf_op jit(solution)/shard_map/ppermute | solution.py:392
  105.1 6.9 %collective-permute-start.24 = (bf16[256,256]{1,0:T(8,128)(2,1)S(1)}, bf16[256,256]{1,0:T(8,128)(2,1)S(1)}, u32[]{:S(2)}, u32[]{:S(2)}) collective-permute-start(bf16[256,256]{1,0:T(8,128)(2,1)S(1)} %heads.1.refs_0_), channel_id=1, source_target_pairs={{0,6},{2,4},{4,2},{6,0},{1,7},{3,5},{5,3},{7,1},{8,14},{10,12},{12... | collective-permute-start | bytes 393224 | tf_op jit(solution)/shard_map/ppermute | solution.py:392
  106.1 5.9 %collective-permute-start.23 = (bf16[256,256]{1,0:T(8,128)(2,1)S(1)}, bf16[256,256]{1,0:T(8,128)(2,1)S(1)}, u32[]{:S(2)}, u32[]{:S(2)}) collective-permute-start(bf16[256,256]{1,0:T(8,128)(2,1)S(1)} %heads.1.refs_0_), channel_id=1, source_target_pairs={{0,4},{2,6},{4,0},{6,2},{1,5},{3,7},{5,1},{7,3},{8,12},{10,14},{12... | collective-permute-start | bytes 393224 | tf_op jit(solution)/shard_map/ppermute | solution.py:392
  107.2 6.5 %collective-permute-start.22 = (bf16[256,256]{1,0:T(8,128)(2,1)S(1)}, bf16[256,256]{1,0:T(8,128)(2,1)S(1)}, u32[]{:S(2)}, u32[]{:S(2)}) collective-permute-start(bf16[256,256]{1,0:T(8,128)(2,1)S(1)} %heads.1.refs_0_), channel_id=1, source_target_pairs={{0,2},{2,0},{4,6},{6,4},{1,3},{3,1},{5,7},{7,5},{8,10},{10,8},{12,... | collective-permute-start | bytes 393224 | tf_op jit(solution)/shard_map/ppermute | solution.py:392
  113.8 3.7 %collective-permute-start.25 = (bf16[4,256,256]{2,1,0:T(8,128)(2,1)S(1)}, bf16[4,256,256]{2,1,0:T(8,128)(2,1)S(1)}, u32[]{:S(2)}, u32[]{:S(2)}) collective-permute-start(bf16[4,256,256]{2,1,0:T(8,128)(2,1)S(1)} %pad_maximum_fusion), channel_id=1, source_target_pairs={{0,1},{1,0},{2,3},{3,2},{4,5},{5,4},{6,7},{7,6},{8,9},{9,8},{10,11... | collective-permute-start | bytes 1572872 | tf_op jit(solution)/shard_map/ppermute | solution.py:392

commit v4 on v3

--- a/solution.py
+++ b/solution.py
@@ -35,6 +35,20 @@
 TAIL = 16
 
 
+def fill_members(meta, ids, assignment):
+    for i in range(SPARE):
+        meta[i] = 0
+
+    def one_request(i, carry):
+        owner = assignment[i]
+        rank = meta[COUNT + owner]
+        meta[COUNT + owner] = rank + 1
+        meta[jnp.where(owner == ids[0], MEMBER + rank, SPARE)] = i
+        return carry
+
+    lax.fori_loop(0, assignment.shape[0], one_request, 0)
+
+
 def fill_table(meta, ids, table, lengths, preempted, assignment, *, groups, block, pages_dev):
     group, column = ids[0], ids[1]
     blocks = table.shape[0]
@@ -42,39 +56,38 @@
     me = group * columns + column
     place = column & (NXC - 1)
     plane = lax.shift_right_logical(column, NXC.bit_length() - 1)
-    for i in range(SPARE):
-        meta[i] = 0
     meta[PLACE] = place
     meta[SPOT] = lax.shift_right_logical(place, NC.bit_length() - 1)
 
     def one_request(i, carry):
         slot = preempted[i]
         owner = assignment[i]
-        rank = meta[COUNT + owner]
-        meta[COUNT + owner] = rank + 1
         ahead = SEND + ((owner - group) & (groups - 1))
         for b in range(blocks):
             page = table[b, slot]
             holder = lax.shift_right_logical(page, pages_dev.bit_length() - 1)
             meta[jnp.where(holder == me, ahead, SPARE)] = page & (pages_dev - 1)
 
-        @pl.when(owner == group)
-        def _():
-            length = lengths[slot]
-            meta[MEMBER + rank] = i
-            for b in range(blocks):
-                holder = lax.shift_right_logical(table[b, slot], pages_dev.bit_length() - 1)
-                col = holder & (columns - 1)
-                row = lax.shift_right_logical(holder, columns.bit_length() - 1)
-                z = (lax.shift_right_logical(col, NXC.bit_length() - 1) - plane) & (NZ - 1)
-                near = (col & (NXC - 1)) == place
-                meta[jnp.where(near, RANK + z, SPARE)] = rank
-                meta[jnp.where(near, VALID + z, SPARE)] = jnp.clip(length - b * block, 0, block)
-                meta[jnp.where(col == column, PICK, SPARE)] = (group - row) & (groups - 1)
-
         return carry
 
     lax.fori_loop(0, preempted.shape[0], one_request, 0)
+
+    def one_member(rank, carry):
+        slot = preempted[meta[MEMBER + rank]]
+        length = lengths[slot]
+        for b in range(blocks):
+            holder = lax.shift_right_logical(table[b, slot], pages_dev.bit_length() - 1)
+            col = holder & (columns - 1)
+            row = lax.shift_right_logical(holder, columns.bit_length() - 1)
+            z = (lax.shift_right_logical(col, NXC.bit_length() - 1) - plane) & (NZ - 1)
+            near = (col & (NXC - 1)) == place
+            meta[jnp.where(near, RANK + z, SPARE)] = rank
+            meta[jnp.where(near, VALID + z, SPARE)] = jnp.clip(length - b * block, 0, block)
+            meta[jnp.where(col == column, PICK, SPARE)] = (group - row) & (groups - 1)
+
+        return carry
+
+    lax.fori_loop(0, preempted.shape[0] // groups, one_member, 0)
 
 
 def prepare_kernel(ids, *refs, groups):
@@ -111,10 +124,7 @@
         load.start()
     for load in first:
         load.wait()
-    fill_table(
-        meta, ids, table, lengths, preempted, assignment,
-        groups=groups, block=block, pages_dev=pages_dev,
-    )
+    fill_members(meta, ids, assignment)
     moves = []
     for r in range(rows // q_rows):
         start = pl.multiple_of(meta[MEMBER + r] * q_rows, q_rows)
@@ -129,6 +139,10 @@
             )
     for move in moves:
         move.start()
+    fill_table(
+        meta, ids, table, lengths, preempted, assignment,
+        groups=groups, block=block, pages_dev=pages_dev,
+    )
     for load in loads:
         load.wait()
     for k, out in enumerate(outs):
@@ -369,14 +383,21 @@
             out[s, z * share : (z + 1) * share, :] = tall[at : at + share, :]
 
 
-def output_kernel(meta, weights, *refs):
-    near, far, out = refs[:NX], *refs[NX:]
+def near_kernel(meta, weights, *refs):
+    near, out = refs[:NX], refs[-1]
     mixed = None
-    for s in range(NXC):
-        heads = near[s // NC][...] if s % NC == 0 else far[s // NC]
-        weight = weights[meta[PLACE] ^ s]
-        term = lax.dot_general(weight, heads, NT, preferred_element_type=F32)
+    for k in range(NX):
+        weight = weights[meta[PLACE] ^ (k * NC)]
+        term = lax.dot_general(weight, near[k][...], NT, preferred_element_type=F32)
         mixed = term if mixed is None else mixed + term
+    out[...] = mixed
+
+
+def output_kernel(meta, weights, half, far, out):
+    mixed = half[...]
+    for k in range(NX):
+        weight = weights[meta[PLACE] ^ (k * NC + 1)]
+        mixed = mixed + lax.dot_general(weight, far[k], NT, preferred_element_type=F32)
     out[...] = mixed.astype(BF16)
 
 
@@ -547,14 +568,22 @@
     heads, weights = lax.optimization_barrier((heads, weights))
     near = [heads] + [sent(heads, "x", NX, k) for k in range(1, NX)]
     far = sent(jnp.stack(near), "c", NC, 1)
+    half = pl.pallas_call(
+        near_kernel,
+        out_shape=jax.ShapeDtypeStruct((NZ * share, rows), F32),
+        in_specs=[spec(SMEM)] + [spec(VMEM)] * (NX + 1),
+        out_specs=spec(VMEM),
+        compiler_params=small,
+        name="near",
+    )(meta, weights, *near)
     mixed = pl.pallas_call(
         output_kernel,
         out_shape=jax.ShapeDtypeStruct((NZ * share, rows), BF16),
-        in_specs=[spec(SMEM)] + [spec(VMEM)] * (NX + 2),
+        in_specs=[spec(SMEM)] + [spec(VMEM)] * 3,
         out_specs=spec(VMEM),
         compiler_params=small,
         name="output",
-    )(meta, weights, *near, far)
+    )(meta, weights, half, far)
     mixed = lax.all_to_all(mixed, "z", split_axis=0, concat_axis=0, tiled=True)
     mixed = mixed.reshape(NZ, -1, rows).astype(F32).sum(axis=0)
     return mixed.T.astype(BF16)

time: 143 us -> 144 us (level)
  waiting for transfers between devices: 35.6 us -> 34 us
    pallas_call x0 -> x1, Pallas kernels: none -> 2.72 us  [local(): pl.pallas_call(near_kernel, out_shape=jax.ShapeDtypeStruct((NZ * share, r...]
    ppermute x9, waiting for transfers between devices: 21.6 us -> 20.1 us  [sent(): return lax.ppermute(x, axis, [(i, i ^ k) for i in range(size)])]
  transfers between devices with their start and end apart: 28 -> 28, of which waited for: 13 -> 12; matrix products, arithmetic and copies ran while one was open for 0% -> 0% of each run, Pallas kernels for 16% -> 17%
where the time goes in v4:
time: 144 us
  starting transfers between devices  51.8 us (36%)
  waiting for transfers between devices  34 us (24%)
  Pallas kernels  33 us (23%)
  blocking collectives  22.4 us (16%)
  local copies, waits for them, and re-layouts  1.77 us (1%)
    all_to_all x1, blocking collectives, local(): mixed = lax.all_to_all(mixed, 'z', split_axis=0, concat_axis=0, tiled=True)  22.4 us
    ppermute x14, starting transfers between devices, shifted(): return lax.ppermute(x, 'z', [(i, (i + k) % NZ) for i in range(NZ)])  21.3 us
    ppermute x9, waiting for transfers between devices, sent(): return lax.ppermute(x, axis, [(i, i ^ k) for i in range(size)])  20.1 us
    ppermute x9, starting transfers between devices, sent(): return lax.ppermute(x, axis, [(i, i ^ k) for i in range(size)])  15 us
    pallas_call x1, Pallas kernels, local(): pl.pallas_call(functools.partial(attention_kernel, scale=scale), out_shap...  12.6 us
    ppermute x14, waiting for transfers between devices, shifted(): return lax.ppermute(x, 'z', [(i, (i + k) % NZ) for i in range(NZ)])  7.11 us
    ppermute x3, waiting for transfers between devices, local(): lax.ppermute(packed[k], 'grp', [(i, (i + k) % groups) for i in range(grou...  6.83 us
    ppermute x3, starting transfers between devices, local(): lax.ppermute(packed[k], 'grp', [(i, (i + k) % groups) for i in range(grou...  5.7 us
  transfers between devices with their start and end apart: 28, of which 12 were waited for; matrix products, arithmetic and copies ran while one was open for 0% of the time, Pallas kernels for 17%

profile of v4, /device:TPU:1, one launch (start us, length us, event | category | flops | bytes accessed | tf_op | source)
XLA Modules:
  0.0 144.1 jit_solution(17081901047809610479)
XLA Ops:
  0.1 5.7 %prepare.1 = (s32[41]{0:T(128)S(1)}, bf16[4,2816,128]{2,1,0:T(8,128)(2,1)}, bf16[288,512]{1,0:T(8,128)(2,1)S(1)}, bf16[288,512]{1,0:T(8,128)(2,1)S(1)}, bf16[288...) custom-call(s32[2]{0:T(128)S(1)} %pad_add_fusion.ids, s32[8,64]{1,0:T(8,128)} %bitcast.14, s32[64]{0:T(128)} %refs_1_.1, ...), custom_call_target="tpu_custom_call" | custom-call | tf_op jit(solution)/shard_map/prepare/pallas_call | solution.py:450
  5.8 4.9 %all-to-all-start = ((bf16[4,2816,128]{2,1,0:T(8,128)(2,1)}), bf16[4,2816,128]{2,1,0:T(8,128)(2,1)}, u32[]{:S(2)}, u32[]{:S(2)}) async-start(bf16[4,2816,128]{2,1,0:T(8,128)(2,1)} %get-tuple-element.30), calls=%async_computation | async-start | bytes 5767168 | tf_op jit(solution)/shard_map/all_to_all | solution.py:479
  10.6 2.0 %collective-permute-start = (bf16[288,512]{1,0:T(8,128)(2,1)S(1)}, bf16[288,512]{1,0:T(8,128)(2,1)S(1)}, u32[]{:S(2)}, u32[]{:S(2)}) collective-permute-start(bf16[288,512]{1,0:T(8,128)(2,1)S(1)} %get-tuple-element.32), channel_id=1, source_target_pairs={{0,64},{64,128},{128,192},{192,0},{1,65},{65,129},{129,193},{193,1... | collective-permute-start | bytes 884744 | tf_op jit(solution)/shard_map/ppermute | solution.py:476
  12.6 2.6 %collective-permute-start.1 = (bf16[288,512]{1,0:T(8,128)(2,1)S(1)}, bf16[288,512]{1,0:T(8,128)(2,1)S(1)}, u32[]{:S(2)}, u32[]{:S(2)}) collective-permute-start(bf16[288,512]{1,0:T(8,128)(2,1)S(1)} %get-tuple-element.33), channel_id=1, source_target_pairs={{0,128},{64,192},{128,0},{192,64},{1,129},{65,193},{129,1},{193,65... | collective-permute-start | bytes 884744 | tf_op jit(solution)/shard_map/ppermute | solution.py:476
  16.3 3.0 %columns.1 = bf16[8,896,256]{2,1,0:T(8,128)(2,1)S(1)} custom-call(bf16[256,7168]{1,0:T(8,128)(2,1)} %w_hbm), custom_call_target="tpu_custom_call" | custom-call | tf_op jit(solution)/shard_map/columns/pallas_call | solution.py:482
  19.4 1.8 %copy-done = bf16[8,896,256]{2,1,0:T(8,128)(2,1)} copy-done((bf16[8,896,256]{2,1,0:T(8,128)(2,1)}, bf16[8,896,256]{2,1,0:T(8,128)(2,1)S(1)}, u32[]{:S(2)}) %copy-start) | copy-done | bytes 3670040
  21.2 6.8 %collective-permute-done.1.rest_2_ = bf16[288,512]{1,0:T(8,128)(2,1)S(1)} collective-permute-done((bf16[288,512]{1,0:T(8,128)(2,1)S(1)}, bf16[288,512]{1,0:T(8,128)(2,1)S(1)}, u32[]{:S(2)}, u32[]{:S(2)}) %collective-permute-start.1) | collective-permute-done | bytes 294944 | tf_op jit(solution)/shard_map/ppermute | solution.py:476
  28.6 1.7 %collective-permute-start.7 = (bf16[144,512]{1,0:T(8,128)(2,1)S(1)}, bf16[144,512]{1,0:T(8,128)(2,1)S(1)}, u32[]{:S(2)}, u32[]{:S(2)}) collective-permute-start(bf16[144,512]{1,0:T(8,128)(2,1)S(1)} %get-tuple-element.40.rest_2_), channel_id=1, source_target_pairs={{0,8},{8,16},{16,24},{24,32},{32,40},{40,48},{48,56},{56,0},{1,9},... | collective-permute-start | bytes 442376 | tf_op jit(solution)/shard_map/ppermute | solution.py:417
  30.3 4.0 %collective-permute-start.3 = (bf16[144,512]{1,0:T(8,128)(2,1)S(1)}, bf16[144,512]{1,0:T(8,128)(2,1)S(1)}, u32[]{:S(2)}, u32[]{:S(2)}) collective-permute-start(bf16[144,512]{1,0:T(8,128)(2,1)S(1)} %get-tuple-element.40.rest_2_), channel_id=1, source_target_pairs={{0,56},{8,0},{16,8},{24,16},{32,24},{40,32},{48,40},{56,48},{1,57}... | collective-permute-start | bytes 442376 | tf_op jit(solution)/shard_map/ppermute | solution.py:417
  34.3 2.7 %collective-permute-start.5 = (bf16[144,512]{1,0:T(8,128)(2,1)S(1)}, bf16[144,512]{1,0:T(8,128)(2,1)S(1)}, u32[]{:S(2)}, u32[]{:S(2)}) collective-permute-start(bf16[144,512]{1,0:T(8,128)(2,1)S(1)} %get-tuple-element.41.rest_10_), channel_id=1, source_target_pairs={{0,56},{8,0},{16,8},{24,16},{32,24},{40,32},{48,40},{56,48},{1,57}... | collective-permute-start | bytes 442376 | tf_op jit(solution)/shard_map/ppermute | solution.py:417
  37.2 2.8 %collective-permute-start.4 = (bf16[144,512]{1,0:T(8,128)(2,1)S(1)}, bf16[144,512]{1,0:T(8,128)(2,1)S(1)}, u32[]{:S(2)}, u32[]{:S(2)}) collective-permute-start(bf16[144,512]{1,0:T(8,128)(2,1)S(1)} %collective-permute-done.3.rest_3_), channel_id=1, source_target_pairs={{0,56},{8,0},{16,8},{24,16},{32,24},{40,32},{48,40},{56,48},{1,57}... | collective-permute-start | bytes 442376 | tf_op jit(solution)/shard_map/ppermute | solution.py:417
  40.5 3.0 %collective-permute-start.6 = (bf16[144,512]{1,0:T(8,128)(2,1)S(1)}, bf16[144,512]{1,0:T(8,128)(2,1)S(1)}, u32[]{:S(2)}, u32[]{:S(2)}) collective-permute-start(bf16[144,512]{1,0:T(8,128)(2,1)S(1)} %collective-permute-done.5.rest_11_), channel_id=1, source_target_pairs={{0,56},{8,0},{16,8},{24,16},{32,24},{40,32},{48,40},{56,48},{1,57}... | collective-permute-start | bytes 442376 | tf_op jit(solution)/shard_map/ppermute | solution.py:417
  43.8 3.2 %collective-permute-done.10.rest_16_ = bf16[144,512]{1,0:T(8,128)(2,1)S(1)} collective-permute-done((bf16[144,512]{1,0:T(8,128)(2,1)S(1)}, bf16[144,512]{1,0:T(8,128)(2,1)S(1)}, u32[]{:S(2)}, u32[]{:S(2)}) %collective-permute-start.10) | collective-permute-done | bytes 147488 | tf_op jit(solution)/shard_map/ppermute | solution.py:417
  47.1 2.9 %collective-permute-start.11 = (bf16[4,2816,128]{2,1,0:T(8,128)(2,1)}, bf16[4,2816,128]{2,1,0:T(8,128)(2,1)}, u32[]{:S(2)}, u32[]{:S(2)}) collective-permute-start(bf16[4,2816,128]{2,1,0:T(8,128)(2,1)} %all-to-all-done.near.rest_0_), channel_id=1, source_target_pairs={{0,1},{1,0},{2,3},{3,2},{4,5},{5,4},{6,7},{7,6},{8,9},{9,8},{10,11... | collective-permute-start | bytes 8650760 | tf_op jit(solution)/shard_map/ppermute | solution.py:413
  50.0 4.9 %all-to-all-start.1 = ((bf16[8,896,256]{2,1,0:T(8,128)(2,1)}), bf16[8,896,256]{2,1,0:T(8,128)(2,1)}, u32[]{:S(2)}, u32[]{:S(2)}) async-start(bf16[8,896,256]{2,1,0:T(8,128)(2,1)} %copy-done), calls=%async_computation.1 | async-start | bytes 7340032 | tf_op jit(solution)/shard_map/all_to_all | solution.py:516
  54.9 3.0 %collective-permute-start.15 = (bf16[144,512]{1,0:T(8,128)(2,1)S(1)}, bf16[144,512]{1,0:T(8,128)(2,1)S(1)}, u32[]{:S(2)}, u32[]{:S(2)}) collective-permute-start(bf16[144,512]{1,0:T(8,128)(2,1)S(1)} %collective-permute-done.6.rest_12_), channel_id=1, source_target_pairs={{0,56},{8,0},{16,8},{24,16},{32,24},{40,32},{48,40},{56,48},{1,57}... | collective-permute-start | bytes 442376 | tf_op jit(solution)/shard_map/ppermute | solution.py:417
  57.9 1.4 %collective-permute-start.12 = (bf16[144,512]{1,0:T(8,128)(2,1)S(1)}, bf16[144,512]{1,0:T(8,128)(2,1)S(1)}, u32[]{:S(2)}, u32[]{:S(2)}) collective-permute-start(bf16[144,512]{1,0:T(8,128)(2,1)S(1)} %collective-permute-done.4.rest_4_), channel_id=1, source_target_pairs={{0,56},{8,0},{16,8},{24,16},{32,24},{40,32},{48,40},{56,48},{1,57}... | collective-permute-start | bytes 442376 | tf_op jit(solution)/shard_map/ppermute | solution.py:417
  59.3 2.8 %collective-permute-done.13.rest_7_ = bf16[144,512]{1,0:T(8,128)(2,1)S(1)} collective-permute-done((bf16[144,512]{1,0:T(8,128)(2,1)S(1)}, bf16[144,512]{1,0:T(8,128)(2,1)S(1)}, u32[]{:S(2)}, u32[]{:S(2)}) %collective-permute-start.13) | collective-permute-done | bytes 147488 | tf_op jit(solution)/shard_map/ppermute | solution.py:417
  62.2 2.7 %collective-permute-start.16 = (bf16[144,512]{1,0:T(8,128)(2,1)S(1)}, bf16[144,512]{1,0:T(8,128)(2,1)S(1)}, u32[]{:S(2)}, u32[]{:S(2)}) collective-permute-start(bf16[144,512]{1,0:T(8,128)(2,1)S(1)} %collective-permute-done.15.rest_13_), channel_id=1, source_target_pairs={{0,56},{8,0},{16,8},{24,16},{32,24},{40,32},{48,40},{56,48},{1,57}... | collective-permute-start | bytes 442376 | tf_op jit(solution)/shard_map/ppermute | solution.py:417
  64.9 4.2 %query.1 = bf16[8,512,640]{2,1,0:T(8,128)(2,1)S(1)} custom-call(s32[41]{0:T(128)S(1)} %get-tuple-element.29.meta, bf16[4,2816,128]{2,1,0:T(8,128)(2,1)} %all-to-all-done.near.rest_0_, bf16[4,2816,128]{2,1,0:T(8,128)(2,1)} %collective-permute-done.11.far.rest_1_), custom_call_target="tpu_custom_call" | custom-call | tf_op jit(solution)/shard_map/query/pallas_call | solution.py:518
  69.1 12.6 %attention.1 = (bf16[4,272,256]{2,1,0:T(8,128)(2,1)S(1)}, bf16[4,272,256]{2,1,0:T(8,128)(2,1)S(1)}) custom-call(s32[41]{0:T(128)S(1)} %get-tuple-element.29.meta, bf16[8,512,640]{2,1,0:T(8,128)(2,1)S(1)} %query.1, bf16[4,2816,128]{2,1,0:T(8,128)(2,1)} %all-to-all-done.near.rest_0_, bf16[4,2816,128]{2,1,0:T(8,128)(2,1)} %collective-permute-done.11.far.rest_1_, ...), custom_call_target="tpu_custom_call" | custom-call | tf_op jit(solution)/shard_map/attention/pallas_call | solution.py:532
  81.7 2.7 %collective-permute-start.18 = (bf16[4,272,256]{2,1,0:T(8,128)(2,1)S(1)}, bf16[4,272,256]{2,1,0:T(8,128)(2,1)S(1)}, u32[]{:S(2)}, u32[]{:S(2)}) collective-permute-start(bf16[4,272,256]{2,1,0:T(8,128)(2,1)S(1)} %get-tuple-element.44), channel_id=1, source_target_pairs={{0,1},{1,0},{2,3},{3,2},{4,5},{5,4},{6,7},{7,6},{8,9},{9,8},{10,11... | collective-permute-start | bytes 1671176 | tf_op jit(solution)/shard_map/ppermute | solution.py:413
  84.5 1.6 %collective-permute-done.18.got = bf16[4,272,256]{2,1,0:T(8,128)(2,1)S(1)} collective-permute-done((bf16[4,272,256]{2,1,0:T(8,128)(2,1)S(1)}, bf16[4,272,256]{2,1,0:T(8,128)(2,1)S(1)}, u32[]{:S(2)}, u32[]{:S(2)}) %collective-permute-start.18) | collective-permute-done | bytes 557088 | tf_op jit(solution)/shard_map/ppermute | solution.py:413
  87.5 3.3 %collective-permute-start.21 = (bf16[272,256]{1,0:T(8,128)(2,1)S(1)}, bf16[272,256]{1,0:T(8,128)(2,1)S(1)}, u32[]{:S(2)}, u32[]{:S(2)}) collective-permute-start(bf16[272,256]{1,0:T(8,128)(2,1)S(1)} %get-tuple-element.48), channel_id=1, source_target_pairs={{0,6},{2,4},{4,2},{6,0},{1,7},{3,5},{5,3},{7,1},{8,14},{10,12},{12... | collective-permute-start | bytes 417800 | tf_op jit(solution)/shard_map/ppermute | solution.py:413
  90.9 8.7 %collective-permute-done.19.refs_1_ = bf16[272,256]{1,0:T(8,128)(2,1)S(1)} collective-permute-done((bf16[272,256]{1,0:T(8,128)(2,1)S(1)}, bf16[272,256]{1,0:T(8,128)(2,1)S(1)}, u32[]{:S(2)}, u32[]{:S(2)}) %collective-permute-start.19) | collective-permute-done | bytes 139296 | tf_op jit(solution)/shard_map/ppermute | solution.py:413
  99.6 4.5 %collective-permute-done.20.refs_2_ = bf16[272,256]{1,0:T(8,128)(2,1)S(1)} collective-permute-done((bf16[272,256]{1,0:T(8,128)(2,1)S(1)}, bf16[272,256]{1,0:T(8,128)(2,1)S(1)}, u32[]{:S(2)}, u32[]{:S(2)}) %collective-permute-start.20) | collective-permute-done | bytes 139296 | tf_op jit(solution)/shard_map/ppermute | solution.py:413
  108.0 3.6 %collective-permute-done.24.refs_3_ = bf16[256,256]{1,0:T(8,128)(2,1)S(1)} collective-permute-done((bf16[256,256]{1,0:T(8,128)(2,1)S(1)}, bf16[256,256]{1,0:T(8,128)(2,1)S(1)}, u32[]{:S(2)}, u32[]{:S(2)}) %collective-permute-start.24) | collective-permute-done | bytes 131104 | tf_op jit(solution)/shard_map/ppermute | solution.py:413
  111.6 1.7 %collective-permute-done.22.refs_1_ = bf16[256,256]{1,0:T(8,128)(2,1)S(1)} collective-permute-done((bf16[256,256]{1,0:T(8,128)(2,1)S(1)}, bf16[256,256]{1,0:T(8,128)(2,1)S(1)}, u32[]{:S(2)}, u32[]{:S(2)}) %collective-permute-start.22) | collective-permute-done | bytes 131104 | tf_op jit(solution)/shard_map/ppermute | solution.py:413
  113.4 2.1 %collective-permute-start.25 = (bf16[4,256,256]{2,1,0:T(8,128)(2,1)S(1)}, bf16[4,256,256]{2,1,0:T(8,128)(2,1)S(1)}, u32[]{:S(2)}, u32[]{:S(2)}) collective-permute-start(bf16[4,256,256]{2,1,0:T(8,128)(2,1)S(1)} %pad_maximum_fusion), channel_id=1, source_target_pairs={{0,1},{1,0},{2,3},{3,2},{4,5},{5,4},{6,7},{7,6},{8,9},{9,8},{10,11... | collective-permute-start | bytes 1572872 | tf_op jit(solution)/shard_map/ppermute | solution.py:413
  115.5 2.7 %near.1.half = f32[896,256]{1,0:T(8,128)S(1)} custom-call(s32[41]{0:T(128)S(1)} %get-tuple-element.29.meta, bf16[8,896,256]{2,1,0:T(8,128)(2,1)} %all-to-all-done.1.weights, bf16[256,256]{1,0:T(8,128)(2,1)S(1)} %heads.1.refs_0_, bf16[256,256]{1,0:T(8,128)(2,1)S(1)} %collective-permute-done.22.refs_1_, bf16[256,256]{1,0:T(8,128)(2,1)S(1)} %collective-permute-done.23.refs_2_, ...), custom_call_target="tpu_custom_call" | custom-call | tf_op jit(solution)/shard_map/near/pallas_call | solution.py:571
  118.2 2.7 %output.1 = bf16[896,256]{1,0:T(8,128)(2,1)S(1)} custom-call(s32[41]{0:T(128)S(1)} %get-tuple-element.29.meta, bf16[8,896,256]{2,1,0:T(8,128)(2,1)} %all-to-all-done.1.weights, f32[896,256]{1,0:T(8,128)S(1)} %near.1.half, bf16[4,256,256]{2,1,0:T(8,128)(2,1)S(1)} %collective-permute-done.25.far), custom_call_target="tpu_custom_call" | custom-call | tf_op jit(solution)/shard_map/output/pallas_call | solution.py:579
  120.9 22.4 %all_to_all.19 = bf16[8,112,256]{2,1,0:T(8,128)(2,1)S(1)} all-to-all(bf16[8,112,256]{2,1,0:T(8,128)(2,1)S(1)} %bitcast.9), channel_id=1, replica_groups=mesh['grp'=4,'z'=8,'x'=4,'c'=2] {'z'}, dimensions={0} | all-to-all | bytes 917504 | tf_op jit(solution)/shard_map/all_to_all | solution.py:587
  (39 shorter events, 9.0 us)
Async XLA Ops:
  5.8 41.3 %all-to-all-start = ((bf16[4,2816,128]{2,1,0:T(8,128)(2,1)}), bf16[4,2816,128]{2,1,0:T(8,128)(2,1)}, u32[]{:S(2)}, u32[]{:S(2)}) async-start(bf16[4,2816,128]{2,1,0:T(8,128)(2,1)} %get-tuple-element.30), calls=%async_computation | async-start | bytes 5767168 | tf_op jit(solution)/shard_map/all_to_all | solution.py:479
  10.6 10.5 %collective-permute-start = (bf16[288,512]{1,0:T(8,128)(2,1)S(1)}, bf16[288,512]{1,0:T(8,128)(2,1)S(1)}, u32[]{:S(2)}, u32[]{:S(2)}) collective-permute-start(bf16[288,512]{1,0:T(8,128)(2,1)S(1)} %get-tuple-element.32), channel_id=1, source_target_pairs={{0,64},{64,128},{128,192},{192,0},{1,65},{65,129},{129,193},{193,1... | collective-permute-start | bytes 884744 | tf_op jit(solution)/shard_map/ppermute | solution.py:476
  12.6 15.4 %collective-permute-start.1 = (bf16[288,512]{1,0:T(8,128)(2,1)S(1)}, bf16[288,512]{1,0:T(8,128)(2,1)S(1)}, u32[]{:S(2)}, u32[]{:S(2)}) collective-permute-start(bf16[288,512]{1,0:T(8,128)(2,1)S(1)} %get-tuple-element.33), channel_id=1, source_target_pairs={{0,128},{64,192},{128,0},{192,64},{1,129},{65,193},{129,1},{193,65... | collective-permute-start | bytes 884744 | tf_op jit(solution)/shard_map/ppermute | solution.py:476
  15.3 12.7 %collective-permute-start.2 = (bf16[288,512]{1,0:T(8,128)(2,1)S(1)}, bf16[288,512]{1,0:T(8,128)(2,1)S(1)}, u32[]{:S(2)}, u32[]{:S(2)}) collective-permute-start(bf16[288,512]{1,0:T(8,128)(2,1)S(1)} %get-tuple-element.34), channel_id=1, source_target_pairs={{0,192},{64,0},{128,64},{192,128},{1,193},{65,1},{129,65},{193,129... | collective-permute-start | bytes 884744 | tf_op jit(solution)/shard_map/ppermute | solution.py:476
  19.4 1.8 %copy-start = (bf16[8,896,256]{2,1,0:T(8,128)(2,1)}, bf16[8,896,256]{2,1,0:T(8,128)(2,1)S(1)}, u32[]{:S(2)}) copy-start(bf16[8,896,256]{2,1,0:T(8,128)(2,1)S(1)} %columns.1) | copy-start | bytes 11010052
  28.6 8.6 %collective-permute-start.7 = (bf16[144,512]{1,0:T(8,128)(2,1)S(1)}, bf16[144,512]{1,0:T(8,128)(2,1)S(1)}, u32[]{:S(2)}, u32[]{:S(2)}) collective-permute-start(bf16[144,512]{1,0:T(8,128)(2,1)S(1)} %get-tuple-element.40.rest_2_), channel_id=1, source_target_pairs={{0,8},{8,16},{16,24},{24,32},{32,40},{40,48},{48,56},{56,0},{1,9},... | collective-permute-start | bytes 442376 | tf_op jit(solution)/shard_map/ppermute | solution.py:417
  30.3 6.9 %collective-permute-start.3 = (bf16[144,512]{1,0:T(8,128)(2,1)S(1)}, bf16[144,512]{1,0:T(8,128)(2,1)S(1)}, u32[]{:S(2)}, u32[]{:S(2)}) collective-permute-start(bf16[144,512]{1,0:T(8,128)(2,1)S(1)} %get-tuple-element.40.rest_2_), channel_id=1, source_target_pairs={{0,56},{8,0},{16,8},{24,16},{32,24},{40,32},{48,40},{56,48},{1,57}... | collective-permute-start | bytes 442376 | tf_op jit(solution)/shard_map/ppermute | solution.py:417
  34.3 6.2 %collective-permute-start.9 = (bf16[144,512]{1,0:T(8,128)(2,1)S(1)}, bf16[144,512]{1,0:T(8,128)(2,1)S(1)}, u32[]{:S(2)}, u32[]{:S(2)}) collective-permute-start(bf16[144,512]{1,0:T(8,128)(2,1)S(1)} %get-tuple-element.41.rest_10_), channel_id=1, source_target_pairs={{0,8},{8,16},{16,24},{24,32},{32,40},{40,48},{48,56},{56,0},{1,9},... | collective-permute-start | bytes 442376 | tf_op jit(solution)/shard_map/ppermute | solution.py:417
  34.3 6.2 %collective-permute-start.5 = (bf16[144,512]{1,0:T(8,128)(2,1)S(1)}, bf16[144,512]{1,0:T(8,128)(2,1)S(1)}, u32[]{:S(2)}, u32[]{:S(2)}) collective-permute-start(bf16[144,512]{1,0:T(8,128)(2,1)S(1)} %get-tuple-element.41.rest_10_), channel_id=1, source_target_pairs={{0,56},{8,0},{16,8},{24,16},{32,24},{40,32},{48,40},{56,48},{1,57}... | collective-permute-start | bytes 442376 | tf_op jit(solution)/shard_map/ppermute | solution.py:417
  37.2 6.6 %collective-permute-start.8 = (bf16[144,512]{1,0:T(8,128)(2,1)S(1)}, bf16[144,512]{1,0:T(8,128)(2,1)S(1)}, u32[]{:S(2)}, u32[]{:S(2)}) collective-permute-start(bf16[144,512]{1,0:T(8,128)(2,1)S(1)} %collective-permute-done.7.rest_9_), channel_id=1, source_target_pairs={{0,8},{8,16},{16,24},{24,32},{32,40},{40,48},{48,56},{56,0},{1,9},... | collective-permute-start | bytes 442376 | tf_op jit(solution)/shard_map/ppermute | solution.py:417
  37.2 6.6 %collective-permute-start.4 = (bf16[144,512]{1,0:T(8,128)(2,1)S(1)}, bf16[144,512]{1,0:T(8,128)(2,1)S(1)}, u32[]{:S(2)}, u32[]{:S(2)}) collective-permute-start(bf16[144,512]{1,0:T(8,128)(2,1)S(1)} %collective-permute-done.3.rest_3_), channel_id=1, source_target_pairs={{0,56},{8,0},{16,8},{24,16},{32,24},{40,32},{48,40},{56,48},{1,57}... | collective-permute-start | bytes 442376 | tf_op jit(solution)/shard_map/ppermute | solution.py:417
  40.5 6.5 %collective-permute-start.10 = (bf16[144,512]{1,0:T(8,128)(2,1)S(1)}, bf16[144,512]{1,0:T(8,128)(2,1)S(1)}, u32[]{:S(2)}, u32[]{:S(2)}) collective-permute-start(bf16[144,512]{1,0:T(8,128)(2,1)S(1)} %collective-permute-done.9.rest_17_), channel_id=1, source_target_pairs={{0,8},{8,16},{16,24},{24,32},{32,40},{40,48},{48,56},{56,0},{1,9},... | collective-permute-start | bytes 442376 | tf_op jit(solution)/shard_map/ppermute | solution.py:417
  40.5 6.6 %collective-permute-start.6 = (bf16[144,512]{1,0:T(8,128)(2,1)S(1)}, bf16[144,512]{1,0:T(8,128)(2,1)S(1)}, u32[]{:S(2)}, u32[]{:S(2)}) collective-permute-start(bf16[144,512]{1,0:T(8,128)(2,1)S(1)} %collective-permute-done.5.rest_11_), channel_id=1, source_target_pairs={{0,56},{8,0},{16,8},{24,16},{32,24},{40,32},{48,40},{56,48},{1,57}... | collective-permute-start | bytes 442376 | tf_op jit(solution)/shard_map/ppermute | solution.py:417
  47.1 17.8 %collective-permute-start.11 = (bf16[4,2816,128]{2,1,0:T(8,128)(2,1)}, bf16[4,2816,128]{2,1,0:T(8,128)(2,1)}, u32[]{:S(2)}, u32[]{:S(2)}) collective-permute-start(bf16[4,2816,128]{2,1,0:T(8,128)(2,1)} %all-to-all-done.near.rest_0_), channel_id=1, source_target_pairs={{0,1},{1,0},{2,3},{3,2},{4,5},{5,4},{6,7},{7,6},{8,9},{9,8},{10,11... | collective-permute-start | bytes 8650760 | tf_op jit(solution)/shard_map/ppermute | solution.py:413
  50.0 54.7 %all-to-all-start.1 = ((bf16[8,896,256]{2,1,0:T(8,128)(2,1)}), bf16[8,896,256]{2,1,0:T(8,128)(2,1)}, u32[]{:S(2)}, u32[]{:S(2)}) async-start(bf16[8,896,256]{2,1,0:T(8,128)(2,1)} %copy-done), calls=%async_computation.1 | async-start | bytes 7340032 | tf_op jit(solution)/shard_map/all_to_all | solution.py:516
  54.9 7.3 %collective-permute-start.13 = (bf16[144,512]{1,0:T(8,128)(2,1)S(1)}, bf16[144,512]{1,0:T(8,128)(2,1)S(1)}, u32[]{:S(2)}, u32[]{:S(2)}) collective-permute-start(bf16[144,512]{1,0:T(8,128)(2,1)S(1)} %collective-permute-done.8.rest_8_), channel_id=1, source_target_pairs={{0,8},{8,16},{16,24},{24,32},{32,40},{40,48},{48,56},{56,0},{1,9},... | collective-permute-start | bytes 442376 | tf_op jit(solution)/shard_map/ppermute | solution.py:417
  54.9 7.3 %collective-permute-start.15 = (bf16[144,512]{1,0:T(8,128)(2,1)S(1)}, bf16[144,512]{1,0:T(8,128)(2,1)S(1)}, u32[]{:S(2)}, u32[]{:S(2)}) collective-permute-start(bf16[144,512]{1,0:T(8,128)(2,1)S(1)} %collective-permute-done.6.rest_12_), channel_id=1, source_target_pairs={{0,56},{8,0},{16,8},{24,16},{32,24},{40,32},{48,40},{56,48},{1,57}... | collective-permute-start | bytes 442376 | tf_op jit(solution)/shard_map/ppermute | solution.py:417
  57.9 11.2 %collective-permute-start.12 = (bf16[144,512]{1,0:T(8,128)(2,1)S(1)}, bf16[144,512]{1,0:T(8,128)(2,1)S(1)}, u32[]{:S(2)}, u32[]{:S(2)}) collective-permute-start(bf16[144,512]{1,0:T(8,128)(2,1)S(1)} %collective-permute-done.4.rest_4_), channel_id=1, source_target_pairs={{0,56},{8,0},{16,8},{24,16},{32,24},{40,32},{48,40},{56,48},{1,57}... | collective-permute-start | bytes 442376 | tf_op jit(solution)/shard_map/ppermute | solution.py:417
  59.3 9.7 %collective-permute-start.17 = (bf16[144,512]{1,0:T(8,128)(2,1)S(1)}, bf16[144,512]{1,0:T(8,128)(2,1)S(1)}, u32[]{:S(2)}, u32[]{:S(2)}) collective-permute-start(bf16[144,512]{1,0:T(8,128)(2,1)S(1)} %collective-permute-done.10.rest_16_), channel_id=1, source_target_pairs={{0,8},{8,16},{16,24},{24,32},{32,40},{40,48},{48,56},{56,0},{1,9},... | collective-permute-start | bytes 442376 | tf_op jit(solution)/shard_map/ppermute | solution.py:417
  62.2 6.9 %collective-permute-start.14 = (bf16[144,512]{1,0:T(8,128)(2,1)S(1)}, bf16[144,512]{1,0:T(8,128)(2,1)S(1)}, u32[]{:S(2)}, u32[]{:S(2)}) collective-permute-start(bf16[144,512]{1,0:T(8,128)(2,1)S(1)} %collective-permute-done.13.rest_7_), channel_id=1, source_target_pairs={{0,8},{8,16},{16,24},{24,32},{32,40},{40,48},{48,56},{56,0},{1,9},... | collective-permute-start | bytes 442376 | tf_op jit(solution)/shard_map/ppermute | solution.py:417
  62.2 6.9 %collective-permute-start.16 = (bf16[144,512]{1,0:T(8,128)(2,1)S(1)}, bf16[144,512]{1,0:T(8,128)(2,1)S(1)}, u32[]{:S(2)}, u32[]{:S(2)}) collective-permute-start(bf16[144,512]{1,0:T(8,128)(2,1)S(1)} %collective-permute-done.15.rest_13_), channel_id=1, source_target_pairs={{0,56},{8,0},{16,8},{24,16},{32,24},{40,32},{48,40},{56,48},{1,57}... | collective-permute-start | bytes 442376 | tf_op jit(solution)/shard_map/ppermute | solution.py:417
  81.7 4.3 %collective-permute-start.18 = (bf16[4,272,256]{2,1,0:T(8,128)(2,1)S(1)}, bf16[4,272,256]{2,1,0:T(8,128)(2,1)S(1)}, u32[]{:S(2)}, u32[]{:S(2)}) collective-permute-start(bf16[4,272,256]{2,1,0:T(8,128)(2,1)S(1)} %get-tuple-element.44), channel_id=1, source_target_pairs={{0,1},{1,0},{2,3},{3,2},{4,5},{5,4},{6,7},{7,6},{8,9},{9,8},{10,11... | collective-permute-start | bytes 1671176 | tf_op jit(solution)/shard_map/ppermute | solution.py:413
  86.9 12.7 %collective-permute-start.19 = (bf16[272,256]{1,0:T(8,128)(2,1)S(1)}, bf16[272,256]{1,0:T(8,128)(2,1)S(1)}, u32[]{:S(2)}, u32[]{:S(2)}) collective-permute-start(bf16[272,256]{1,0:T(8,128)(2,1)S(1)} %get-tuple-element.46), channel_id=1, source_target_pairs={{0,2},{2,0},{4,6},{6,4},{1,3},{3,1},{5,7},{7,5},{8,10},{10,8},{12,... | collective-permute-start | bytes 417800 | tf_op jit(solution)/shard_map/ppermute | solution.py:413
  87.0 17.1 %collective-permute-start.20 = (bf16[272,256]{1,0:T(8,128)(2,1)S(1)}, bf16[272,256]{1,0:T(8,128)(2,1)S(1)}, u32[]{:S(2)}, u32[]{:S(2)}) collective-permute-start(bf16[272,256]{1,0:T(8,128)(2,1)S(1)} %get-tuple-element.47), channel_id=1, source_target_pairs={{0,4},{2,6},{4,0},{6,2},{1,5},{3,7},{5,1},{7,3},{8,12},{10,14},{12... | collective-permute-start | bytes 417800 | tf_op jit(solution)/shard_map/ppermute | solution.py:413
  87.5 16.6 %collective-permute-start.21 = (bf16[272,256]{1,0:T(8,128)(2,1)S(1)}, bf16[272,256]{1,0:T(8,128)(2,1)S(1)}, u32[]{:S(2)}, u32[]{:S(2)}) collective-permute-start(bf16[272,256]{1,0:T(8,128)(2,1)S(1)} %get-tuple-element.48), channel_id=1, source_target_pairs={{0,6},{2,4},{4,2},{6,0},{1,7},{3,5},{5,3},{7,1},{8,14},{10,12},{12... | collective-permute-start | bytes 417800 | tf_op jit(solution)/shard_map/ppermute | solution.py:413
  104.7 6.9 %collective-permute-start.24 = (bf16[256,256]{1,0:T(8,128)(2,1)S(1)}, bf16[256,256]{1,0:T(8,128)(2,1)S(1)}, u32[]{:S(2)}, u32[]{:S(2)}) collective-permute-start(bf16[256,256]{1,0:T(8,128)(2,1)S(1)} %heads.1.refs_0_), channel_id=1, source_target_pairs={{0,6},{2,4},{4,2},{6,0},{1,7},{3,5},{5,3},{7,1},{8,14},{10,12},{12... | collective-permute-start | bytes 393224 | tf_op jit(solution)/shard_map/ppermute | solution.py:413
  105.6 5.9 %collective-permute-start.23 = (bf16[256,256]{1,0:T(8,128)(2,1)S(1)}, bf16[256,256]{1,0:T(8,128)(2,1)S(1)}, u32[]{:S(2)}, u32[]{:S(2)}) collective-permute-start(bf16[256,256]{1,0:T(8,128)(2,1)S(1)} %heads.1.refs_0_), channel_id=1, source_target_pairs={{0,4},{2,6},{4,0},{6,2},{1,5},{3,7},{5,1},{7,3},{8,12},{10,14},{12... | collective-permute-start | bytes 393224 | tf_op jit(solution)/shard_map/ppermute | solution.py:413
  106.8 6.5 %collective-permute-start.22 = (bf16[256,256]{1,0:T(8,128)(2,1)S(1)}, bf16[256,256]{1,0:T(8,128)(2,1)S(1)}, u32[]{:S(2)}, u32[]{:S(2)}) collective-permute-start(bf16[256,256]{1,0:T(8,128)(2,1)S(1)} %heads.1.refs_0_), channel_id=1, source_target_pairs={{0,2},{2,0},{4,6},{6,4},{1,3},{3,1},{5,7},{7,5},{8,10},{10,8},{12,... | collective-permute-start | bytes 393224 | tf_op jit(solution)/shard_map/ppermute | solution.py:413
  113.4 4.8 %collective-permute-start.25 = (bf16[4,256,256]{2,1,0:T(8,128)(2,1)S(1)}, bf16[4,256,256]{2,1,0:T(8,128)(2,1)S(1)}, u32[]{:S(2)}, u32[]{:S(2)}) collective-permute-start(bf16[4,256,256]{2,1,0:T(8,128)(2,1)S(1)} %pad_maximum_fusion), channel_id=1, source_target_pairs={{0,1},{1,0},{2,3},{3,2},{4,5},{5,4},{6,7},{7,6},{8,9},{9,8},{10,11... | collective-permute-start | bytes 1572872 | tf_op jit(solution)/shard_map/ppermute | solution.py:413

commit v5 on v4

--- a/solution.py
+++ b/solution.py
@@ -90,18 +90,12 @@
     lax.fori_loop(0, preempted.shape[0] // groups, one_member, 0)
 
 
-def prepare_kernel(ids, *refs, groups):
-    tables_hbm, (latent_hbm, rope_hbm, q_nope, q_rope, w_uk, w_uv), rest = refs[:4], refs[4:10], refs[10:]
-    meta, copies = rest[:2]
-    outs = rest[2 : 2 + groups]
-    table, lengths, preempted, assignment, latent, rope, sem, row_sem, table_sem, w_sem = rest[2 + groups :]
-    tables = (table, lengths, preempted, assignment)
-    pages_dev, block, _ = latent.shape
-    half = rope.shape[1] // 2
-    q_rows = q_nope.shape[0] // preempted.shape[0]
+def package_kernel(ids, owners, q_nope, q_rope, w_uk, w_uv, copies, assignment, meta, row_sem, w_sem, sem):
     depth = w_uk.shape[0]
     queries = copies.shape[1] - 4 * depth
     rows = queries // 3
+    q_rows = q_nope.shape[0] // assignment.shape[0]
+    first = pltpu.make_async_copy(owners, assignment, sem)
     for_all = [
         pltpu.make_async_copy(
             w.at[:, pl.ds(h * DN, DN)],
@@ -112,18 +106,9 @@
         for h in range(2)
         for k in range(copies.shape[0])
     ]
-    loads = [
-        pltpu.make_async_copy(latent_hbm, latent, sem.at[0]),
-        pltpu.make_async_copy(rope_hbm, rope, sem.at[1]),
-    ]
-    first = [
-        pltpu.make_async_copy(src, dst, table_sem.at[i])
-        for i, (src, dst) in enumerate(zip(tables_hbm, tables))
-    ]
-    for load in first + loads + for_all:
+    for load in [first] + for_all:
         load.start()
-    for load in first:
-        load.wait()
+    first.wait()
     fill_members(meta, ids, assignment)
     moves = []
     for r in range(rows // q_rows):
@@ -139,6 +124,34 @@
             )
     for move in moves:
         move.start()
+    for move in moves:
+        move.wait()
+    for k in range(1, copies.shape[0]):
+        copies[k, :queries, :] = copies[0, :queries, :]
+    for load in for_all:
+        load.wait()
+
+
+def prepare_kernel(ids, *refs, groups):
+    tables_hbm, (latent_hbm, rope_hbm), rest = refs[:4], refs[4:6], refs[6:]
+    meta, outs = rest[0], rest[1 : 1 + groups]
+    table, lengths, preempted, assignment, latent, rope, sem, table_sem = rest[1 + groups :]
+    tables = (table, lengths, preempted, assignment)
+    pages_dev, block, _ = latent.shape
+    half = rope.shape[1] // 2
+    loads = [
+        pltpu.make_async_copy(latent_hbm, latent, sem.at[0]),
+        pltpu.make_async_copy(rope_hbm, rope, sem.at[1]),
+    ]
+    first = [
+        pltpu.make_async_copy(src, dst, table_sem.at[i])
+        for i, (src, dst) in enumerate(zip(tables_hbm, tables))
+    ]
+    for load in first + loads:
+        load.start()
+    for load in first:
+        load.wait()
+    fill_members(meta, ids, assignment)
     fill_table(
         meta, ids, table, lengths, preempted, assignment,
         groups=groups, block=block, pages_dev=pages_dev,
@@ -150,12 +163,6 @@
         out[:block, :] = latent[page]
         out[block:, :block] = rope[page, :half, :]
         out[block:, block:] = rope[page, half:, :]
-    for move in moves:
-        move.wait()
-    for k in range(1, copies.shape[0]):
-        copies[k, :queries, :] = copies[0, :queries, :]
-    for load in for_all:
-        load.wait()
 
 
 def pick_kernel(meta, *rest):
@@ -383,22 +390,18 @@
             out[s, z * share : (z + 1) * share, :] = tall[at : at + share, :]
 
 
-def near_kernel(meta, weights, *refs):
-    near, out = refs[:NX], refs[-1]
-    mixed = None
-    for k in range(NX):
-        weight = weights[meta[PLACE] ^ (k * NC)]
-        term = lax.dot_general(weight, near[k][...], NT, preferred_element_type=F32)
-        mixed = term if mixed is None else mixed + term
-    out[...] = mixed
-
-
-def output_kernel(meta, weights, half, far, out):
-    mixed = half[...]
-    for k in range(NX):
-        weight = weights[meta[PLACE] ^ (k * NC + 1)]
-        mixed = mixed + lax.dot_general(weight, far[k], NT, preferred_element_type=F32)
-    out[...] = mixed.astype(BF16)
+def output_kernel(meta, weights, *refs):
+    near, far, out = refs[:NX], *refs[NX:]
+    block = out.shape[0] // NX
+    for i in range(NX):
+        part = slice(i * block, (i + 1) * block)
+        mixed = None
+        for s in range(NXC):
+            heads = near[s // NC][...] if s % NC == 0 else far[s // NC]
+            weight = weights[meta[PLACE] ^ s, part, :]
+            term = lax.dot_general(weight, heads, NT, preferred_element_type=F32)
+            mixed = term if mixed is None else mixed + term
+        out[part, :] = mixed.astype(BF16)
 
 
 def after(x, *others):
@@ -447,15 +450,27 @@
     small = pltpu.CompilerParams(vmem_limit_bytes=16 << 20)
     ids = jnp.stack([group, column]).astype(jnp.int32)
     page_type = jax.ShapeDtypeStruct((page_rows, width), BF16)
-    meta, copies, *packed = pl.pallas_call(
+    copies = pl.pallas_call(
+        package_kernel,
+        out_shape=jax.ShapeDtypeStruct((NX, 3 * rows + 4 * width, DN), BF16),
+        in_specs=[spec(SMEM)] + [spec(pltpu.HBM)] * 5,
+        out_specs=spec(VMEM),
+        scratch_shapes=[
+            SMEM(assignment.shape, jnp.int32),
+            SMEM((META,), jnp.int32),
+            pltpu.SemaphoreType.DMA((per_group, 3)),
+            pltpu.SemaphoreType.DMA((NX, 4)),
+            pltpu.SemaphoreType.DMA,
+        ],
+        compiler_params=small,
+        name="package",
+    )(ids, *[in_hbm(a) for a in (assignment, q_nope, q_rope, w_uk, w_uv)])
+
+    meta, *packed = pl.pallas_call(
         functools.partial(prepare_kernel, groups=groups),
-        out_shape=[
-            jax.ShapeDtypeStruct((META,), jnp.int32),
-            jax.ShapeDtypeStruct((NX, 3 * rows + 4 * width, DN), BF16),
-        ]
-        + [page_type] * groups,
-        in_specs=[spec(SMEM)] + [spec(pltpu.HBM)] * 10,
-        out_specs=[spec(SMEM)] + [spec(VMEM)] * (1 + groups),
+        out_shape=[jax.ShapeDtypeStruct((META,), jnp.int32)] + [page_type] * groups,
+        in_specs=[spec(SMEM)] + [spec(pltpu.HBM)] * 6,
+        out_specs=[spec(SMEM)] + [spec(VMEM)] * groups,
         scratch_shapes=[
             SMEM(block_table.T.shape, jnp.int32),
             SMEM(lengths.shape, jnp.int32),
@@ -464,13 +479,11 @@
             VMEM(pool_latent.shape, BF16),
             VMEM(pool_rope.shape, BF16),
             pltpu.SemaphoreType.DMA((2,)),
-            pltpu.SemaphoreType.DMA((per_group, 3)),
             pltpu.SemaphoreType.DMA((4,)),
-            pltpu.SemaphoreType.DMA((NX, 4)),
         ],
         compiler_params=small,
         name="prepare",
-    )(ids, *[in_hbm(a) for a in (block_table.T, lengths, preempted, assignment, pool_latent, pool_rope, q_nope, q_rope, w_uk, w_uv)])
+    )(ids, *[in_hbm(a) for a in (block_table.T, lengths, preempted, assignment, pool_latent, pool_rope)])
 
     arrived = [packed[0]] + [
         lax.ppermute(packed[k], "grp", [(i, (i + k) % groups) for i in range(groups)])
@@ -511,7 +524,7 @@
     middle = [shifted(below[-1][0], 1), shifted(above[-1][1], -1)]
     pages = [halves] + above[1:] + [middle] + below[:0:-1]
 
-    far_x = sent(after(near_x, above[2], below[2]), "c", NC, 1)
+    far_x = sent(after(near_x, above[1], below[1]), "c", NC, 1)
     w_cols = after(w_cols, near_x)
     weights = lax.all_to_all(w_cols, XC, split_axis=0, concat_axis=0)
 
@@ -568,22 +581,14 @@
     heads, weights = lax.optimization_barrier((heads, weights))
     near = [heads] + [sent(heads, "x", NX, k) for k in range(1, NX)]
     far = sent(jnp.stack(near), "c", NC, 1)
-    half = pl.pallas_call(
-        near_kernel,
-        out_shape=jax.ShapeDtypeStruct((NZ * share, rows), F32),
-        in_specs=[spec(SMEM)] + [spec(VMEM)] * (NX + 1),
-        out_specs=spec(VMEM),
-        compiler_params=small,
-        name="near",
-    )(meta, weights, *near)
     mixed = pl.pallas_call(
         output_kernel,
         out_shape=jax.ShapeDtypeStruct((NZ * share, rows), BF16),
-        in_specs=[spec(SMEM)] + [spec(VMEM)] * 3,
+        in_specs=[spec(SMEM)] + [spec(VMEM)] * (NX + 2),
         out_specs=spec(VMEM),
         compiler_params=small,
         name="output",
-    )(meta, weights, half, far)
+    )(meta, weights, *near, far)
     mixed = lax.all_to_all(mixed, "z", split_axis=0, concat_axis=0, tiled=True)
     mixed = mixed.reshape(NZ, -1, rows).astype(F32).sum(axis=0)
     return mixed.T.astype(BF16)

time: 144 us -> 145 us (level); the launches traced: 144 us -> 142 us
  waiting for transfers between devices: 34 us -> 30.2 us
  Pallas kernels: 33 us -> 35.6 us
  blocking collectives: 22.4 us -> 20 us
    ppermute x9, waiting for transfers between devices: 20.1 us -> 15.2 us  [sent(): return lax.ppermute(x, axis, [(i, i ^ k) for i in range(size)])]
    ppermute x14, starting transfers between devices: 21.3 us -> 24.3 us  [shifted(): return lax.ppermute(x, 'z', [(i, (i + k) % NZ) for i in range(NZ)])]
    all_to_all x1, blocking collectives: 22.4 us -> 20 us  [local(): mixed = lax.all_to_all(mixed, 'z', split_axis=0, concat_axis=0, tiled=True)]
    pallas_call x1, Pallas kernels: 2.72 us -> 4.84 us  [local(): pl.pallas_call(package_kernel, out_shape=jax.ShapeDtypeStruct((NX, 3 * ro...]
    pallas_call x1, Pallas kernels: 5.69 us -> 4.05 us  [local(): pl.pallas_call(functools.partial(prepare_kernel, groups=groups), out_shap...]
  transfers between devices with their start and end apart: 28 -> 28, of which waited for: 12 -> 14; matrix products, arithmetic and copies ran while one was open for 0% -> 0% of each run, Pallas kernels for 17% -> 19%
where the time goes in v5:
time: 145 us; the launch traced here: 142 us
  starting transfers between devices  53.2 us (37%)
  Pallas kernels  35.6 us (25%)
  waiting for transfers between devices  30.2 us (21%)
  blocking collectives  20 us (14%)
  local copies, waits for them, and re-layouts  1.77 us (1%)
    ppermute x14, starting transfers between devices, shifted(): return lax.ppermute(x, 'z', [(i, (i + k) % NZ) for i in range(NZ)])  24.3 us
    all_to_all x1, blocking collectives, local(): mixed = lax.all_to_all(mixed, 'z', split_axis=0, concat_axis=0, tiled=True)  20 us
    ppermute x9, waiting for transfers between devices, sent(): return lax.ppermute(x, axis, [(i, i ^ k) for i in range(size)])  15.2 us
    pallas_call x1, Pallas kernels, local(): pl.pallas_call(functools.partial(attention_kernel, scale=scale), out_shap...  14 us
    ppermute x9, starting transfers between devices, sent(): return lax.ppermute(x, axis, [(i, i ^ k) for i in range(size)])  13.9 us
    ppermute x14, waiting for transfers between devices, shifted(): return lax.ppermute(x, 'z', [(i, (i + k) % NZ) for i in range(NZ)])  8.18 us
    ppermute x3, waiting for transfers between devices, local(): lax.ppermute(packed[k], 'grp', [(i, (i + k) % groups) for i in range(grou...  6.83 us
    ppermute x3, starting transfers between devices, local(): lax.ppermute(packed[k], 'grp', [(i, (i + k) % groups) for i in range(grou...  5.71 us
  transfers between devices with their start and end apart: 28, of which 14 were waited for; matrix products, arithmetic and copies ran while one was open for 0% of the time, Pallas kernels for 19%

profile of v5, /device:TPU:1, one launch (start us, length us, event | category | flops | bytes accessed | tf_op | source)
XLA Modules:
  0.0 141.8 jit_solution(17432966822929479495)
XLA Ops:
  0.1 4.8 %package.1 = bf16[4,2816,128]{2,1,0:T(8,128)(2,1)} custom-call(s32[2]{0:T(128)S(1)} %pad_add_fusion.ids, s32[32]{0:T(128)} %owners.1, bf16[1024,256]{1,0:T(8,128)(2,1)} %q_nope.1, bf16[1024,128]{1,0:T(8,128)(2,1)} %q_rope.1, bf16[512,256]{1,0:T(8,128)(2,1)} %w_uk.1, bf16[512,256]{1,0:T(8,128)(2,1)} %w_uv.1), custom_call_target="tpu_custom_call" | custom-call | tf_op jit(solution)/shard_map/package/pallas_call | solution.py:453
  4.9 4.9 %all-to-all-start = ((bf16[4,2816,128]{2,1,0:T(8,128)(2,1)}), bf16[4,2816,128]{2,1,0:T(8,128)(2,1)}, u32[]{:S(2)}, u32[]{:S(2)}) async-start(bf16[4,2816,128]{2,1,0:T(8,128)(2,1)} %package.1), calls=%async_computation | async-start | bytes 5767168 | tf_op jit(solution)/shard_map/all_to_all | solution.py:492
  9.8 4.0 %prepare.1 = (s32[41]{0:T(128)S(1)}, bf16[288,512]{1,0:T(8,128)(2,1)S(1)}, bf16[288,512]{1,0:T(8,128)(2,1)S(1)}, bf16[288,512]{1,0:T(8,128)(2,1)S(1)}, bf16[288,512]{1,0:T(8,128)(2,1)S(1)}) custom-call(s32[2]{0:T(128)S(1)} %pad_add_fusion.ids, s32[8,64]{1,0:T(8,128)} %bitcast.14, s32[64]{0:T(128)} %refs_1_.1, s32[32]{0:T(128)} %refs_2_.1, s32[32]{0:T(128)} %owners.1, ...), custom_call_target="tpu_custom_call" | custom-call | tf_op jit(solution)/shard_map/prepare/pallas_call | solution.py:469
  13.8 2.0 %collective-permute-start = (bf16[288,512]{1,0:T(8,128)(2,1)S(1)}, bf16[288,512]{1,0:T(8,128)(2,1)S(1)}, u32[]{:S(2)}, u32[]{:S(2)}) collective-permute-start(bf16[288,512]{1,0:T(8,128)(2,1)S(1)} %get-tuple-element.30), channel_id=1, source_target_pairs={{0,64},{64,128},{128,192},{192,0},{1,65},{65,129},{129,193},{193,1... | collective-permute-start | bytes 884744 | tf_op jit(solution)/shard_map/ppermute | solution.py:489
  15.9 2.6 %collective-permute-start.1 = (bf16[288,512]{1,0:T(8,128)(2,1)S(1)}, bf16[288,512]{1,0:T(8,128)(2,1)S(1)}, u32[]{:S(2)}, u32[]{:S(2)}) collective-permute-start(bf16[288,512]{1,0:T(8,128)(2,1)S(1)} %get-tuple-element.31), channel_id=1, source_target_pairs={{0,128},{64,192},{128,0},{192,64},{1,129},{65,193},{129,1},{193,65... | collective-permute-start | bytes 884744 | tf_op jit(solution)/shard_map/ppermute | solution.py:489
  19.5 3.0 %columns.1 = bf16[8,896,256]{2,1,0:T(8,128)(2,1)S(1)} custom-call(bf16[256,7168]{1,0:T(8,128)(2,1)} %w_hbm), custom_call_target="tpu_custom_call" | custom-call | tf_op jit(solution)/shard_map/columns/pallas_call | solution.py:495
  22.6 1.8 %copy-done = bf16[8,896,256]{2,1,0:T(8,128)(2,1)} copy-done((bf16[8,896,256]{2,1,0:T(8,128)(2,1)}, bf16[8,896,256]{2,1,0:T(8,128)(2,1)S(1)}, u32[]{:S(2)}) %copy-start) | copy-done | bytes 3670040
  24.4 6.8 %collective-permute-done.1.rest_2_ = bf16[288,512]{1,0:T(8,128)(2,1)S(1)} collective-permute-done((bf16[288,512]{1,0:T(8,128)(2,1)S(1)}, bf16[288,512]{1,0:T(8,128)(2,1)S(1)}, u32[]{:S(2)}, u32[]{:S(2)}) %collective-permute-start.1) | collective-permute-done | bytes 294944 | tf_op jit(solution)/shard_map/ppermute | solution.py:489
  31.8 1.7 %collective-permute-start.5 = (bf16[144,512]{1,0:T(8,128)(2,1)S(1)}, bf16[144,512]{1,0:T(8,128)(2,1)S(1)}, u32[]{:S(2)}, u32[]{:S(2)}) collective-permute-start(bf16[144,512]{1,0:T(8,128)(2,1)S(1)} %get-tuple-element.38.rest_2_), channel_id=1, source_target_pairs={{0,8},{8,16},{16,24},{24,32},{32,40},{40,48},{48,56},{56,0},{1,9},... | collective-permute-start | bytes 442376 | tf_op jit(solution)/shard_map/ppermute | solution.py:420
  33.5 4.0 %collective-permute-start.3 = (bf16[144,512]{1,0:T(8,128)(2,1)S(1)}, bf16[144,512]{1,0:T(8,128)(2,1)S(1)}, u32[]{:S(2)}, u32[]{:S(2)}) collective-permute-start(bf16[144,512]{1,0:T(8,128)(2,1)S(1)} %get-tuple-element.38.rest_2_), channel_id=1, source_target_pairs={{0,56},{8,0},{16,8},{24,16},{32,24},{40,32},{48,40},{56,48},{1,57}... | collective-permute-start | bytes 442376 | tf_op jit(solution)/shard_map/ppermute | solution.py:420
  37.6 2.7 %collective-permute-start.4 = (bf16[144,512]{1,0:T(8,128)(2,1)S(1)}, bf16[144,512]{1,0:T(8,128)(2,1)S(1)}, u32[]{:S(2)}, u32[]{:S(2)}) collective-permute-start(bf16[144,512]{1,0:T(8,128)(2,1)S(1)} %get-tuple-element.39.rest_10_), channel_id=1, source_target_pairs={{0,56},{8,0},{16,8},{24,16},{32,24},{40,32},{48,40},{56,48},{1,57}... | collective-permute-start | bytes 442376 | tf_op jit(solution)/shard_map/ppermute | solution.py:420
  40.4 3.3 %collective-permute-done.6.rest_17_ = bf16[144,512]{1,0:T(8,128)(2,1)S(1)} collective-permute-done((bf16[144,512]{1,0:T(8,128)(2,1)S(1)}, bf16[144,512]{1,0:T(8,128)(2,1)S(1)}, u32[]{:S(2)}, u32[]{:S(2)}) %collective-permute-start.6) | collective-permute-done | bytes 147488 | tf_op jit(solution)/shard_map/ppermute | solution.py:420
  43.7 2.2 %collective-permute-start.7 = (bf16[4,2816,128]{2,1,0:T(8,128)(2,1)}, bf16[4,2816,128]{2,1,0:T(8,128)(2,1)}, u32[]{:S(2)}, u32[]{:S(2)}) collective-permute-start(bf16[4,2816,128]{2,1,0:T(8,128)(2,1)} %all-to-all-done.near.rest_0_), channel_id=1, source_target_pairs={{0,1},{1,0},{2,3},{3,2},{4,5},{5,4},{6,7},{7,6},{8,9},{9,8},{10,11... | collective-permute-start | bytes 8650760 | tf_op jit(solution)/shard_map/ppermute | solution.py:416
  45.9 4.5 %all-to-all-start.1 = ((bf16[8,896,256]{2,1,0:T(8,128)(2,1)}), bf16[8,896,256]{2,1,0:T(8,128)(2,1)}, u32[]{:S(2)}, u32[]{:S(2)}) async-start(bf16[8,896,256]{2,1,0:T(8,128)(2,1)} %copy-done), calls=%async_computation.1 | async-start | bytes 7340032 | tf_op jit(solution)/shard_map/all_to_all | solution.py:529
  50.4 2.0 %collective-permute-start.10 = (bf16[144,512]{1,0:T(8,128)(2,1)S(1)}, bf16[144,512]{1,0:T(8,128)(2,1)S(1)}, u32[]{:S(2)}, u32[]{:S(2)}) collective-permute-start(bf16[144,512]{1,0:T(8,128)(2,1)S(1)} %collective-permute-done.5.rest_9_), channel_id=1, source_target_pairs={{0,8},{8,16},{16,24},{24,32},{32,40},{40,48},{48,56},{56,0},{1,9},... | collective-permute-start | bytes 442376 | tf_op jit(solution)/shard_map/ppermute | solution.py:420
  52.4 4.0 %collective-permute-start.13 = (bf16[144,512]{1,0:T(8,128)(2,1)S(1)}, bf16[144,512]{1,0:T(8,128)(2,1)S(1)}, u32[]{:S(2)}, u32[]{:S(2)}) collective-permute-start(bf16[144,512]{1,0:T(8,128)(2,1)S(1)} %collective-permute-done.4.rest_11_), channel_id=1, source_target_pairs={{0,56},{8,0},{16,8},{24,16},{32,24},{40,32},{48,40},{56,48},{1,57}... | collective-permute-start | bytes 442376 | tf_op jit(solution)/shard_map/ppermute | solution.py:420
  57.9 2.7 %collective-permute-done.10.rest_8_ = bf16[144,512]{1,0:T(8,128)(2,1)S(1)} collective-permute-done((bf16[144,512]{1,0:T(8,128)(2,1)S(1)}, bf16[144,512]{1,0:T(8,128)(2,1)S(1)}, u32[]{:S(2)}, u32[]{:S(2)}) %collective-permute-start.10) | collective-permute-done | bytes 147488 | tf_op jit(solution)/shard_map/ppermute | solution.py:420
  60.6 2.7 %collective-permute-start.14 = (bf16[144,512]{1,0:T(8,128)(2,1)S(1)}, bf16[144,512]{1,0:T(8,128)(2,1)S(1)}, u32[]{:S(2)}, u32[]{:S(2)}) collective-permute-start(bf16[144,512]{1,0:T(8,128)(2,1)S(1)} %collective-permute-done.13.rest_12_), channel_id=1, source_target_pairs={{0,56},{8,0},{16,8},{24,16},{32,24},{40,32},{48,40},{56,48},{1,57}... | collective-permute-start | bytes 442376 | tf_op jit(solution)/shard_map/ppermute | solution.py:420
  63.3 3.0 %collective-permute-start.9 = (bf16[144,512]{1,0:T(8,128)(2,1)S(1)}, bf16[144,512]{1,0:T(8,128)(2,1)S(1)}, u32[]{:S(2)}, u32[]{:S(2)}) collective-permute-start(bf16[144,512]{1,0:T(8,128)(2,1)S(1)} %collective-permute-done.8.rest_4_), channel_id=1, source_target_pairs={{0,56},{8,0},{16,8},{24,16},{32,24},{40,32},{48,40},{56,48},{1,57}... | collective-permute-start | bytes 442376 | tf_op jit(solution)/shard_map/ppermute | solution.py:420
  67.4 2.7 %collective-permute-start.15 = (bf16[144,512]{1,0:T(8,128)(2,1)S(1)}, bf16[144,512]{1,0:T(8,128)(2,1)S(1)}, u32[]{:S(2)}, u32[]{:S(2)}) collective-permute-start(bf16[144,512]{1,0:T(8,128)(2,1)S(1)} %collective-permute-done.14.rest_13_), channel_id=1, source_target_pairs={{0,56},{8,0},{16,8},{24,16},{32,24},{40,32},{48,40},{56,48},{1,57}... | collective-permute-start | bytes 442376 | tf_op jit(solution)/shard_map/ppermute | solution.py:420
  70.1 4.2 %query.1 = bf16[8,512,640]{2,1,0:T(8,128)(2,1)S(1)} custom-call(s32[41]{0:T(128)S(1)} %get-tuple-element.28.meta, bf16[4,2816,128]{2,1,0:T(8,128)(2,1)} %all-to-all-done.near.rest_0_, bf16[4,2816,128]{2,1,0:T(8,128)(2,1)} %collective-permute-done.7.far.rest_1_), custom_call_target="tpu_custom_call" | custom-call | tf_op jit(solution)/shard_map/query/pallas_call | solution.py:531
  75.2 14.0 %attention.1 = (bf16[4,272,256]{2,1,0:T(8,128)(2,1)S(1)}, bf16[4,272,256]{2,1,0:T(8,128)(2,1)S(1)}) custom-call(s32[41]{0:T(128)S(1)} %get-tuple-element.28.meta, bf16[8,512,640]{2,1,0:T(8,128)(2,1)S(1)} %query.1, bf16[4,2816,128]{2,1,0:T(8,128)(2,1)} %all-to-all-done.near.rest_0_, bf16[4,2816,128]{2,1,0:T(8,128)(2,1)} %collective-permute-done.7.far.rest_1_, ...), custom_call_target="tpu_custom_call" | custom-call | tf_op jit(solution)/shard_map/attention/pallas_call | solution.py:545
  89.2 1.9 %collective-permute-start.18 = (bf16[4,272,256]{2,1,0:T(8,128)(2,1)S(1)}, bf16[4,272,256]{2,1,0:T(8,128)(2,1)S(1)}, u32[]{:S(2)}, u32[]{:S(2)}) collective-permute-start(bf16[4,272,256]{2,1,0:T(8,128)(2,1)S(1)} %get-tuple-element.42), channel_id=1, source_target_pairs={{0,1},{1,0},{2,3},{3,2},{4,5},{5,4},{6,7},{7,6},{8,9},{9,8},{10,11... | collective-permute-start | bytes 1671176 | tf_op jit(solution)/shard_map/ppermute | solution.py:416
  91.1 1.6 %collective-permute-done.18.got = bf16[4,272,256]{2,1,0:T(8,128)(2,1)S(1)} collective-permute-done((bf16[4,272,256]{2,1,0:T(8,128)(2,1)S(1)}, bf16[4,272,256]{2,1,0:T(8,128)(2,1)S(1)}, u32[]{:S(2)}, u32[]{:S(2)}) %collective-permute-start.18) | collective-permute-done | bytes 557088 | tf_op jit(solution)/shard_map/ppermute | solution.py:416
  94.0 3.5 %collective-permute-start.21 = (bf16[272,256]{1,0:T(8,128)(2,1)S(1)}, bf16[272,256]{1,0:T(8,128)(2,1)S(1)}, u32[]{:S(2)}, u32[]{:S(2)}) collective-permute-start(bf16[272,256]{1,0:T(8,128)(2,1)S(1)} %get-tuple-element.46), channel_id=1, source_target_pairs={{0,6},{2,4},{4,2},{6,0},{1,7},{3,5},{5,3},{7,1},{8,14},{10,12},{12... | collective-permute-start | bytes 417800 | tf_op jit(solution)/shard_map/ppermute | solution.py:416
  98.5 1.8 %collective-permute-done.20.refs_2_ = bf16[272,256]{1,0:T(8,128)(2,1)S(1)} collective-permute-done((bf16[272,256]{1,0:T(8,128)(2,1)S(1)}, bf16[272,256]{1,0:T(8,128)(2,1)S(1)}, u32[]{:S(2)}, u32[]{:S(2)}) %collective-permute-start.20) | collective-permute-done | bytes 139296 | tf_op jit(solution)/shard_map/ppermute | solution.py:416
  100.4 3.7 %collective-permute-done.21.refs_3_ = bf16[272,256]{1,0:T(8,128)(2,1)S(1)} collective-permute-done((bf16[272,256]{1,0:T(8,128)(2,1)S(1)}, bf16[272,256]{1,0:T(8,128)(2,1)S(1)}, u32[]{:S(2)}, u32[]{:S(2)}) %collective-permute-start.21) | collective-permute-done | bytes 139296 | tf_op jit(solution)/shard_map/ppermute | solution.py:416
  104.6 2.5 %collective-permute-start.24 = (bf16[256,256]{1,0:T(8,128)(2,1)S(1)}, bf16[256,256]{1,0:T(8,128)(2,1)S(1)}, u32[]{:S(2)}, u32[]{:S(2)}) collective-permute-start(bf16[256,256]{1,0:T(8,128)(2,1)S(1)} %heads.1.refs_0_), channel_id=1, source_target_pairs={{0,6},{2,4},{4,2},{6,0},{1,7},{3,5},{5,3},{7,1},{8,14},{10,12},{12... | collective-permute-start | bytes 393224 | tf_op jit(solution)/shard_map/ppermute | solution.py:416
  108.0 4.1 %collective-permute-done.24.refs_3_ = bf16[256,256]{1,0:T(8,128)(2,1)S(1)} collective-permute-done((bf16[256,256]{1,0:T(8,128)(2,1)S(1)}, bf16[256,256]{1,0:T(8,128)(2,1)S(1)}, u32[]{:S(2)}, u32[]{:S(2)}) %collective-permute-start.24) | collective-permute-done | bytes 131104 | tf_op jit(solution)/shard_map/ppermute | solution.py:416
  113.6 2.6 %collective-permute-start.25 = (bf16[4,256,256]{2,1,0:T(8,128)(2,1)S(1)}, bf16[4,256,256]{2,1,0:T(8,128)(2,1)S(1)}, u32[]{:S(2)}, u32[]{:S(2)}) collective-permute-start(bf16[4,256,256]{2,1,0:T(8,128)(2,1)S(1)} %pad_maximum_fusion), channel_id=1, source_target_pairs={{0,1},{1,0},{2,3},{3,2},{4,5},{5,4},{6,7},{7,6},{8,9},{9,8},{10,11... | collective-permute-start | bytes 1572872 | tf_op jit(solution)/shard_map/ppermute | solution.py:416
  117.7 3.4 %output.1 = bf16[896,256]{1,0:T(8,128)(2,1)S(1)} custom-call(s32[41]{0:T(128)S(1)} %get-tuple-element.28.meta, bf16[8,896,256]{2,1,0:T(8,128)(2,1)} %all-to-all-done.1.weights, bf16[256,256]{1,0:T(8,128)(2,1)S(1)} %heads.1.refs_0_, bf16[256,256]{1,0:T(8,128)(2,1)S(1)} %collective-permute-done.22.refs_1_, ...), custom_call_target="tpu_custom_call" | custom-call | tf_op jit(solution)/shard_map/output/pallas_call | solution.py:584
  121.1 20.0 %all_to_all.19 = bf16[8,112,256]{2,1,0:T(8,128)(2,1)S(1)} all-to-all(bf16[8,112,256]{2,1,0:T(8,128)(2,1)S(1)} %bitcast.9), channel_id=1, replica_groups=mesh['grp'=4,'z'=8,'x'=4,'c'=2] {'z'}, dimensions={0} | all-to-all | bytes 917504 | tf_op jit(solution)/shard_map/all_to_all | solution.py:592
  (39 shorter events, 12.9 us)
Async XLA Ops:
  4.9 38.8 %all-to-all-start = ((bf16[4,2816,128]{2,1,0:T(8,128)(2,1)}), bf16[4,2816,128]{2,1,0:T(8,128)(2,1)}, u32[]{:S(2)}, u32[]{:S(2)}) async-start(bf16[4,2816,128]{2,1,0:T(8,128)(2,1)} %package.1), calls=%async_computation | async-start | bytes 5767168 | tf_op jit(solution)/shard_map/all_to_all | solution.py:492
  13.8 10.6 %collective-permute-start = (bf16[288,512]{1,0:T(8,128)(2,1)S(1)}, bf16[288,512]{1,0:T(8,128)(2,1)S(1)}, u32[]{:S(2)}, u32[]{:S(2)}) collective-permute-start(bf16[288,512]{1,0:T(8,128)(2,1)S(1)} %get-tuple-element.30), channel_id=1, source_target_pairs={{0,64},{64,128},{128,192},{192,0},{1,65},{65,129},{129,193},{193,1... | collective-permute-start | bytes 884744 | tf_op jit(solution)/shard_map/ppermute | solution.py:489
  15.9 15.4 %collective-permute-start.1 = (bf16[288,512]{1,0:T(8,128)(2,1)S(1)}, bf16[288,512]{1,0:T(8,128)(2,1)S(1)}, u32[]{:S(2)}, u32[]{:S(2)}) collective-permute-start(bf16[288,512]{1,0:T(8,128)(2,1)S(1)} %get-tuple-element.31), channel_id=1, source_target_pairs={{0,128},{64,192},{128,0},{192,64},{1,129},{65,193},{129,1},{193,65... | collective-permute-start | bytes 884744 | tf_op jit(solution)/shard_map/ppermute | solution.py:489
  18.5 12.7 %collective-permute-start.2 = (bf16[288,512]{1,0:T(8,128)(2,1)S(1)}, bf16[288,512]{1,0:T(8,128)(2,1)S(1)}, u32[]{:S(2)}, u32[]{:S(2)}) collective-permute-start(bf16[288,512]{1,0:T(8,128)(2,1)S(1)} %get-tuple-element.32), channel_id=1, source_target_pairs={{0,192},{64,0},{128,64},{192,128},{1,193},{65,1},{129,65},{193,129... | collective-permute-start | bytes 884744 | tf_op jit(solution)/shard_map/ppermute | solution.py:489
  22.6 1.8 %copy-start = (bf16[8,896,256]{2,1,0:T(8,128)(2,1)}, bf16[8,896,256]{2,1,0:T(8,128)(2,1)S(1)}, u32[]{:S(2)}) copy-start(bf16[8,896,256]{2,1,0:T(8,128)(2,1)S(1)} %columns.1) | copy-start | bytes 11010052
  31.8 8.6 %collective-permute-start.5 = (bf16[144,512]{1,0:T(8,128)(2,1)S(1)}, bf16[144,512]{1,0:T(8,128)(2,1)S(1)}, u32[]{:S(2)}, u32[]{:S(2)}) collective-permute-start(bf16[144,512]{1,0:T(8,128)(2,1)S(1)} %get-tuple-element.38.rest_2_), channel_id=1, source_target_pairs={{0,8},{8,16},{16,24},{24,32},{32,40},{40,48},{48,56},{56,0},{1,9},... | collective-permute-start | bytes 442376 | tf_op jit(solution)/shard_map/ppermute | solution.py:420
  33.5 6.9 %collective-permute-start.3 = (bf16[144,512]{1,0:T(8,128)(2,1)S(1)}, bf16[144,512]{1,0:T(8,128)(2,1)S(1)}, u32[]{:S(2)}, u32[]{:S(2)}) collective-permute-start(bf16[144,512]{1,0:T(8,128)(2,1)S(1)} %get-tuple-element.38.rest_2_), channel_id=1, source_target_pairs={{0,56},{8,0},{16,8},{24,16},{32,24},{40,32},{48,40},{56,48},{1,57}... | collective-permute-start | bytes 442376 | tf_op jit(solution)/shard_map/ppermute | solution.py:420
  37.5 6.2 %collective-permute-start.6 = (bf16[144,512]{1,0:T(8,128)(2,1)S(1)}, bf16[144,512]{1,0:T(8,128)(2,1)S(1)}, u32[]{:S(2)}, u32[]{:S(2)}) collective-permute-start(bf16[144,512]{1,0:T(8,128)(2,1)S(1)} %get-tuple-element.39.rest_10_), channel_id=1, source_target_pairs={{0,8},{8,16},{16,24},{24,32},{32,40},{40,48},{48,56},{56,0},{1,9},... | collective-permute-start | bytes 442376 | tf_op jit(solution)/shard_map/ppermute | solution.py:420
  37.6 6.2 %collective-permute-start.4 = (bf16[144,512]{1,0:T(8,128)(2,1)S(1)}, bf16[144,512]{1,0:T(8,128)(2,1)S(1)}, u32[]{:S(2)}, u32[]{:S(2)}) collective-permute-start(bf16[144,512]{1,0:T(8,128)(2,1)S(1)} %get-tuple-element.39.rest_10_), channel_id=1, source_target_pairs={{0,56},{8,0},{16,8},{24,16},{32,24},{40,32},{48,40},{56,48},{1,57}... | collective-permute-start | bytes 442376 | tf_op jit(solution)/shard_map/ppermute | solution.py:420
  43.7 26.4 %collective-permute-start.7 = (bf16[4,2816,128]{2,1,0:T(8,128)(2,1)}, bf16[4,2816,128]{2,1,0:T(8,128)(2,1)}, u32[]{:S(2)}, u32[]{:S(2)}) collective-permute-start(bf16[4,2816,128]{2,1,0:T(8,128)(2,1)} %all-to-all-done.near.rest_0_), channel_id=1, source_target_pairs={{0,1},{1,0},{2,3},{3,2},{4,5},{5,4},{6,7},{7,6},{8,9},{9,8},{10,11... | collective-permute-start | bytes 8650760 | tf_op jit(solution)/shard_map/ppermute | solution.py:416
  45.9 58.7 %all-to-all-start.1 = ((bf16[8,896,256]{2,1,0:T(8,128)(2,1)}), bf16[8,896,256]{2,1,0:T(8,128)(2,1)}, u32[]{:S(2)}, u32[]{:S(2)}) async-start(bf16[8,896,256]{2,1,0:T(8,128)(2,1)} %copy-done), calls=%async_computation.1 | async-start | bytes 7340032 | tf_op jit(solution)/shard_map/all_to_all | solution.py:529
  50.4 10.2 %collective-permute-start.10 = (bf16[144,512]{1,0:T(8,128)(2,1)S(1)}, bf16[144,512]{1,0:T(8,128)(2,1)S(1)}, u32[]{:S(2)}, u32[]{:S(2)}) collective-permute-start(bf16[144,512]{1,0:T(8,128)(2,1)S(1)} %collective-permute-done.5.rest_9_), channel_id=1, source_target_pairs={{0,8},{8,16},{16,24},{24,32},{32,40},{40,48},{48,56},{56,0},{1,9},... | collective-permute-start | bytes 442376 | tf_op jit(solution)/shard_map/ppermute | solution.py:420
  52.4 8.2 %collective-permute-start.13 = (bf16[144,512]{1,0:T(8,128)(2,1)S(1)}, bf16[144,512]{1,0:T(8,128)(2,1)S(1)}, u32[]{:S(2)}, u32[]{:S(2)}) collective-permute-start(bf16[144,512]{1,0:T(8,128)(2,1)S(1)} %collective-permute-done.4.rest_11_), channel_id=1, source_target_pairs={{0,56},{8,0},{16,8},{24,16},{32,24},{40,32},{48,40},{56,48},{1,57}... | collective-permute-start | bytes 442376 | tf_op jit(solution)/shard_map/ppermute | solution.py:420
  56.4 6.9 %collective-permute-start.8 = (bf16[144,512]{1,0:T(8,128)(2,1)S(1)}, bf16[144,512]{1,0:T(8,128)(2,1)S(1)}, u32[]{:S(2)}, u32[]{:S(2)}) collective-permute-start(bf16[144,512]{1,0:T(8,128)(2,1)S(1)} %collective-permute-done.3.rest_3_), channel_id=1, source_target_pairs={{0,56},{8,0},{16,8},{24,16},{32,24},{40,32},{48,40},{56,48},{1,57}... | collective-permute-start | bytes 442376 | tf_op jit(solution)/shard_map/ppermute | solution.py:420
  57.8 8.5 %collective-permute-start.16 = (bf16[144,512]{1,0:T(8,128)(2,1)S(1)}, bf16[144,512]{1,0:T(8,128)(2,1)S(1)}, u32[]{:S(2)}, u32[]{:S(2)}) collective-permute-start(bf16[144,512]{1,0:T(8,128)(2,1)S(1)} %collective-permute-done.6.rest_17_), channel_id=1, source_target_pairs={{0,8},{8,16},{16,24},{24,32},{32,40},{40,48},{48,56},{56,0},{1,9},... | collective-permute-start | bytes 442376 | tf_op jit(solution)/shard_map/ppermute | solution.py:420
  60.6 6.8 %collective-permute-start.11 = (bf16[144,512]{1,0:T(8,128)(2,1)S(1)}, bf16[144,512]{1,0:T(8,128)(2,1)S(1)}, u32[]{:S(2)}, u32[]{:S(2)}) collective-permute-start(bf16[144,512]{1,0:T(8,128)(2,1)S(1)} %collective-permute-done.10.rest_8_), channel_id=1, source_target_pairs={{0,8},{8,16},{16,24},{24,32},{32,40},{40,48},{48,56},{56,0},{1,9},... | collective-permute-start | bytes 442376 | tf_op jit(solution)/shard_map/ppermute | solution.py:420
  60.6 6.8 %collective-permute-start.14 = (bf16[144,512]{1,0:T(8,128)(2,1)S(1)}, bf16[144,512]{1,0:T(8,128)(2,1)S(1)}, u32[]{:S(2)}, u32[]{:S(2)}) collective-permute-start(bf16[144,512]{1,0:T(8,128)(2,1)S(1)} %collective-permute-done.13.rest_12_), channel_id=1, source_target_pairs={{0,56},{8,0},{16,8},{24,16},{32,24},{40,32},{48,40},{56,48},{1,57}... | collective-permute-start | bytes 442376 | tf_op jit(solution)/shard_map/ppermute | solution.py:420
  63.3 11.0 %collective-permute-start.9 = (bf16[144,512]{1,0:T(8,128)(2,1)S(1)}, bf16[144,512]{1,0:T(8,128)(2,1)S(1)}, u32[]{:S(2)}, u32[]{:S(2)}) collective-permute-start(bf16[144,512]{1,0:T(8,128)(2,1)S(1)} %collective-permute-done.8.rest_4_), channel_id=1, source_target_pairs={{0,56},{8,0},{16,8},{24,16},{32,24},{40,32},{48,40},{56,48},{1,57}... | collective-permute-start | bytes 442376 | tf_op jit(solution)/shard_map/ppermute | solution.py:420
  66.3 7.9 %collective-permute-start.17 = (bf16[144,512]{1,0:T(8,128)(2,1)S(1)}, bf16[144,512]{1,0:T(8,128)(2,1)S(1)}, u32[]{:S(2)}, u32[]{:S(2)}) collective-permute-start(bf16[144,512]{1,0:T(8,128)(2,1)S(1)} %collective-permute-done.16.rest_16_), channel_id=1, source_target_pairs={{0,8},{8,16},{16,24},{24,32},{32,40},{40,48},{48,56},{56,0},{1,9},... | collective-permute-start | bytes 442376 | tf_op jit(solution)/shard_map/ppermute | solution.py:420
  67.4 7.8 %collective-permute-start.12 = (bf16[144,512]{1,0:T(8,128)(2,1)S(1)}, bf16[144,512]{1,0:T(8,128)(2,1)S(1)}, u32[]{:S(2)}, u32[]{:S(2)}) collective-permute-start(bf16[144,512]{1,0:T(8,128)(2,1)S(1)} %collective-permute-done.11.rest_7_), channel_id=1, source_target_pairs={{0,8},{8,16},{16,24},{24,32},{32,40},{40,48},{48,56},{56,0},{1,9},... | collective-permute-start | bytes 442376 | tf_op jit(solution)/shard_map/ppermute | solution.py:420
  67.4 7.8 %collective-permute-start.15 = (bf16[144,512]{1,0:T(8,128)(2,1)S(1)}, bf16[144,512]{1,0:T(8,128)(2,1)S(1)}, u32[]{:S(2)}, u32[]{:S(2)}) collective-permute-start(bf16[144,512]{1,0:T(8,128)(2,1)S(1)} %collective-permute-done.14.rest_13_), channel_id=1, source_target_pairs={{0,56},{8,0},{16,8},{24,16},{32,24},{40,32},{48,40},{56,48},{1,57}... | collective-permute-start | bytes 442376 | tf_op jit(solution)/shard_map/ppermute | solution.py:420
  89.2 3.5 %collective-permute-start.18 = (bf16[4,272,256]{2,1,0:T(8,128)(2,1)S(1)}, bf16[4,272,256]{2,1,0:T(8,128)(2,1)S(1)}, u32[]{:S(2)}, u32[]{:S(2)}) collective-permute-start(bf16[4,272,256]{2,1,0:T(8,128)(2,1)S(1)} %get-tuple-element.42), channel_id=1, source_target_pairs={{0,1},{1,0},{2,3},{3,2},{4,5},{5,4},{6,7},{7,6},{8,9},{9,8},{10,11... | collective-permute-start | bytes 1671176 | tf_op jit(solution)/shard_map/ppermute | solution.py:416
  93.6 5.0 %collective-permute-start.19 = (bf16[272,256]{1,0:T(8,128)(2,1)S(1)}, bf16[272,256]{1,0:T(8,128)(2,1)S(1)}, u32[]{:S(2)}, u32[]{:S(2)}) collective-permute-start(bf16[272,256]{1,0:T(8,128)(2,1)S(1)} %get-tuple-element.44), channel_id=1, source_target_pairs={{0,2},{2,0},{4,6},{6,4},{1,3},{3,1},{5,7},{7,5},{8,10},{10,8},{12,... | collective-permute-start | bytes 417800 | tf_op jit(solution)/shard_map/ppermute | solution.py:416
  93.7 6.7 %collective-permute-start.20 = (bf16[272,256]{1,0:T(8,128)(2,1)S(1)}, bf16[272,256]{1,0:T(8,128)(2,1)S(1)}, u32[]{:S(2)}, u32[]{:S(2)}) collective-permute-start(bf16[272,256]{1,0:T(8,128)(2,1)S(1)} %get-tuple-element.45), channel_id=1, source_target_pairs={{0,4},{2,6},{4,0},{6,2},{1,5},{3,7},{5,1},{7,3},{8,12},{10,14},{12... | collective-permute-start | bytes 417800 | tf_op jit(solution)/shard_map/ppermute | solution.py:416
  94.0 10.1 %collective-permute-start.21 = (bf16[272,256]{1,0:T(8,128)(2,1)S(1)}, bf16[272,256]{1,0:T(8,128)(2,1)S(1)}, u32[]{:S(2)}, u32[]{:S(2)}) collective-permute-start(bf16[272,256]{1,0:T(8,128)(2,1)S(1)} %get-tuple-element.46), channel_id=1, source_target_pairs={{0,6},{2,4},{4,2},{6,0},{1,7},{3,5},{5,3},{7,1},{8,14},{10,12},{12... | collective-permute-start | bytes 417800 | tf_op jit(solution)/shard_map/ppermute | solution.py:416
  104.6 7.4 %collective-permute-start.24 = (bf16[256,256]{1,0:T(8,128)(2,1)S(1)}, bf16[256,256]{1,0:T(8,128)(2,1)S(1)}, u32[]{:S(2)}, u32[]{:S(2)}) collective-permute-start(bf16[256,256]{1,0:T(8,128)(2,1)S(1)} %heads.1.refs_0_), channel_id=1, source_target_pairs={{0,6},{2,4},{4,2},{6,0},{1,7},{3,5},{5,3},{7,1},{8,14},{10,12},{12... | collective-permute-start | bytes 393224 | tf_op jit(solution)/shard_map/ppermute | solution.py:416
  107.1 5.4 %collective-permute-start.23 = (bf16[256,256]{1,0:T(8,128)(2,1)S(1)}, bf16[256,256]{1,0:T(8,128)(2,1)S(1)}, u32[]{:S(2)}, u32[]{:S(2)}) collective-permute-start(bf16[256,256]{1,0:T(8,128)(2,1)S(1)} %heads.1.refs_0_), channel_id=1, source_target_pairs={{0,4},{2,6},{4,0},{6,2},{1,5},{3,7},{5,1},{7,3},{8,12},{10,14},{12... | collective-permute-start | bytes 393224 | tf_op jit(solution)/shard_map/ppermute | solution.py:416
  107.1 6.4 %collective-permute-start.22 = (bf16[256,256]{1,0:T(8,128)(2,1)S(1)}, bf16[256,256]{1,0:T(8,128)(2,1)S(1)}, u32[]{:S(2)}, u32[]{:S(2)}) collective-permute-start(bf16[256,256]{1,0:T(8,128)(2,1)S(1)} %heads.1.refs_0_), channel_id=1, source_target_pairs={{0,2},{2,0},{4,6},{6,4},{1,3},{3,1},{5,7},{7,5},{8,10},{10,8},{12,... | collective-permute-start | bytes 393224 | tf_op jit(solution)/shard_map/ppermute | solution.py:416
  113.6 4.1 %collective-permute-start.25 = (bf16[4,256,256]{2,1,0:T(8,128)(2,1)S(1)}, bf16[4,256,256]{2,1,0:T(8,128)(2,1)S(1)}, u32[]{:S(2)}, u32[]{:S(2)}) collective-permute-start(bf16[4,256,256]{2,1,0:T(8,128)(2,1)S(1)} %pad_maximum_fusion), channel_id=1, source_target_pairs={{0,1},{1,0},{2,3},{3,2},{4,5},{5,4},{6,7},{7,6},{8,9},{9,8},{10,11... | collective-permute-start | bytes 1572872 | tf_op jit(solution)/shard_map/ppermute | solution.py:416

commit v6 on v4

--- a/solution.py
+++ b/solution.py
@@ -383,22 +383,23 @@
             out[s, z * share : (z + 1) * share, :] = tall[at : at + share, :]
 
 
-def near_kernel(meta, weights, *refs):
-    near, out = refs[:NX], refs[-1]
-    mixed = None
-    for k in range(NX):
-        weight = weights[meta[PLACE] ^ (k * NC)]
-        term = lax.dot_general(weight, near[k][...], NT, preferred_element_type=F32)
-        mixed = term if mixed is None else mixed + term
-    out[...] = mixed
-
-
-def output_kernel(meta, weights, half, far, out):
-    mixed = half[...]
-    for k in range(NX):
-        weight = weights[meta[PLACE] ^ (k * NC + 1)]
-        mixed = mixed + lax.dot_general(weight, far[k], NT, preferred_element_type=F32)
-    out[...] = mixed.astype(BF16)
+def output_kernel(meta, weights, near, far, out):
+    block = out.shape[0] // NX
+    spot = meta[SPOT]
+    for c, sides in enumerate(((near, far), (far, near))):
+
+        @pl.when((meta[PLACE] & (NC - 1)) == c)
+        def _():
+            heads = [sides[s % NC][spot ^ (s // NC)] for s in range(NXC)]
+            for i in range(NX):
+                part = slice(i * block, (i + 1) * block)
+                mixed = None
+                for s in range(NXC):
+                    term = lax.dot_general(
+                        weights[s, part, :], heads[s], NT, preferred_element_type=F32
+                    )
+                    mixed = term if mixed is None else mixed + term
+                out[part, :] = mixed.astype(BF16)
 
 
 def after(x, *others):
@@ -567,15 +568,7 @@
     )(chip[0], *[sent(chip[k], "x", NX, k) for k in range(1, NX)])
     heads, weights = lax.optimization_barrier((heads, weights))
     near = [heads] + [sent(heads, "x", NX, k) for k in range(1, NX)]
-    far = sent(jnp.stack(near), "c", NC, 1)
-    half = pl.pallas_call(
-        near_kernel,
-        out_shape=jax.ShapeDtypeStruct((NZ * share, rows), F32),
-        in_specs=[spec(SMEM)] + [spec(VMEM)] * (NX + 1),
-        out_specs=spec(VMEM),
-        compiler_params=small,
-        name="near",
-    )(meta, weights, *near)
+    near = jnp.stack(near)
     mixed = pl.pallas_call(
         output_kernel,
         out_shape=jax.ShapeDtypeStruct((NZ * share, rows), BF16),
@@ -583,7 +576,7 @@
         out_specs=spec(VMEM),
         compiler_params=small,
         name="output",
-    )(meta, weights, half, far)
+    )(meta, weights, near, sent(near, "c", NC, 1))
     mixed = lax.all_to_all(mixed, "z", split_axis=0, concat_axis=0, tiled=True)
     mixed = mixed.reshape(NZ, -1, rows).astype(F32).sum(axis=0)
     return mixed.T.astype(BF16)

time: 144 us -> 143 us (level)
  waiting for transfers between devices: 34 us -> 35.6 us
    pallas_call x1 -> x0, Pallas kernels: 2.72 us -> none  [local(): pl.pallas_call(near_kernel, out_shape=jax.ShapeDtypeStruct((NZ * share, r...]
    ppermute x9, waiting for transfers between devices: 20.1 us -> 21.6 us  [sent(): return lax.ppermute(x, axis, [(i, i ^ k) for i in range(size)])]
  transfers between devices with their start and end apart: 28 -> 28, of which waited for: 12 -> 13; matrix products, arithmetic and copies ran while one was open for 0% -> 0% of each run, Pallas kernels for 17% -> 16%
where the time goes in v6:
time: 143 us; the launch traced here: 142 us
  starting transfers between devices  50.4 us (35%)
  waiting for transfers between devices  35.6 us (25%)
  Pallas kernels  32.4 us (23%)
  blocking collectives  21.1 us (15%)
  local copies, waits for them, and re-layouts  1.77 us (1%)
    ppermute x9, waiting for transfers between devices, sent(): return lax.ppermute(x, axis, [(i, i ^ k) for i in range(size)])  21.6 us
    ppermute x14, starting transfers between devices, shifted(): return lax.ppermute(x, 'z', [(i, (i + k) % NZ) for i in range(NZ)])  21.3 us
    all_to_all x1, blocking collectives, local(): mixed = lax.all_to_all(mixed, 'z', split_axis=0, concat_axis=0, tiled=True)  21.1 us
    pallas_call x1, Pallas kernels, local(): pl.pallas_call(functools.partial(attention_kernel, scale=scale), out_shap...  14.1 us
    ppermute x9, starting transfers between devices, sent(): return lax.ppermute(x, axis, [(i, i ^ k) for i in range(size)])  13.6 us
    ppermute x14, waiting for transfers between devices, shifted(): return lax.ppermute(x, 'z', [(i, (i + k) % NZ) for i in range(NZ)])  7.11 us
    ppermute x3, waiting for transfers between devices, local(): lax.ppermute(packed[k], 'grp', [(i, (i + k) % groups) for i in range(grou...  6.83 us
    ppermute x3, starting transfers between devices, local(): lax.ppermute(packed[k], 'grp', [(i, (i + k) % groups) for i in range(grou...  5.7 us
  transfers between devices with their start and end apart: 28, of which 13 were waited for; matrix products, arithmetic and copies ran while one was open for 0% of the time, Pallas kernels for 16%

profile of v6, /device:TPU:1, one launch (start us, length us, event | category | flops | bytes accessed | tf_op | source)
XLA Modules:
  0.0 142.2 jit_solution(13033598019454764186)
XLA Ops:
  0.1 5.7 %prepare.1 = (s32[41]{0:T(128)S(1)}, bf16[4,2816,128]{2,1,0:T(8,128)(2,1)}, bf16[288,512]{1,0:T(8,128)(2,1)S(1)}, bf16[288,512]{1,0:T(8,128)(2,1)S(1)}, bf16[288...) custom-call(s32[2]{0:T(128)S(1)} %pad_add_fusion.ids, s32[8,64]{1,0:T(8,128)} %bitcast.14, s32[64]{0:T(128)} %refs_1_.1, ...), custom_call_target="tpu_custom_call" | custom-call | tf_op jit(solution)/shard_map/prepare/pallas_call | solution.py:451
  5.8 4.9 %all-to-all-start = ((bf16[4,2816,128]{2,1,0:T(8,128)(2,1)}), bf16[4,2816,128]{2,1,0:T(8,128)(2,1)}, u32[]{:S(2)}, u32[]{:S(2)}) async-start(bf16[4,2816,128]{2,1,0:T(8,128)(2,1)} %get-tuple-element.30), calls=%async_computation | async-start | bytes 5767168 | tf_op jit(solution)/shard_map/all_to_all | solution.py:480
  10.6 2.0 %collective-permute-start = (bf16[288,512]{1,0:T(8,128)(2,1)S(1)}, bf16[288,512]{1,0:T(8,128)(2,1)S(1)}, u32[]{:S(2)}, u32[]{:S(2)}) collective-permute-start(bf16[288,512]{1,0:T(8,128)(2,1)S(1)} %get-tuple-element.32), channel_id=1, source_target_pairs={{0,64},{64,128},{128,192},{192,0},{1,65},{65,129},{129,193},{193,1... | collective-permute-start | bytes 884744 | tf_op jit(solution)/shard_map/ppermute | solution.py:477
  12.6 2.6 %collective-permute-start.1 = (bf16[288,512]{1,0:T(8,128)(2,1)S(1)}, bf16[288,512]{1,0:T(8,128)(2,1)S(1)}, u32[]{:S(2)}, u32[]{:S(2)}) collective-permute-start(bf16[288,512]{1,0:T(8,128)(2,1)S(1)} %get-tuple-element.33), channel_id=1, source_target_pairs={{0,128},{64,192},{128,0},{192,64},{1,129},{65,193},{129,1},{193,65... | collective-permute-start | bytes 884744 | tf_op jit(solution)/shard_map/ppermute | solution.py:477
  16.3 3.0 %columns.1 = bf16[8,896,256]{2,1,0:T(8,128)(2,1)S(1)} custom-call(bf16[256,7168]{1,0:T(8,128)(2,1)} %w_hbm), custom_call_target="tpu_custom_call" | custom-call | tf_op jit(solution)/shard_map/columns/pallas_call | solution.py:483
  19.4 1.8 %copy-done = bf16[8,896,256]{2,1,0:T(8,128)(2,1)} copy-done((bf16[8,896,256]{2,1,0:T(8,128)(2,1)}, bf16[8,896,256]{2,1,0:T(8,128)(2,1)S(1)}, u32[]{:S(2)}) %copy-start) | copy-done | bytes 3670040
  21.2 6.8 %collective-permute-done.1.rest_2_ = bf16[288,512]{1,0:T(8,128)(2,1)S(1)} collective-permute-done((bf16[288,512]{1,0:T(8,128)(2,1)S(1)}, bf16[288,512]{1,0:T(8,128)(2,1)S(1)}, u32[]{:S(2)}, u32[]{:S(2)}) %collective-permute-start.1) | collective-permute-done | bytes 294944 | tf_op jit(solution)/shard_map/ppermute | solution.py:477
  28.6 1.7 %collective-permute-start.7 = (bf16[144,512]{1,0:T(8,128)(2,1)S(1)}, bf16[144,512]{1,0:T(8,128)(2,1)S(1)}, u32[]{:S(2)}, u32[]{:S(2)}) collective-permute-start(bf16[144,512]{1,0:T(8,128)(2,1)S(1)} %get-tuple-element.40.rest_2_), channel_id=1, source_target_pairs={{0,8},{8,16},{16,24},{24,32},{32,40},{40,48},{48,56},{56,0},{1,9},... | collective-permute-start | bytes 442376 | tf_op jit(solution)/shard_map/ppermute | solution.py:418
  30.3 4.0 %collective-permute-start.3 = (bf16[144,512]{1,0:T(8,128)(2,1)S(1)}, bf16[144,512]{1,0:T(8,128)(2,1)S(1)}, u32[]{:S(2)}, u32[]{:S(2)}) collective-permute-start(bf16[144,512]{1,0:T(8,128)(2,1)S(1)} %get-tuple-element.40.rest_2_), channel_id=1, source_target_pairs={{0,56},{8,0},{16,8},{24,16},{32,24},{40,32},{48,40},{56,48},{1,57}... | collective-permute-start | bytes 442376 | tf_op jit(solution)/shard_map/ppermute | solution.py:418
  34.3 2.7 %collective-permute-start.5 = (bf16[144,512]{1,0:T(8,128)(2,1)S(1)}, bf16[144,512]{1,0:T(8,128)(2,1)S(1)}, u32[]{:S(2)}, u32[]{:S(2)}) collective-permute-start(bf16[144,512]{1,0:T(8,128)(2,1)S(1)} %get-tuple-element.41.rest_10_), channel_id=1, source_target_pairs={{0,56},{8,0},{16,8},{24,16},{32,24},{40,32},{48,40},{56,48},{1,57}... | collective-permute-start | bytes 442376 | tf_op jit(solution)/shard_map/ppermute | solution.py:418
  37.2 2.8 %collective-permute-start.4 = (bf16[144,512]{1,0:T(8,128)(2,1)S(1)}, bf16[144,512]{1,0:T(8,128)(2,1)S(1)}, u32[]{:S(2)}, u32[]{:S(2)}) collective-permute-start(bf16[144,512]{1,0:T(8,128)(2,1)S(1)} %collective-permute-done.3.rest_3_), channel_id=1, source_target_pairs={{0,56},{8,0},{16,8},{24,16},{32,24},{40,32},{48,40},{56,48},{1,57}... | collective-permute-start | bytes 442376 | tf_op jit(solution)/shard_map/ppermute | solution.py:418
  40.5 3.0 %collective-permute-start.6 = (bf16[144,512]{1,0:T(8,128)(2,1)S(1)}, bf16[144,512]{1,0:T(8,128)(2,1)S(1)}, u32[]{:S(2)}, u32[]{:S(2)}) collective-permute-start(bf16[144,512]{1,0:T(8,128)(2,1)S(1)} %collective-permute-done.5.rest_11_), channel_id=1, source_target_pairs={{0,56},{8,0},{16,8},{24,16},{32,24},{40,32},{48,40},{56,48},{1,57}... | collective-permute-start | bytes 442376 | tf_op jit(solution)/shard_map/ppermute | solution.py:418
  43.8 3.2 %collective-permute-done.10.rest_16_ = bf16[144,512]{1,0:T(8,128)(2,1)S(1)} collective-permute-done((bf16[144,512]{1,0:T(8,128)(2,1)S(1)}, bf16[144,512]{1,0:T(8,128)(2,1)S(1)}, u32[]{:S(2)}, u32[]{:S(2)}) %collective-permute-start.10) | collective-permute-done | bytes 147488 | tf_op jit(solution)/shard_map/ppermute | solution.py:418
  47.1 2.9 %collective-permute-start.11 = (bf16[4,2816,128]{2,1,0:T(8,128)(2,1)}, bf16[4,2816,128]{2,1,0:T(8,128)(2,1)}, u32[]{:S(2)}, u32[]{:S(2)}) collective-permute-start(bf16[4,2816,128]{2,1,0:T(8,128)(2,1)} %all-to-all-done.near.rest_0_), channel_id=1, source_target_pairs={{0,1},{1,0},{2,3},{3,2},{4,5},{5,4},{6,7},{7,6},{8,9},{9,8},{10,11... | collective-permute-start | bytes 8650760 | tf_op jit(solution)/shard_map/ppermute | solution.py:414
  50.0 4.9 %all-to-all-start.1 = ((bf16[8,896,256]{2,1,0:T(8,128)(2,1)}), bf16[8,896,256]{2,1,0:T(8,128)(2,1)}, u32[]{:S(2)}, u32[]{:S(2)}) async-start(bf16[8,896,256]{2,1,0:T(8,128)(2,1)} %copy-done), calls=%async_computation.1 | async-start | bytes 7340032 | tf_op jit(solution)/shard_map/all_to_all | solution.py:517
  54.9 3.0 %collective-permute-start.15 = (bf16[144,512]{1,0:T(8,128)(2,1)S(1)}, bf16[144,512]{1,0:T(8,128)(2,1)S(1)}, u32[]{:S(2)}, u32[]{:S(2)}) collective-permute-start(bf16[144,512]{1,0:T(8,128)(2,1)S(1)} %collective-permute-done.6.rest_12_), channel_id=1, source_target_pairs={{0,56},{8,0},{16,8},{24,16},{32,24},{40,32},{48,40},{56,48},{1,57}... | collective-permute-start | bytes 442376 | tf_op jit(solution)/shard_map/ppermute | solution.py:418
  57.9 1.4 %collective-permute-start.12 = (bf16[144,512]{1,0:T(8,128)(2,1)S(1)}, bf16[144,512]{1,0:T(8,128)(2,1)S(1)}, u32[]{:S(2)}, u32[]{:S(2)}) collective-permute-start(bf16[144,512]{1,0:T(8,128)(2,1)S(1)} %collective-permute-done.4.rest_4_), channel_id=1, source_target_pairs={{0,56},{8,0},{16,8},{24,16},{32,24},{40,32},{48,40},{56,48},{1,57}... | collective-permute-start | bytes 442376 | tf_op jit(solution)/shard_map/ppermute | solution.py:418
  59.3 2.8 %collective-permute-done.13.rest_7_ = bf16[144,512]{1,0:T(8,128)(2,1)S(1)} collective-permute-done((bf16[144,512]{1,0:T(8,128)(2,1)S(1)}, bf16[144,512]{1,0:T(8,128)(2,1)S(1)}, u32[]{:S(2)}, u32[]{:S(2)}) %collective-permute-start.13) | collective-permute-done | bytes 147488 | tf_op jit(solution)/shard_map/ppermute | solution.py:418
  62.2 2.7 %collective-permute-start.16 = (bf16[144,512]{1,0:T(8,128)(2,1)S(1)}, bf16[144,512]{1,0:T(8,128)(2,1)S(1)}, u32[]{:S(2)}, u32[]{:S(2)}) collective-permute-start(bf16[144,512]{1,0:T(8,128)(2,1)S(1)} %collective-permute-done.15.rest_13_), channel_id=1, source_target_pairs={{0,56},{8,0},{16,8},{24,16},{32,24},{40,32},{48,40},{56,48},{1,57}... | collective-permute-start | bytes 442376 | tf_op jit(solution)/shard_map/ppermute | solution.py:418
  64.9 4.2 %query.1 = bf16[8,512,640]{2,1,0:T(8,128)(2,1)S(1)} custom-call(s32[41]{0:T(128)S(1)} %get-tuple-element.29.meta, bf16[4,2816,128]{2,1,0:T(8,128)(2,1)} %all-to-all-done.near.rest_0_, bf16[4,2816,128]{2,1,0:T(8,128)(2,1)} %collective-permute-done.11.far.rest_1_), custom_call_target="tpu_custom_call" | custom-call | tf_op jit(solution)/shard_map/query/pallas_call | solution.py:519
  69.1 14.1 %attention.1 = (bf16[4,272,256]{2,1,0:T(8,128)(2,1)S(1)}, bf16[4,272,256]{2,1,0:T(8,128)(2,1)S(1)}) custom-call(s32[41]{0:T(128)S(1)} %get-tuple-element.29.meta, bf16[8,512,640]{2,1,0:T(8,128)(2,1)S(1)} %query.1, bf16[4,2816,128]{2,1,0:T(8,128)(2,1)} %all-to-all-done.near.rest_0_, bf16[4,2816,128]{2,1,0:T(8,128)(2,1)} %collective-permute-done.11.far.rest_1_, ...), custom_call_target="tpu_custom_call" | custom-call | tf_op jit(solution)/shard_map/attention/pallas_call | solution.py:533
  83.1 1.3 collective-permute-start.18
  84.5 1.6 %collective-permute-done.18.got = bf16[4,272,256]{2,1,0:T(8,128)(2,1)S(1)} collective-permute-done((bf16[4,272,256]{2,1,0:T(8,128)(2,1)S(1)}, bf16[4,272,256]{2,1,0:T(8,128)(2,1)S(1)}, u32[]{:S(2)}, u32[]{:S(2)}) %collective-permute-start.18) | collective-permute-done | bytes 557088 | tf_op jit(solution)/shard_map/ppermute | solution.py:414
  88.0 2.9 %collective-permute-start.21 = (bf16[272,256]{1,0:T(8,128)(2,1)S(1)}, bf16[272,256]{1,0:T(8,128)(2,1)S(1)}, u32[]{:S(2)}, u32[]{:S(2)}) collective-permute-start(bf16[272,256]{1,0:T(8,128)(2,1)S(1)} %get-tuple-element.48), channel_id=1, source_target_pairs={{0,6},{2,4},{4,2},{6,0},{1,7},{3,5},{5,3},{7,1},{8,14},{10,12},{12... | collective-permute-start | bytes 417800 | tf_op jit(solution)/shard_map/ppermute | solution.py:414
  90.9 8.7 %collective-permute-done.19.refs_1_ = bf16[272,256]{1,0:T(8,128)(2,1)S(1)} collective-permute-done((bf16[272,256]{1,0:T(8,128)(2,1)S(1)}, bf16[272,256]{1,0:T(8,128)(2,1)S(1)}, u32[]{:S(2)}, u32[]{:S(2)}) %collective-permute-start.19) | collective-permute-done | bytes 139296 | tf_op jit(solution)/shard_map/ppermute | solution.py:414
  99.6 4.5 %collective-permute-done.20.refs_2_ = bf16[272,256]{1,0:T(8,128)(2,1)S(1)} collective-permute-done((bf16[272,256]{1,0:T(8,128)(2,1)S(1)}, bf16[272,256]{1,0:T(8,128)(2,1)S(1)}, u32[]{:S(2)}, u32[]{:S(2)}) %collective-permute-start.20) | collective-permute-done | bytes 139296 | tf_op jit(solution)/shard_map/ppermute | solution.py:414
  108.0 3.6 %collective-permute-done.24 = bf16[256,256]{1,0:T(8,128)(2,1)S(1)} collective-permute-done((bf16[256,256]{1,0:T(8,128)(2,1)S(1)}, bf16[256,256]{1,0:T(8,128)(2,1)S(1)}, u32[]{:S(2)}, u32[]{:S(2)}) %collective-permute-start.24) | collective-permute-done | bytes 131104 | tf_op jit(solution)/shard_map/ppermute | solution.py:414
  111.6 1.7 %collective-permute-done.22 = bf16[256,256]{1,0:T(8,128)(2,1)S(1)} collective-permute-done((bf16[256,256]{1,0:T(8,128)(2,1)S(1)}, bf16[256,256]{1,0:T(8,128)(2,1)S(1)}, u32[]{:S(2)}, u32[]{:S(2)}) %collective-permute-start.22) | collective-permute-done | bytes 131104 | tf_op jit(solution)/shard_map/ppermute | solution.py:414
  113.4 2.1 %collective-permute-start.25 = (bf16[4,256,256]{2,1,0:T(8,128)(2,1)S(1)}, bf16[4,256,256]{2,1,0:T(8,128)(2,1)S(1)}, u32[]{:S(2)}, u32[]{:S(2)}) collective-permute-start(bf16[4,256,256]{2,1,0:T(8,128)(2,1)S(1)} %pad_maximum_fusion.near), channel_id=1, source_target_pairs={{0,1},{1,0},{2,3},{3,2},{4,5},{5,4},{6,7},{7,6},{8,9},{9,8},{10,11... | collective-permute-start | bytes 1572872 | tf_op jit(solution)/shard_map/ppermute | solution.py:414
  115.5 1.5 %collective-permute-done.25.far = bf16[4,256,256]{2,1,0:T(8,128)(2,1)S(1)} collective-permute-done((bf16[4,256,256]{2,1,0:T(8,128)(2,1)S(1)}, bf16[4,256,256]{2,1,0:T(8,128)(2,1)S(1)}, u32[]{:S(2)}, u32[]{:S(2)}) %collective-permute-start.25) | collective-permute-done | bytes 524320 | tf_op jit(solution)/shard_map/ppermute | solution.py:414
  117.0 3.5 %output.1 = bf16[896,256]{1,0:T(8,128)(2,1)S(1)} custom-call(s32[41]{0:T(128)S(1)} %get-tuple-element.29.meta, bf16[8,896,256]{2,1,0:T(8,128)(2,1)} %all-to-all-done.1.weights, bf16[4,256,256]{2,1,0:T(8,128)(2,1)S(1)} %pad_maximum_fusion.near, bf16[4,256,256]{2,1,0:T(8,128)(2,1)S(1)} %collective-permute-done.25.far), custom_call_target="tpu_custom_call" | custom-call | tf_op jit(solution)/shard_map/output/pallas_call | solution.py:572
  120.5 21.1 %all_to_all.19 = bf16[8,112,256]{2,1,0:T(8,128)(2,1)S(1)} all-to-all(bf16[8,112,256]{2,1,0:T(8,128)(2,1)S(1)} %bitcast.9), channel_id=1, replica_groups=mesh['grp'=4,'z'=8,'x'=4,'c'=2] {'z'}, dimensions={0} | all-to-all | bytes 917504 | tf_op jit(solution)/shard_map/all_to_all | solution.py:580
  (38 shorter events, 9.5 us)
Async XLA Ops:
  5.8 41.3 %all-to-all-start = ((bf16[4,2816,128]{2,1,0:T(8,128)(2,1)}), bf16[4,2816,128]{2,1,0:T(8,128)(2,1)}, u32[]{:S(2)}, u32[]{:S(2)}) async-start(bf16[4,2816,128]{2,1,0:T(8,128)(2,1)} %get-tuple-element.30), calls=%async_computation | async-start | bytes 5767168 | tf_op jit(solution)/shard_map/all_to_all | solution.py:480
  10.6 10.5 %collective-permute-start = (bf16[288,512]{1,0:T(8,128)(2,1)S(1)}, bf16[288,512]{1,0:T(8,128)(2,1)S(1)}, u32[]{:S(2)}, u32[]{:S(2)}) collective-permute-start(bf16[288,512]{1,0:T(8,128)(2,1)S(1)} %get-tuple-element.32), channel_id=1, source_target_pairs={{0,64},{64,128},{128,192},{192,0},{1,65},{65,129},{129,193},{193,1... | collective-permute-start | bytes 884744 | tf_op jit(solution)/shard_map/ppermute | solution.py:477
  12.6 15.4 %collective-permute-start.1 = (bf16[288,512]{1,0:T(8,128)(2,1)S(1)}, bf16[288,512]{1,0:T(8,128)(2,1)S(1)}, u32[]{:S(2)}, u32[]{:S(2)}) collective-permute-start(bf16[288,512]{1,0:T(8,128)(2,1)S(1)} %get-tuple-element.33), channel_id=1, source_target_pairs={{0,128},{64,192},{128,0},{192,64},{1,129},{65,193},{129,1},{193,65... | collective-permute-start | bytes 884744 | tf_op jit(solution)/shard_map/ppermute | solution.py:477
  15.3 12.7 %collective-permute-start.2 = (bf16[288,512]{1,0:T(8,128)(2,1)S(1)}, bf16[288,512]{1,0:T(8,128)(2,1)S(1)}, u32[]{:S(2)}, u32[]{:S(2)}) collective-permute-start(bf16[288,512]{1,0:T(8,128)(2,1)S(1)} %get-tuple-element.34), channel_id=1, source_target_pairs={{0,192},{64,0},{128,64},{192,128},{1,193},{65,1},{129,65},{193,129... | collective-permute-start | bytes 884744 | tf_op jit(solution)/shard_map/ppermute | solution.py:477
  19.4 1.8 %copy-start = (bf16[8,896,256]{2,1,0:T(8,128)(2,1)}, bf16[8,896,256]{2,1,0:T(8,128)(2,1)S(1)}, u32[]{:S(2)}) copy-start(bf16[8,896,256]{2,1,0:T(8,128)(2,1)S(1)} %columns.1) | copy-start | bytes 11010052
  28.6 8.6 %collective-permute-start.7 = (bf16[144,512]{1,0:T(8,128)(2,1)S(1)}, bf16[144,512]{1,0:T(8,128)(2,1)S(1)}, u32[]{:S(2)}, u32[]{:S(2)}) collective-permute-start(bf16[144,512]{1,0:T(8,128)(2,1)S(1)} %get-tuple-element.40.rest_2_), channel_id=1, source_target_pairs={{0,8},{8,16},{16,24},{24,32},{32,40},{40,48},{48,56},{56,0},{1,9},... | collective-permute-start | bytes 442376 | tf_op jit(solution)/shard_map/ppermute | solution.py:418
  30.3 6.9 %collective-permute-start.3 = (bf16[144,512]{1,0:T(8,128)(2,1)S(1)}, bf16[144,512]{1,0:T(8,128)(2,1)S(1)}, u32[]{:S(2)}, u32[]{:S(2)}) collective-permute-start(bf16[144,512]{1,0:T(8,128)(2,1)S(1)} %get-tuple-element.40.rest_2_), channel_id=1, source_target_pairs={{0,56},{8,0},{16,8},{24,16},{32,24},{40,32},{48,40},{56,48},{1,57}... | collective-permute-start | bytes 442376 | tf_op jit(solution)/shard_map/ppermute | solution.py:418
  34.3 6.2 %collective-permute-start.9 = (bf16[144,512]{1,0:T(8,128)(2,1)S(1)}, bf16[144,512]{1,0:T(8,128)(2,1)S(1)}, u32[]{:S(2)}, u32[]{:S(2)}) collective-permute-start(bf16[144,512]{1,0:T(8,128)(2,1)S(1)} %get-tuple-element.41.rest_10_), channel_id=1, source_target_pairs={{0,8},{8,16},{16,24},{24,32},{32,40},{40,48},{48,56},{56,0},{1,9},... | collective-permute-start | bytes 442376 | tf_op jit(solution)/shard_map/ppermute | solution.py:418
  34.3 6.2 %collective-permute-start.5 = (bf16[144,512]{1,0:T(8,128)(2,1)S(1)}, bf16[144,512]{1,0:T(8,128)(2,1)S(1)}, u32[]{:S(2)}, u32[]{:S(2)}) collective-permute-start(bf16[144,512]{1,0:T(8,128)(2,1)S(1)} %get-tuple-element.41.rest_10_), channel_id=1, source_target_pairs={{0,56},{8,0},{16,8},{24,16},{32,24},{40,32},{48,40},{56,48},{1,57}... | collective-permute-start | bytes 442376 | tf_op jit(solution)/shard_map/ppermute | solution.py:418
  37.2 6.6 %collective-permute-start.8 = (bf16[144,512]{1,0:T(8,128)(2,1)S(1)}, bf16[144,512]{1,0:T(8,128)(2,1)S(1)}, u32[]{:S(2)}, u32[]{:S(2)}) collective-permute-start(bf16[144,512]{1,0:T(8,128)(2,1)S(1)} %collective-permute-done.7.rest_9_), channel_id=1, source_target_pairs={{0,8},{8,16},{16,24},{24,32},{32,40},{40,48},{48,56},{56,0},{1,9},... | collective-permute-start | bytes 442376 | tf_op jit(solution)/shard_map/ppermute | solution.py:418
  37.2 6.6 %collective-permute-start.4 = (bf16[144,512]{1,0:T(8,128)(2,1)S(1)}, bf16[144,512]{1,0:T(8,128)(2,1)S(1)}, u32[]{:S(2)}, u32[]{:S(2)}) collective-permute-start(bf16[144,512]{1,0:T(8,128)(2,1)S(1)} %collective-permute-done.3.rest_3_), channel_id=1, source_target_pairs={{0,56},{8,0},{16,8},{24,16},{32,24},{40,32},{48,40},{56,48},{1,57}... | collective-permute-start | bytes 442376 | tf_op jit(solution)/shard_map/ppermute | solution.py:418
  40.5 6.5 %collective-permute-start.10 = (bf16[144,512]{1,0:T(8,128)(2,1)S(1)}, bf16[144,512]{1,0:T(8,128)(2,1)S(1)}, u32[]{:S(2)}, u32[]{:S(2)}) collective-permute-start(bf16[144,512]{1,0:T(8,128)(2,1)S(1)} %collective-permute-done.9.rest_17_), channel_id=1, source_target_pairs={{0,8},{8,16},{16,24},{24,32},{32,40},{40,48},{48,56},{56,0},{1,9},... | collective-permute-start | bytes 442376 | tf_op jit(solution)/shard_map/ppermute | solution.py:418
  40.5 6.6 %collective-permute-start.6 = (bf16[144,512]{1,0:T(8,128)(2,1)S(1)}, bf16[144,512]{1,0:T(8,128)(2,1)S(1)}, u32[]{:S(2)}, u32[]{:S(2)}) collective-permute-start(bf16[144,512]{1,0:T(8,128)(2,1)S(1)} %collective-permute-done.5.rest_11_), channel_id=1, source_target_pairs={{0,56},{8,0},{16,8},{24,16},{32,24},{40,32},{48,40},{56,48},{1,57}... | collective-permute-start | bytes 442376 | tf_op jit(solution)/shard_map/ppermute | solution.py:418
  47.1 17.8 %collective-permute-start.11 = (bf16[4,2816,128]{2,1,0:T(8,128)(2,1)}, bf16[4,2816,128]{2,1,0:T(8,128)(2,1)}, u32[]{:S(2)}, u32[]{:S(2)}) collective-permute-start(bf16[4,2816,128]{2,1,0:T(8,128)(2,1)} %all-to-all-done.near.rest_0_), channel_id=1, source_target_pairs={{0,1},{1,0},{2,3},{3,2},{4,5},{5,4},{6,7},{7,6},{8,9},{9,8},{10,11... | collective-permute-start | bytes 8650760 | tf_op jit(solution)/shard_map/ppermute | solution.py:414
  50.0 54.7 %all-to-all-start.1 = ((bf16[8,896,256]{2,1,0:T(8,128)(2,1)}), bf16[8,896,256]{2,1,0:T(8,128)(2,1)}, u32[]{:S(2)}, u32[]{:S(2)}) async-start(bf16[8,896,256]{2,1,0:T(8,128)(2,1)} %copy-done), calls=%async_computation.1 | async-start | bytes 7340032 | tf_op jit(solution)/shard_map/all_to_all | solution.py:517
  54.9 7.3 %collective-permute-start.13 = (bf16[144,512]{1,0:T(8,128)(2,1)S(1)}, bf16[144,512]{1,0:T(8,128)(2,1)S(1)}, u32[]{:S(2)}, u32[]{:S(2)}) collective-permute-start(bf16[144,512]{1,0:T(8,128)(2,1)S(1)} %collective-permute-done.8.rest_8_), channel_id=1, source_target_pairs={{0,8},{8,16},{16,24},{24,32},{32,40},{40,48},{48,56},{56,0},{1,9},... | collective-permute-start | bytes 442376 | tf_op jit(solution)/shard_map/ppermute | solution.py:418
  54.9 7.3 %collective-permute-start.15 = (bf16[144,512]{1,0:T(8,128)(2,1)S(1)}, bf16[144,512]{1,0:T(8,128)(2,1)S(1)}, u32[]{:S(2)}, u32[]{:S(2)}) collective-permute-start(bf16[144,512]{1,0:T(8,128)(2,1)S(1)} %collective-permute-done.6.rest_12_), channel_id=1, source_target_pairs={{0,56},{8,0},{16,8},{24,16},{32,24},{40,32},{48,40},{56,48},{1,57}... | collective-permute-start | bytes 442376 | tf_op jit(solution)/shard_map/ppermute | solution.py:418
  57.9 11.2 %collective-permute-start.12 = (bf16[144,512]{1,0:T(8,128)(2,1)S(1)}, bf16[144,512]{1,0:T(8,128)(2,1)S(1)}, u32[]{:S(2)}, u32[]{:S(2)}) collective-permute-start(bf16[144,512]{1,0:T(8,128)(2,1)S(1)} %collective-permute-done.4.rest_4_), channel_id=1, source_target_pairs={{0,56},{8,0},{16,8},{24,16},{32,24},{40,32},{48,40},{56,48},{1,57}... | collective-permute-start | bytes 442376 | tf_op jit(solution)/shard_map/ppermute | solution.py:418
  59.3 9.7 %collective-permute-start.17 = (bf16[144,512]{1,0:T(8,128)(2,1)S(1)}, bf16[144,512]{1,0:T(8,128)(2,1)S(1)}, u32[]{:S(2)}, u32[]{:S(2)}) collective-permute-start(bf16[144,512]{1,0:T(8,128)(2,1)S(1)} %collective-permute-done.10.rest_16_), channel_id=1, source_target_pairs={{0,8},{8,16},{16,24},{24,32},{32,40},{40,48},{48,56},{56,0},{1,9},... | collective-permute-start | bytes 442376 | tf_op jit(solution)/shard_map/ppermute | solution.py:418
  62.2 6.9 %collective-permute-start.14 = (bf16[144,512]{1,0:T(8,128)(2,1)S(1)}, bf16[144,512]{1,0:T(8,128)(2,1)S(1)}, u32[]{:S(2)}, u32[]{:S(2)}) collective-permute-start(bf16[144,512]{1,0:T(8,128)(2,1)S(1)} %collective-permute-done.13.rest_7_), channel_id=1, source_target_pairs={{0,8},{8,16},{16,24},{24,32},{32,40},{40,48},{48,56},{56,0},{1,9},... | collective-permute-start | bytes 442376 | tf_op jit(solution)/shard_map/ppermute | solution.py:418
  62.2 6.9 %collective-permute-start.16 = (bf16[144,512]{1,0:T(8,128)(2,1)S(1)}, bf16[144,512]{1,0:T(8,128)(2,1)S(1)}, u32[]{:S(2)}, u32[]{:S(2)}) collective-permute-start(bf16[144,512]{1,0:T(8,128)(2,1)S(1)} %collective-permute-done.15.rest_13_), channel_id=1, source_target_pairs={{0,56},{8,0},{16,8},{24,16},{32,24},{40,32},{48,40},{56,48},{1,57}... | collective-permute-start | bytes 442376 | tf_op jit(solution)/shard_map/ppermute | solution.py:418
  83.1 2.9 %collective-permute-start.18 = (bf16[4,272,256]{2,1,0:T(8,128)(2,1)S(1)}, bf16[4,272,256]{2,1,0:T(8,128)(2,1)S(1)}, u32[]{:S(2)}, u32[]{:S(2)}) collective-permute-start(bf16[4,272,256]{2,1,0:T(8,128)(2,1)S(1)} %get-tuple-element.44), channel_id=1, source_target_pairs={{0,1},{1,0},{2,3},{3,2},{4,5},{5,4},{6,7},{7,6},{8,9},{9,8},{10,11... | collective-permute-start | bytes 1671176 | tf_op jit(solution)/shard_map/ppermute | solution.py:414
  86.9 12.7 %collective-permute-start.19 = (bf16[272,256]{1,0:T(8,128)(2,1)S(1)}, bf16[272,256]{1,0:T(8,128)(2,1)S(1)}, u32[]{:S(2)}, u32[]{:S(2)}) collective-permute-start(bf16[272,256]{1,0:T(8,128)(2,1)S(1)} %get-tuple-element.46), channel_id=1, source_target_pairs={{0,2},{2,0},{4,6},{6,4},{1,3},{3,1},{5,7},{7,5},{8,10},{10,8},{12,... | collective-permute-start | bytes 417800 | tf_op jit(solution)/shard_map/ppermute | solution.py:414
  88.0 16.1 %collective-permute-start.20 = (bf16[272,256]{1,0:T(8,128)(2,1)S(1)}, bf16[272,256]{1,0:T(8,128)(2,1)S(1)}, u32[]{:S(2)}, u32[]{:S(2)}) collective-permute-start(bf16[272,256]{1,0:T(8,128)(2,1)S(1)} %get-tuple-element.47), channel_id=1, source_target_pairs={{0,4},{2,6},{4,0},{6,2},{1,5},{3,7},{5,1},{7,3},{8,12},{10,14},{12... | collective-permute-start | bytes 417800 | tf_op jit(solution)/shard_map/ppermute | solution.py:414
  88.0 16.1 %collective-permute-start.21 = (bf16[272,256]{1,0:T(8,128)(2,1)S(1)}, bf16[272,256]{1,0:T(8,128)(2,1)S(1)}, u32[]{:S(2)}, u32[]{:S(2)}) collective-permute-start(bf16[272,256]{1,0:T(8,128)(2,1)S(1)} %get-tuple-element.48), channel_id=1, source_target_pairs={{0,6},{2,4},{4,2},{6,0},{1,7},{3,5},{5,3},{7,1},{8,14},{10,12},{12... | collective-permute-start | bytes 417800 | tf_op jit(solution)/shard_map/ppermute | solution.py:414
  104.7 6.9 %collective-permute-start.24 = (bf16[256,256]{1,0:T(8,128)(2,1)S(1)}, bf16[256,256]{1,0:T(8,128)(2,1)S(1)}, u32[]{:S(2)}, u32[]{:S(2)}) collective-permute-start(bf16[256,256]{1,0:T(8,128)(2,1)S(1)} %heads.1), channel_id=1, source_target_pairs={{0,6},{2,4},{4,2},{6,0},{1,7},{3,5},{5,3},{7,1},{8,14},{10,12},{12... | collective-permute-start | bytes 393224 | tf_op jit(solution)/shard_map/ppermute | solution.py:414
  105.6 5.9 %collective-permute-start.23 = (bf16[256,256]{1,0:T(8,128)(2,1)S(1)}, bf16[256,256]{1,0:T(8,128)(2,1)S(1)}, u32[]{:S(2)}, u32[]{:S(2)}) collective-permute-start(bf16[256,256]{1,0:T(8,128)(2,1)S(1)} %heads.1), channel_id=1, source_target_pairs={{0,4},{2,6},{4,0},{6,2},{1,5},{3,7},{5,1},{7,3},{8,12},{10,14},{12... | collective-permute-start | bytes 393224 | tf_op jit(solution)/shard_map/ppermute | solution.py:414
  106.8 6.5 %collective-permute-start.22 = (bf16[256,256]{1,0:T(8,128)(2,1)S(1)}, bf16[256,256]{1,0:T(8,128)(2,1)S(1)}, u32[]{:S(2)}, u32[]{:S(2)}) collective-permute-start(bf16[256,256]{1,0:T(8,128)(2,1)S(1)} %heads.1), channel_id=1, source_target_pairs={{0,2},{2,0},{4,6},{6,4},{1,3},{3,1},{5,7},{7,5},{8,10},{10,8},{12,... | collective-permute-start | bytes 393224 | tf_op jit(solution)/shard_map/ppermute | solution.py:414
  113.4 3.7 %collective-permute-start.25 = (bf16[4,256,256]{2,1,0:T(8,128)(2,1)S(1)}, bf16[4,256,256]{2,1,0:T(8,128)(2,1)S(1)}, u32[]{:S(2)}, u32[]{:S(2)}) collective-permute-start(bf16[4,256,256]{2,1,0:T(8,128)(2,1)S(1)} %pad_maximum_fusion.near), channel_id=1, source_target_pairs={{0,1},{1,0},{2,3},{3,2},{4,5},{5,4},{6,7},{7,6},{8,9},{9,8},{10,11... | collective-permute-start | bytes 1572872 | tf_op jit(solution)/shard_map/ppermute | solution.py:414

commit v7 on v6

--- a/solution.py
+++ b/solution.py
@@ -385,18 +385,19 @@
 
 def output_kernel(meta, weights, near, far, out):
     block = out.shape[0] // NX
-    spot = meta[SPOT]
-    for c, sides in enumerate(((near, far), (far, near))):
-
-        @pl.when((meta[PLACE] & (NC - 1)) == c)
+    for place in range(NXC):
+
+        @pl.when(meta[PLACE] == place)
         def _():
-            heads = [sides[s % NC][spot ^ (s // NC)] for s in range(NXC)]
             for i in range(NX):
                 part = slice(i * block, (i + 1) * block)
                 mixed = None
                 for s in range(NXC):
                     term = lax.dot_general(
-                        weights[s, part, :], heads[s], NT, preferred_element_type=F32
+                        weights[place ^ s, part, :],
+                        (near, far)[s % NC][s // NC],
+                        NT,
+                        preferred_element_type=F32,
                     )
                     mixed = term if mixed is None else mixed + term
                 out[part, :] = mixed.astype(BF16)

time: 143 us -> 143 us (level)
  no operation moved by 1% of the time
where the time goes in v7:
time: 143 us; the launch traced here: 142 us
  starting transfers between devices  50.4 us (35%)
  waiting for transfers between devices  35.6 us (25%)
  Pallas kernels  32.5 us (23%)
  blocking collectives  21.1 us (15%)
  local copies, waits for them, and re-layouts  1.77 us (1%)
    ppermute x9, waiting for transfers between devices, sent(): return lax.ppermute(x, axis, [(i, i ^ k) for i in range(size)])  21.6 us
    ppermute x14, starting transfers between devices, shifted(): return lax.ppermute(x, 'z', [(i, (i + k) % NZ) for i in range(NZ)])  21.3 us
    all_to_all x1, blocking collectives, local(): mixed = lax.all_to_all(mixed, 'z', split_axis=0, concat_axis=0, tiled=True)  21.1 us
    pallas_call x1, Pallas kernels, local(): pl.pallas_call(functools.partial(attention_kernel, scale=scale), out_shap...  14.1 us
    ppermute x9, starting transfers between devices, sent(): return lax.ppermute(x, axis, [(i, i ^ k) for i in range(size)])  13.6 us
    ppermute x14, waiting for transfers between devices, shifted(): return lax.ppermute(x, 'z', [(i, (i + k) % NZ) for i in range(NZ)])  7.11 us
    ppermute x3, waiting for transfers between devices, local(): lax.ppermute(packed[k], 'grp', [(i, (i + k) % groups) for i in range(grou...  6.83 us
    ppermute x3, starting transfers between devices, local(): lax.ppermute(packed[k], 'grp', [(i, (i + k) % groups) for i in range(grou...  5.7 us
  transfers between devices with their start and end apart: 28, of which 13 were waited for; matrix products, arithmetic and copies ran while one was open for 0% of the time, Pallas kernels for 16%

profile of v7, /device:TPU:1, one launch (start us, length us, event | category | flops | bytes accessed | tf_op | source)
XLA Modules:
  0.0 142.3 jit_solution(2805043505680884292)
XLA Ops:
  0.1 5.7 %prepare.1 = (s32[41]{0:T(128)S(1)}, bf16[4,2816,128]{2,1,0:T(8,128)(2,1)}, bf16[288,512]{1,0:T(8,128)(2,1)S(1)}, bf16[288,512]{1,0:T(8,128)(2,1)S(1)}, bf16[288...) custom-call(s32[2]{0:T(128)S(1)} %pad_add_fusion.ids, s32[8,64]{1,0:T(8,128)} %bitcast.14, s32[64]{0:T(128)} %refs_1_.1, ...), custom_call_target="tpu_custom_call" | custom-call | tf_op jit(solution)/shard_map/prepare/pallas_call | solution.py:452
  5.8 4.9 %all-to-all-start = ((bf16[4,2816,128]{2,1,0:T(8,128)(2,1)}), bf16[4,2816,128]{2,1,0:T(8,128)(2,1)}, u32[]{:S(2)}, u32[]{:S(2)}) async-start(bf16[4,2816,128]{2,1,0:T(8,128)(2,1)} %get-tuple-element.30), calls=%async_computation | async-start | bytes 5767168 | tf_op jit(solution)/shard_map/all_to_all | solution.py:481
  10.6 2.0 %collective-permute-start = (bf16[288,512]{1,0:T(8,128)(2,1)S(1)}, bf16[288,512]{1,0:T(8,128)(2,1)S(1)}, u32[]{:S(2)}, u32[]{:S(2)}) collective-permute-start(bf16[288,512]{1,0:T(8,128)(2,1)S(1)} %get-tuple-element.32), channel_id=1, source_target_pairs={{0,64},{64,128},{128,192},{192,0},{1,65},{65,129},{129,193},{193,1... | collective-permute-start | bytes 884744 | tf_op jit(solution)/shard_map/ppermute | solution.py:478
  12.6 2.6 %collective-permute-start.1 = (bf16[288,512]{1,0:T(8,128)(2,1)S(1)}, bf16[288,512]{1,0:T(8,128)(2,1)S(1)}, u32[]{:S(2)}, u32[]{:S(2)}) collective-permute-start(bf16[288,512]{1,0:T(8,128)(2,1)S(1)} %get-tuple-element.33), channel_id=1, source_target_pairs={{0,128},{64,192},{128,0},{192,64},{1,129},{65,193},{129,1},{193,65... | collective-permute-start | bytes 884744 | tf_op jit(solution)/shard_map/ppermute | solution.py:478
  16.3 3.0 %columns.1 = bf16[8,896,256]{2,1,0:T(8,128)(2,1)S(1)} custom-call(bf16[256,7168]{1,0:T(8,128)(2,1)} %w_hbm), custom_call_target="tpu_custom_call" | custom-call | tf_op jit(solution)/shard_map/columns/pallas_call | solution.py:484
  19.4 1.8 %copy-done = bf16[8,896,256]{2,1,0:T(8,128)(2,1)} copy-done((bf16[8,896,256]{2,1,0:T(8,128)(2,1)}, bf16[8,896,256]{2,1,0:T(8,128)(2,1)S(1)}, u32[]{:S(2)}) %copy-start) | copy-done | bytes 3670040
  21.2 6.8 %collective-permute-done.1.rest_2_ = bf16[288,512]{1,0:T(8,128)(2,1)S(1)} collective-permute-done((bf16[288,512]{1,0:T(8,128)(2,1)S(1)}, bf16[288,512]{1,0:T(8,128)(2,1)S(1)}, u32[]{:S(2)}, u32[]{:S(2)}) %collective-permute-start.1) | collective-permute-done | bytes 294944 | tf_op jit(solution)/shard_map/ppermute | solution.py:478
  28.6 1.7 %collective-permute-start.7 = (bf16[144,512]{1,0:T(8,128)(2,1)S(1)}, bf16[144,512]{1,0:T(8,128)(2,1)S(1)}, u32[]{:S(2)}, u32[]{:S(2)}) collective-permute-start(bf16[144,512]{1,0:T(8,128)(2,1)S(1)} %get-tuple-element.40.rest_2_), channel_id=1, source_target_pairs={{0,8},{8,16},{16,24},{24,32},{32,40},{40,48},{48,56},{56,0},{1,9},... | collective-permute-start | bytes 442376 | tf_op jit(solution)/shard_map/ppermute | solution.py:419
  30.3 4.0 %collective-permute-start.3 = (bf16[144,512]{1,0:T(8,128)(2,1)S(1)}, bf16[144,512]{1,0:T(8,128)(2,1)S(1)}, u32[]{:S(2)}, u32[]{:S(2)}) collective-permute-start(bf16[144,512]{1,0:T(8,128)(2,1)S(1)} %get-tuple-element.40.rest_2_), channel_id=1, source_target_pairs={{0,56},{8,0},{16,8},{24,16},{32,24},{40,32},{48,40},{56,48},{1,57}... | collective-permute-start | bytes 442376 | tf_op jit(solution)/shard_map/ppermute | solution.py:419
  34.3 2.7 %collective-permute-start.5 = (bf16[144,512]{1,0:T(8,128)(2,1)S(1)}, bf16[144,512]{1,0:T(8,128)(2,1)S(1)}, u32[]{:S(2)}, u32[]{:S(2)}) collective-permute-start(bf16[144,512]{1,0:T(8,128)(2,1)S(1)} %get-tuple-element.41.rest_10_), channel_id=1, source_target_pairs={{0,56},{8,0},{16,8},{24,16},{32,24},{40,32},{48,40},{56,48},{1,57}... | collective-permute-start | bytes 442376 | tf_op jit(solution)/shard_map/ppermute | solution.py:419
  37.2 2.8 %collective-permute-start.4 = (bf16[144,512]{1,0:T(8,128)(2,1)S(1)}, bf16[144,512]{1,0:T(8,128)(2,1)S(1)}, u32[]{:S(2)}, u32[]{:S(2)}) collective-permute-start(bf16[144,512]{1,0:T(8,128)(2,1)S(1)} %collective-permute-done.3.rest_3_), channel_id=1, source_target_pairs={{0,56},{8,0},{16,8},{24,16},{32,24},{40,32},{48,40},{56,48},{1,57}... | collective-permute-start | bytes 442376 | tf_op jit(solution)/shard_map/ppermute | solution.py:419
  40.5 3.0 %collective-permute-start.6 = (bf16[144,512]{1,0:T(8,128)(2,1)S(1)}, bf16[144,512]{1,0:T(8,128)(2,1)S(1)}, u32[]{:S(2)}, u32[]{:S(2)}) collective-permute-start(bf16[144,512]{1,0:T(8,128)(2,1)S(1)} %collective-permute-done.5.rest_11_), channel_id=1, source_target_pairs={{0,56},{8,0},{16,8},{24,16},{32,24},{40,32},{48,40},{56,48},{1,57}... | collective-permute-start | bytes 442376 | tf_op jit(solution)/shard_map/ppermute | solution.py:419
  43.8 3.2 %collective-permute-done.10.rest_16_ = bf16[144,512]{1,0:T(8,128)(2,1)S(1)} collective-permute-done((bf16[144,512]{1,0:T(8,128)(2,1)S(1)}, bf16[144,512]{1,0:T(8,128)(2,1)S(1)}, u32[]{:S(2)}, u32[]{:S(2)}) %collective-permute-start.10) | collective-permute-done | bytes 147488 | tf_op jit(solution)/shard_map/ppermute | solution.py:419
  47.1 2.9 %collective-permute-start.11 = (bf16[4,2816,128]{2,1,0:T(8,128)(2,1)}, bf16[4,2816,128]{2,1,0:T(8,128)(2,1)}, u32[]{:S(2)}, u32[]{:S(2)}) collective-permute-start(bf16[4,2816,128]{2,1,0:T(8,128)(2,1)} %all-to-all-done.near.rest_0_), channel_id=1, source_target_pairs={{0,1},{1,0},{2,3},{3,2},{4,5},{5,4},{6,7},{7,6},{8,9},{9,8},{10,11... | collective-permute-start | bytes 8650760 | tf_op jit(solution)/shard_map/ppermute | solution.py:415
  50.0 4.9 %all-to-all-start.1 = ((bf16[8,896,256]{2,1,0:T(8,128)(2,1)}), bf16[8,896,256]{2,1,0:T(8,128)(2,1)}, u32[]{:S(2)}, u32[]{:S(2)}) async-start(bf16[8,896,256]{2,1,0:T(8,128)(2,1)} %copy-done), calls=%async_computation.1 | async-start | bytes 7340032 | tf_op jit(solution)/shard_map/all_to_all | solution.py:518
  54.9 3.0 %collective-permute-start.15 = (bf16[144,512]{1,0:T(8,128)(2,1)S(1)}, bf16[144,512]{1,0:T(8,128)(2,1)S(1)}, u32[]{:S(2)}, u32[]{:S(2)}) collective-permute-start(bf16[144,512]{1,0:T(8,128)(2,1)S(1)} %collective-permute-done.6.rest_12_), channel_id=1, source_target_pairs={{0,56},{8,0},{16,8},{24,16},{32,24},{40,32},{48,40},{56,48},{1,57}... | collective-permute-start | bytes 442376 | tf_op jit(solution)/shard_map/ppermute | solution.py:419
  57.9 1.4 %collective-permute-start.12 = (bf16[144,512]{1,0:T(8,128)(2,1)S(1)}, bf16[144,512]{1,0:T(8,128)(2,1)S(1)}, u32[]{:S(2)}, u32[]{:S(2)}) collective-permute-start(bf16[144,512]{1,0:T(8,128)(2,1)S(1)} %collective-permute-done.4.rest_4_), channel_id=1, source_target_pairs={{0,56},{8,0},{16,8},{24,16},{32,24},{40,32},{48,40},{56,48},{1,57}... | collective-permute-start | bytes 442376 | tf_op jit(solution)/shard_map/ppermute | solution.py:419
  59.3 2.8 %collective-permute-done.13.rest_7_ = bf16[144,512]{1,0:T(8,128)(2,1)S(1)} collective-permute-done((bf16[144,512]{1,0:T(8,128)(2,1)S(1)}, bf16[144,512]{1,0:T(8,128)(2,1)S(1)}, u32[]{:S(2)}, u32[]{:S(2)}) %collective-permute-start.13) | collective-permute-done | bytes 147488 | tf_op jit(solution)/shard_map/ppermute | solution.py:419
  62.2 2.7 %collective-permute-start.16 = (bf16[144,512]{1,0:T(8,128)(2,1)S(1)}, bf16[144,512]{1,0:T(8,128)(2,1)S(1)}, u32[]{:S(2)}, u32[]{:S(2)}) collective-permute-start(bf16[144,512]{1,0:T(8,128)(2,1)S(1)} %collective-permute-done.15.rest_13_), channel_id=1, source_target_pairs={{0,56},{8,0},{16,8},{24,16},{32,24},{40,32},{48,40},{56,48},{1,57}... | collective-permute-start | bytes 442376 | tf_op jit(solution)/shard_map/ppermute | solution.py:419
  64.9 4.2 %query.1 = bf16[8,512,640]{2,1,0:T(8,128)(2,1)S(1)} custom-call(s32[41]{0:T(128)S(1)} %get-tuple-element.29.meta, bf16[4,2816,128]{2,1,0:T(8,128)(2,1)} %all-to-all-done.near.rest_0_, bf16[4,2816,128]{2,1,0:T(8,128)(2,1)} %collective-permute-done.11.far.rest_1_), custom_call_target="tpu_custom_call" | custom-call | tf_op jit(solution)/shard_map/query/pallas_call | solution.py:520
  69.1 14.1 %attention.1 = (bf16[4,272,256]{2,1,0:T(8,128)(2,1)S(1)}, bf16[4,272,256]{2,1,0:T(8,128)(2,1)S(1)}) custom-call(s32[41]{0:T(128)S(1)} %get-tuple-element.29.meta, bf16[8,512,640]{2,1,0:T(8,128)(2,1)S(1)} %query.1, bf16[4,2816,128]{2,1,0:T(8,128)(2,1)} %all-to-all-done.near.rest_0_, bf16[4,2816,128]{2,1,0:T(8,128)(2,1)} %collective-permute-done.11.far.rest_1_, ...), custom_call_target="tpu_custom_call" | custom-call | tf_op jit(solution)/shard_map/attention/pallas_call | solution.py:534
  83.1 1.3 collective-permute-start.18
  84.5 1.6 %collective-permute-done.18.got = bf16[4,272,256]{2,1,0:T(8,128)(2,1)S(1)} collective-permute-done((bf16[4,272,256]{2,1,0:T(8,128)(2,1)S(1)}, bf16[4,272,256]{2,1,0:T(8,128)(2,1)S(1)}, u32[]{:S(2)}, u32[]{:S(2)}) %collective-permute-start.18) | collective-permute-done | bytes 557088 | tf_op jit(solution)/shard_map/ppermute | solution.py:415
  88.0 2.9 %collective-permute-start.21 = (bf16[272,256]{1,0:T(8,128)(2,1)S(1)}, bf16[272,256]{1,0:T(8,128)(2,1)S(1)}, u32[]{:S(2)}, u32[]{:S(2)}) collective-permute-start(bf16[272,256]{1,0:T(8,128)(2,1)S(1)} %get-tuple-element.48), channel_id=1, source_target_pairs={{0,6},{2,4},{4,2},{6,0},{1,7},{3,5},{5,3},{7,1},{8,14},{10,12},{12... | collective-permute-start | bytes 417800 | tf_op jit(solution)/shard_map/ppermute | solution.py:415
  90.9 8.7 %collective-permute-done.19.refs_1_ = bf16[272,256]{1,0:T(8,128)(2,1)S(1)} collective-permute-done((bf16[272,256]{1,0:T(8,128)(2,1)S(1)}, bf16[272,256]{1,0:T(8,128)(2,1)S(1)}, u32[]{:S(2)}, u32[]{:S(2)}) %collective-permute-start.19) | collective-permute-done | bytes 139296 | tf_op jit(solution)/shard_map/ppermute | solution.py:415
  99.6 4.5 %collective-permute-done.20.refs_2_ = bf16[272,256]{1,0:T(8,128)(2,1)S(1)} collective-permute-done((bf16[272,256]{1,0:T(8,128)(2,1)S(1)}, bf16[272,256]{1,0:T(8,128)(2,1)S(1)}, u32[]{:S(2)}, u32[]{:S(2)}) %collective-permute-start.20) | collective-permute-done | bytes 139296 | tf_op jit(solution)/shard_map/ppermute | solution.py:415
  108.0 3.6 %collective-permute-done.24 = bf16[256,256]{1,0:T(8,128)(2,1)S(1)} collective-permute-done((bf16[256,256]{1,0:T(8,128)(2,1)S(1)}, bf16[256,256]{1,0:T(8,128)(2,1)S(1)}, u32[]{:S(2)}, u32[]{:S(2)}) %collective-permute-start.24) | collective-permute-done | bytes 131104 | tf_op jit(solution)/shard_map/ppermute | solution.py:415
  111.6 1.7 %collective-permute-done.22 = bf16[256,256]{1,0:T(8,128)(2,1)S(1)} collective-permute-done((bf16[256,256]{1,0:T(8,128)(2,1)S(1)}, bf16[256,256]{1,0:T(8,128)(2,1)S(1)}, u32[]{:S(2)}, u32[]{:S(2)}) %collective-permute-start.22) | collective-permute-done | bytes 131104 | tf_op jit(solution)/shard_map/ppermute | solution.py:415
  113.4 2.1 %collective-permute-start.25 = (bf16[4,256,256]{2,1,0:T(8,128)(2,1)S(1)}, bf16[4,256,256]{2,1,0:T(8,128)(2,1)S(1)}, u32[]{:S(2)}, u32[]{:S(2)}) collective-permute-start(bf16[4,256,256]{2,1,0:T(8,128)(2,1)S(1)} %pad_maximum_fusion.near), channel_id=1, source_target_pairs={{0,1},{1,0},{2,3},{3,2},{4,5},{5,4},{6,7},{7,6},{8,9},{9,8},{10,11... | collective-permute-start | bytes 1572872 | tf_op jit(solution)/shard_map/ppermute | solution.py:415
  115.5 1.5 %collective-permute-done.25.far = bf16[4,256,256]{2,1,0:T(8,128)(2,1)S(1)} collective-permute-done((bf16[4,256,256]{2,1,0:T(8,128)(2,1)S(1)}, bf16[4,256,256]{2,1,0:T(8,128)(2,1)S(1)}, u32[]{:S(2)}, u32[]{:S(2)}) %collective-permute-start.25) | collective-permute-done | bytes 524320 | tf_op jit(solution)/shard_map/ppermute | solution.py:415
  117.0 3.5 %output.1 = bf16[896,256]{1,0:T(8,128)(2,1)S(1)} custom-call(s32[41]{0:T(128)S(1)} %get-tuple-element.29.meta, bf16[8,896,256]{2,1,0:T(8,128)(2,1)} %all-to-all-done.1.weights, bf16[4,256,256]{2,1,0:T(8,128)(2,1)S(1)} %pad_maximum_fusion.near, bf16[4,256,256]{2,1,0:T(8,128)(2,1)S(1)} %collective-permute-done.25.far), custom_call_target="tpu_custom_call" | custom-call | tf_op jit(solution)/shard_map/output/pallas_call | solution.py:573
  120.5 21.1 %all_to_all.19 = bf16[8,112,256]{2,1,0:T(8,128)(2,1)S(1)} all-to-all(bf16[8,112,256]{2,1,0:T(8,128)(2,1)S(1)} %bitcast.9), channel_id=1, replica_groups=mesh['grp'=4,'z'=8,'x'=4,'c'=2] {'z'}, dimensions={0} | all-to-all | bytes 917504 | tf_op jit(solution)/shard_map/all_to_all | solution.py:581
  (38 shorter events, 9.5 us)
Async XLA Ops:
  5.8 41.3 %all-to-all-start = ((bf16[4,2816,128]{2,1,0:T(8,128)(2,1)}), bf16[4,2816,128]{2,1,0:T(8,128)(2,1)}, u32[]{:S(2)}, u32[]{:S(2)}) async-start(bf16[4,2816,128]{2,1,0:T(8,128)(2,1)} %get-tuple-element.30), calls=%async_computation | async-start | bytes 5767168 | tf_op jit(solution)/shard_map/all_to_all | solution.py:481
  10.6 10.5 %collective-permute-start = (bf16[288,512]{1,0:T(8,128)(2,1)S(1)}, bf16[288,512]{1,0:T(8,128)(2,1)S(1)}, u32[]{:S(2)}, u32[]{:S(2)}) collective-permute-start(bf16[288,512]{1,0:T(8,128)(2,1)S(1)} %get-tuple-element.32), channel_id=1, source_target_pairs={{0,64},{64,128},{128,192},{192,0},{1,65},{65,129},{129,193},{193,1... | collective-permute-start | bytes 884744 | tf_op jit(solution)/shard_map/ppermute | solution.py:478
  12.6 15.4 %collective-permute-start.1 = (bf16[288,512]{1,0:T(8,128)(2,1)S(1)}, bf16[288,512]{1,0:T(8,128)(2,1)S(1)}, u32[]{:S(2)}, u32[]{:S(2)}) collective-permute-start(bf16[288,512]{1,0:T(8,128)(2,1)S(1)} %get-tuple-element.33), channel_id=1, source_target_pairs={{0,128},{64,192},{128,0},{192,64},{1,129},{65,193},{129,1},{193,65... | collective-permute-start | bytes 884744 | tf_op jit(solution)/shard_map/ppermute | solution.py:478
  15.3 12.7 %collective-permute-start.2 = (bf16[288,512]{1,0:T(8,128)(2,1)S(1)}, bf16[288,512]{1,0:T(8,128)(2,1)S(1)}, u32[]{:S(2)}, u32[]{:S(2)}) collective-permute-start(bf16[288,512]{1,0:T(8,128)(2,1)S(1)} %get-tuple-element.34), channel_id=1, source_target_pairs={{0,192},{64,0},{128,64},{192,128},{1,193},{65,1},{129,65},{193,129... | collective-permute-start | bytes 884744 | tf_op jit(solution)/shard_map/ppermute | solution.py:478
  19.4 1.8 %copy-start = (bf16[8,896,256]{2,1,0:T(8,128)(2,1)}, bf16[8,896,256]{2,1,0:T(8,128)(2,1)S(1)}, u32[]{:S(2)}) copy-start(bf16[8,896,256]{2,1,0:T(8,128)(2,1)S(1)} %columns.1) | copy-start | bytes 11010052
  28.6 8.6 %collective-permute-start.7 = (bf16[144,512]{1,0:T(8,128)(2,1)S(1)}, bf16[144,512]{1,0:T(8,128)(2,1)S(1)}, u32[]{:S(2)}, u32[]{:S(2)}) collective-permute-start(bf16[144,512]{1,0:T(8,128)(2,1)S(1)} %get-tuple-element.40.rest_2_), channel_id=1, source_target_pairs={{0,8},{8,16},{16,24},{24,32},{32,40},{40,48},{48,56},{56,0},{1,9},... | collective-permute-start | bytes 442376 | tf_op jit(solution)/shard_map/ppermute | solution.py:419
  30.3 6.9 %collective-permute-start.3 = (bf16[144,512]{1,0:T(8,128)(2,1)S(1)}, bf16[144,512]{1,0:T(8,128)(2,1)S(1)}, u32[]{:S(2)}, u32[]{:S(2)}) collective-permute-start(bf16[144,512]{1,0:T(8,128)(2,1)S(1)} %get-tuple-element.40.rest_2_), channel_id=1, source_target_pairs={{0,56},{8,0},{16,8},{24,16},{32,24},{40,32},{48,40},{56,48},{1,57}... | collective-permute-start | bytes 442376 | tf_op jit(solution)/shard_map/ppermute | solution.py:419
  34.3 6.2 %collective-permute-start.9 = (bf16[144,512]{1,0:T(8,128)(2,1)S(1)}, bf16[144,512]{1,0:T(8,128)(2,1)S(1)}, u32[]{:S(2)}, u32[]{:S(2)}) collective-permute-start(bf16[144,512]{1,0:T(8,128)(2,1)S(1)} %get-tuple-element.41.rest_10_), channel_id=1, source_target_pairs={{0,8},{8,16},{16,24},{24,32},{32,40},{40,48},{48,56},{56,0},{1,9},... | collective-permute-start | bytes 442376 | tf_op jit(solution)/shard_map/ppermute | solution.py:419
  34.3 6.2 %collective-permute-start.5 = (bf16[144,512]{1,0:T(8,128)(2,1)S(1)}, bf16[144,512]{1,0:T(8,128)(2,1)S(1)}, u32[]{:S(2)}, u32[]{:S(2)}) collective-permute-start(bf16[144,512]{1,0:T(8,128)(2,1)S(1)} %get-tuple-element.41.rest_10_), channel_id=1, source_target_pairs={{0,56},{8,0},{16,8},{24,16},{32,24},{40,32},{48,40},{56,48},{1,57}... | collective-permute-start | bytes 442376 | tf_op jit(solution)/shard_map/ppermute | solution.py:419
  37.2 6.6 %collective-permute-start.8 = (bf16[144,512]{1,0:T(8,128)(2,1)S(1)}, bf16[144,512]{1,0:T(8,128)(2,1)S(1)}, u32[]{:S(2)}, u32[]{:S(2)}) collective-permute-start(bf16[144,512]{1,0:T(8,128)(2,1)S(1)} %collective-permute-done.7.rest_9_), channel_id=1, source_target_pairs={{0,8},{8,16},{16,24},{24,32},{32,40},{40,48},{48,56},{56,0},{1,9},... | collective-permute-start | bytes 442376 | tf_op jit(solution)/shard_map/ppermute | solution.py:419
  37.2 6.6 %collective-permute-start.4 = (bf16[144,512]{1,0:T(8,128)(2,1)S(1)}, bf16[144,512]{1,0:T(8,128)(2,1)S(1)}, u32[]{:S(2)}, u32[]{:S(2)}) collective-permute-start(bf16[144,512]{1,0:T(8,128)(2,1)S(1)} %collective-permute-done.3.rest_3_), channel_id=1, source_target_pairs={{0,56},{8,0},{16,8},{24,16},{32,24},{40,32},{48,40},{56,48},{1,57}... | collective-permute-start | bytes 442376 | tf_op jit(solution)/shard_map/ppermute | solution.py:419
  40.5 6.5 %collective-permute-start.10 = (bf16[144,512]{1,0:T(8,128)(2,1)S(1)}, bf16[144,512]{1,0:T(8,128)(2,1)S(1)}, u32[]{:S(2)}, u32[]{:S(2)}) collective-permute-start(bf16[144,512]{1,0:T(8,128)(2,1)S(1)} %collective-permute-done.9.rest_17_), channel_id=1, source_target_pairs={{0,8},{8,16},{16,24},{24,32},{32,40},{40,48},{48,56},{56,0},{1,9},... | collective-permute-start | bytes 442376 | tf_op jit(solution)/shard_map/ppermute | solution.py:419
  40.5 6.6 %collective-permute-start.6 = (bf16[144,512]{1,0:T(8,128)(2,1)S(1)}, bf16[144,512]{1,0:T(8,128)(2,1)S(1)}, u32[]{:S(2)}, u32[]{:S(2)}) collective-permute-start(bf16[144,512]{1,0:T(8,128)(2,1)S(1)} %collective-permute-done.5.rest_11_), channel_id=1, source_target_pairs={{0,56},{8,0},{16,8},{24,16},{32,24},{40,32},{48,40},{56,48},{1,57}... | collective-permute-start | bytes 442376 | tf_op jit(solution)/shard_map/ppermute | solution.py:419
  47.1 17.8 %collective-permute-start.11 = (bf16[4,2816,128]{2,1,0:T(8,128)(2,1)}, bf16[4,2816,128]{2,1,0:T(8,128)(2,1)}, u32[]{:S(2)}, u32[]{:S(2)}) collective-permute-start(bf16[4,2816,128]{2,1,0:T(8,128)(2,1)} %all-to-all-done.near.rest_0_), channel_id=1, source_target_pairs={{0,1},{1,0},{2,3},{3,2},{4,5},{5,4},{6,7},{7,6},{8,9},{9,8},{10,11... | collective-permute-start | bytes 8650760 | tf_op jit(solution)/shard_map/ppermute | solution.py:415
  50.0 54.7 %all-to-all-start.1 = ((bf16[8,896,256]{2,1,0:T(8,128)(2,1)}), bf16[8,896,256]{2,1,0:T(8,128)(2,1)}, u32[]{:S(2)}, u32[]{:S(2)}) async-start(bf16[8,896,256]{2,1,0:T(8,128)(2,1)} %copy-done), calls=%async_computation.1 | async-start | bytes 7340032 | tf_op jit(solution)/shard_map/all_to_all | solution.py:518
  54.9 7.3 %collective-permute-start.13 = (bf16[144,512]{1,0:T(8,128)(2,1)S(1)}, bf16[144,512]{1,0:T(8,128)(2,1)S(1)}, u32[]{:S(2)}, u32[]{:S(2)}) collective-permute-start(bf16[144,512]{1,0:T(8,128)(2,1)S(1)} %collective-permute-done.8.rest_8_), channel_id=1, source_target_pairs={{0,8},{8,16},{16,24},{24,32},{32,40},{40,48},{48,56},{56,0},{1,9},... | collective-permute-start | bytes 442376 | tf_op jit(solution)/shard_map/ppermute | solution.py:419
  54.9 7.3 %collective-permute-start.15 = (bf16[144,512]{1,0:T(8,128)(2,1)S(1)}, bf16[144,512]{1,0:T(8,128)(2,1)S(1)}, u32[]{:S(2)}, u32[]{:S(2)}) collective-permute-start(bf16[144,512]{1,0:T(8,128)(2,1)S(1)} %collective-permute-done.6.rest_12_), channel_id=1, source_target_pairs={{0,56},{8,0},{16,8},{24,16},{32,24},{40,32},{48,40},{56,48},{1,57}... | collective-permute-start | bytes 442376 | tf_op jit(solution)/shard_map/ppermute | solution.py:419
  57.9 11.2 %collective-permute-start.12 = (bf16[144,512]{1,0:T(8,128)(2,1)S(1)}, bf16[144,512]{1,0:T(8,128)(2,1)S(1)}, u32[]{:S(2)}, u32[]{:S(2)}) collective-permute-start(bf16[144,512]{1,0:T(8,128)(2,1)S(1)} %collective-permute-done.4.rest_4_), channel_id=1, source_target_pairs={{0,56},{8,0},{16,8},{24,16},{32,24},{40,32},{48,40},{56,48},{1,57}... | collective-permute-start | bytes 442376 | tf_op jit(solution)/shard_map/ppermute | solution.py:419
  59.3 9.7 %collective-permute-start.17 = (bf16[144,512]{1,0:T(8,128)(2,1)S(1)}, bf16[144,512]{1,0:T(8,128)(2,1)S(1)}, u32[]{:S(2)}, u32[]{:S(2)}) collective-permute-start(bf16[144,512]{1,0:T(8,128)(2,1)S(1)} %collective-permute-done.10.rest_16_), channel_id=1, source_target_pairs={{0,8},{8,16},{16,24},{24,32},{32,40},{40,48},{48,56},{56,0},{1,9},... | collective-permute-start | bytes 442376 | tf_op jit(solution)/shard_map/ppermute | solution.py:419
  62.2 6.9 %collective-permute-start.14 = (bf16[144,512]{1,0:T(8,128)(2,1)S(1)}, bf16[144,512]{1,0:T(8,128)(2,1)S(1)}, u32[]{:S(2)}, u32[]{:S(2)}) collective-permute-start(bf16[144,512]{1,0:T(8,128)(2,1)S(1)} %collective-permute-done.13.rest_7_), channel_id=1, source_target_pairs={{0,8},{8,16},{16,24},{24,32},{32,40},{40,48},{48,56},{56,0},{1,9},... | collective-permute-start | bytes 442376 | tf_op jit(solution)/shard_map/ppermute | solution.py:419
  62.2 6.9 %collective-permute-start.16 = (bf16[144,512]{1,0:T(8,128)(2,1)S(1)}, bf16[144,512]{1,0:T(8,128)(2,1)S(1)}, u32[]{:S(2)}, u32[]{:S(2)}) collective-permute-start(bf16[144,512]{1,0:T(8,128)(2,1)S(1)} %collective-permute-done.15.rest_13_), channel_id=1, source_target_pairs={{0,56},{8,0},{16,8},{24,16},{32,24},{40,32},{48,40},{56,48},{1,57}... | collective-permute-start | bytes 442376 | tf_op jit(solution)/shard_map/ppermute | solution.py:419
  83.1 2.9 %collective-permute-start.18 = (bf16[4,272,256]{2,1,0:T(8,128)(2,1)S(1)}, bf16[4,272,256]{2,1,0:T(8,128)(2,1)S(1)}, u32[]{:S(2)}, u32[]{:S(2)}) collective-permute-start(bf16[4,272,256]{2,1,0:T(8,128)(2,1)S(1)} %get-tuple-element.44), channel_id=1, source_target_pairs={{0,1},{1,0},{2,3},{3,2},{4,5},{5,4},{6,7},{7,6},{8,9},{9,8},{10,11... | collective-permute-start | bytes 1671176 | tf_op jit(solution)/shard_map/ppermute | solution.py:415
  86.9 12.7 %collective-permute-start.19 = (bf16[272,256]{1,0:T(8,128)(2,1)S(1)}, bf16[272,256]{1,0:T(8,128)(2,1)S(1)}, u32[]{:S(2)}, u32[]{:S(2)}) collective-permute-start(bf16[272,256]{1,0:T(8,128)(2,1)S(1)} %get-tuple-element.46), channel_id=1, source_target_pairs={{0,2},{2,0},{4,6},{6,4},{1,3},{3,1},{5,7},{7,5},{8,10},{10,8},{12,... | collective-permute-start | bytes 417800 | tf_op jit(solution)/shard_map/ppermute | solution.py:415
  88.0 16.1 %collective-permute-start.20 = (bf16[272,256]{1,0:T(8,128)(2,1)S(1)}, bf16[272,256]{1,0:T(8,128)(2,1)S(1)}, u32[]{:S(2)}, u32[]{:S(2)}) collective-permute-start(bf16[272,256]{1,0:T(8,128)(2,1)S(1)} %get-tuple-element.47), channel_id=1, source_target_pairs={{0,4},{2,6},{4,0},{6,2},{1,5},{3,7},{5,1},{7,3},{8,12},{10,14},{12... | collective-permute-start | bytes 417800 | tf_op jit(solution)/shard_map/ppermute | solution.py:415
  88.0 16.1 %collective-permute-start.21 = (bf16[272,256]{1,0:T(8,128)(2,1)S(1)}, bf16[272,256]{1,0:T(8,128)(2,1)S(1)}, u32[]{:S(2)}, u32[]{:S(2)}) collective-permute-start(bf16[272,256]{1,0:T(8,128)(2,1)S(1)} %get-tuple-element.48), channel_id=1, source_target_pairs={{0,6},{2,4},{4,2},{6,0},{1,7},{3,5},{5,3},{7,1},{8,14},{10,12},{12... | collective-permute-start | bytes 417800 | tf_op jit(solution)/shard_map/ppermute | solution.py:415
  104.7 6.9 %collective-permute-start.24 = (bf16[256,256]{1,0:T(8,128)(2,1)S(1)}, bf16[256,256]{1,0:T(8,128)(2,1)S(1)}, u32[]{:S(2)}, u32[]{:S(2)}) collective-permute-start(bf16[256,256]{1,0:T(8,128)(2,1)S(1)} %heads.1), channel_id=1, source_target_pairs={{0,6},{2,4},{4,2},{6,0},{1,7},{3,5},{5,3},{7,1},{8,14},{10,12},{12... | collective-permute-start | bytes 393224 | tf_op jit(solution)/shard_map/ppermute | solution.py:415
  105.6 5.9 %collective-permute-start.23 = (bf16[256,256]{1,0:T(8,128)(2,1)S(1)}, bf16[256,256]{1,0:T(8,128)(2,1)S(1)}, u32[]{:S(2)}, u32[]{:S(2)}) collective-permute-start(bf16[256,256]{1,0:T(8,128)(2,1)S(1)} %heads.1), channel_id=1, source_target_pairs={{0,4},{2,6},{4,0},{6,2},{1,5},{3,7},{5,1},{7,3},{8,12},{10,14},{12... | collective-permute-start | bytes 393224 | tf_op jit(solution)/shard_map/ppermute | solution.py:415
  106.8 6.5 %collective-permute-start.22 = (bf16[256,256]{1,0:T(8,128)(2,1)S(1)}, bf16[256,256]{1,0:T(8,128)(2,1)S(1)}, u32[]{:S(2)}, u32[]{:S(2)}) collective-permute-start(bf16[256,256]{1,0:T(8,128)(2,1)S(1)} %heads.1), channel_id=1, source_target_pairs={{0,2},{2,0},{4,6},{6,4},{1,3},{3,1},{5,7},{7,5},{8,10},{10,8},{12,... | collective-permute-start | bytes 393224 | tf_op jit(solution)/shard_map/ppermute | solution.py:415
  113.4 3.7 %collective-permute-start.25 = (bf16[4,256,256]{2,1,0:T(8,128)(2,1)S(1)}, bf16[4,256,256]{2,1,0:T(8,128)(2,1)S(1)}, u32[]{:S(2)}, u32[]{:S(2)}) collective-permute-start(bf16[4,256,256]{2,1,0:T(8,128)(2,1)S(1)} %pad_maximum_fusion.near), channel_id=1, source_target_pairs={{0,1},{1,0},{2,3},{3,2},{4,5},{5,4},{6,7},{7,6},{8,9},{9,8},{10,11... | collective-permute-start | bytes 1572872 | tf_op jit(solution)/shard_map/ppermute | solution.py:415

commit v8 on v6

--- a/solution.py
+++ b/solution.py
@@ -306,9 +306,10 @@
 
         return carry
 
-    for load in [load for pair in loads for load in pair]:
-        load.wait()
-    lax.fori_loop(0, NZ, one_step, 0)
+    for lo, hi in ((0, 2), (2, NZ)):
+        for load in [load for pair in loads[lo:hi] for load in pair]:
+            load.wait()
+        lax.fori_loop(lo, hi, one_step, 0)
 
     lane = lax.broadcasted_iota(jnp.int32, (rows, total.shape[2]), 1)
     weights = jnp.zeros(lane.shape, F32)

time: 143 us -> 143 us (level)
  no operation moved by 1% of the time
where the time goes in v8:
time: 143 us; the launch traced here: 142 us
  starting transfers between devices  50.6 us (35%)
  waiting for transfers between devices  35.3 us (25%)
  Pallas kernels  32.4 us (23%)
  blocking collectives  21.1 us (15%)
  local copies, waits for them, and re-layouts  1.77 us (1%)
    ppermute x9, waiting for transfers between devices, sent(): return lax.ppermute(x, axis, [(i, i ^ k) for i in range(size)])  21.4 us
    ppermute x14, starting transfers between devices, shifted(): return lax.ppermute(x, 'z', [(i, (i + k) % NZ) for i in range(NZ)])  21.3 us
    all_to_all x1, blocking collectives, local(): mixed = lax.all_to_all(mixed, 'z', split_axis=0, concat_axis=0, tiled=True)  21.1 us
    pallas_call x1, Pallas kernels, local(): pl.pallas_call(functools.partial(attention_kernel, scale=scale), out_shap...  14.1 us
    ppermute x9, starting transfers between devices, sent(): return lax.ppermute(x, axis, [(i, i ^ k) for i in range(size)])  13.8 us
    ppermute x14, waiting for transfers between devices, shifted(): return lax.ppermute(x, 'z', [(i, (i + k) % NZ) for i in range(NZ)])  7.11 us
    ppermute x3, waiting for transfers between devices, local(): lax.ppermute(packed[k], 'grp', [(i, (i + k) % groups) for i in range(grou...  6.83 us
    ppermute x3, starting transfers between devices, local(): lax.ppermute(packed[k], 'grp', [(i, (i + k) % groups) for i in range(grou...  5.7 us
  transfers between devices with their start and end apart: 28, of which 13 were waited for; matrix products, arithmetic and copies ran while one was open for 0% of the time, Pallas kernels for 16%

profile of v8, /device:TPU:1, one launch (start us, length us, event | category | flops | bytes accessed | tf_op | source)
XLA Modules:
  0.0 142.2 jit_solution(12057307721441706518)
XLA Ops:
  0.1 5.7 %prepare.1 = (s32[41]{0:T(128)S(1)}, bf16[4,2816,128]{2,1,0:T(8,128)(2,1)}, bf16[288,512]{1,0:T(8,128)(2,1)S(1)}, bf16[288,512]{1,0:T(8,128)(2,1)S(1)}, bf16[288...) custom-call(s32[2]{0:T(128)S(1)} %pad_add_fusion.ids, s32[8,64]{1,0:T(8,128)} %bitcast.14, s32[64]{0:T(128)} %refs_1_.1, ...), custom_call_target="tpu_custom_call" | custom-call | tf_op jit(solution)/shard_map/prepare/pallas_call | solution.py:452
  5.8 4.9 %all-to-all-start = ((bf16[4,2816,128]{2,1,0:T(8,128)(2,1)}), bf16[4,2816,128]{2,1,0:T(8,128)(2,1)}, u32[]{:S(2)}, u32[]{:S(2)}) async-start(bf16[4,2816,128]{2,1,0:T(8,128)(2,1)} %get-tuple-element.30), calls=%async_computation | async-start | bytes 5767168 | tf_op jit(solution)/shard_map/all_to_all | solution.py:481
  10.6 2.0 %collective-permute-start = (bf16[288,512]{1,0:T(8,128)(2,1)S(1)}, bf16[288,512]{1,0:T(8,128)(2,1)S(1)}, u32[]{:S(2)}, u32[]{:S(2)}) collective-permute-start(bf16[288,512]{1,0:T(8,128)(2,1)S(1)} %get-tuple-element.32), channel_id=1, source_target_pairs={{0,64},{64,128},{128,192},{192,0},{1,65},{65,129},{129,193},{193,1... | collective-permute-start | bytes 884744 | tf_op jit(solution)/shard_map/ppermute | solution.py:478
  12.6 2.6 %collective-permute-start.1 = (bf16[288,512]{1,0:T(8,128)(2,1)S(1)}, bf16[288,512]{1,0:T(8,128)(2,1)S(1)}, u32[]{:S(2)}, u32[]{:S(2)}) collective-permute-start(bf16[288,512]{1,0:T(8,128)(2,1)S(1)} %get-tuple-element.33), channel_id=1, source_target_pairs={{0,128},{64,192},{128,0},{192,64},{1,129},{65,193},{129,1},{193,65... | collective-permute-start | bytes 884744 | tf_op jit(solution)/shard_map/ppermute | solution.py:478
  16.3 3.0 %columns.1 = bf16[8,896,256]{2,1,0:T(8,128)(2,1)S(1)} custom-call(bf16[256,7168]{1,0:T(8,128)(2,1)} %w_hbm), custom_call_target="tpu_custom_call" | custom-call | tf_op jit(solution)/shard_map/columns/pallas_call | solution.py:484
  19.4 1.8 %copy-done = bf16[8,896,256]{2,1,0:T(8,128)(2,1)} copy-done((bf16[8,896,256]{2,1,0:T(8,128)(2,1)}, bf16[8,896,256]{2,1,0:T(8,128)(2,1)S(1)}, u32[]{:S(2)}) %copy-start) | copy-done | bytes 3670040
  21.2 6.8 %collective-permute-done.1.rest_2_ = bf16[288,512]{1,0:T(8,128)(2,1)S(1)} collective-permute-done((bf16[288,512]{1,0:T(8,128)(2,1)S(1)}, bf16[288,512]{1,0:T(8,128)(2,1)S(1)}, u32[]{:S(2)}, u32[]{:S(2)}) %collective-permute-start.1) | collective-permute-done | bytes 294944 | tf_op jit(solution)/shard_map/ppermute | solution.py:478
  28.6 1.7 %collective-permute-start.7 = (bf16[144,512]{1,0:T(8,128)(2,1)S(1)}, bf16[144,512]{1,0:T(8,128)(2,1)S(1)}, u32[]{:S(2)}, u32[]{:S(2)}) collective-permute-start(bf16[144,512]{1,0:T(8,128)(2,1)S(1)} %get-tuple-element.40.rest_2_), channel_id=1, source_target_pairs={{0,8},{8,16},{16,24},{24,32},{32,40},{40,48},{48,56},{56,0},{1,9},... | collective-permute-start | bytes 442376 | tf_op jit(solution)/shard_map/ppermute | solution.py:419
  30.3 4.0 %collective-permute-start.3 = (bf16[144,512]{1,0:T(8,128)(2,1)S(1)}, bf16[144,512]{1,0:T(8,128)(2,1)S(1)}, u32[]{:S(2)}, u32[]{:S(2)}) collective-permute-start(bf16[144,512]{1,0:T(8,128)(2,1)S(1)} %get-tuple-element.40.rest_2_), channel_id=1, source_target_pairs={{0,56},{8,0},{16,8},{24,16},{32,24},{40,32},{48,40},{56,48},{1,57}... | collective-permute-start | bytes 442376 | tf_op jit(solution)/shard_map/ppermute | solution.py:419
  34.3 2.7 %collective-permute-start.5 = (bf16[144,512]{1,0:T(8,128)(2,1)S(1)}, bf16[144,512]{1,0:T(8,128)(2,1)S(1)}, u32[]{:S(2)}, u32[]{:S(2)}) collective-permute-start(bf16[144,512]{1,0:T(8,128)(2,1)S(1)} %get-tuple-element.41.rest_10_), channel_id=1, source_target_pairs={{0,56},{8,0},{16,8},{24,16},{32,24},{40,32},{48,40},{56,48},{1,57}... | collective-permute-start | bytes 442376 | tf_op jit(solution)/shard_map/ppermute | solution.py:419
  37.2 2.8 %collective-permute-start.4 = (bf16[144,512]{1,0:T(8,128)(2,1)S(1)}, bf16[144,512]{1,0:T(8,128)(2,1)S(1)}, u32[]{:S(2)}, u32[]{:S(2)}) collective-permute-start(bf16[144,512]{1,0:T(8,128)(2,1)S(1)} %collective-permute-done.3.rest_3_), channel_id=1, source_target_pairs={{0,56},{8,0},{16,8},{24,16},{32,24},{40,32},{48,40},{56,48},{1,57}... | collective-permute-start | bytes 442376 | tf_op jit(solution)/shard_map/ppermute | solution.py:419
  40.5 3.0 %collective-permute-start.6 = (bf16[144,512]{1,0:T(8,128)(2,1)S(1)}, bf16[144,512]{1,0:T(8,128)(2,1)S(1)}, u32[]{:S(2)}, u32[]{:S(2)}) collective-permute-start(bf16[144,512]{1,0:T(8,128)(2,1)S(1)} %collective-permute-done.5.rest_11_), channel_id=1, source_target_pairs={{0,56},{8,0},{16,8},{24,16},{32,24},{40,32},{48,40},{56,48},{1,57}... | collective-permute-start | bytes 442376 | tf_op jit(solution)/shard_map/ppermute | solution.py:419
  43.8 3.2 %collective-permute-done.10.rest_16_ = bf16[144,512]{1,0:T(8,128)(2,1)S(1)} collective-permute-done((bf16[144,512]{1,0:T(8,128)(2,1)S(1)}, bf16[144,512]{1,0:T(8,128)(2,1)S(1)}, u32[]{:S(2)}, u32[]{:S(2)}) %collective-permute-start.10) | collective-permute-done | bytes 147488 | tf_op jit(solution)/shard_map/ppermute | solution.py:419
  47.1 2.9 %collective-permute-start.11 = (bf16[4,2816,128]{2,1,0:T(8,128)(2,1)}, bf16[4,2816,128]{2,1,0:T(8,128)(2,1)}, u32[]{:S(2)}, u32[]{:S(2)}) collective-permute-start(bf16[4,2816,128]{2,1,0:T(8,128)(2,1)} %all-to-all-done.near.rest_0_), channel_id=1, source_target_pairs={{0,1},{1,0},{2,3},{3,2},{4,5},{5,4},{6,7},{7,6},{8,9},{9,8},{10,11... | collective-permute-start | bytes 8650760 | tf_op jit(solution)/shard_map/ppermute | solution.py:415
  50.0 4.9 %all-to-all-start.1 = ((bf16[8,896,256]{2,1,0:T(8,128)(2,1)}), bf16[8,896,256]{2,1,0:T(8,128)(2,1)}, u32[]{:S(2)}, u32[]{:S(2)}) async-start(bf16[8,896,256]{2,1,0:T(8,128)(2,1)} %copy-done), calls=%async_computation.1 | async-start | bytes 7340032 | tf_op jit(solution)/shard_map/all_to_all | solution.py:518
  54.9 3.0 %collective-permute-start.15 = (bf16[144,512]{1,0:T(8,128)(2,1)S(1)}, bf16[144,512]{1,0:T(8,128)(2,1)S(1)}, u32[]{:S(2)}, u32[]{:S(2)}) collective-permute-start(bf16[144,512]{1,0:T(8,128)(2,1)S(1)} %collective-permute-done.6.rest_12_), channel_id=1, source_target_pairs={{0,56},{8,0},{16,8},{24,16},{32,24},{40,32},{48,40},{56,48},{1,57}... | collective-permute-start | bytes 442376 | tf_op jit(solution)/shard_map/ppermute | solution.py:419
  57.9 1.4 %collective-permute-start.12 = (bf16[144,512]{1,0:T(8,128)(2,1)S(1)}, bf16[144,512]{1,0:T(8,128)(2,1)S(1)}, u32[]{:S(2)}, u32[]{:S(2)}) collective-permute-start(bf16[144,512]{1,0:T(8,128)(2,1)S(1)} %collective-permute-done.4.rest_4_), channel_id=1, source_target_pairs={{0,56},{8,0},{16,8},{24,16},{32,24},{40,32},{48,40},{56,48},{1,57}... | collective-permute-start | bytes 442376 | tf_op jit(solution)/shard_map/ppermute | solution.py:419
  59.3 2.8 %collective-permute-done.13.rest_7_ = bf16[144,512]{1,0:T(8,128)(2,1)S(1)} collective-permute-done((bf16[144,512]{1,0:T(8,128)(2,1)S(1)}, bf16[144,512]{1,0:T(8,128)(2,1)S(1)}, u32[]{:S(2)}, u32[]{:S(2)}) %collective-permute-start.13) | collective-permute-done | bytes 147488 | tf_op jit(solution)/shard_map/ppermute | solution.py:419
  62.2 2.7 %collective-permute-start.16 = (bf16[144,512]{1,0:T(8,128)(2,1)S(1)}, bf16[144,512]{1,0:T(8,128)(2,1)S(1)}, u32[]{:S(2)}, u32[]{:S(2)}) collective-permute-start(bf16[144,512]{1,0:T(8,128)(2,1)S(1)} %collective-permute-done.15.rest_13_), channel_id=1, source_target_pairs={{0,56},{8,0},{16,8},{24,16},{32,24},{40,32},{48,40},{56,48},{1,57}... | collective-permute-start | bytes 442376 | tf_op jit(solution)/shard_map/ppermute | solution.py:419
  64.9 4.2 %query.1 = bf16[8,512,640]{2,1,0:T(8,128)(2,1)S(1)} custom-call(s32[41]{0:T(128)S(1)} %get-tuple-element.29.meta, bf16[4,2816,128]{2,1,0:T(8,128)(2,1)} %all-to-all-done.near.rest_0_, bf16[4,2816,128]{2,1,0:T(8,128)(2,1)} %collective-permute-done.11.far.rest_1_), custom_call_target="tpu_custom_call" | custom-call | tf_op jit(solution)/shard_map/query/pallas_call | solution.py:520
  69.1 14.1 %attention.1 = (bf16[4,272,256]{2,1,0:T(8,128)(2,1)S(1)}, bf16[4,272,256]{2,1,0:T(8,128)(2,1)S(1)}) custom-call(s32[41]{0:T(128)S(1)} %get-tuple-element.29.meta, bf16[8,512,640]{2,1,0:T(8,128)(2,1)S(1)} %query.1, bf16[4,2816,128]{2,1,0:T(8,128)(2,1)} %all-to-all-done.near.rest_0_, bf16[4,2816,128]{2,1,0:T(8,128)(2,1)} %collective-permute-done.11.far.rest_1_, ...), custom_call_target="tpu_custom_call" | custom-call | tf_op jit(solution)/shard_map/attention/pallas_call | solution.py:534
  83.1 1.5 %collective-permute-start.18 = (bf16[4,272,256]{2,1,0:T(8,128)(2,1)S(1)}, bf16[4,272,256]{2,1,0:T(8,128)(2,1)S(1)}, u32[]{:S(2)}, u32[]{:S(2)}) collective-permute-start(bf16[4,272,256]{2,1,0:T(8,128)(2,1)S(1)} %get-tuple-element.44), channel_id=1, source_target_pairs={{0,1},{1,0},{2,3},{3,2},{4,5},{5,4},{6,7},{7,6},{8,9},{9,8},{10,11... | collective-permute-start | bytes 1671176 | tf_op jit(solution)/shard_map/ppermute | solution.py:415
  84.7 1.6 %collective-permute-done.18.got = bf16[4,272,256]{2,1,0:T(8,128)(2,1)S(1)} collective-permute-done((bf16[4,272,256]{2,1,0:T(8,128)(2,1)S(1)}, bf16[4,272,256]{2,1,0:T(8,128)(2,1)S(1)}, u32[]{:S(2)}, u32[]{:S(2)}) %collective-permute-start.18) | collective-permute-done | bytes 557088 | tf_op jit(solution)/shard_map/ppermute | solution.py:415
  88.2 2.9 %collective-permute-start.21 = (bf16[272,256]{1,0:T(8,128)(2,1)S(1)}, bf16[272,256]{1,0:T(8,128)(2,1)S(1)}, u32[]{:S(2)}, u32[]{:S(2)}) collective-permute-start(bf16[272,256]{1,0:T(8,128)(2,1)S(1)} %get-tuple-element.48), channel_id=1, source_target_pairs={{0,6},{2,4},{4,2},{6,0},{1,7},{3,5},{5,3},{7,1},{8,14},{10,12},{12... | collective-permute-start | bytes 417800 | tf_op jit(solution)/shard_map/ppermute | solution.py:415
  91.1 8.5 %collective-permute-done.19.refs_1_ = bf16[272,256]{1,0:T(8,128)(2,1)S(1)} collective-permute-done((bf16[272,256]{1,0:T(8,128)(2,1)S(1)}, bf16[272,256]{1,0:T(8,128)(2,1)S(1)}, u32[]{:S(2)}, u32[]{:S(2)}) %collective-permute-start.19) | collective-permute-done | bytes 139296 | tf_op jit(solution)/shard_map/ppermute | solution.py:415
  99.6 4.5 %collective-permute-done.20.refs_2_ = bf16[272,256]{1,0:T(8,128)(2,1)S(1)} collective-permute-done((bf16[272,256]{1,0:T(8,128)(2,1)S(1)}, bf16[272,256]{1,0:T(8,128)(2,1)S(1)}, u32[]{:S(2)}, u32[]{:S(2)}) %collective-permute-start.20) | collective-permute-done | bytes 139296 | tf_op jit(solution)/shard_map/ppermute | solution.py:415
  108.0 3.6 %collective-permute-done.24 = bf16[256,256]{1,0:T(8,128)(2,1)S(1)} collective-permute-done((bf16[256,256]{1,0:T(8,128)(2,1)S(1)}, bf16[256,256]{1,0:T(8,128)(2,1)S(1)}, u32[]{:S(2)}, u32[]{:S(2)}) %collective-permute-start.24) | collective-permute-done | bytes 131104 | tf_op jit(solution)/shard_map/ppermute | solution.py:415
  111.6 1.7 %collective-permute-done.22 = bf16[256,256]{1,0:T(8,128)(2,1)S(1)} collective-permute-done((bf16[256,256]{1,0:T(8,128)(2,1)S(1)}, bf16[256,256]{1,0:T(8,128)(2,1)S(1)}, u32[]{:S(2)}, u32[]{:S(2)}) %collective-permute-start.22) | collective-permute-done | bytes 131104 | tf_op jit(solution)/shard_map/ppermute | solution.py:415
  113.4 2.1 %collective-permute-start.25 = (bf16[4,256,256]{2,1,0:T(8,128)(2,1)S(1)}, bf16[4,256,256]{2,1,0:T(8,128)(2,1)S(1)}, u32[]{:S(2)}, u32[]{:S(2)}) collective-permute-start(bf16[4,256,256]{2,1,0:T(8,128)(2,1)S(1)} %pad_maximum_fusion.near), channel_id=1, source_target_pairs={{0,1},{1,0},{2,3},{3,2},{4,5},{5,4},{6,7},{7,6},{8,9},{9,8},{10,11... | collective-permute-start | bytes 1572872 | tf_op jit(solution)/shard_map/ppermute | solution.py:415
  115.5 1.5 %collective-permute-done.25.far = bf16[4,256,256]{2,1,0:T(8,128)(2,1)S(1)} collective-permute-done((bf16[4,256,256]{2,1,0:T(8,128)(2,1)S(1)}, bf16[4,256,256]{2,1,0:T(8,128)(2,1)S(1)}, u32[]{:S(2)}, u32[]{:S(2)}) %collective-permute-start.25) | collective-permute-done | bytes 524320 | tf_op jit(solution)/shard_map/ppermute | solution.py:415
  117.0 3.5 %output.1 = bf16[896,256]{1,0:T(8,128)(2,1)S(1)} custom-call(s32[41]{0:T(128)S(1)} %get-tuple-element.29.meta, bf16[8,896,256]{2,1,0:T(8,128)(2,1)} %all-to-all-done.1.weights, bf16[4,256,256]{2,1,0:T(8,128)(2,1)S(1)} %pad_maximum_fusion.near, bf16[4,256,256]{2,1,0:T(8,128)(2,1)S(1)} %collective-permute-done.25.far), custom_call_target="tpu_custom_call" | custom-call | tf_op jit(solution)/shard_map/output/pallas_call | solution.py:573
  120.5 21.1 %all_to_all.19 = bf16[8,112,256]{2,1,0:T(8,128)(2,1)S(1)} all-to-all(bf16[8,112,256]{2,1,0:T(8,128)(2,1)S(1)} %bitcast.9), channel_id=1, replica_groups=mesh['grp'=4,'z'=8,'x'=4,'c'=2] {'z'}, dimensions={0} | all-to-all | bytes 917504 | tf_op jit(solution)/shard_map/all_to_all | solution.py:581
  (38 shorter events, 9.5 us)
Async XLA Ops:
  5.8 41.3 %all-to-all-start = ((bf16[4,2816,128]{2,1,0:T(8,128)(2,1)}), bf16[4,2816,128]{2,1,0:T(8,128)(2,1)}, u32[]{:S(2)}, u32[]{:S(2)}) async-start(bf16[4,2816,128]{2,1,0:T(8,128)(2,1)} %get-tuple-element.30), calls=%async_computation | async-start | bytes 5767168 | tf_op jit(solution)/shard_map/all_to_all | solution.py:481
  10.6 10.5 %collective-permute-start = (bf16[288,512]{1,0:T(8,128)(2,1)S(1)}, bf16[288,512]{1,0:T(8,128)(2,1)S(1)}, u32[]{:S(2)}, u32[]{:S(2)}) collective-permute-start(bf16[288,512]{1,0:T(8,128)(2,1)S(1)} %get-tuple-element.32), channel_id=1, source_target_pairs={{0,64},{64,128},{128,192},{192,0},{1,65},{65,129},{129,193},{193,1... | collective-permute-start | bytes 884744 | tf_op jit(solution)/shard_map/ppermute | solution.py:478
  12.6 15.4 %collective-permute-start.1 = (bf16[288,512]{1,0:T(8,128)(2,1)S(1)}, bf16[288,512]{1,0:T(8,128)(2,1)S(1)}, u32[]{:S(2)}, u32[]{:S(2)}) collective-permute-start(bf16[288,512]{1,0:T(8,128)(2,1)S(1)} %get-tuple-element.33), channel_id=1, source_target_pairs={{0,128},{64,192},{128,0},{192,64},{1,129},{65,193},{129,1},{193,65... | collective-permute-start | bytes 884744 | tf_op jit(solution)/shard_map/ppermute | solution.py:478
  15.3 12.7 %collective-permute-start.2 = (bf16[288,512]{1,0:T(8,128)(2,1)S(1)}, bf16[288,512]{1,0:T(8,128)(2,1)S(1)}, u32[]{:S(2)}, u32[]{:S(2)}) collective-permute-start(bf16[288,512]{1,0:T(8,128)(2,1)S(1)} %get-tuple-element.34), channel_id=1, source_target_pairs={{0,192},{64,0},{128,64},{192,128},{1,193},{65,1},{129,65},{193,129... | collective-permute-start | bytes 884744 | tf_op jit(solution)/shard_map/ppermute | solution.py:478
  19.4 1.8 %copy-start = (bf16[8,896,256]{2,1,0:T(8,128)(2,1)}, bf16[8,896,256]{2,1,0:T(8,128)(2,1)S(1)}, u32[]{:S(2)}) copy-start(bf16[8,896,256]{2,1,0:T(8,128)(2,1)S(1)} %columns.1) | copy-start | bytes 11010052
  28.6 8.6 %collective-permute-start.7 = (bf16[144,512]{1,0:T(8,128)(2,1)S(1)}, bf16[144,512]{1,0:T(8,128)(2,1)S(1)}, u32[]{:S(2)}, u32[]{:S(2)}) collective-permute-start(bf16[144,512]{1,0:T(8,128)(2,1)S(1)} %get-tuple-element.40.rest_2_), channel_id=1, source_target_pairs={{0,8},{8,16},{16,24},{24,32},{32,40},{40,48},{48,56},{56,0},{1,9},... | collective-permute-start | bytes 442376 | tf_op jit(solution)/shard_map/ppermute | solution.py:419
  30.3 6.9 %collective-permute-start.3 = (bf16[144,512]{1,0:T(8,128)(2,1)S(1)}, bf16[144,512]{1,0:T(8,128)(2,1)S(1)}, u32[]{:S(2)}, u32[]{:S(2)}) collective-permute-start(bf16[144,512]{1,0:T(8,128)(2,1)S(1)} %get-tuple-element.40.rest_2_), channel_id=1, source_target_pairs={{0,56},{8,0},{16,8},{24,16},{32,24},{40,32},{48,40},{56,48},{1,57}... | collective-permute-start | bytes 442376 | tf_op jit(solution)/shard_map/ppermute | solution.py:419
  34.3 6.2 %collective-permute-start.9 = (bf16[144,512]{1,0:T(8,128)(2,1)S(1)}, bf16[144,512]{1,0:T(8,128)(2,1)S(1)}, u32[]{:S(2)}, u32[]{:S(2)}) collective-permute-start(bf16[144,512]{1,0:T(8,128)(2,1)S(1)} %get-tuple-element.41.rest_10_), channel_id=1, source_target_pairs={{0,8},{8,16},{16,24},{24,32},{32,40},{40,48},{48,56},{56,0},{1,9},... | collective-permute-start | bytes 442376 | tf_op jit(solution)/shard_map/ppermute | solution.py:419
  34.3 6.2 %collective-permute-start.5 = (bf16[144,512]{1,0:T(8,128)(2,1)S(1)}, bf16[144,512]{1,0:T(8,128)(2,1)S(1)}, u32[]{:S(2)}, u32[]{:S(2)}) collective-permute-start(bf16[144,512]{1,0:T(8,128)(2,1)S(1)} %get-tuple-element.41.rest_10_), channel_id=1, source_target_pairs={{0,56},{8,0},{16,8},{24,16},{32,24},{40,32},{48,40},{56,48},{1,57}... | collective-permute-start | bytes 442376 | tf_op jit(solution)/shard_map/ppermute | solution.py:419
  37.2 6.6 %collective-permute-start.8 = (bf16[144,512]{1,0:T(8,128)(2,1)S(1)}, bf16[144,512]{1,0:T(8,128)(2,1)S(1)}, u32[]{:S(2)}, u32[]{:S(2)}) collective-permute-start(bf16[144,512]{1,0:T(8,128)(2,1)S(1)} %collective-permute-done.7.rest_9_), channel_id=1, source_target_pairs={{0,8},{8,16},{16,24},{24,32},{32,40},{40,48},{48,56},{56,0},{1,9},... | collective-permute-start | bytes 442376 | tf_op jit(solution)/shard_map/ppermute | solution.py:419
  37.2 6.6 %collective-permute-start.4 = (bf16[144,512]{1,0:T(8,128)(2,1)S(1)}, bf16[144,512]{1,0:T(8,128)(2,1)S(1)}, u32[]{:S(2)}, u32[]{:S(2)}) collective-permute-start(bf16[144,512]{1,0:T(8,128)(2,1)S(1)} %collective-permute-done.3.rest_3_), channel_id=1, source_target_pairs={{0,56},{8,0},{16,8},{24,16},{32,24},{40,32},{48,40},{56,48},{1,57}... | collective-permute-start | bytes 442376 | tf_op jit(solution)/shard_map/ppermute | solution.py:419
  40.5 6.5 %collective-permute-start.10 = (bf16[144,512]{1,0:T(8,128)(2,1)S(1)}, bf16[144,512]{1,0:T(8,128)(2,1)S(1)}, u32[]{:S(2)}, u32[]{:S(2)}) collective-permute-start(bf16[144,512]{1,0:T(8,128)(2,1)S(1)} %collective-permute-done.9.rest_17_), channel_id=1, source_target_pairs={{0,8},{8,16},{16,24},{24,32},{32,40},{40,48},{48,56},{56,0},{1,9},... | collective-permute-start | bytes 442376 | tf_op jit(solution)/shard_map/ppermute | solution.py:419
  40.5 6.6 %collective-permute-start.6 = (bf16[144,512]{1,0:T(8,128)(2,1)S(1)}, bf16[144,512]{1,0:T(8,128)(2,1)S(1)}, u32[]{:S(2)}, u32[]{:S(2)}) collective-permute-start(bf16[144,512]{1,0:T(8,128)(2,1)S(1)} %collective-permute-done.5.rest_11_), channel_id=1, source_target_pairs={{0,56},{8,0},{16,8},{24,16},{32,24},{40,32},{48,40},{56,48},{1,57}... | collective-permute-start | bytes 442376 | tf_op jit(solution)/shard_map/ppermute | solution.py:419
  47.1 17.8 %collective-permute-start.11 = (bf16[4,2816,128]{2,1,0:T(8,128)(2,1)}, bf16[4,2816,128]{2,1,0:T(8,128)(2,1)}, u32[]{:S(2)}, u32[]{:S(2)}) collective-permute-start(bf16[4,2816,128]{2,1,0:T(8,128)(2,1)} %all-to-all-done.near.rest_0_), channel_id=1, source_target_pairs={{0,1},{1,0},{2,3},{3,2},{4,5},{5,4},{6,7},{7,6},{8,9},{9,8},{10,11... | collective-permute-start | bytes 8650760 | tf_op jit(solution)/shard_map/ppermute | solution.py:415
  50.0 54.7 %all-to-all-start.1 = ((bf16[8,896,256]{2,1,0:T(8,128)(2,1)}), bf16[8,896,256]{2,1,0:T(8,128)(2,1)}, u32[]{:S(2)}, u32[]{:S(2)}) async-start(bf16[8,896,256]{2,1,0:T(8,128)(2,1)} %copy-done), calls=%async_computation.1 | async-start | bytes 7340032 | tf_op jit(solution)/shard_map/all_to_all | solution.py:518
  54.9 7.3 %collective-permute-start.13 = (bf16[144,512]{1,0:T(8,128)(2,1)S(1)}, bf16[144,512]{1,0:T(8,128)(2,1)S(1)}, u32[]{:S(2)}, u32[]{:S(2)}) collective-permute-start(bf16[144,512]{1,0:T(8,128)(2,1)S(1)} %collective-permute-done.8.rest_8_), channel_id=1, source_target_pairs={{0,8},{8,16},{16,24},{24,32},{32,40},{40,48},{48,56},{56,0},{1,9},... | collective-permute-start | bytes 442376 | tf_op jit(solution)/shard_map/ppermute | solution.py:419
  54.9 7.3 %collective-permute-start.15 = (bf16[144,512]{1,0:T(8,128)(2,1)S(1)}, bf16[144,512]{1,0:T(8,128)(2,1)S(1)}, u32[]{:S(2)}, u32[]{:S(2)}) collective-permute-start(bf16[144,512]{1,0:T(8,128)(2,1)S(1)} %collective-permute-done.6.rest_12_), channel_id=1, source_target_pairs={{0,56},{8,0},{16,8},{24,16},{32,24},{40,32},{48,40},{56,48},{1,57}... | collective-permute-start | bytes 442376 | tf_op jit(solution)/shard_map/ppermute | solution.py:419
  57.9 11.2 %collective-permute-start.12 = (bf16[144,512]{1,0:T(8,128)(2,1)S(1)}, bf16[144,512]{1,0:T(8,128)(2,1)S(1)}, u32[]{:S(2)}, u32[]{:S(2)}) collective-permute-start(bf16[144,512]{1,0:T(8,128)(2,1)S(1)} %collective-permute-done.4.rest_4_), channel_id=1, source_target_pairs={{0,56},{8,0},{16,8},{24,16},{32,24},{40,32},{48,40},{56,48},{1,57}... | collective-permute-start | bytes 442376 | tf_op jit(solution)/shard_map/ppermute | solution.py:419
  59.3 9.7 %collective-permute-start.17 = (bf16[144,512]{1,0:T(8,128)(2,1)S(1)}, bf16[144,512]{1,0:T(8,128)(2,1)S(1)}, u32[]{:S(2)}, u32[]{:S(2)}) collective-permute-start(bf16[144,512]{1,0:T(8,128)(2,1)S(1)} %collective-permute-done.10.rest_16_), channel_id=1, source_target_pairs={{0,8},{8,16},{16,24},{24,32},{32,40},{40,48},{48,56},{56,0},{1,9},... | collective-permute-start | bytes 442376 | tf_op jit(solution)/shard_map/ppermute | solution.py:419
  62.2 6.9 %collective-permute-start.14 = (bf16[144,512]{1,0:T(8,128)(2,1)S(1)}, bf16[144,512]{1,0:T(8,128)(2,1)S(1)}, u32[]{:S(2)}, u32[]{:S(2)}) collective-permute-start(bf16[144,512]{1,0:T(8,128)(2,1)S(1)} %collective-permute-done.13.rest_7_), channel_id=1, source_target_pairs={{0,8},{8,16},{16,24},{24,32},{32,40},{40,48},{48,56},{56,0},{1,9},... | collective-permute-start | bytes 442376 | tf_op jit(solution)/shard_map/ppermute | solution.py:419
  62.2 6.9 %collective-permute-start.16 = (bf16[144,512]{1,0:T(8,128)(2,1)S(1)}, bf16[144,512]{1,0:T(8,128)(2,1)S(1)}, u32[]{:S(2)}, u32[]{:S(2)}) collective-permute-start(bf16[144,512]{1,0:T(8,128)(2,1)S(1)} %collective-permute-done.15.rest_13_), channel_id=1, source_target_pairs={{0,56},{8,0},{16,8},{24,16},{32,24},{40,32},{48,40},{56,48},{1,57}... | collective-permute-start | bytes 442376 | tf_op jit(solution)/shard_map/ppermute | solution.py:419
  83.1 3.1 %collective-permute-start.18 = (bf16[4,272,256]{2,1,0:T(8,128)(2,1)S(1)}, bf16[4,272,256]{2,1,0:T(8,128)(2,1)S(1)}, u32[]{:S(2)}, u32[]{:S(2)}) collective-permute-start(bf16[4,272,256]{2,1,0:T(8,128)(2,1)S(1)} %get-tuple-element.44), channel_id=1, source_target_pairs={{0,1},{1,0},{2,3},{3,2},{4,5},{5,4},{6,7},{7,6},{8,9},{9,8},{10,11... | collective-permute-start | bytes 1671176 | tf_op jit(solution)/shard_map/ppermute | solution.py:415
  87.1 12.5 %collective-permute-start.19 = (bf16[272,256]{1,0:T(8,128)(2,1)S(1)}, bf16[272,256]{1,0:T(8,128)(2,1)S(1)}, u32[]{:S(2)}, u32[]{:S(2)}) collective-permute-start(bf16[272,256]{1,0:T(8,128)(2,1)S(1)} %get-tuple-element.46), channel_id=1, source_target_pairs={{0,2},{2,0},{4,6},{6,4},{1,3},{3,1},{5,7},{7,5},{8,10},{10,8},{12,... | collective-permute-start | bytes 417800 | tf_op jit(solution)/shard_map/ppermute | solution.py:415
  88.2 15.9 %collective-permute-start.20 = (bf16[272,256]{1,0:T(8,128)(2,1)S(1)}, bf16[272,256]{1,0:T(8,128)(2,1)S(1)}, u32[]{:S(2)}, u32[]{:S(2)}) collective-permute-start(bf16[272,256]{1,0:T(8,128)(2,1)S(1)} %get-tuple-element.47), channel_id=1, source_target_pairs={{0,4},{2,6},{4,0},{6,2},{1,5},{3,7},{5,1},{7,3},{8,12},{10,14},{12... | collective-permute-start | bytes 417800 | tf_op jit(solution)/shard_map/ppermute | solution.py:415
  88.2 15.9 %collective-permute-start.21 = (bf16[272,256]{1,0:T(8,128)(2,1)S(1)}, bf16[272,256]{1,0:T(8,128)(2,1)S(1)}, u32[]{:S(2)}, u32[]{:S(2)}) collective-permute-start(bf16[272,256]{1,0:T(8,128)(2,1)S(1)} %get-tuple-element.48), channel_id=1, source_target_pairs={{0,6},{2,4},{4,2},{6,0},{1,7},{3,5},{5,3},{7,1},{8,14},{10,12},{12... | collective-permute-start | bytes 417800 | tf_op jit(solution)/shard_map/ppermute | solution.py:415
  104.7 6.9 %collective-permute-start.24 = (bf16[256,256]{1,0:T(8,128)(2,1)S(1)}, bf16[256,256]{1,0:T(8,128)(2,1)S(1)}, u32[]{:S(2)}, u32[]{:S(2)}) collective-permute-start(bf16[256,256]{1,0:T(8,128)(2,1)S(1)} %heads.1), channel_id=1, source_target_pairs={{0,6},{2,4},{4,2},{6,0},{1,7},{3,5},{5,3},{7,1},{8,14},{10,12},{12... | collective-permute-start | bytes 393224 | tf_op jit(solution)/shard_map/ppermute | solution.py:415
  105.6 5.9 %collective-permute-start.23 = (bf16[256,256]{1,0:T(8,128)(2,1)S(1)}, bf16[256,256]{1,0:T(8,128)(2,1)S(1)}, u32[]{:S(2)}, u32[]{:S(2)}) collective-permute-start(bf16[256,256]{1,0:T(8,128)(2,1)S(1)} %heads.1), channel_id=1, source_target_pairs={{0,4},{2,6},{4,0},{6,2},{1,5},{3,7},{5,1},{7,3},{8,12},{10,14},{12... | collective-permute-start | bytes 393224 | tf_op jit(solution)/shard_map/ppermute | solution.py:415
  106.8 6.5 %collective-permute-start.22 = (bf16[256,256]{1,0:T(8,128)(2,1)S(1)}, bf16[256,256]{1,0:T(8,128)(2,1)S(1)}, u32[]{:S(2)}, u32[]{:S(2)}) collective-permute-start(bf16[256,256]{1,0:T(8,128)(2,1)S(1)} %heads.1), channel_id=1, source_target_pairs={{0,2},{2,0},{4,6},{6,4},{1,3},{3,1},{5,7},{7,5},{8,10},{10,8},{12,... | collective-permute-start | bytes 393224 | tf_op jit(solution)/shard_map/ppermute | solution.py:415
  113.4 3.7 %collective-permute-start.25 = (bf16[4,256,256]{2,1,0:T(8,128)(2,1)S(1)}, bf16[4,256,256]{2,1,0:T(8,128)(2,1)S(1)}, u32[]{:S(2)}, u32[]{:S(2)}) collective-permute-start(bf16[4,256,256]{2,1,0:T(8,128)(2,1)S(1)} %pad_maximum_fusion.near), channel_id=1, source_target_pairs={{0,1},{1,0},{2,3},{3,2},{4,5},{5,4},{6,7},{7,6},{8,9},{9,8},{10,11... | collective-permute-start | bytes 1572872 | tf_op jit(solution)/shard_map/ppermute | solution.py:415
